TPU v7x, 256 devices: a whole 4x4x8 slice. The times are simulated.
256 devices in a mesh: seq: 32 (over z, x), head: 8 (over y, core).
Axes of the slice: x: 4, y: 4, z: 8, core: 2. Of those that a mesh axis runs over, the one named last changes fastest.
Arguments:
- tokens: bfloat16 [8192, 2560], P(('seq', 'head')), may hold values from -6 to 6
- w_xz: bfloat16 [2560, 2, 5120], P(None, None, 'head'), may hold values from -0.125 to 0.125
- w_bc: bfloat16 [2560, 256], replicated, may hold values from -0.125 to 0.125
- w_dt: bfloat16 [2560, 80], P(None, 'head'), may hold values from -0.125 to 0.125
- dt_bias: float32 [80], P('head'), may hold values from -2 to 1
- a_log: float32 [80], P('head'), may hold values from -16 to 0
- conv_x: bfloat16 [4, 5120], P(None, 'head'), may hold values from -3 to 3
- conv_bc: bfloat16 [4, 256], replicated, may hold values from -3 to 3
- norm_gain: float32 [5120], P('head'), may hold values from 0.5 to 1.5
- w_out: bfloat16 [5120, 2560], P('head'), may hold values from -0.078125 to 0.078125
Outputs:
- layer_out: bfloat16 [8192, 2560], P(('seq', 'head'))
All inputs are finite; a program needn't handle non-finite values.
Results may differ from a plain program's by a relative error of at most 0.02.
Values may be sent and summed in bfloat16 or wider, within the bound.
No kernel may reach another device: no remote copies, remote signals or barrier semaphores. Data moves between devices by JAX's collectives and lax.ppermute only.
A program may use at most 64 MiB of HBM per device.

v0:
```python
import jax
import jax.numpy as jnp
from jax import lax
from jax.sharding import Mesh
from jax.sharding import PartitionSpec as P

SPAN = 256
DI = 5120
SEQ = ("seq_0", "seq_1")
SEQ_HEAD = ("seq_0", "seq_1", "head")


def in_order(pieces, dim):
    pieces = jnp.moveaxis(pieces, 0, dim)
    shape = pieces.shape
    return pieces.reshape(*shape[:dim], shape[dim] * shape[dim + 1], *shape[dim + 2 :])


def sent_to_all(value, axis):
    size = lax.axis_size(axis)
    return lax.all_to_all(
        jnp.broadcast_to(value[None], (size, *value.shape)), axis, 0, 0, tiled=True
    )


def collect(value, axis, dim):
    return in_order(sent_to_all(value, axis), dim)


def passed_along(value, axis, steps):
    count = lax.axis_size(axis)
    leading, last = (max(0, -steps), min(count, count - steps))
    return lax.ppermute(value, axis, [(source, source + steps) for source in range(leading, last)])


def neutral_like(value, identity):
    return jax.tree.map(
        lambda a, e: jnp.broadcast_to(jnp.asarray(e, a.dtype), a.shape), value, identity
    )


def carried_in(value, axes, combine, identity):
    before = start = neutral_like(value, identity)
    so_far = value
    for axis in reversed(axes):
        size, here = (lax.axis_size(axis), lax.axis_index(axis))
        pieces = jax.tree.map(
            lambda part, kind: lax.all_gather(part.astype(kind), axis),
            so_far,
            (jnp.bfloat16, jnp.bfloat16),
        )
        inside, so_far = (start, start)
        for k in range(size):
            passed = k < here
            so_far = combine(
                so_far, jax.tree.map(lambda part, own: part[k].astype(own.dtype), pieces, value)
            )
            inside = jax.tree.map(lambda new, old: jnp.where(passed, new, old), so_far, inside)
        before = combine(inside, before)
    return before


def taken_together(value, axis):
    everything = sent_to_all(value, axis)
    return jnp.sum(everything, axis=0)


def split_up(value, dim, size):
    shape = value.shape
    pieces = value.reshape(*shape[:dim], size, shape[dim] // size, *shape[dim + 1 :])
    return jnp.moveaxis(pieces, dim, 0)


def sum_at_owner(value, axis, dim):
    size = lax.axis_size(axis)
    pieces = lax.all_to_all(split_up(value, dim, size), axis, 0, 0, tiled=True)
    return jnp.sum(pieces.astype(jnp.float32), axis=0)


def causal_mix(values, tail_rows, kernel):
    kernel_size = kernel.shape[0]
    row_count = values.shape[0]
    padded = jnp.concatenate([tail_rows, values], axis=0)
    summed = jnp.zeros(values.shape, jnp.float32)
    for offset in range(kernel_size):
        summed = summed + kernel[offset].astype(jnp.float32) * padded[
            offset : offset + row_count
        ].astype(jnp.float32)
    return jax.nn.silu(summed).astype(jnp.bfloat16)


def span_update(carried, inputs):
    value_block, b_block, c_block, step_block, decay_block = inputs
    block_len = value_block.shape[0]
    cumulative = jnp.cumsum(decay_block, axis=0)
    cum_heads = cumulative.T
    differ = cum_heads[:, :, None] - cum_heads[:, None, :]
    causal_mask = (jnp.arange(block_len)[:, None] >= jnp.arange(block_len)[None, :])[None]
    scores = jnp.dot(c_block, b_block.T, preferred_element_type=jnp.float32)
    weights = jnp.where(causal_mask, jnp.exp(jnp.where(causal_mask, differ, 0.0)), 0.0)
    weights = (weights * scores[None] * step_block.T[:, None, :]).astype(jnp.bfloat16)
    start_state = carried.astype(jnp.bfloat16)
    inside = jnp.einsum("hts,shp->thp", weights, value_block, preferred_element_type=jnp.float32)
    carried_out = jnp.exp(cumulative)[:, :, None] * jnp.einsum(
        "tn,hpn->thp", c_block, start_state, preferred_element_type=jnp.float32
    )
    final_decay = cumulative[-1]
    tail_weight = jnp.exp(final_decay[None] - cumulative) * step_block
    scaled = (tail_weight[:, :, None] * value_block.astype(jnp.float32)).astype(jnp.bfloat16)
    new_state = jnp.exp(final_decay)[:, None, None] * carried + jnp.einsum(
        "shp,sn->hpn", scaled, b_block, preferred_element_type=jnp.float32
    )
    return (new_state, inside + carried_out)


def combine_pairs(earlier, latter):
    return (earlier[0] + latter[0], jnp.exp(latter[0])[:, None, None] * earlier[1] + latter[1])


def body(tokens, w_xz, w_bc, w_dt, dt_bias, a_log, conv_x, conv_bc, norm_gain, w_out):
    model_width = tokens.shape[1]
    inner_width = w_xz.shape[2]
    head_count = w_dt.shape[1]
    head_width = inner_width // head_count
    state_width = w_bc.shape[1] // 2
    kernel_size = conv_x.shape[0]
    flat_xz = w_xz.reshape(model_width, 2 * inner_width)
    token_piece = collect(tokens, "head", 0)
    projected = jnp.concatenate(
        [
            jnp.dot(token_piece, flat_xz, preferred_element_type=jnp.float32),
            jnp.dot(token_piece, w_bc, preferred_element_type=jnp.float32),
            jnp.dot(token_piece, w_dt, preferred_element_type=jnp.float32),
        ],
        axis=1,
    )
    row_count = projected.shape[0]
    value_pre = projected[:, :inner_width].astype(jnp.bfloat16)
    gate_pre = projected[:, inner_width : 2 * inner_width].astype(jnp.bfloat16)
    bc_pre = projected[:, 2 * inner_width : 2 * inner_width + 2 * state_width].astype(jnp.bfloat16)
    step_size = jax.nn.softplus(projected[:, 2 * inner_width + 2 * state_width :] + dt_bias[None])
    first_tail = row_count - kernel_size + 1
    value_tail, bc_tail = passed_along((value_pre[first_tail:], bc_pre[first_tail:]), SEQ, 1)
    values = causal_mix(value_pre, value_tail, conv_x)
    bc_mixed = causal_mix(bc_pre, bc_tail, conv_bc)
    b_input = bc_mixed[:, :state_width]
    c_input = bc_mixed[:, state_width:]
    log_decay = step_size * (-jnp.exp(a_log))[None]
    blocks = row_count // SPAN
    inputs = (
        values.reshape(blocks, SPAN, head_count, head_width),
        b_input.reshape(blocks, SPAN, state_width),
        c_input.reshape(blocks, SPAN, state_width),
        step_size.reshape(blocks, SPAN, head_count),
        log_decay.reshape(blocks, SPAN, head_count),
    )
    zero_state = jnp.zeros((head_count, head_width, state_width), jnp.float32)
    local_state, outputs = lax.scan(span_update, zero_state, inputs)
    decay_total = jnp.sum(log_decay, axis=0)
    cumulative = jnp.cumsum(log_decay, axis=0)
    _, incoming = carried_in(
        (decay_total, local_state), SEQ, combine_pairs, (jnp.zeros_like(decay_total), zero_state)
    )
    correction = jnp.exp(cumulative)[:, :, None] * jnp.einsum(
        "tn,hpn->thp", c_input, incoming.astype(jnp.bfloat16), preferred_element_type=jnp.float32
    )
    ssm_out = (outputs.reshape(row_count, head_count, head_width) + correction).reshape(
        row_count, inner_width
    )
    gated = ssm_out * jax.nn.silu(gate_pre.astype(jnp.float32))
    square_sum = taken_together(jnp.sum(gated * gated, axis=1), "head")
    scale = lax.rsqrt(square_sum / DI + 1.0)[:, None]
    normed = (gated * scale * norm_gain[None]).astype(jnp.bfloat16)
    return sum_at_owner(
        jnp.dot(normed, w_out, preferred_element_type=jnp.float32).astype(jnp.bfloat16), "head", 0
    ).astype(jnp.bfloat16)


def solution(mesh):
    split = Mesh(mesh.devices.reshape(8, 4, mesh.shape["head"]), ("seq_0", "seq_1", "head"))
    in_specs = (
        P(SEQ_HEAD, None),
        P(None, None, "head"),
        P(),
        P(None, "head"),
        P("head"),
        P("head"),
        P(None, "head"),
        P(),
        P("head"),
        P("head", None),
    )
    out_specs = P(SEQ_HEAD, None)
    return jax.shard_map(body, mesh=split, in_specs=in_specs, out_specs=out_specs, check_vma=False)
```

profile of v0, /device:TPU:1, one launch (start us, length us, event | category | flops | bytes accessed | tf_op | source)
XLA Modules:
  0.0 174.9 jit_solution(15404712217844710359)
XLA Ops:
  6.5 2.3 %broadcast_in_dim.53 = bf16[8,32,2560]{2,1,0:T(8,128)(2,1)} broadcast(bf16[32,2560]{1,0:T(8,128)(2,1)} %param.10), dimensions={1,2} | broadcast | bytes 1474560 | tf_op jit(solution)/shard_map/broadcast_in_dim | solution.py:22
  8.9 7.3 %all-to-all-start = ((bf16[8,32,2560]{2,1,0:T(8,128)(2,1)}), bf16[8,32,2560]{2,1,0:T(8,128)(2,1)}, u32[]{:S(2)}, u32[]{:S(2)}) async-start(bf16[8,32,2560]{2,1,0:T(8,128)(2,1)} %broadcast_in_dim.53), calls=%async_computation | async-start | bytes 2621440 | tf_op jit(solution)/shard_map/all_to_all | solution.py:21
  16.2 6.7 %copy.34 = bf16[320,8,2,640]{3,1,2,0:T(8,128)(2,1)} copy(bf16[320,8,2,640]{3,2,1,0:T(2,128)(2,1)} %bitcast.150) | data formatting | bytes 13107200
  25.5 8.6 %all-to-all-done = bf16[8,32,2560]{2,1,0:T(8,128)(2,1)} async-done(((bf16[8,32,2560]{2,1,0:T(8,128)(2,1)}), bf16[8,32,2560]{2,1,0:T(8,128)(2,1)}, u32[]{:S(2)}, u32[]{:S(2)}) %all-to-all-start) | async-done | bytes 1310752 | tf_op jit(solution)/shard_map/all_to_all | solution.py:21
  34.1 5.2 %convolution_convert_fusion.1 = bf16[256,1280]{1,0:T(8,128)(2,1)S(1)} fusion(bf16[256,2560]{1,0:T(8,128)(2,1)} %bitcast, bf16[2560,1280]{1,0:T(8,128)(2,1)} %bitcast.151), kind=kOutput, calls=%fused_computation.2 | convolution fusion | flops 1678049280 | bytes 8519680 | tf_op jit(solution)/shard_map/dot_general | solution.py:131
  40.0 2.4 %collective-permute-start = (bf16[3,640]{1,0:T(4,128)(2,1)}, bf16[3,640]{1,0:T(4,128)(2,1)}, u32[]{:S(2)}, u32[]{:S(2)}) collective-permute-start(bf16[3,640]{1,0:T(4,128)(2,1)} %slice.210), channel_id=1, source_target_pairs={{0,8},{8,16},{16,24},{24,32},{32,40},{40,48},{48,56},{56,64},{64,7... | collective-permute-start | bytes 11528 | tf_op jit(solution)/shard_map/ppermute | solution.py:33
  42.4 1.8 %convolution_convert_fusion.2 = bf16[256,256]{1,0:T(8,128)(2,1)S(1)} fusion(bf16[256,2560]{1,0:T(8,128)(2,1)} %bitcast, bf16[2560,256]{1,0:T(8,128)(2,1)S(1)} %copy-done.21), kind=kOutput, calls=%fused_computation.17 | convolution fusion | flops 335609856 | bytes 2752512 | tf_op jit(solution)/shard_map/dot_general | solution.py:132
  44.3 2.5 %collective-permute-start.1 = (bf16[3,256]{1,0:T(4,128)(2,1)S(1)}, bf16[3,256]{1,0:T(4,128)(2,1)S(1)}, u32[]{:S(2)}, u32[]{:S(2)}) collective-permute-start(bf16[3,256]{1,0:T(4,128)(2,1)S(1)} %slice.217), channel_id=1, source_target_pairs={{0,8},{8,16},{16,24},{24,32},{32,40},{40,48},{48,56},{56,64},{64,7... | collective-permute-start | bytes 4616 | tf_op jit(solution)/shard_map/ppermute | solution.py:33
  46.8 2.4 %broadcast_multiply_fusion = (f32[10,256]{1,0:T(8,128)S(1)}, f32[10,256]{1,0:T(8,128)}, f32[256,10]{0,1:T(8,128)S(1)}) fusion(f32[10]{0:T(128)S(1)} %exponential_negate_fusion, f32[10]{0:T(128)S(1)} %copy-done.15, bf16[256,2560]{1,0:T(8,128)(2,1)} %bitcast, bf16[2560,10]{0,1:T(8,128)(2,1)S(1)} %copy-done.3), kind=kOutput, calls=%fused_computation.146 | convolution fusion | flops 13127680 | bytes 1392720 | tf_op jit(solution)/shard_map/dot_general | solution.py:133
  51.4 8.8 %all-reduce = bf16[40]{0:T(256)(128)(2,1)S(1)} all-reduce(bf16[40]{0:T(256)(128)(2,1)S(1)} %dynamic-update-slice), channel_id=2, replica_groups=mesh['seq_0'=8,'seq_1'=4,'head'=8] {'seq_1'}, use_global_device_ids=true, to_apply=%add | all-reduce | flops 40 | bytes 160
  64.7 2.0 %multiply_convert_fusion.6 = bf16[256,640]{1,0:T(8,128)(2,1)} fusion(bf16[256,640]{1,0:T(8,128)(2,1)S(1)} %slice.211, bf16[3,640]{1,0:T(4,128)(2,1)} %collective-permute-done, f32[640]{0:T(1024)} %get-tuple-element.21, f32[640]{0:T(1024)} %get-tuple-element.22, f32[640]{0:T(1024)} %get-tuple-element.20, f32[640]{0:T(1024)} %get-tuple-element.19), kind=kLoop, calls=%fused_computation.28 | loop fusion | flops 4096000 | bytes 669440 | tf_op jit(solution)/shard_map/convert_element_type | solution.py:89
  66.7 1.9 %copy.28 = bf16[256,640]{0,1:T(8,128)(2,1)} copy(bf16[256,640]{1,0:T(8,128)(2,1)} %multiply_convert_fusion.6) | data formatting | bytes 655360 | tf_op jit(solution)/shard_map/convert_element_type | solution.py:89
  68.6 1.2 fusion.10
  69.8 11.8 %all-gather.1 = bf16[40,64,128]{2,1,0:T(8,128)(2,1)S(1)} all-gather(bf16[10,64,128]{2,1,0:T(8,128)(2,1)S(1)} %fusion.10), channel_id=3, replica_groups=mesh['seq_0'=8,'seq_1'=4,'head'=8] {'seq_1'}, dimensions={0}, use_global_device_ids=true | all-gather | bytes 819200 | tf_op jit(solution)/shard_map/all_gather | solution.py:48
  83.5 13.3 %all-gather.2 = bf16[8,1,10]{2,1,0:T(2,128)(2,1)S(1)} all-gather(bf16[1,1,10]{2,1,0:T(2,128)(2,1)S(1)} %copy-done.14), channel_id=1, replica_groups=mesh['seq_0'=8,'seq_1'=4,'head'=8] {'seq_0'}, dimensions={0}, use_global_device_ids=true | all-gather | bytes 180 | tf_op jit(solution)/shard_map/all_gather | solution.py:48
  97.6 1.9 %fusion.7 = f32[256,10,64]{0,2,1:T(8,128)S(1)} fusion(bf16[256,10,64]{0,2,1:T(8,128)(2,1)} %bitcast.155, f32[10,256]{1,0:T(8,128)S(1)} %copy-done.6, f32[256,256]{1,0:T(8,128)S(1)} %fusion.83, f32[10,256]{1,0:T(8,128)S(1)} %bitcast.158, pred[256,256]{1,0:T(8,128)(4,1)S(1)} %iota_compare_fusion), kind=kOutput, calls=%fused_computation.10 | convolution fusion | flops 87818240 | bytes 1331200 | tf_op jit(solution)/shard_map/while/body/eval_jaxpr/hts,shp->thp/dot_general | solution.py:103
  100.6 19.6 %all-gather.5.cloned.1.call-done = bf16[8,10,64,128]{3,2,1,0:T(8,128)(2,1)} async-done(((bf16[1,10,64,128]{3,2,1,0:T(8,128)(2,1)}), bf16[8,10,64,128]{3,2,1,0:T(8,128)(2,1)}) %all-gather.5.cloned.1.call-update) | async-done | bytes 1310736 | tf_op jit(solution)/shard_map/all_gather | solution.py:48
  120.2 3.4 %fusion.8 = f32[256,10,64]{0,2,1:T(8,128)} fusion(f32[256,10,64]{0,2,1:T(8,128)} %fusion.9, f32[256,10]{0,1:T(8,128)S(1)} %copy-done.4, bf16[8,10,64,128]{3,2,1,0:T(8,128)(2,1)} %all-gather.5.cloned.1.call-done, f32[10]{0:T(128)S(1)} %copy-done.16, f32[10]{0:T(128)S(1)} %copy-done.11, f32[10]{0:T(128)S(1)} %copy-done.10, f32[10]{0:T(128)S(1)} %copy-done.13, ...), kind=kOutput, calls=%fused_computation.12 | convolution fusion | flops 46284800 | bytes 3365388 | tf_op jit(solution)/shard_map/tn,hpn->thp/dot_general | solution.py:164
  123.7 2.2 %copy.31 = f32[256,640]{1,0:T(8,128)} copy(f32[256,640]{0,1:T(8,128)} %bitcast.153) | data formatting | bytes 1310720 | tf_op jit(solution)/shard_map/reshape | solution.py:167
  125.8 1.5 multiply_reduce_fusion
  127.3 14.5 %all_to_all.16 = f32[8,1,256]{2,1,0:T(1,128)S(1)} all-to-all(f32[8,1,256]{2,1,0:T(1,128)S(1)} %broadcast_in_dim.58), channel_id=1, replica_groups=mesh['seq_0'=8,'seq_1'=4,'head'=8] {'head'}, dimensions={0} | all-to-all | bytes 16384 | tf_op jit(solution)/shard_map/all_to_all | solution.py:21
  141.8 2.5 %convolution_convert_fusion = bf16[256,2560]{1,0:T(8,128)(2,1)S(1)} fusion(bf16[640,2560]{1,0:T(8,128)(2,1)S(1)} %copy-done, f32[640]{0:T(1024)S(1)} %copy-done.22, f32[256]{0:T(256)S(1)} %add_rsqrt_fusion, f32[256,640]{1,0:T(8,128)} %copy.31, bf16[256,1280]{1,0:T(8,128)(2,1)} %copy-done.2), kind=kOutput, calls=%fused_computation | convolution fusion | flops 840990720 | bytes 5574144 | tf_op jit(solution)/shard_map/dot_general | solution.py:175
  144.3 21.6 %all_to_all.17 = bf16[8,32,2560]{2,1,0:T(8,128)(2,1)} all-to-all(bf16[8,32,2560]{2,1,0:T(8,128)(2,1)S(1)} %bitcast.152), channel_id=1, replica_groups=mesh['seq_0'=8,'seq_1'=4,'head'=8] {'head'}, dimensions={0} | all-to-all | bytes 2621440 | tf_op jit(solution)/shard_map/all_to_all | solution.py:76
  165.9 2.2 %reduce_sum.42 = bf16[32,2560]{1,0:T(8,128)(2,1)} reduce(bf16[8,32,2560]{2,1,0:T(8,128)(2,1)} %all_to_all.17, bf16[]{:T(256)} %constant.31.clone.1), dimensions={0}, to_apply=%region_5.6 | reduce | flops 573440 | bytes 1474562 | tf_op jit(solution)/shard_map/reduce_sum | solution.py:77
  (89 shorter events, 12.9 us)
Async XLA Ops:
  6.5 135.3 %copy-start = (bf16[640,2560]{1,0:T(8,128)(2,1)S(1)}, bf16[640,2560]{1,0:T(8,128)(2,1)}, u32[]{:S(2)}) copy-start(bf16[640,2560]{1,0:T(8,128)(2,1)} %param.19) | copy-start | bytes 9830404
  8.9 25.3 %all-to-all-start = ((bf16[8,32,2560]{2,1,0:T(8,128)(2,1)}), bf16[8,32,2560]{2,1,0:T(8,128)(2,1)}, u32[]{:S(2)}, u32[]{:S(2)}) async-start(bf16[8,32,2560]{2,1,0:T(8,128)(2,1)} %broadcast_in_dim.53), calls=%async_computation | async-start | bytes 2621440 | tf_op jit(solution)/shard_map/all_to_all | solution.py:21
  16.2 104.0 %all-gather.5.cloned.1.call-start = ((), (), s32[]{:S(2)}) async-start(), calls=%async_computation.3 | async-start | bytes 1474560 | tf_op jit(solution)/shard_map/all_gather | solution.py:48
  16.2 6.8 %copy-start.24 = (u32[256]{0:T(256)S(1)}, u32[256]{0:T(256)}, u32[]{:S(2)}) copy-start(u32[256]{0:T(256)} %constant.72) | copy-start | bytes 3076
  16.2 8.0 %copy-start.5 = (bf16[4,640]{1,0:T(4,128)(2,1)S(1)}, bf16[4,640]{1,0:T(4,128)(2,1)}, u32[]{:S(2)}) copy-start(bf16[4,640]{1,0:T(4,128)(2,1)} %param.16) | copy-start | bytes 15364
  16.2 8.6 %copy-start.23 = (f32[10]{0:T(128)S(1)}, f32[10]{0:T(128)}, u32[]{:S(2)}) copy-start(f32[10]{0:T(128)} %param.15) | copy-start | bytes 124
  16.2 8.6 %copy-start.8 = (bf16[4,256]{1,0:T(4,128)(2,1)S(1)}, bf16[4,256]{1,0:T(4,128)(2,1)}, u32[]{:S(2)}) copy-start(bf16[4,256]{1,0:T(4,128)(2,1)} %param.17) | copy-start | bytes 6148
  34.1 8.3 %copy-start.21 = (bf16[2560,256]{1,0:T(8,128)(2,1)S(1)}, bf16[2560,256]{1,0:T(8,128)(2,1)}, u32[]{:S(2)}) copy-start(bf16[2560,256]{1,0:T(8,128)(2,1)} %param.12) | copy-start | bytes 3932164
  40.0 6.8 %copy-start.3 = (bf16[2560,10]{0,1:T(8,128)(2,1)S(1)}, bf16[2560,10]{0,1:T(8,128)(2,1)}, u32[]{:S(2)}) copy-start(bf16[2560,10]{0,1:T(8,128)(2,1)} %param.13) | copy-start | bytes 153604
  40.0 6.8 %copy-start.15 = (f32[10]{0:T(128)S(1)}, f32[10]{0:T(128)}, u32[]{:S(2)}) copy-start(f32[10]{0:T(128)} %param.14) | copy-start | bytes 124
  40.0 24.7 %collective-permute-start = (bf16[3,640]{1,0:T(4,128)(2,1)}, bf16[3,640]{1,0:T(4,128)(2,1)}, u32[]{:S(2)}, u32[]{:S(2)}) collective-permute-start(bf16[3,640]{1,0:T(4,128)(2,1)} %slice.210), channel_id=1, source_target_pairs={{0,8},{8,16},{16,24},{24,32},{32,40},{40,48},{48,56},{56,64},{64,7... | collective-permute-start | bytes 11528 | tf_op jit(solution)/shard_map/ppermute | solution.py:33
  44.3 18.8 %collective-permute-start.1 = (bf16[3,256]{1,0:T(4,128)(2,1)S(1)}, bf16[3,256]{1,0:T(4,128)(2,1)S(1)}, u32[]{:S(2)}, u32[]{:S(2)}) collective-permute-start(bf16[3,256]{1,0:T(4,128)(2,1)S(1)} %slice.217), channel_id=1, source_target_pairs={{0,8},{8,16},{16,24},{24,32},{32,40},{40,48},{48,56},{56,64},{64,7... | collective-permute-start | bytes 4616 | tf_op jit(solution)/shard_map/ppermute | solution.py:33
  64.7 17.8 %copy-start.10 = (f32[10]{0:T(128)S(1)}, f32[10]{0:T(128)}, u32[]{:S(2)}) copy-start(f32[10]{0:T(128)} %get-tuple-element.53) | copy-start | bytes 124
  64.7 17.8 %copy-start.11 = (f32[10]{0:T(128)S(1)}, f32[10]{0:T(128)}, u32[]{:S(2)}) copy-start(f32[10]{0:T(128)} %get-tuple-element.54) | copy-start | bytes 124
  64.7 17.8 %copy-start.12 = (f32[10]{0:T(128)S(1)}, f32[10]{0:T(128)}, u32[]{:S(2)}) copy-start(f32[10]{0:T(128)} %get-tuple-element.55) | copy-start | bytes 124
  64.7 17.8 %copy-start.13 = (f32[10]{0:T(128)S(1)}, f32[10]{0:T(128)}, u32[]{:S(2)}) copy-start(f32[10]{0:T(128)} %get-tuple-element.56) | copy-start | bytes 124
  68.6 14.9 %copy-start.14 = (bf16[1,1,10]{2,1,0:T(2,128)(2,1)S(1)}, bf16[1,1,10]{2,1,0:T(2,128)(2,1)}, u32[]{:S(2)}) copy-start(bf16[1,1,10]{2,1,0:T(2,128)(2,1)} %get-tuple-element.23) | copy-start | bytes 64
  69.8 27.7 %copy-start.6 = (f32[10,256]{1,0:T(8,128)S(1)}, f32[10,256]{1,0:T(8,128)}, u32[]{:S(2)}) copy-start(f32[10,256]{1,0:T(8,128)} %get-tuple-element.39) | copy-start | bytes 30724
  99.5 20.7 %copy-start.16 = (f32[10]{0:T(128)S(1)}, f32[10]{0:T(128)}, u32[]{:S(2)}) copy-start(f32[10]{0:T(128)} %get-tuple-element.52) | copy-start | bytes 124
  99.5 20.7 %copy-start.17 = (f32[10]{0:T(128)S(1)}, f32[10]{0:T(128)}, u32[]{:S(2)}) copy-start(f32[10]{0:T(128)} %get-tuple-element.44) | copy-start | bytes 124
  99.5 20.7 %copy-start.18 = (f32[10]{0:T(128)S(1)}, f32[10]{0:T(128)}, u32[]{:S(2)}) copy-start(f32[10]{0:T(128)} %get-tuple-element.45) | copy-start | bytes 124
  99.5 20.7 %copy-start.19 = (f32[10]{0:T(128)S(1)}, f32[10]{0:T(128)}, u32[]{:S(2)}) copy-start(f32[10]{0:T(128)} %get-tuple-element.46) | copy-start | bytes 124
  99.5 20.7 %copy-start.20 = (f32[10]{0:T(128)S(1)}, f32[10]{0:T(128)}, u32[]{:S(2)}) copy-start(f32[10]{0:T(128)} %get-tuple-element.47) | copy-start | bytes 124
  123.7 18.1 %copy-start.22 = (f32[640]{0:T(1024)S(1)}, f32[640]{0:T(1024)}, u32[]{:S(2)}) copy-start(f32[640]{0:T(1024)} %param.18) | copy-start | bytes 7684
  (6 other events, 16.2 us)
Sparse Core Ops, SparseCore 0:
  83.6 36.5 all-gather.4
where the time goes:
time: 176 us; the launch traced here: 175 us
  blocking collectives  69.9 us (40%)
  waiting for transfers between devices  28.2 us (16%)
  matrix products  19.8 us (11%)
  local copies, waits for them, and re-layouts  17.5 us (10%)
  between operations  14.4 us (8%)
  other arithmetic  12.8 us (7%)
  starting transfers between devices  12.3 us (7%)
    all_gather x2, blocking collectives, carried_in(): lax.all_gather(part.astype(kind), axis)  25.1 us
    all_to_all x1, blocking collectives, sum_at_owner(): pieces = lax.all_to_all(split_up(value, dim, size), axis, 0, 0, tiled=True)  21.6 us
    all_gather x1, waiting for transfers between devices, carried_in(): lax.all_gather(part.astype(kind), axis)  19.6 us
    all_to_all x1, blocking collectives, sent_to_all(): lax.all_to_all(jnp.broadcast_to(value[None], (size, *value.shape)), axis,...  14.5 us
    unnamed x58, local copies, waits for them, and re-layouts  9.1 us
    unnamed x1, blocking collectives  8.79 us
    all_to_all x1, waiting for transfers between devices, sent_to_all(): lax.all_to_all(jnp.broadcast_to(value[None], (size, *value.shape)), axis,...  8.64 us
    all_to_all x1, starting transfers between devices, sent_to_all(): lax.all_to_all(jnp.broadcast_to(value[None], (size, *value.shape)), axis,...  7.34 us
  transfers between devices with their start and end apart: 4, of which 2 were waited for; matrix products, arithmetic and copies ran while one was open for 13% of the time, Pallas kernels for 0%

commit v1 on v0

v1 whole, which is shorter than its diff:
```python
import jax
import jax.numpy as jnp
from jax import lax
from jax.experimental import pallas as pl
from jax.experimental.pallas import tpu as pltpu
from jax.sharding import Mesh
from jax.sharding import PartitionSpec as P

DI = 5120
SEQ = ("z", "x")
ALL = ("z", "x", "y", "c")
HEAD = ("y", "c")
BF = jnp.bfloat16
F32 = jnp.float32
ROWS = 32
BLOCK = 256
WIDTH = 640
STATE = 128
PRE = WIDTH + 2 * STATE
MODEL = 2560
WIDE = MODEL + 128
PIECE = 40


def whole(count):
    return [pl.BlockSpec(memory_space=pltpu.VMEM)] * count


def call(body, outs, args, scratch=(), flops=0, name=None):
    return pl.pallas_call(
        body,
        out_shape=[jax.ShapeDtypeStruct(s, t) for s, t in outs],
        in_specs=whole(len(args)),
        out_specs=whole(len(outs)),
        scratch_shapes=[pltpu.VMEM(s, t) for s, t in scratch],
        compiler_params=pltpu.CompilerParams(vmem_limit_bytes=24 << 20),
        cost_estimate=pl.CostEstimate(flops=flops, transcendentals=0, bytes_accessed=flops // 500),
        name=name,
    )(*args)


def shifted(value, axis, steps):
    size = lax.axis_size(axis)
    return lax.ppermute(value, axis, [(i, (i + steps) % size) for i in range(size)])


def row_at(index, rows):
    return pl.ds(pl.multiple_of(index * rows, rows), rows)


def project_kernel(t0, t1, t2, t3, o0, o1, o2, o3, w, all_out, pre_out, tail_out, dt_out):
    y, c = lax.axis_index("y"), lax.axis_index("c")
    for d, (own, other) in enumerate(((t0, o0), (t1, o1), (t2, o2), (t3, o3))):
        source = lax.rem(y + 4 - d, 4)
        all_out[row_at(source * 2 + c, ROWS), :] = own[...]
        all_out[row_at(source * 2 + 1 - c, ROWS), :] = other[...]
    tokens = all_out[...]
    for n in range(4):
        cols = slice(256 * n, 256 * n + 256)
        part = jnp.dot(tokens, w[:, cols], preferred_element_type=F32)
        if n < 3:
            pre_out[:, cols] = part.astype(BF)
            tail_out[:, cols] = part[BLOCK - 8 :].astype(BF)
        else:
            pre_out[:, 768:896] = part[:, :128].astype(BF)
            tail_out[:, 768:896] = part[BLOCK - 8 :, :128].astype(BF)
            dt_out[...] = part[:, 128:]


def gate_kernel(tokens, w, out):
    gate = jnp.dot(tokens[...], w[...], preferred_element_type=F32).astype(BF).astype(F32)
    out[...] = jax.nn.silu(gate)


def spread(value, pair):
    rows = value.shape[0]
    lane = lax.broadcasted_iota(jnp.int32, (rows, 128), 1)
    left = jnp.broadcast_to(value[:, 2 * pair : 2 * pair + 1], (rows, 128))
    right = jnp.broadcast_to(value[:, 2 * pair + 1 : 2 * pair + 2], (rows, 128))
    return jnp.where(lane < 64, left, right)


def halves(value):
    high = value.astype(BF)
    return high, (value - high.astype(F32)).astype(BF)


def decay_rows(factor):
    high, low = halves(factor)
    row = lax.broadcasted_iota(jnp.int32, factor.shape, 0)
    return jnp.where(row == 0, high.astype(F32), jnp.where(row == 1, low.astype(F32), 0.0)).astype(BF)


def local_kernel(
    pre, tail, dt_pre, conv_x, conv_bc, bias, a_log, v_out, b_out, c_out, dt_out, cum_out, p0, p1, p2, p3, ext, state
):
    x = lax.axis_index("x")
    ext[0:8, :] = tail[...].astype(F32)
    ext[8 : 8 + BLOCK, :] = pre[...].astype(F32)
    step = jax.nn.softplus(dt_pre[...] + bias[...])
    decay = step * (-jnp.exp(a_log[...]))
    row = lax.broadcasted_iota(jnp.int32, decay.shape, 0)
    cum = decay
    for k in (1, 2, 4, 8, 16, 32, 64, 128):
        cum = cum + jnp.where(row >= k, pltpu.roll(cum, k, 0), 0.0)
    dt_out[...] = step
    cum_out[...] = cum
    last = cum[BLOCK - 1 : BLOCK, :]
    tail_weight = jnp.exp(last - cum) * step

    def mixed(first, kernel, lo):
        total = jnp.zeros((BLOCK, 128), F32)
        for k in range(4):
            total = total + kernel[k : k + 1, lo : lo + 128].astype(F32) * ext[5 + k : 5 + k + BLOCK, first : first + 128]
        return jax.nn.silu(total).astype(BF)

    b = mixed(WIDTH, conv_bc, 0)
    b_out[...] = b
    c_out[...] = mixed(WIDTH + STATE, conv_bc, STATE)
    factor = jnp.broadcast_to(jnp.exp(last), (8, 128))
    b_rows = b.astype(F32).T.astype(BF)
    for pair in range(5):
        cols = slice(128 * pair, 128 * pair + 128)
        v = mixed(128 * pair, conv_x, 128 * pair)
        v_out[:, cols] = v
        scaled = (spread(tail_weight, pair) * v.astype(F32)).astype(BF)
        state[:, cols] = jnp.dot(b_rows, scaled, preferred_element_type=F32)
        extra = decay_rows(spread(factor, pair))
        for out in (p0, p1, p2, p3):
            out[32:40, cols] = extra
    for d, out in enumerate((p0, p1, p2, p3)):
        out[0:32, :] = state[row_at(lax.rem(x + d, 4), 32), :].astype(BF)


def inside_kernel(v, b, c, step, cum, out):
    scores = jnp.dot(c[...], b[...].astype(F32).T.astype(BF), preferred_element_type=F32)
    t = lax.broadcasted_iota(jnp.int32, (BLOCK, BLOCK), 0)
    s = lax.broadcasted_iota(jnp.int32, (BLOCK, BLOCK), 1)
    scores = jnp.where(t >= s, scores, 0.0)
    cum_all = cum[...]
    cum_rows = cum_all.T
    step_rows = step[...].T
    lane = lax.broadcasted_iota(jnp.int32, (BLOCK, 128), 1)
    for pair in range(5):
        cols = slice(128 * pair, 128 * pair + 128)
        value = v[:, cols]
        parts = []
        for h in (2 * pair, 2 * pair + 1):
            differ = jnp.broadcast_to(cum_all[:, h : h + 1], (BLOCK, BLOCK)) - cum_rows[h : h + 1, :]
            weight = jnp.exp(jnp.minimum(differ, 0.0)) * (scores * step_rows[h : h + 1, :])
            parts.append(jnp.dot(weight.astype(BF), value, preferred_element_type=F32))
        out[:, cols] = jnp.where(lane < 64, parts[0], parts[1])


def load_rows(pieces, held):
    x = lax.axis_index("x")
    for d, piece in enumerate(pieces):
        held[lax.rem(x + 4 - d, 4)] = piece[...].astype(F32)


def factor_of(held, k):
    return held[k, 32:33, :] + held[k, 33:34, :]


def row_total_kernel(q0, q1, q2, q3, out, held):
    load_rows((q0, q1, q2, q3), held)
    total, factor = held[0, 0:32, :], factor_of(held, 0)
    for k in range(1, 4):
        a = factor_of(held, k)
        total = total * a + held[k, 0:32, :]
        factor = factor * a
    extra = decay_rows(jnp.broadcast_to(factor, (8, WIDTH)))
    for k in range(8):
        out[k, 0:32, :] = total.astype(BF)
        out[k, 32:40, :] = extra


def incoming_kernel(q0, q1, q2, q3, totals, e0, e1, e2, e3, held, ready):
    z, x = lax.axis_index("z"), lax.axis_index("x")
    load_rows((q0, q1, q2, q3), held)
    carry = jnp.zeros((32, WIDTH), F32)
    for k in range(7):
        a = totals[k, 32:33, :].astype(F32) + totals[k, 33:34, :].astype(F32)
        carry = jnp.where(k < z, carry * a + totals[k, 0:32, :].astype(F32), carry)
    ready[0] = carry
    for k in range(3):
        carry = carry * factor_of(held, k) + held[k, 0:32, :]
        ready[k + 1] = carry
    for d, out in enumerate((e0, e1, e2, e3)):
        out[...] = ready[lax.rem(x + d, 4)].astype(BF)


def gated_kernel(e0, e1, e2, e3, c, cum, inside, gate, gain, w, g_out, sq_out, send_out, state, pick):
    x, core = lax.axis_index("x"), lax.axis_index("c")
    for d, piece in enumerate((e0, e1, e2, e3)):
        state[row_at(lax.rem(x + 4 - d, 4), 32), :] = piece[...]
    grown = jnp.exp(cum[...])
    squares = jnp.zeros((BLOCK, 128), F32)
    for pair in range(5):
        cols = slice(128 * pair, 128 * pair + 128)
        came = jnp.dot(c[...], state[:, cols], preferred_element_type=F32)
        gated = (inside[:, cols] + spread(grown, pair) * came) * gate[:, cols]
        squares = squares + gated * gated
        g_out[:, cols] = (gated * gain[:, cols]).astype(BF)
    sq_out[...] = jnp.broadcast_to(jnp.sum(squares, axis=1, keepdims=True), (BLOCK, 128))
    for k in range(4):
        rows = row_at(2 * k + 1 - core, ROWS)
        pick[32 * k : 32 * k + 32, :] = g_out[rows, :]
        send_out[32 * k : 32 * k + 32, MODEL:] = square_cols(sq_out[rows, :])
    left = pick[...]
    for n in range(10):
        cols = slice(256 * n, 256 * n + 256)
        send_out[:, cols] = jnp.dot(left, w[:, cols], preferred_element_type=F32).astype(BF)


def square_cols(total):
    high, low = halves(total)
    lane = lax.broadcasted_iota(jnp.int32, total.shape, 1)
    return jnp.where(lane == 0, high.astype(F32), jnp.where(lane == 1, low.astype(F32), 0.0)).astype(BF)


def own_kernel(g, sq, w, out, pick):
    core = lax.axis_index("c")
    lane = lax.broadcasted_iota(jnp.int32, (ROWS, 128), 1)
    for k in range(4):
        rows = row_at(2 * k + core, ROWS)
        pick[32 * k : 32 * k + 32, :] = g[rows, :]
        out[32 * k : 32 * k + 32, MODEL:] = jnp.where(lane == 0, sq[rows, :], 0.0)
    left = pick[...]
    for n in range(10):
        cols = slice(256 * n, 256 * n + 256)
        out[:, cols] = jnp.dot(left, w[:, cols], preferred_element_type=F32)


def pair_kernel(own, came, f0, f1, f2, f3):
    y = lax.axis_index("y")
    for d, out in enumerate((f0, f1, f2, f3)):
        rows = row_at(lax.rem(y + d, 4), ROWS)
        total = own[rows, :] + came[rows, :].astype(F32)
        out[:, :MODEL] = total[:, :MODEL].astype(out.dtype)
        both = jnp.sum(total[:, MODEL:], axis=1, keepdims=True)
        out[:, MODEL:] = square_cols(jnp.broadcast_to(both, (ROWS, 128))).astype(out.dtype)


def finish_kernel(f0, g1, g2, g3, out):
    total = f0[...] + g1[...].astype(F32) + g2[...].astype(F32) + g3[...].astype(F32)
    squares = jnp.sum(total[:, MODEL:], axis=1, keepdims=True)
    out[...] = (total[:, :MODEL] * lax.rsqrt(squares / DI + 1.0)).astype(BF)


def body(tokens, w_xz, w_bc, w_dt, dt_bias, a_log, conv_x, conv_bc, norm_gain, w_out):
    heads = w_dt.shape[1]
    lanes = ((0, 0), (0, 128 - heads))
    near = [tokens] + [shifted(tokens, "y", d) for d in (1, 2, 3)]
    far = [shifted(piece, "c", 1) for piece in near]
    w_first = jnp.concatenate([w_xz[:, 0], w_bc, jnp.pad(w_dt, lanes)], axis=1)
    w_gate = w_xz[:, 1]
    bias = jnp.pad(dt_bias[None], lanes)
    rates = jnp.pad(a_log[None], lanes)
    everything, pre, tail, dt_pre = call(
        project_kernel,
        [((BLOCK, MODEL), BF), ((BLOCK, PRE), BF), ((8, PRE), BF), ((BLOCK, 128), F32)],
        [*near, *far, w_first],
        flops=2 * BLOCK * MODEL * 1024,
        name="project",
    )
    tail = lax.ppermute(tail, SEQ, [(i, i + 1) for i in range(31)])
    (gate,) = call(gate_kernel, [((BLOCK, WIDTH), F32)], [everything, w_gate], flops=2 * BLOCK * MODEL * WIDTH, name="gate")
    v, b, c, step, cum, p0, p1, p2, p3 = call(
        local_kernel,
        [((BLOCK, WIDTH), BF), ((BLOCK, STATE), BF), ((BLOCK, STATE), BF), ((BLOCK, 128), F32), ((BLOCK, 128), F32)]
        + [((PIECE, WIDTH), BF)] * 4,
        [pre, tail, dt_pre, conv_x, conv_bc, bias, rates],
        scratch=[((BLOCK + 8, PRE), F32), ((STATE, WIDTH), F32)],
        flops=2 * BLOCK * STATE * WIDTH,
        name="local",
    )
    rows = [p0] + [shifted(piece, "x", d) for d, piece in ((1, p1), (2, p2), (3, p3))]
    (inside,) = call(
        inside_kernel, [((BLOCK, WIDTH), F32)], [v, b, c, step, cum], flops=20 * BLOCK * BLOCK * 256, name="inside"
    )
    (totals,) = call(row_total_kernel, [((8, PIECE, WIDTH), BF)], rows, scratch=[((4, PIECE, WIDTH), F32)], name="rowtotal")
    totals = lax.all_to_all(totals, "z", 0, 0, tiled=True)
    e0, e1, e2, e3 = call(
        incoming_kernel,
        [((32, WIDTH), BF)] * 4,
        [*rows, totals],
        scratch=[((4, PIECE, WIDTH), F32), ((4, 32, WIDTH), F32)],
        name="incoming",
    )
    states = [e0] + [shifted(piece, "x", d) for d, piece in ((1, e1), (2, e2), (3, e3))]
    g, squares, send = call(
        gated_kernel,
        [((BLOCK, WIDTH), BF), ((BLOCK, 128), F32), ((128, WIDE), BF)],
        [*states, c, cum, inside, gate, norm_gain[None], w_out],
        scratch=[((STATE, WIDTH), BF), ((128, WIDTH), BF)],
        flops=2 * 128 * WIDTH * MODEL,
        name="gated",
    )
    came = shifted(send, "c", 1)
    (own,) = call(
        own_kernel, [((128, WIDE), F32)], [g, squares, w_out], scratch=[((128, WIDTH), BF)], flops=2 * 128 * WIDTH * MODEL, name="own"
    )
    f0, f1, f2, f3 = call(pair_kernel, [((ROWS, WIDE), F32)] + [((ROWS, WIDE), BF)] * 3, [own, came], name="pair")
    parts = [f0] + [shifted(piece, "y", d) for d, piece in ((1, f1), (2, f2), (3, f3))]
    (out,) = call(finish_kernel, [((ROWS, MODEL), BF)], parts, name="finish")
    return out


def solution(mesh):
    split = Mesh(mesh.devices.reshape(8, 4, 4, 2), ALL)
    in_specs = (
        P(ALL, None),
        P(None, None, HEAD),
        P(),
        P(None, HEAD),
        P(HEAD),
        P(HEAD),
        P(None, HEAD),
        P(),
        P(HEAD),
        P(HEAD, None),
    )
    return jax.shard_map(body, mesh=split, in_specs=in_specs, out_specs=P(ALL, None), check_vma=False)
```

time: 176 us -> 103 us (0.59)
  blocking collectives: 69.9 us -> 0 us
  starting transfers between devices: 12.3 us -> 38.2 us
  matrix products: 19.8 us -> 0 us
  local copies, waits for them, and re-layouts: 17.5 us -> 32.4 us
  between operations: 14.4 us -> 0.31 us
  Pallas kernels: 0 us -> 10.1 us
  waiting for transfers between devices: 28.2 us -> 18.4 us
  other arithmetic: 12.8 us -> 3.11 us
    all_to_all x2 -> x0, blocking collectives: 36 us -> none  [the longest x1 21.6 us: sum_at_owner(): pieces = lax.all_to_all(split_up(value, dim, size), axis, 0, 0, tiled=True)]
    all_gather x2 -> x0, blocking collectives: 25.1 us -> none  [carried_in(): lax.all_gather(part.astype(kind), axis)]
    ppermute x2 -> x18, starting transfers between devices: 4.96 us -> 27.8 us  [the longest x17 24.7 us: shifted(): lax.ppermute(value, axis, [(i, (i + steps) % size) for i in range(size)])]
    dot_general x9 -> x0, matrix products: 19.8 us -> none  [the longest x1 5.21 us: body(): jnp.dot(token_piece, flat_xz, preferred_element_type=jnp.float32)]
    all_gather x1 -> x0, waiting for transfers between devices: 19.6 us -> none  [carried_in(): lax.all_gather(part.astype(kind), axis)]
    ppermute x2 -> x18, waiting for transfers between devices: 0.01 us -> 12.9 us  [the longest x17 12.1 us: shifted(): lax.ppermute(value, axis, [(i, (i + steps) % size) for i in range(size)])]
    slice x4 -> x1, local copies, waits for them, and re-layouts: 1.83 us -> 14 us  [body(): w_gate = w_xz[:, 1]]
    pallas_call x0 -> x10, Pallas kernels: none -> 10.1 us  [call(): pl.pallas_call(body, out_shape=[jax.ShapeDtypeStruct(s, t) for s, t in ou...]
  transfers between devices with their start and end apart: 4 -> 19, of which waited for: 2 -> 6; matrix products, arithmetic and copies ran while one was open for 13% -> 24% of each run, Pallas kernels for 0% -> 3%
where the time goes in v1:
time: 103 us
  starting transfers between devices  38.2 us (37%)
  local copies, waits for them, and re-layouts  32.4 us (31%)
  waiting for transfers between devices  18.4 us (18%)
  Pallas kernels  10.1 us (10%)
  other arithmetic  3.11 us (3%)
    ppermute x17, starting transfers between devices, shifted(): lax.ppermute(value, axis, [(i, (i + steps) % size) for i in range(size)])  24.7 us
    unnamed x51, local copies, waits for them, and re-layouts  18.4 us
    slice x1, local copies, waits for them, and re-layouts, body(): w_gate = w_xz[:, 1]  14 us
    ppermute x17, waiting for transfers between devices, shifted(): lax.ppermute(value, axis, [(i, (i + steps) % size) for i in range(size)])  12.1 us
    all_to_all x1, starting transfers between devices, body(): totals = lax.all_to_all(totals, 'z', 0, 0, tiled=True)  10.4 us
    pallas_call x10, Pallas kernels, call(): pl.pallas_call(body, out_shape=[jax.ShapeDtypeStruct(s, t) for s, t in ou...  10.1 us
    all_to_all x1, waiting for transfers between devices, body(): totals = lax.all_to_all(totals, 'z', 0, 0, tiled=True)  5.53 us
    concatenate x1, other arithmetic, body(): w_first = jnp.concatenate([w_xz[:, 0], w_bc, jnp.pad(w_dt, lanes)], axis=1)  3.11 us
  transfers between devices with their start and end apart: 19, of which 6 were waited for; matrix products, arithmetic and copies ran while one was open for 24% of the time, Pallas kernels for 3%

profile of v1, /device:TPU:1, one launch (start us, length us, event | category | flops | bytes accessed | tf_op | source)
XLA Modules:
  0.0 102.5 jit_solution(12465051217696612459)
XLA Ops:
  0.0 2.1 %collective-permute-start = (bf16[32,2560]{1,0:T(8,128)(2,1)}, bf16[32,2560]{1,0:T(8,128)(2,1)S(1)}, u32[]{:S(2)}, u32[]{:S(2)}) collective-permute-start(bf16[32,2560]{1,0:T(8,128)(2,1)} %t0.1), channel_id=1, source_target_pairs={{0,2},{2,4},{4,6},{6,0},{1,3},{3,5},{5,7},{7,1},{8,10},{10,12},{12... | collective-permute-start | bytes 491528 | tf_op jit(solution)/shard_map/ppermute | solution.py:44
  2.1 2.6 %collective-permute-start.1 = (bf16[32,2560]{1,0:T(8,128)(2,1)}, bf16[32,2560]{1,0:T(8,128)(2,1)S(1)}, u32[]{:S(2)}, u32[]{:S(2)}) collective-permute-start(bf16[32,2560]{1,0:T(8,128)(2,1)} %t0.1), channel_id=1, source_target_pairs={{0,4},{2,6},{4,0},{6,2},{1,5},{3,7},{5,1},{7,3},{8,12},{10,14},{12... | collective-permute-start | bytes 491528 | tf_op jit(solution)/shard_map/ppermute | solution.py:44
  5.8 1.5 %collective-permute-start.3 = (bf16[32,2560]{1,0:T(8,128)(2,1)}, bf16[32,2560]{1,0:T(8,128)(2,1)S(1)}, u32[]{:S(2)}, u32[]{:S(2)}) collective-permute-start(bf16[32,2560]{1,0:T(8,128)(2,1)} %t0.1), channel_id=1, source_target_pairs={{0,1},{1,0},{2,3},{3,2},{4,5},{5,4},{6,7},{7,6},{8,9},{9,8},{10,11... | collective-permute-start | bytes 491528 | tf_op jit(solution)/shard_map/ppermute | solution.py:44
  7.3 14.0 %fusion.2 = (bf16[2560,1,640]{2,1,0:T(2,128)(2,1)}, bf16[2560,1,640]{2,1,0:T(2,128)(2,1)S(1)}) fusion(bf16[2560,2,640]{2,1,0:T(2,128)(2,1)} %param.11), kind=kLoop, calls=%fused_computation.5 | loop fusion | bytes 13107200 | tf_op jit(solution)/shard_map/slice | solution.py:257
  21.3 2.3 %copy.19 = bf16[2560,1,640]{2,0,1:T(8,128)(2,1)} copy(bf16[2560,1,640]{2,1,0:T(2,128)(2,1)S(1)} %get-tuple-element.54) | data formatting | bytes 6553600
  24.7 3.1 %fusion.1.w = bf16[2560,1024]{1,0:T(8,128)(2,1)S(1)} fusion(bf16[2560,10]{1,0:T(8,128)(2,1)S(1)} %copy.12, bf16[2560,256]{1,0:T(8,128)(2,1)S(1)} %copy-done.19, bf16[2560,640]{1,0:T(8,128)(2,1)} %bitcast.9), kind=kLoop, calls=%fused_computation.2 | loop fusion | flops 20971520 | bytes 9881600 | tf_op jit(solution)/shard_map/concatenate | solution.py:256
  27.9 1.6 %project.1 = (bf16[256,2560]{1,0:T(8,128)(2,1)S(1)}, bf16[256,896]{1,0:T(8,128)(2,1)S(1)}, bf16[8,896]{1,0:T(8,128)(2,1)S(1)}, f32[256,128]{1,0:T(8,128)S(1)}) custom-call(bf16[32,2560]{1,0:T(8,128)(2,1)S(1)} %copy-done.12, bf16[32,2560]{1,0:T(8,128)(2,1)S(1)} %collective-permute-done.t1, bf16[32,2560]{1,0:T(8,128)(2,1)S(1)} %collective-permute-done.1.t2, ...), custom_call_target="tpu_custom_call" | custom-call | flops 1342177280 | bytes 2684354 | tf_op jit(solution)/shard_map/project/pallas_call | solution.py:30
  30.6 3.1 %collective-permute-start.7 = (bf16[8,896]{1,0:T(8,128)(2,1)S(1)}, bf16[8,896]{1,0:T(8,128)(2,1)S(1)}, u32[]{:S(2)}, u32[]{:S(2)}) collective-permute-start(bf16[8,896]{1,0:T(8,128)(2,1)S(1)} %get-tuple-element.30), channel_id=1, source_target_pairs={{0,8},{8,16},{16,24},{24,32},{32,40},{40,48},{48,56},{56,64},{64,7... | collective-permute-start | bytes 43016 | tf_op jit(solution)/shard_map/ppermute | solution.py:267
  34.5 1.4 %local.1 = (bf16[256,640]{1,0:T(8,128)(2,1)S(1)}, bf16[256,128]{1,0:T(8,128)(2,1)S(1)}, bf16[256,128]{1,0:T(8,128)(2,1)S(1)}, f32[256,128]{1,0:T(8,128)S(1)}, f3...) custom-call(bf16[256,896]{1,0:T(8,128)(2,1)S(1)} %get-tuple-element., ...), custom_call_target="tpu_custom_call" | custom-call | flops 41943040 | bytes 83886 | tf_op jit(solution)/shard_map/local/pallas_call | solution.py:30
  38.0 3.0 %collective-permute-start.10 = (bf16[40,640]{1,0:T(8,128)(2,1)S(1)}, bf16[40,640]{1,0:T(8,128)(2,1)S(1)}, u32[]{:S(2)}, u32[]{:S(2)}) collective-permute-start(bf16[40,640]{1,0:T(8,128)(2,1)S(1)} %get-tuple-element.35), channel_id=1, source_target_pairs={{0,24},{8,0},{16,8},{24,16},{1,25},{9,1},{17,9},{25,17},{2,26},{10... | collective-permute-start | bytes 153608 | tf_op jit(solution)/shard_map/ppermute | solution.py:44
  41.0 1.7 %collective-permute-start.9 = (bf16[40,640]{1,0:T(8,128)(2,1)S(1)}, bf16[40,640]{1,0:T(8,128)(2,1)S(1)}, u32[]{:S(2)}, u32[]{:S(2)}) collective-permute-start(bf16[40,640]{1,0:T(8,128)(2,1)S(1)} %get-tuple-element.34), channel_id=1, source_target_pairs={{0,16},{8,24},{16,0},{24,8},{1,17},{9,25},{17,1},{25,9},{2,18},{10... | collective-permute-start | bytes 153608 | tf_op jit(solution)/shard_map/ppermute | solution.py:44
  42.7 3.0 %collective-permute-done.8.q1 = bf16[40,640]{1,0:T(8,128)(2,1)S(1)} collective-permute-done((bf16[40,640]{1,0:T(8,128)(2,1)S(1)}, bf16[40,640]{1,0:T(8,128)(2,1)S(1)}, u32[]{:S(2)}, u32[]{:S(2)}) %collective-permute-start.8) | collective-permute-done | bytes 51232 | tf_op jit(solution)/shard_map/ppermute | solution.py:44
  48.4 10.4 %all-to-all-start = ((bf16[8,40,640]{2,1,0:T(8,128)(2,1)}), bf16[8,40,640]{2,1,0:T(8,128)(2,1)}, u32[]{:S(2)}, u32[]{:S(2)}) async-start(bf16[8,40,640]{2,1,0:T(8,128)(2,1)} %rowtotal.1), calls=%async_computation | async-start | bytes 819200 | tf_op jit(solution)/shard_map/all_to_all | solution.py:283
  58.8 5.1 %copy.18 = bf16[2560,1,640]{2,0,1:T(8,128)(2,1)} copy(bf16[2560,1,640]{2,1,0:T(2,128)(2,1)} %get-tuple-element.53) | data formatting | bytes 6553600
  64.0 5.5 %all-to-all-done.totals = bf16[8,40,640]{2,1,0:T(8,128)(2,1)} async-done(((bf16[8,40,640]{2,1,0:T(8,128)(2,1)}), bf16[8,40,640]{2,1,0:T(8,128)(2,1)}, u32[]{:S(2)}, u32[]{:S(2)}) %all-to-all-start) | async-done | bytes 409632 | tf_op jit(solution)/shard_map/all_to_all | solution.py:283
  71.9 1.2 %incoming.1 = (bf16[32,640]{1,0:T(8,128)(2,1)S(1)}, bf16[32,640]{1,0:T(8,128)(2,1)S(1)}, bf16[32,640]{1,0:T(8,128)(2,1)S(1)}, bf16[32,640]{1,0:T(8,128)(2,1)S(1)}) custom-call(bf16[40,640]{1,0:T(8,128)(2,1)S(1)} %get-tuple-element.32.q0, bf16[40,640]{1,0:T(8,128)(2,1)S(1)} %copy-done.9, bf16[40,640]{1,0:T(8,128)(2,1)S(1)} %copy-done.11, ...), custom_call_target="tpu_custom_call" | custom-call | tf_op jit(solution)/shard_map/incoming/pallas_call | solution.py:30
  74.1 3.0 %collective-permute-start.12 = (bf16[32,640]{1,0:T(8,128)(2,1)S(1)}, bf16[32,640]{1,0:T(8,128)(2,1)S(1)}, u32[]{:S(2)}, u32[]{:S(2)}) collective-permute-start(bf16[32,640]{1,0:T(8,128)(2,1)S(1)} %get-tuple-element.38), channel_id=1, source_target_pairs={{0,16},{8,24},{16,0},{24,8},{1,17},{9,25},{17,1},{25,9},{2,18},{10... | collective-permute-start | bytes 122888 | tf_op jit(solution)/shard_map/ppermute | solution.py:44
  77.1 1.9 %copy-done.1 = bf16[2560,1,640]{2,0,1:T(8,128)(2,1)S(1)} copy-done((bf16[2560,1,640]{2,0,1:T(8,128)(2,1)S(1)}, bf16[2560,1,640]{2,0,1:T(8,128)(2,1)}, u32[]{:S(2)}) %copy-start.1) | copy-done | bytes 3276824
  79.0 1.3 %copy-done.3 = bf16[256,2560]{1,0:T(8,128)(2,1)S(1)} copy-done((bf16[256,2560]{1,0:T(8,128)(2,1)S(1)}, bf16[256,2560]{1,0:T(8,128)(2,1)}, u32[]{:S(2)}) %copy-start.3) | copy-done | bytes 1310744
  80.4 1.2 %gate.1 = f32[256,640]{1,0:T(8,128)S(1)} custom-call(bf16[256,2560]{1,0:T(8,128)(2,1)S(1)} %copy-done.3, bf16[2560,640]{1,0:T(8,128)(2,1)S(1)} %bitcast.8), custom_call_target="tpu_custom_call" | custom-call | flops 838860800 | bytes 1677721 | tf_op jit(solution)/shard_map/gate/pallas_call | solution.py:30
  82.6 1.2 %gated.1 = (bf16[256,640]{1,0:T(8,128)(2,1)S(1)}, f32[256,128]{1,0:T(8,128)S(1)}, bf16[128,2688]{1,0:T(8,128)(2,1)S(1)}) custom-call(bf16[32,640]{1,0:T(8,128)(2,1)S(1)} %get-tuple-element.36.e0, bf16[32,640]{1,0:T(8,128)(2,1)S(1)} %collective-permute-done.11.e1, bf16[32,640]{1,0:T(8,128)(2,1)S(1)} %collective-permute-done.12.e2, ...), custom_call_target="tpu_custom_call" | custom-call | flops 419430400 | bytes 838860 | tf_op jit(solution)/shard_map/gated/pallas_call | solution.py:30
  83.8 5.0 %collective-permute-start.14 = (bf16[128,2688]{1,0:T(8,128)(2,1)S(1)}, bf16[128,2688]{1,0:T(8,128)(2,1)S(1)}, u32[]{:S(2)}, u32[]{:S(2)}) collective-permute-start(bf16[128,2688]{1,0:T(8,128)(2,1)S(1)} %get-tuple-element.48), channel_id=1, source_target_pairs={{0,1},{1,0},{2,3},{3,2},{4,5},{5,4},{6,7},{7,6},{8,9},{9,8},{10,11... | collective-permute-start | bytes 2064392 | tf_op jit(solution)/shard_map/ppermute | solution.py:44
  91.8 2.0 %collective-permute-start.17 = (bf16[32,2688]{1,0:T(8,128)(2,1)S(1)}, bf16[32,2688]{1,0:T(8,128)(2,1)S(1)}, u32[]{:S(2)}, u32[]{:S(2)}) collective-permute-start(bf16[32,2688]{1,0:T(8,128)(2,1)S(1)} %get-tuple-element.52), channel_id=1, source_target_pairs={{0,6},{2,0},{4,2},{6,4},{1,7},{3,1},{5,3},{7,5},{8,14},{10,8},{12,... | collective-permute-start | bytes 516104 | tf_op jit(solution)/shard_map/ppermute | solution.py:44
  93.8 7.6 %collective-permute-done.15.g1 = bf16[32,2688]{1,0:T(8,128)(2,1)S(1)} collective-permute-done((bf16[32,2688]{1,0:T(8,128)(2,1)S(1)}, bf16[32,2688]{1,0:T(8,128)(2,1)S(1)}, u32[]{:S(2)}, u32[]{:S(2)}) %collective-permute-start.15) | collective-permute-done | bytes 172064 | tf_op jit(solution)/shard_map/ppermute | solution.py:44
  (80 shorter events, 17.3 us)
Async XLA Ops:
  0.0 24.0 %collective-permute-start = (bf16[32,2560]{1,0:T(8,128)(2,1)}, bf16[32,2560]{1,0:T(8,128)(2,1)S(1)}, u32[]{:S(2)}, u32[]{:S(2)}) collective-permute-start(bf16[32,2560]{1,0:T(8,128)(2,1)} %t0.1), channel_id=1, source_target_pairs={{0,2},{2,4},{4,6},{6,0},{1,3},{3,5},{5,7},{7,1},{8,10},{10,12},{12... | collective-permute-start | bytes 491528 | tf_op jit(solution)/shard_map/ppermute | solution.py:44
  2.1 22.0 %collective-permute-start.1 = (bf16[32,2560]{1,0:T(8,128)(2,1)}, bf16[32,2560]{1,0:T(8,128)(2,1)S(1)}, u32[]{:S(2)}, u32[]{:S(2)}) collective-permute-start(bf16[32,2560]{1,0:T(8,128)(2,1)} %t0.1), channel_id=1, source_target_pairs={{0,4},{2,6},{4,0},{6,2},{1,5},{3,7},{5,1},{7,3},{8,12},{10,14},{12... | collective-permute-start | bytes 491528 | tf_op jit(solution)/shard_map/ppermute | solution.py:44
  4.7 19.8 %collective-permute-start.2 = (bf16[32,2560]{1,0:T(8,128)(2,1)}, bf16[32,2560]{1,0:T(8,128)(2,1)S(1)}, u32[]{:S(2)}, u32[]{:S(2)}) collective-permute-start(bf16[32,2560]{1,0:T(8,128)(2,1)} %t0.1), channel_id=1, source_target_pairs={{0,6},{2,0},{4,2},{6,4},{1,7},{3,1},{5,3},{7,5},{8,14},{10,8},{12,... | collective-permute-start | bytes 491528 | tf_op jit(solution)/shard_map/ppermute | solution.py:44
  5.8 22.1 %collective-permute-start.3 = (bf16[32,2560]{1,0:T(8,128)(2,1)}, bf16[32,2560]{1,0:T(8,128)(2,1)S(1)}, u32[]{:S(2)}, u32[]{:S(2)}) collective-permute-start(bf16[32,2560]{1,0:T(8,128)(2,1)} %t0.1), channel_id=1, source_target_pairs={{0,1},{1,0},{2,3},{3,2},{4,5},{5,4},{6,7},{7,6},{8,9},{9,8},{10,11... | collective-permute-start | bytes 491528 | tf_op jit(solution)/shard_map/ppermute | solution.py:44
  24.0 3.9 %collective-permute-start.4 = (bf16[32,2560]{1,0:T(8,128)(2,1)S(1)}, bf16[32,2560]{1,0:T(8,128)(2,1)S(1)}, u32[]{:S(2)}, u32[]{:S(2)}) collective-permute-start(bf16[32,2560]{1,0:T(8,128)(2,1)S(1)} %collective-permute-done.t1), channel_id=1, source_target_pairs={{0,1},{1,0},{2,3},{3,2},{4,5},{5,4},{6,7},{7,6},{8,9},{9,8},{10,11... | collective-permute-start | bytes 491528 | tf_op jit(solution)/shard_map/ppermute | solution.py:44
  24.1 3.8 %collective-permute-start.5 = (bf16[32,2560]{1,0:T(8,128)(2,1)S(1)}, bf16[32,2560]{1,0:T(8,128)(2,1)S(1)}, u32[]{:S(2)}, u32[]{:S(2)}) collective-permute-start(bf16[32,2560]{1,0:T(8,128)(2,1)S(1)} %collective-permute-done.1.t2), channel_id=1, source_target_pairs={{0,1},{1,0},{2,3},{3,2},{4,5},{5,4},{6,7},{7,6},{8,9},{9,8},{10,11... | collective-permute-start | bytes 491528 | tf_op jit(solution)/shard_map/ppermute | solution.py:44
  24.6 3.3 %collective-permute-start.6 = (bf16[32,2560]{1,0:T(8,128)(2,1)S(1)}, bf16[32,2560]{1,0:T(8,128)(2,1)S(1)}, u32[]{:S(2)}, u32[]{:S(2)}) collective-permute-start(bf16[32,2560]{1,0:T(8,128)(2,1)S(1)} %collective-permute-done.2.t3), channel_id=1, source_target_pairs={{0,1},{1,0},{2,3},{3,2},{4,5},{5,4},{6,7},{7,6},{8,9},{9,8},{10,11... | collective-permute-start | bytes 491528 | tf_op jit(solution)/shard_map/ppermute | solution.py:44
  27.8 5.9 %copy-start.23 = (f32[10]{0:T(128)S(1)}, f32[10]{0:T(128)}, u32[]{:S(2)}) copy-start(f32[10]{0:T(128)} %param.15) | copy-start | bytes 124
  27.8 6.7 %copy-start.17 = (bf16[4,640]{1,0:T(4,128)(2,1)S(1)}, bf16[4,640]{1,0:T(4,128)(2,1)}, u32[]{:S(2)}) copy-start(bf16[4,640]{1,0:T(4,128)(2,1)} %conv_x.1) | copy-start | bytes 15364
  27.9 6.7 %copy-start.18 = (bf16[4,256]{1,0:T(4,128)(2,1)S(1)}, bf16[4,256]{1,0:T(4,128)(2,1)}, u32[]{:S(2)}) copy-start(bf16[4,256]{1,0:T(4,128)(2,1)} %conv_bc.1) | copy-start | bytes 6148
  30.6 3.9 %collective-permute-start.7 = (bf16[8,896]{1,0:T(8,128)(2,1)S(1)}, bf16[8,896]{1,0:T(8,128)(2,1)S(1)}, u32[]{:S(2)}, u32[]{:S(2)}) collective-permute-start(bf16[8,896]{1,0:T(8,128)(2,1)S(1)} %get-tuple-element.30), channel_id=1, source_target_pairs={{0,8},{8,16},{16,24},{24,32},{32,40},{40,48},{48,56},{56,64},{64,7... | collective-permute-start | bytes 43016 | tf_op jit(solution)/shard_map/ppermute | solution.py:267
  38.0 4.7 %collective-permute-start.10 = (bf16[40,640]{1,0:T(8,128)(2,1)S(1)}, bf16[40,640]{1,0:T(8,128)(2,1)S(1)}, u32[]{:S(2)}, u32[]{:S(2)}) collective-permute-start(bf16[40,640]{1,0:T(8,128)(2,1)S(1)} %get-tuple-element.35), channel_id=1, source_target_pairs={{0,24},{8,0},{16,8},{24,16},{1,25},{9,1},{17,9},{25,17},{2,26},{10... | collective-permute-start | bytes 153608 | tf_op jit(solution)/shard_map/ppermute | solution.py:44
  41.0 4.7 %collective-permute-start.8 = (bf16[40,640]{1,0:T(8,128)(2,1)S(1)}, bf16[40,640]{1,0:T(8,128)(2,1)S(1)}, u32[]{:S(2)}, u32[]{:S(2)}) collective-permute-start(bf16[40,640]{1,0:T(8,128)(2,1)S(1)} %get-tuple-element.33), channel_id=1, source_target_pairs={{0,8},{8,16},{16,24},{24,0},{1,9},{9,17},{17,25},{25,1},{2,10},{10... | collective-permute-start | bytes 153608 | tf_op jit(solution)/shard_map/ppermute | solution.py:44
  41.0 4.7 %collective-permute-start.9 = (bf16[40,640]{1,0:T(8,128)(2,1)S(1)}, bf16[40,640]{1,0:T(8,128)(2,1)S(1)}, u32[]{:S(2)}, u32[]{:S(2)}) collective-permute-start(bf16[40,640]{1,0:T(8,128)(2,1)S(1)} %get-tuple-element.34), channel_id=1, source_target_pairs={{0,16},{8,24},{16,0},{24,8},{1,17},{9,25},{17,1},{25,9},{2,18},{10... | collective-permute-start | bytes 153608 | tf_op jit(solution)/shard_map/ppermute | solution.py:44
  48.4 15.5 %copy-start.21 = (f32[640]{0:T(1024)S(1)}, f32[640]{0:T(1024)}, u32[]{:S(2)}) copy-start(f32[640]{0:T(1024)} %param.18) | copy-start | bytes 7684
  48.4 21.1 %all-to-all-start = ((bf16[8,40,640]{2,1,0:T(8,128)(2,1)}), bf16[8,40,640]{2,1,0:T(8,128)(2,1)}, u32[]{:S(2)}, u32[]{:S(2)}) async-start(bf16[8,40,640]{2,1,0:T(8,128)(2,1)} %rowtotal.1), calls=%async_computation | async-start | bytes 819200 | tf_op jit(solution)/shard_map/all_to_all | solution.py:283
  64.0 18.6 %copy-start = (bf16[640,2560]{1,0:T(8,128)(2,1)S(1)}, bf16[640,2560]{1,0:T(8,128)(2,1)}, u32[]{:S(2)}) copy-start(bf16[640,2560]{1,0:T(8,128)(2,1)} %w.3) | copy-start | bytes 9830404
  73.1 9.5 %collective-permute-start.11 = (bf16[32,640]{1,0:T(8,128)(2,1)S(1)}, bf16[32,640]{1,0:T(8,128)(2,1)S(1)}, u32[]{:S(2)}, u32[]{:S(2)}) collective-permute-start(bf16[32,640]{1,0:T(8,128)(2,1)S(1)} %get-tuple-element.37), channel_id=1, source_target_pairs={{0,8},{8,16},{16,24},{24,0},{1,9},{9,17},{17,25},{25,1},{2,10},{10... | collective-permute-start | bytes 122888 | tf_op jit(solution)/shard_map/ppermute | solution.py:44
  74.1 8.5 %collective-permute-start.12 = (bf16[32,640]{1,0:T(8,128)(2,1)S(1)}, bf16[32,640]{1,0:T(8,128)(2,1)S(1)}, u32[]{:S(2)}, u32[]{:S(2)}) collective-permute-start(bf16[32,640]{1,0:T(8,128)(2,1)S(1)} %get-tuple-element.38), channel_id=1, source_target_pairs={{0,16},{8,24},{16,0},{24,8},{1,17},{9,25},{17,1},{25,9},{2,18},{10... | collective-permute-start | bytes 122888 | tf_op jit(solution)/shard_map/ppermute | solution.py:44
  77.1 5.5 %collective-permute-start.13 = (bf16[32,640]{1,0:T(8,128)(2,1)S(1)}, bf16[32,640]{1,0:T(8,128)(2,1)S(1)}, u32[]{:S(2)}, u32[]{:S(2)}) collective-permute-start(bf16[32,640]{1,0:T(8,128)(2,1)S(1)} %get-tuple-element.39), channel_id=1, source_target_pairs={{0,24},{8,0},{16,8},{24,16},{1,25},{9,1},{17,9},{25,17},{2,26},{10... | collective-permute-start | bytes 122888 | tf_op jit(solution)/shard_map/ppermute | solution.py:44
  83.8 6.8 %collective-permute-start.14 = (bf16[128,2688]{1,0:T(8,128)(2,1)S(1)}, bf16[128,2688]{1,0:T(8,128)(2,1)S(1)}, u32[]{:S(2)}, u32[]{:S(2)}) collective-permute-start(bf16[128,2688]{1,0:T(8,128)(2,1)S(1)} %get-tuple-element.48), channel_id=1, source_target_pairs={{0,1},{1,0},{2,3},{3,2},{4,5},{5,4},{6,7},{7,6},{8,9},{9,8},{10,11... | collective-permute-start | bytes 2064392 | tf_op jit(solution)/shard_map/ppermute | solution.py:44
  90.8 10.5 %collective-permute-start.15 = (bf16[32,2688]{1,0:T(8,128)(2,1)S(1)}, bf16[32,2688]{1,0:T(8,128)(2,1)S(1)}, u32[]{:S(2)}, u32[]{:S(2)}) collective-permute-start(bf16[32,2688]{1,0:T(8,128)(2,1)S(1)} %get-tuple-element.50), channel_id=1, source_target_pairs={{0,2},{2,4},{4,6},{6,0},{1,3},{3,5},{5,7},{7,1},{8,10},{10,12},{12... | collective-permute-start | bytes 516104 | tf_op jit(solution)/shard_map/ppermute | solution.py:44
  91.3 10.1 %collective-permute-start.16 = (bf16[32,2688]{1,0:T(8,128)(2,1)S(1)}, bf16[32,2688]{1,0:T(8,128)(2,1)S(1)}, u32[]{:S(2)}, u32[]{:S(2)}) collective-permute-start(bf16[32,2688]{1,0:T(8,128)(2,1)S(1)} %get-tuple-element.51), channel_id=1, source_target_pairs={{0,4},{2,6},{4,0},{6,2},{1,5},{3,7},{5,1},{7,3},{8,12},{10,14},{12... | collective-permute-start | bytes 516104 | tf_op jit(solution)/shard_map/ppermute | solution.py:44
  91.8 9.9 %collective-permute-start.17 = (bf16[32,2688]{1,0:T(8,128)(2,1)S(1)}, bf16[32,2688]{1,0:T(8,128)(2,1)S(1)}, u32[]{:S(2)}, u32[]{:S(2)}) collective-permute-start(bf16[32,2688]{1,0:T(8,128)(2,1)S(1)} %get-tuple-element.52), channel_id=1, source_target_pairs={{0,6},{2,0},{4,2},{6,4},{1,7},{3,1},{5,3},{7,5},{8,14},{10,8},{12,... | collective-permute-start | bytes 516104 | tf_op jit(solution)/shard_map/ppermute | solution.py:44
  (19 other events, 29.1 us)

commit v2 on v1

--- a/solution.py
+++ b/solution.py
@@ -48,28 +48,29 @@
     return pl.ds(pl.multiple_of(index * rows, rows), rows)
 
 
-def project_kernel(t0, t1, t2, t3, o0, o1, o2, o3, w, all_out, pre_out, tail_out, dt_out):
+def project_kernel(t0, t1, t2, t3, o0, o1, o2, o3, w, w_bc, w_dt, early, all_out, pre_out, tail_out, dt_out, w_steps):
     y, c = lax.axis_index("y"), lax.axis_index("c")
     for d, (own, other) in enumerate(((t0, o0), (t1, o1), (t2, o2), (t3, o3))):
         source = lax.rem(y + 4 - d, 4)
         all_out[row_at(source * 2 + c, ROWS), :] = own[...]
         all_out[row_at(source * 2 + 1 - c, ROWS), :] = other[...]
     tokens = all_out[...]
-    for n in range(4):
-        cols = slice(256 * n, 256 * n + 256)
-        part = jnp.dot(tokens, w[:, cols], preferred_element_type=F32)
-        if n < 3:
-            pre_out[:, cols] = part.astype(BF)
-            tail_out[:, cols] = part[BLOCK - 8 :].astype(BF)
-        else:
-            pre_out[:, 768:896] = part[:, :128].astype(BF)
-            tail_out[:, 768:896] = part[BLOCK - 8 :, :128].astype(BF)
-            dt_out[...] = part[:, 128:]
+    w_steps[...] = jnp.zeros(w_steps.shape, BF)
+    w_steps[0 : w_dt.shape[0], :] = w_dt[...]
+    for lo, hi in ((0, 256), (256, 512), (512, WIDTH)):
+        part = jnp.dot(tokens, w[:, lo:hi], preferred_element_type=F32).astype(BF)
+        pre_out[:, lo:hi] = part
+        tail_out[:, lo:hi] = part[BLOCK - 8 :]
+    part = jnp.dot(tokens, w_bc[...], preferred_element_type=F32).astype(BF)
+    pre_out[:, WIDTH:] = part
+    tail_out[:, WIDTH:] = part[BLOCK - 8 :]
+    dt_out[...] = lax.dot_general(tokens, w_steps[...], (((1,), (1,)), ((), ())), preferred_element_type=F32)
 
 
 def gate_kernel(tokens, w, out):
-    gate = jnp.dot(tokens[...], w[...], preferred_element_type=F32).astype(BF).astype(F32)
-    out[...] = jax.nn.silu(gate)
+    for lo, hi in ((0, 256), (256, 512), (512, WIDTH)):
+        gate = jnp.dot(tokens[...], w[:, WIDTH + lo : WIDTH + hi], preferred_element_type=F32)
+        out[:, lo:hi] = jax.nn.silu(gate.astype(BF).astype(F32))
 
 
 def spread(value, pair):
@@ -92,13 +93,35 @@
 
 
 def local_kernel(
-    pre, tail, dt_pre, conv_x, conv_bc, bias, a_log, v_out, b_out, c_out, dt_out, cum_out, p0, p1, p2, p3, ext, state
+    pre,
+    tail,
+    dt_pre,
+    conv_x,
+    conv_bc,
+    bias,
+    a_log,
+    before,
+    v_out,
+    b_out,
+    c_out,
+    dt_out,
+    cum_out,
+    p0,
+    p1,
+    p2,
+    p3,
+    ext,
+    state,
+    small,
 ):
     x = lax.axis_index("x")
     ext[0:8, :] = tail[...].astype(F32)
     ext[8 : 8 + BLOCK, :] = pre[...].astype(F32)
-    step = jax.nn.softplus(dt_pre[...] + bias[...])
-    decay = step * (-jnp.exp(a_log[...]))
+    small[...] = jnp.zeros(small.shape, F32)
+    small[0:1, 0 : bias.shape[1]] = bias[...]
+    small[1:2, 0 : bias.shape[1]] = a_log[...]
+    step = jax.nn.softplus(dt_pre[...] + small[0:1, :])
+    decay = step * (-jnp.exp(small[1:2, :]))
     row = lax.broadcasted_iota(jnp.int32, decay.shape, 0)
     cum = decay
     for k in (1, 2, 4, 8, 16, 32, 64, 128):
@@ -162,7 +185,7 @@
     return held[k, 32:33, :] + held[k, 33:34, :]
 
 
-def row_total_kernel(q0, q1, q2, q3, out, held):
+def row_total_kernel(q0, q1, q2, q3, before, out, held):
     load_rows((q0, q1, q2, q3), held)
     total, factor = held[0, 0:32, :], factor_of(held, 0)
     for k in range(1, 4):
@@ -249,29 +272,27 @@
 
 
 def body(tokens, w_xz, w_bc, w_dt, dt_bias, a_log, conv_x, conv_bc, norm_gain, w_out):
-    heads = w_dt.shape[1]
-    lanes = ((0, 0), (0, 128 - heads))
     near = [tokens] + [shifted(tokens, "y", d) for d in (1, 2, 3)]
+    w_both = w_xz.reshape(MODEL, 2 * WIDTH)
+    near[1:] = [lax.optimization_barrier((piece, w_both))[0] for piece in near[1:]]
     far = [shifted(piece, "c", 1) for piece in near]
-    w_first = jnp.concatenate([w_xz[:, 0], w_bc, jnp.pad(w_dt, lanes)], axis=1)
-    w_gate = w_xz[:, 1]
-    bias = jnp.pad(dt_bias[None], lanes)
-    rates = jnp.pad(a_log[None], lanes)
+    gain = norm_gain[None]
     everything, pre, tail, dt_pre = call(
         project_kernel,
         [((BLOCK, MODEL), BF), ((BLOCK, PRE), BF), ((8, PRE), BF), ((BLOCK, 128), F32)],
-        [*near, *far, w_first],
+        [*near, *far, w_both, w_bc, w_dt.T, gain],
+        scratch=[((128, MODEL), BF)],
         flops=2 * BLOCK * MODEL * 1024,
         name="project",
     )
     tail = lax.ppermute(tail, SEQ, [(i, i + 1) for i in range(31)])
-    (gate,) = call(gate_kernel, [((BLOCK, WIDTH), F32)], [everything, w_gate], flops=2 * BLOCK * MODEL * WIDTH, name="gate")
+    (gate,) = call(gate_kernel, [((BLOCK, WIDTH), F32)], [everything, w_both], flops=2 * BLOCK * MODEL * WIDTH, name="gate")
     v, b, c, step, cum, p0, p1, p2, p3 = call(
         local_kernel,
         [((BLOCK, WIDTH), BF), ((BLOCK, STATE), BF), ((BLOCK, STATE), BF), ((BLOCK, 128), F32), ((BLOCK, 128), F32)]
         + [((PIECE, WIDTH), BF)] * 4,
-        [pre, tail, dt_pre, conv_x, conv_bc, bias, rates],
-        scratch=[((BLOCK + 8, PRE), F32), ((STATE, WIDTH), F32)],
+        [pre, tail, dt_pre, conv_x, conv_bc, dt_bias[None], a_log[None], gate],
+        scratch=[((BLOCK + 8, PRE), F32), ((STATE, WIDTH), F32), ((8, 128), F32)],
         flops=2 * BLOCK * STATE * WIDTH,
         name="local",
     )
@@ -279,7 +300,7 @@
     (inside,) = call(
         inside_kernel, [((BLOCK, WIDTH), F32)], [v, b, c, step, cum], flops=20 * BLOCK * BLOCK * 256, name="inside"
     )
-    (totals,) = call(row_total_kernel, [((8, PIECE, WIDTH), BF)], rows, scratch=[((4, PIECE, WIDTH), F32)], name="rowtotal")
+    (totals,) = call(row_total_kernel, [((8, PIECE, WIDTH), BF)], [*rows, inside], scratch=[((4, PIECE, WIDTH), F32)], name="rowtotal")
     totals = lax.all_to_all(totals, "z", 0, 0, tiled=True)
     e0, e1, e2, e3 = call(
         incoming_kernel,
@@ -292,7 +313,7 @@
     g, squares, send = call(
         gated_kernel,
         [((BLOCK, WIDTH), BF), ((BLOCK, 128), F32), ((128, WIDE), BF)],
-        [*states, c, cum, inside, gate, norm_gain[None], w_out],
+        [*states, c, cum, inside, gate, gain, w_out],
         scratch=[((STATE, WIDTH), BF), ((128, WIDTH), BF)],
         flops=2 * 128 * WIDTH * MODEL,
         name="gated",

time: 103 us -> 80.9 us (0.79)
  local copies, waits for them, and re-layouts: 32.4 us -> 4.15 us
  blocking collectives: 0 us -> 20.9 us
  starting transfers between devices: 38.2 us -> 28.4 us
  other arithmetic: 3.11 us -> 0 us
  Pallas kernels: 10.1 us -> 8.71 us
    all_to_all x0 -> x1, blocking collectives: none -> 20.9 us  [body(): totals = lax.all_to_all(totals, 'z', 0, 0, tiled=True)]
    unnamed x51 -> x19, local copies, waits for them, and re-layouts: 18.4 us -> 4.15 us
    slice x1 -> x0, local copies, waits for them, and re-layouts: 14 us -> none  [body(): w_gate = w_xz[:, 1]]
    all_to_all x1 -> x0, starting transfers between devices: 10.4 us -> none  [body(): totals = lax.all_to_all(totals, 'z', 0, 0, tiled=True)]
    ppermute x17, waiting for transfers between devices: 12.1 us -> 18.5 us  [shifted(): lax.ppermute(value, axis, [(i, (i + steps) % size) for i in range(size)])]
    all_to_all x1 -> x0, waiting for transfers between devices: 5.53 us -> none  [body(): totals = lax.all_to_all(totals, 'z', 0, 0, tiled=True)]
    concatenate x1 -> x0, other arithmetic: 3.11 us -> none  [body(): w_first = jnp.concatenate([w_xz[:, 0], w_bc, jnp.pad(w_dt, lanes)], axis=1)]
    pallas_call x10, Pallas kernels: 10.1 us -> 8.71 us  [call(): pl.pallas_call(body, out_shape=[jax.ShapeDtypeStruct(s, t) for s, t in ou...]
  transfers between devices with their start and end apart: 19 -> 18, of which waited for: 6 -> 10; matrix products, arithmetic and copies ran while one was open for 24% -> 5% of each run, Pallas kernels for 3% -> 4%
where the time goes in v2:
time: 80.9 us; the launch traced here: 80.8 us
  starting transfers between devices  28.4 us (35%)
  blocking collectives  20.9 us (26%)
  waiting for transfers between devices  18.5 us (23%)
  Pallas kernels  8.71 us (11%)
  local copies, waits for them, and re-layouts  4.15 us (5%)
    ppermute x17, starting transfers between devices, shifted(): lax.ppermute(value, axis, [(i, (i + steps) % size) for i in range(size)])  25.3 us
    all_to_all x1, blocking collectives, body(): totals = lax.all_to_all(totals, 'z', 0, 0, tiled=True)  20.9 us
    ppermute x17, waiting for transfers between devices, shifted(): lax.ppermute(value, axis, [(i, (i + steps) % size) for i in range(size)])  18.5 us
    pallas_call x10, Pallas kernels, call(): pl.pallas_call(body, out_shape=[jax.ShapeDtypeStruct(s, t) for s, t in ou...  8.71 us
    unnamed x19, local copies, waits for them, and re-layouts  4.15 us
    ppermute x1, starting transfers between devices, body(): tail = lax.ppermute(tail, SEQ, [(i, i + 1) for i in range(31)])  3.12 us
  transfers between devices with their start and end apart: 18, of which 10 were waited for; matrix products, arithmetic and copies ran while one was open for 5% of the time, Pallas kernels for 4%

profile of v2, /device:TPU:1, one launch (start us, length us, event | category | flops | bytes accessed | tf_op | source)
XLA Modules:
  0.0 80.8 jit_solution(13425311133293637494)
XLA Ops:
  0.0 3.6 %collective-permute-start.2 = (bf16[32,2560]{1,0:T(8,128)(2,1)}, bf16[32,2560]{1,0:T(8,128)(2,1)S(1)}, u32[]{:S(2)}, u32[]{:S(2)}) collective-permute-start(bf16[32,2560]{1,0:T(8,128)(2,1)} %t0.1), channel_id=1, source_target_pairs={{0,6},{2,0},{4,2},{6,4},{1,7},{3,1},{5,3},{7,5},{8,14},{10,8},{12,... | collective-permute-start | bytes 491528 | tf_op jit(solution)/shard_map/ppermute | solution.py:44
  4.6 1.5 %collective-permute-start.3 = (bf16[32,2560]{1,0:T(8,128)(2,1)}, bf16[32,2560]{1,0:T(8,128)(2,1)S(1)}, u32[]{:S(2)}, u32[]{:S(2)}) collective-permute-start(bf16[32,2560]{1,0:T(8,128)(2,1)} %t0.1), channel_id=1, source_target_pairs={{0,1},{1,0},{2,3},{3,2},{4,5},{5,4},{6,7},{7,6},{8,9},{9,8},{10,11... | collective-permute-start | bytes 491528 | tf_op jit(solution)/shard_map/ppermute | solution.py:44
  6.1 4.1 %copy.11 = bf16[320,8,2,640]{3,1,2,0:T(8,128)(2,1)S(1)} copy(bf16[320,8,2,640]{3,2,1,0:T(2,128)(2,1)} %bitcast.10) | data formatting | bytes 13107200
  10.2 4.7 %collective-permute-done.t1 = bf16[32,2560]{1,0:T(8,128)(2,1)S(1)} collective-permute-done((bf16[32,2560]{1,0:T(8,128)(2,1)}, bf16[32,2560]{1,0:T(8,128)(2,1)S(1)}, u32[]{:S(2)}, u32[]{:S(2)}) %collective-permute-start) | collective-permute-done | bytes 163872 | tf_op jit(solution)/shard_map/ppermute | solution.py:44
  17.0 1.9 %project.1 = (bf16[256,2560]{1,0:T(8,128)(2,1)S(1)}, bf16[256,896]{1,0:T(8,128)(2,1)S(1)}, bf16[8,896]{1,0:T(8,128)(2,1)S(1)}, f32[256,128]{1,0:T(8,128)S(1)}) custom-call(bf16[32,2560]{1,0:T(8,128)(2,1)S(1)} %copy-done.2, bf16[32,2560]{1,0:T(8,128)(2,1)S(1)} %collective-permute-done.t1, bf16[32,2560]{1,0:T(8,128)(2,1)S(1)} %collective-permute-done.1.t2, ...), custom_call_target="tpu_custom_call" | custom-call | flops 1342177280 | bytes 2684354 | tf_op jit(solution)/shard_map/project/pallas_call | solution.py:30
  19.0 3.1 %collective-permute-start.7 = (bf16[8,896]{1,0:T(8,128)(2,1)S(1)}, bf16[8,896]{1,0:T(8,128)(2,1)S(1)}, u32[]{:S(2)}, u32[]{:S(2)}) collective-permute-start(bf16[8,896]{1,0:T(8,128)(2,1)S(1)} %get-tuple-element.36), channel_id=1, source_target_pairs={{0,8},{8,16},{16,24},{24,32},{32,40},{40,48},{48,56},{56,64},{64,7... | collective-permute-start | bytes 43016 | tf_op jit(solution)/shard_map/ppermute | solution.py:288
  22.2 1.2 %gate.1.before = f32[256,640]{1,0:T(8,128)S(1)} custom-call(bf16[256,2560]{1,0:T(8,128)(2,1)S(1)} %get-tuple-element.38.tokens, bf16[2560,1280]{1,0:T(8,128)(2,1)S(1)} %bitcast.6), custom_call_target="tpu_custom_call" | custom-call | flops 838860800 | bytes 1677721 | tf_op jit(solution)/shard_map/gate/pallas_call | solution.py:30
  23.4 1.5 %local.1 = (bf16[256,640]{1,0:T(8,128)(2,1)S(1)}, bf16[256,128]{1,0:T(8,128)(2,1)S(1)}, bf16[256,128]{1,0:T(8,128)(2,1)S(1)}, f32[256,128]{1,0:T(8,128)S(1)}, f3...) custom-call(bf16[256,896]{1,0:T(8,128)(2,1)S(1)} %get-tuple-element., ...), custom_call_target="tpu_custom_call" | custom-call | flops 41943040 | bytes 83886 | tf_op jit(solution)/shard_map/local/pallas_call | solution.py:30
  24.9 1.3 %collective-permute-start.8 = (bf16[40,640]{1,0:T(8,128)(2,1)S(1)}, bf16[40,640]{1,0:T(8,128)(2,1)S(1)}, u32[]{:S(2)}, u32[]{:S(2)}) collective-permute-start(bf16[40,640]{1,0:T(8,128)(2,1)S(1)} %get-tuple-element.40), channel_id=1, source_target_pairs={{0,8},{8,16},{16,24},{24,0},{1,9},{9,17},{17,25},{25,1},{2,10},{10... | collective-permute-start | bytes 153608 | tf_op jit(solution)/shard_map/ppermute | solution.py:44
  26.2 2.8 %collective-permute-start.9 = (bf16[40,640]{1,0:T(8,128)(2,1)S(1)}, bf16[40,640]{1,0:T(8,128)(2,1)S(1)}, u32[]{:S(2)}, u32[]{:S(2)}) collective-permute-start(bf16[40,640]{1,0:T(8,128)(2,1)S(1)} %get-tuple-element.41), channel_id=1, source_target_pairs={{0,16},{8,24},{16,0},{24,8},{1,17},{9,25},{17,1},{25,9},{2,18},{10... | collective-permute-start | bytes 153608 | tf_op jit(solution)/shard_map/ppermute | solution.py:44
  29.0 0.8 %collective-permute-start.10 = (bf16[40,640]{1,0:T(8,128)(2,1)S(1)}, bf16[40,640]{1,0:T(8,128)(2,1)S(1)}, u32[]{:S(2)}, u32[]{:S(2)}) collective-permute-start(bf16[40,640]{1,0:T(8,128)(2,1)S(1)} %get-tuple-element.42), channel_id=1, source_target_pairs={{0,24},{8,0},{16,8},{24,16},{1,25},{9,1},{17,9},{25,17},{2,26},{10... | collective-permute-start | bytes 153608 | tf_op jit(solution)/shard_map/ppermute | solution.py:44
  29.8 1.0 %inside.1.before = f32[256,640]{1,0:T(8,128)S(1)} custom-call(bf16[256,640]{1,0:T(8,128)(2,1)S(1)} %get-tuple-element.43.v, bf16[256,128]{1,0:T(8,128)(2,1)S(1)} %get-tuple-element.44.b, bf16[256,128]{1,0:T(8,128)(2,1)S(1)} %get-tuple-element.45.c, f32[256,128]{1,0:T(8,128)S(1)} %get-tuple-element.46.step, f32[256,128]{1,0:T(8,128)S(1)} %get-tuple-element.47.cum), custom_call_target="tpu_custom_call" | custom-call | flops 335544320 | bytes 671088 | tf_op jit(solution)/shard_map/inside/pallas_call | solution.py:30
  31.1 1.3 %collective-permute-done.10.q3 = bf16[40,640]{1,0:T(8,128)(2,1)S(1)} collective-permute-done((bf16[40,640]{1,0:T(8,128)(2,1)S(1)}, bf16[40,640]{1,0:T(8,128)(2,1)S(1)}, u32[]{:S(2)}, u32[]{:S(2)}) %collective-permute-start.10) | collective-permute-done | bytes 51232 | tf_op jit(solution)/shard_map/ppermute | solution.py:44
  32.5 20.9 %all_to_all.5.totals = bf16[8,40,640]{2,1,0:T(8,128)(2,1)S(1)} all-to-all(bf16[8,40,640]{2,1,0:T(8,128)(2,1)S(1)} %rowtotal.1), channel_id=1, replica_groups=mesh['z'=8,'x'=4,'y'=4,'c'=2] {'z'}, dimensions={0} | all-to-all | bytes 819200 | tf_op jit(solution)/shard_map/all_to_all | solution.py:304
  53.5 1.8 %collective-permute-start.11 = (bf16[32,640]{1,0:T(8,128)(2,1)S(1)}, bf16[32,640]{1,0:T(8,128)(2,1)S(1)}, u32[]{:S(2)}, u32[]{:S(2)}) collective-permute-start(bf16[32,640]{1,0:T(8,128)(2,1)S(1)} %get-tuple-element.49), channel_id=1, source_target_pairs={{0,8},{8,16},{16,24},{24,0},{1,9},{9,17},{17,25},{25,1},{2,10},{10... | collective-permute-start | bytes 122888 | tf_op jit(solution)/shard_map/ppermute | solution.py:44
  55.4 1.5 %collective-permute-start.12 = (bf16[32,640]{1,0:T(8,128)(2,1)S(1)}, bf16[32,640]{1,0:T(8,128)(2,1)S(1)}, u32[]{:S(2)}, u32[]{:S(2)}) collective-permute-start(bf16[32,640]{1,0:T(8,128)(2,1)S(1)} %get-tuple-element.50), channel_id=1, source_target_pairs={{0,16},{8,24},{16,0},{24,8},{1,17},{9,25},{17,1},{25,9},{2,18},{10... | collective-permute-start | bytes 122888 | tf_op jit(solution)/shard_map/ppermute | solution.py:44
  56.9 1.0 %collective-permute-start.13 = (bf16[32,640]{1,0:T(8,128)(2,1)S(1)}, bf16[32,640]{1,0:T(8,128)(2,1)S(1)}, u32[]{:S(2)}, u32[]{:S(2)}) collective-permute-start(bf16[32,640]{1,0:T(8,128)(2,1)S(1)} %get-tuple-element.51), channel_id=1, source_target_pairs={{0,24},{8,0},{16,8},{24,16},{1,25},{9,1},{17,9},{25,17},{2,26},{10... | collective-permute-start | bytes 122888 | tf_op jit(solution)/shard_map/ppermute | solution.py:44
  57.9 1.9 %collective-permute-done.12.e2 = bf16[32,640]{1,0:T(8,128)(2,1)S(1)} collective-permute-done((bf16[32,640]{1,0:T(8,128)(2,1)S(1)}, bf16[32,640]{1,0:T(8,128)(2,1)S(1)}, u32[]{:S(2)}, u32[]{:S(2)}) %collective-permute-start.12) | collective-permute-done | bytes 40992 | tf_op jit(solution)/shard_map/ppermute | solution.py:44
  59.7 1.2 %gated.1 = (bf16[256,640]{1,0:T(8,128)(2,1)S(1)}, f32[256,128]{1,0:T(8,128)S(1)}, bf16[128,2688]{1,0:T(8,128)(2,1)S(1)}) custom-call(bf16[32,640]{1,0:T(8,128)(2,1)S(1)} %get-tuple-element.48.e0, bf16[32,640]{1,0:T(8,128)(2,1)S(1)} %collective-permute-done.11.e1, bf16[32,640]{1,0:T(8,128)(2,1)S(1)} %collective-permute-done.12.e2, ...), custom_call_target="tpu_custom_call" | custom-call | flops 419430400 | bytes 838860 | tf_op jit(solution)/shard_map/gated/pallas_call | solution.py:30
  61.0 6.1 %collective-permute-start.14 = (bf16[128,2688]{1,0:T(8,128)(2,1)S(1)}, bf16[128,2688]{1,0:T(8,128)(2,1)S(1)}, u32[]{:S(2)}, u32[]{:S(2)}) collective-permute-start(bf16[128,2688]{1,0:T(8,128)(2,1)S(1)} %get-tuple-element.54), channel_id=1, source_target_pairs={{0,1},{1,0},{2,3},{3,2},{4,5},{5,4},{6,7},{7,6},{8,9},{9,8},{10,11... | collective-permute-start | bytes 2064392 | tf_op jit(solution)/shard_map/ppermute | solution.py:44
  67.8 1.1 %collective-permute-done.14.came = bf16[128,2688]{1,0:T(8,128)(2,1)S(1)} collective-permute-done((bf16[128,2688]{1,0:T(8,128)(2,1)S(1)}, bf16[128,2688]{1,0:T(8,128)(2,1)S(1)}, u32[]{:S(2)}, u32[]{:S(2)}) %collective-permute-start.14) | collective-permute-done | bytes 688160 | tf_op jit(solution)/shard_map/ppermute | solution.py:44
  69.2 1.5 %collective-permute-start.16 = (bf16[32,2688]{1,0:T(8,128)(2,1)S(1)}, bf16[32,2688]{1,0:T(8,128)(2,1)S(1)}, u32[]{:S(2)}, u32[]{:S(2)}) collective-permute-start(bf16[32,2688]{1,0:T(8,128)(2,1)S(1)} %get-tuple-element.57), channel_id=1, source_target_pairs={{0,4},{2,6},{4,0},{6,2},{1,5},{3,7},{5,1},{7,3},{8,12},{10,14},{12... | collective-permute-start | bytes 516104 | tf_op jit(solution)/shard_map/ppermute | solution.py:44
  70.7 1.1 %collective-permute-start.17 = (bf16[32,2688]{1,0:T(8,128)(2,1)S(1)}, bf16[32,2688]{1,0:T(8,128)(2,1)S(1)}, u32[]{:S(2)}, u32[]{:S(2)}) collective-permute-start(bf16[32,2688]{1,0:T(8,128)(2,1)S(1)} %get-tuple-element.58), channel_id=1, source_target_pairs={{0,6},{2,0},{4,2},{6,4},{1,7},{3,1},{5,3},{7,5},{8,14},{10,8},{12,... | collective-permute-start | bytes 516104 | tf_op jit(solution)/shard_map/ppermute | solution.py:44
  71.8 7.8 %collective-permute-done.15.g1 = bf16[32,2688]{1,0:T(8,128)(2,1)S(1)} collective-permute-done((bf16[32,2688]{1,0:T(8,128)(2,1)S(1)}, bf16[32,2688]{1,0:T(8,128)(2,1)S(1)}, u32[]{:S(2)}, u32[]{:S(2)}) %collective-permute-start.15) | collective-permute-done | bytes 172064 | tf_op jit(solution)/shard_map/ppermute | solution.py:44
  (43 shorter events, 6.0 us)
Async XLA Ops:
  0.0 10.2 %collective-permute-start.2 = (bf16[32,2560]{1,0:T(8,128)(2,1)}, bf16[32,2560]{1,0:T(8,128)(2,1)S(1)}, u32[]{:S(2)}, u32[]{:S(2)}) collective-permute-start(bf16[32,2560]{1,0:T(8,128)(2,1)} %t0.1), channel_id=1, source_target_pairs={{0,6},{2,0},{4,2},{6,4},{1,7},{3,1},{5,3},{7,5},{8,14},{10,8},{12,... | collective-permute-start | bytes 491528 | tf_op jit(solution)/shard_map/ppermute | solution.py:44
  3.6 6.7 %collective-permute-start.1 = (bf16[32,2560]{1,0:T(8,128)(2,1)}, bf16[32,2560]{1,0:T(8,128)(2,1)S(1)}, u32[]{:S(2)}, u32[]{:S(2)}) collective-permute-start(bf16[32,2560]{1,0:T(8,128)(2,1)} %t0.1), channel_id=1, source_target_pairs={{0,4},{2,6},{4,0},{6,2},{1,5},{3,7},{5,1},{7,3},{8,12},{10,14},{12... | collective-permute-start | bytes 491528 | tf_op jit(solution)/shard_map/ppermute | solution.py:44
  3.9 11.0 %collective-permute-start = (bf16[32,2560]{1,0:T(8,128)(2,1)}, bf16[32,2560]{1,0:T(8,128)(2,1)S(1)}, u32[]{:S(2)}, u32[]{:S(2)}) collective-permute-start(bf16[32,2560]{1,0:T(8,128)(2,1)} %t0.1), channel_id=1, source_target_pairs={{0,2},{2,4},{4,6},{6,0},{1,3},{3,5},{5,7},{7,1},{8,10},{10,12},{12... | collective-permute-start | bytes 491528 | tf_op jit(solution)/shard_map/ppermute | solution.py:44
  4.6 11.3 %collective-permute-start.3 = (bf16[32,2560]{1,0:T(8,128)(2,1)}, bf16[32,2560]{1,0:T(8,128)(2,1)S(1)}, u32[]{:S(2)}, u32[]{:S(2)}) collective-permute-start(bf16[32,2560]{1,0:T(8,128)(2,1)} %t0.1), channel_id=1, source_target_pairs={{0,1},{1,0},{2,3},{3,2},{4,5},{5,4},{6,7},{7,6},{8,9},{9,8},{10,11... | collective-permute-start | bytes 491528 | tf_op jit(solution)/shard_map/ppermute | solution.py:44
  6.1 9.8 %copy-start.8 = (f32[640]{0:T(1024)S(1)}, f32[640]{0:T(1024)}, u32[]{:S(2)}) copy-start(f32[640]{0:T(1024)} %param.18) | copy-start | bytes 7684
  6.1 10.9 %copy-start.1 = (bf16[2560,256]{1,0:T(8,128)(2,1)S(1)}, bf16[2560,256]{1,0:T(8,128)(2,1)}, u32[]{:S(2)}) copy-start(bf16[2560,256]{1,0:T(8,128)(2,1)} %w_bc.1) | copy-start | bytes 3932164
  6.1 10.9 %copy-start.2 = (bf16[32,2560]{1,0:T(8,128)(2,1)S(1)}, bf16[32,2560]{1,0:T(8,128)(2,1)}, u32[]{:S(2)}) copy-start(bf16[32,2560]{1,0:T(8,128)(2,1)} %t0.1) | copy-start | bytes 491524
  6.1 10.9 %copy-start.3 = (bf16[2560,10]{0,1:T(8,128)(2,1)S(1)}, bf16[2560,10]{0,1:T(8,128)(2,1)}, u32[]{:S(2)}) copy-start(bf16[2560,10]{0,1:T(8,128)(2,1)} %param.13) | copy-start | bytes 153604
  14.9 1.5 %collective-permute-start.4 = (bf16[32,2560]{1,0:T(8,128)(2,1)S(1)}, bf16[32,2560]{1,0:T(8,128)(2,1)S(1)}, u32[]{:S(2)}, u32[]{:S(2)}) collective-permute-start(bf16[32,2560]{1,0:T(8,128)(2,1)S(1)} %collective-permute-done.t1), channel_id=1, source_target_pairs={{0,1},{1,0},{2,3},{3,2},{4,5},{5,4},{6,7},{7,6},{8,9},{9,8},{10,11... | collective-permute-start | bytes 491528 | tf_op jit(solution)/shard_map/ppermute | solution.py:44
  15.4 1.4 %collective-permute-start.5 = (bf16[32,2560]{1,0:T(8,128)(2,1)S(1)}, bf16[32,2560]{1,0:T(8,128)(2,1)S(1)}, u32[]{:S(2)}, u32[]{:S(2)}) collective-permute-start(bf16[32,2560]{1,0:T(8,128)(2,1)S(1)} %collective-permute-done.1.t2), channel_id=1, source_target_pairs={{0,1},{1,0},{2,3},{3,2},{4,5},{5,4},{6,7},{7,6},{8,9},{9,8},{10,11... | collective-permute-start | bytes 491528 | tf_op jit(solution)/shard_map/ppermute | solution.py:44
  15.4 1.6 %collective-permute-start.6 = (bf16[32,2560]{1,0:T(8,128)(2,1)S(1)}, bf16[32,2560]{1,0:T(8,128)(2,1)S(1)}, u32[]{:S(2)}, u32[]{:S(2)}) collective-permute-start(bf16[32,2560]{1,0:T(8,128)(2,1)S(1)} %collective-permute-done.2.t3), channel_id=1, source_target_pairs={{0,1},{1,0},{2,3},{3,2},{4,5},{5,4},{6,7},{7,6},{8,9},{9,8},{10,11... | collective-permute-start | bytes 491528 | tf_op jit(solution)/shard_map/ppermute | solution.py:44
  19.0 4.4 %collective-permute-start.7 = (bf16[8,896]{1,0:T(8,128)(2,1)S(1)}, bf16[8,896]{1,0:T(8,128)(2,1)S(1)}, u32[]{:S(2)}, u32[]{:S(2)}) collective-permute-start(bf16[8,896]{1,0:T(8,128)(2,1)S(1)} %get-tuple-element.36), channel_id=1, source_target_pairs={{0,8},{8,16},{16,24},{24,32},{32,40},{40,48},{48,56},{56,64},{64,7... | collective-permute-start | bytes 43016 | tf_op jit(solution)/shard_map/ppermute | solution.py:288
  22.1 1.3 %copy-start.4 = (bf16[4,640]{1,0:T(4,128)(2,1)S(1)}, bf16[4,640]{1,0:T(4,128)(2,1)}, u32[]{:S(2)}) copy-start(bf16[4,640]{1,0:T(4,128)(2,1)} %conv_x.1) | copy-start | bytes 15364
  23.4 36.4 %copy-start = (bf16[640,2560]{1,0:T(8,128)(2,1)S(1)}, bf16[640,2560]{1,0:T(8,128)(2,1)}, u32[]{:S(2)}) copy-start(bf16[640,2560]{1,0:T(8,128)(2,1)} %w.3) | copy-start | bytes 9830404
  24.9 5.9 %collective-permute-start.8 = (bf16[40,640]{1,0:T(8,128)(2,1)S(1)}, bf16[40,640]{1,0:T(8,128)(2,1)S(1)}, u32[]{:S(2)}, u32[]{:S(2)}) collective-permute-start(bf16[40,640]{1,0:T(8,128)(2,1)S(1)} %get-tuple-element.40), channel_id=1, source_target_pairs={{0,8},{8,16},{16,24},{24,0},{1,9},{9,17},{17,25},{25,1},{2,10},{10... | collective-permute-start | bytes 153608 | tf_op jit(solution)/shard_map/ppermute | solution.py:44
  26.2 4.9 %collective-permute-start.9 = (bf16[40,640]{1,0:T(8,128)(2,1)S(1)}, bf16[40,640]{1,0:T(8,128)(2,1)S(1)}, u32[]{:S(2)}, u32[]{:S(2)}) collective-permute-start(bf16[40,640]{1,0:T(8,128)(2,1)S(1)} %get-tuple-element.41), channel_id=1, source_target_pairs={{0,16},{8,24},{16,0},{24,8},{1,17},{9,25},{17,1},{25,9},{2,18},{10... | collective-permute-start | bytes 153608 | tf_op jit(solution)/shard_map/ppermute | solution.py:44
  29.0 3.4 %collective-permute-start.10 = (bf16[40,640]{1,0:T(8,128)(2,1)S(1)}, bf16[40,640]{1,0:T(8,128)(2,1)S(1)}, u32[]{:S(2)}, u32[]{:S(2)}) collective-permute-start(bf16[40,640]{1,0:T(8,128)(2,1)S(1)} %get-tuple-element.42), channel_id=1, source_target_pairs={{0,24},{8,0},{16,8},{24,16},{1,25},{9,1},{17,9},{25,17},{2,26},{10... | collective-permute-start | bytes 153608 | tf_op jit(solution)/shard_map/ppermute | solution.py:44
  53.5 4.3 %collective-permute-start.11 = (bf16[32,640]{1,0:T(8,128)(2,1)S(1)}, bf16[32,640]{1,0:T(8,128)(2,1)S(1)}, u32[]{:S(2)}, u32[]{:S(2)}) collective-permute-start(bf16[32,640]{1,0:T(8,128)(2,1)S(1)} %get-tuple-element.49), channel_id=1, source_target_pairs={{0,8},{8,16},{16,24},{24,0},{1,9},{9,17},{17,25},{25,1},{2,10},{10... | collective-permute-start | bytes 122888 | tf_op jit(solution)/shard_map/ppermute | solution.py:44
  55.4 4.4 %collective-permute-start.12 = (bf16[32,640]{1,0:T(8,128)(2,1)S(1)}, bf16[32,640]{1,0:T(8,128)(2,1)S(1)}, u32[]{:S(2)}, u32[]{:S(2)}) collective-permute-start(bf16[32,640]{1,0:T(8,128)(2,1)S(1)} %get-tuple-element.50), channel_id=1, source_target_pairs={{0,16},{8,24},{16,0},{24,8},{1,17},{9,25},{17,1},{25,9},{2,18},{10... | collective-permute-start | bytes 122888 | tf_op jit(solution)/shard_map/ppermute | solution.py:44
  56.9 2.9 %collective-permute-start.13 = (bf16[32,640]{1,0:T(8,128)(2,1)S(1)}, bf16[32,640]{1,0:T(8,128)(2,1)S(1)}, u32[]{:S(2)}, u32[]{:S(2)}) collective-permute-start(bf16[32,640]{1,0:T(8,128)(2,1)S(1)} %get-tuple-element.51), channel_id=1, source_target_pairs={{0,24},{8,0},{16,8},{24,16},{1,25},{9,1},{17,9},{25,17},{2,26},{10... | collective-permute-start | bytes 122888 | tf_op jit(solution)/shard_map/ppermute | solution.py:44
  61.0 7.9 %collective-permute-start.14 = (bf16[128,2688]{1,0:T(8,128)(2,1)S(1)}, bf16[128,2688]{1,0:T(8,128)(2,1)S(1)}, u32[]{:S(2)}, u32[]{:S(2)}) collective-permute-start(bf16[128,2688]{1,0:T(8,128)(2,1)S(1)} %get-tuple-element.54), channel_id=1, source_target_pairs={{0,1},{1,0},{2,3},{3,2},{4,5},{5,4},{6,7},{7,6},{8,9},{9,8},{10,11... | collective-permute-start | bytes 2064392 | tf_op jit(solution)/shard_map/ppermute | solution.py:44
  69.1 10.5 %collective-permute-start.15 = (bf16[32,2688]{1,0:T(8,128)(2,1)S(1)}, bf16[32,2688]{1,0:T(8,128)(2,1)S(1)}, u32[]{:S(2)}, u32[]{:S(2)}) collective-permute-start(bf16[32,2688]{1,0:T(8,128)(2,1)S(1)} %get-tuple-element.56), channel_id=1, source_target_pairs={{0,2},{2,4},{4,6},{6,0},{1,3},{3,5},{5,7},{7,1},{8,10},{10,12},{12... | collective-permute-start | bytes 516104 | tf_op jit(solution)/shard_map/ppermute | solution.py:44
  69.2 10.4 %collective-permute-start.16 = (bf16[32,2688]{1,0:T(8,128)(2,1)S(1)}, bf16[32,2688]{1,0:T(8,128)(2,1)S(1)}, u32[]{:S(2)}, u32[]{:S(2)}) collective-permute-start(bf16[32,2688]{1,0:T(8,128)(2,1)S(1)} %get-tuple-element.57), channel_id=1, source_target_pairs={{0,4},{2,6},{4,0},{6,2},{1,5},{3,7},{5,1},{7,3},{8,12},{10,14},{12... | collective-permute-start | bytes 516104 | tf_op jit(solution)/shard_map/ppermute | solution.py:44
  70.7 9.3 %collective-permute-start.17 = (bf16[32,2688]{1,0:T(8,128)(2,1)S(1)}, bf16[32,2688]{1,0:T(8,128)(2,1)S(1)}, u32[]{:S(2)}, u32[]{:S(2)}) collective-permute-start(bf16[32,2688]{1,0:T(8,128)(2,1)S(1)} %get-tuple-element.58), channel_id=1, source_target_pairs={{0,6},{2,0},{4,2},{6,4},{1,7},{3,1},{5,3},{7,5},{8,14},{10,8},{12,... | collective-permute-start | bytes 516104 | tf_op jit(solution)/shard_map/ppermute | solution.py:44
  (3 other events, 3.8 us)

commit v3 on v2

--- a/solution.py
+++ b/solution.py
@@ -185,26 +185,54 @@
     return held[k, 32:33, :] + held[k, 33:34, :]
 
 
+def pack(out, total, factor):
+    out[0:32, :] = total.astype(BF)
+    out[32:40, :] = decay_rows(jnp.broadcast_to(factor, (8, WIDTH)))
+
+
+def unpack(ref):
+    return ref[0:32, :].astype(F32), ref[32:33, :].astype(F32) + ref[33:34, :].astype(F32)
+
+
+def follow(earlier, later):
+    return earlier[0] * later[1] + later[0], earlier[1] * later[1]
+
+
+def choose(test, yes, no):
+    return jnp.where(test, yes[0], no[0]), jnp.where(test, yes[1], no[1])
+
+
 def row_total_kernel(q0, q1, q2, q3, before, out, held):
     load_rows((q0, q1, q2, q3), held)
-    total, factor = held[0, 0:32, :], factor_of(held, 0)
+    total = held[0, 0:32, :], factor_of(held, 0)
     for k in range(1, 4):
-        a = factor_of(held, k)
-        total = total * a + held[k, 0:32, :]
-        factor = factor * a
-    extra = decay_rows(jnp.broadcast_to(factor, (8, WIDTH)))
-    for k in range(8):
-        out[k, 0:32, :] = total.astype(BF)
-        out[k, 32:40, :] = extra
-
-
-def incoming_kernel(q0, q1, q2, q3, totals, e0, e1, e2, e3, held, ready):
+        total = follow(total, (held[k, 0:32, :], factor_of(held, k)))
+    pack(out, *total)
+
+
+def two_rows(row, other):
+    odd = lax.rem(lax.axis_index("z"), 2) == 1
+    mine, theirs = unpack(row), unpack(other)
+    return odd, theirs, follow(choose(odd, theirs, mine), choose(odd, mine, theirs))
+
+
+def pair_total_kernel(row, other, out):
+    pack(out, *two_rows(row, other)[2])
+
+
+def quad_total_kernel(row, other, previous, out):
+    pack(out, *follow(unpack(previous), two_rows(row, other)[2]))
+
+
+def incoming_kernel(q0, q1, q2, q3, row, other, previous, low, high, e0, e1, e2, e3, held, ready):
     z, x = lax.axis_index("z"), lax.axis_index("x")
     load_rows((q0, q1, q2, q3), held)
-    carry = jnp.zeros((32, WIDTH), F32)
-    for k in range(7):
-        a = totals[k, 32:33, :].astype(F32) + totals[k, 33:34, :].astype(F32)
-        carry = jnp.where(k < z, carry * a + totals[k, 0:32, :].astype(F32), carry)
+    odd, theirs, _ = two_rows(row, other)
+    carry = choose(odd, theirs, (jnp.zeros((32, WIDTH), F32), jnp.ones((1, WIDTH), F32)))
+    second = lax.rem(z, 4) >= 2
+    carry = choose(second, follow(unpack(previous), carry), carry)
+    quad = choose(second, unpack(high), unpack(low))
+    carry, _ = choose(z >= 4, follow(quad, carry), carry)
     ready[0] = carry
     for k in range(3):
         carry = carry * factor_of(held, k) + held[k, 0:32, :]
@@ -300,12 +328,18 @@
     (inside,) = call(
         inside_kernel, [((BLOCK, WIDTH), F32)], [v, b, c, step, cum], flops=20 * BLOCK * BLOCK * 256, name="inside"
     )
-    (totals,) = call(row_total_kernel, [((8, PIECE, WIDTH), BF)], [*rows, inside], scratch=[((4, PIECE, WIDTH), F32)], name="rowtotal")
-    totals = lax.all_to_all(totals, "z", 0, 0, tiled=True)
+    piece = [((PIECE, WIDTH), BF)]
+    (row,) = call(row_total_kernel, piece, [*rows, inside], scratch=[((4, PIECE, WIDTH), F32)], name="rowtotal")
+    other = lax.ppermute(row, "z", [(i, i ^ 1) for i in range(8)])
+    (two,) = call(pair_total_kernel, piece, [row, other], name="pairtotal")
+    previous = lax.ppermute(two, "z", [(0, 2), (1, 3), (4, 6), (5, 7)])
+    (four,) = call(quad_total_kernel, piece, [row, other, previous], name="quadtotal")
+    low = lax.ppermute(four, "z", [(2, 4), (3, 5)])
+    high = lax.ppermute(four, "z", [(2, 6), (3, 7)])
     e0, e1, e2, e3 = call(
         incoming_kernel,
         [((32, WIDTH), BF)] * 4,
-        [*rows, totals],
+        [*rows, row, other, previous, low, high],
         scratch=[((4, PIECE, WIDTH), F32), ((4, 32, WIDTH), F32)],
         name="incoming",
     )

time: 80.9 us -> 81.4 us (level)
  the two profiles are of different devices: /device:TPU:1 before, /device:TPU:160 now
where the time goes in v3:
time: 81.4 us; the launch traced here: 81.3 us
  waiting for transfers between devices  40.8 us (50%)
  starting transfers between devices  27.3 us (34%)
  Pallas kernels  8.75 us (11%)
  local copies, waits for them, and re-layouts  4.15 us (5%)
    ppermute x17, waiting for transfers between devices, shifted(): lax.ppermute(value, axis, [(i, (i + steps) % size) for i in range(size)])  22.7 us
    ppermute x17, starting transfers between devices, shifted(): lax.ppermute(value, axis, [(i, (i + steps) % size) for i in range(size)])  16.5 us
    ppermute x1, waiting for transfers between devices, body(): low = lax.ppermute(four, 'z', [(2, 4), (3, 5)])  11.2 us
    pallas_call x12, Pallas kernels, call(): pl.pallas_call(body, out_shape=[jax.ShapeDtypeStruct(s, t) for s, t in ou...  8.75 us
    unnamed x19, local copies, waits for them, and re-layouts  4.14 us
    ppermute x1, starting transfers between devices, body(): tail = lax.ppermute(tail, SEQ, [(i, i + 1) for i in range(31)])  3.4 us
    ppermute x1, starting transfers between devices, body(): previous = lax.ppermute(two, 'z', [(0, 2), (1, 3), (4, 6), (5, 7)])  3.18 us
    ppermute x1, waiting for transfers between devices, body(): tail = lax.ppermute(tail, SEQ, [(i, i + 1) for i in range(31)])  3.05 us
  transfers between devices with their start and end apart: 22, of which 18 were waited for; matrix products, arithmetic and copies ran while one was open for 5% of the time, Pallas kernels for 3%

profile of v3, /device:TPU:160, one launch (start us, length us, event | category | flops | bytes accessed | tf_op | source)
XLA Modules:
  0.0 81.3 jit_solution(2637288106060213018)
XLA Ops:
  0.0 3.0 %collective-permute-start.2 = (bf16[32,2560]{1,0:T(8,128)(2,1)}, bf16[32,2560]{1,0:T(8,128)(2,1)S(1)}, u32[]{:S(2)}, u32[]{:S(2)}) collective-permute-start(bf16[32,2560]{1,0:T(8,128)(2,1)} %t0.1), channel_id=1, source_target_pairs={{0,6},{2,0},{4,2},{6,4},{1,7},{3,1},{5,3},{7,5},{8,14},{10,8},{12,... | collective-permute-start | bytes 491528 | tf_op jit(solution)/shard_map/ppermute | solution.py:44
  4.6 4.1 %copy.11 = bf16[320,8,2,640]{3,1,2,0:T(8,128)(2,1)S(1)} copy(bf16[320,8,2,640]{3,2,1,0:T(2,128)(2,1)} %bitcast.10) | data formatting | bytes 13107200
  8.7 1.6 %collective-permute-done.2.t3 = bf16[32,2560]{1,0:T(8,128)(2,1)S(1)} collective-permute-done((bf16[32,2560]{1,0:T(8,128)(2,1)}, bf16[32,2560]{1,0:T(8,128)(2,1)S(1)}, u32[]{:S(2)}, u32[]{:S(2)}) %collective-permute-start.2) | collective-permute-done | bytes 163872 | tf_op jit(solution)/shard_map/ppermute | solution.py:44
  10.3 1.5 %collective-permute-done.1.t2 = bf16[32,2560]{1,0:T(8,128)(2,1)S(1)} collective-permute-done((bf16[32,2560]{1,0:T(8,128)(2,1)}, bf16[32,2560]{1,0:T(8,128)(2,1)S(1)}, u32[]{:S(2)}, u32[]{:S(2)}) %collective-permute-start.1) | collective-permute-done | bytes 163872 | tf_op jit(solution)/shard_map/ppermute | solution.py:44
  11.8 2.1 %collective-permute-done.t1 = bf16[32,2560]{1,0:T(8,128)(2,1)S(1)} collective-permute-done((bf16[32,2560]{1,0:T(8,128)(2,1)}, bf16[32,2560]{1,0:T(8,128)(2,1)S(1)}, u32[]{:S(2)}, u32[]{:S(2)}) %collective-permute-start) | collective-permute-done | bytes 163872 | tf_op jit(solution)/shard_map/ppermute | solution.py:44
  15.8 1.9 %project.1 = (bf16[256,2560]{1,0:T(8,128)(2,1)S(1)}, bf16[256,896]{1,0:T(8,128)(2,1)S(1)}, bf16[8,896]{1,0:T(8,128)(2,1)S(1)}, f32[256,128]{1,0:T(8,128)S(1)}) custom-call(bf16[32,2560]{1,0:T(8,128)(2,1)S(1)} %copy-done.2, bf16[32,2560]{1,0:T(8,128)(2,1)S(1)} %collective-permute-done.t1, bf16[32,2560]{1,0:T(8,128)(2,1)S(1)} %collective-permute-done.1.t2, ...), custom_call_target="tpu_custom_call" | custom-call | flops 1342177280 | bytes 2684354 | tf_op jit(solution)/shard_map/project/pallas_call | solution.py:30
  17.8 3.4 %collective-permute-start.7 = (bf16[8,896]{1,0:T(8,128)(2,1)S(1)}, bf16[8,896]{1,0:T(8,128)(2,1)S(1)}, u32[]{:S(2)}, u32[]{:S(2)}) collective-permute-start(bf16[8,896]{1,0:T(8,128)(2,1)S(1)} %get-tuple-element.36), channel_id=1, source_target_pairs={{0,8},{8,16},{16,24},{24,32},{32,40},{40,48},{48,56},{56,64},{64,7... | collective-permute-start | bytes 43016 | tf_op jit(solution)/shard_map/ppermute | solution.py:316
  22.4 3.0 %collective-permute-done.7.tail = bf16[8,896]{1,0:T(8,128)(2,1)S(1)} collective-permute-done((bf16[8,896]{1,0:T(8,128)(2,1)S(1)}, bf16[8,896]{1,0:T(8,128)(2,1)S(1)}, u32[]{:S(2)}, u32[]{:S(2)}) %collective-permute-start.7) | collective-permute-done | bytes 14368 | tf_op jit(solution)/shard_map/ppermute | solution.py:316
  25.5 1.5 %local.1 = (bf16[256,640]{1,0:T(8,128)(2,1)S(1)}, bf16[256,128]{1,0:T(8,128)(2,1)S(1)}, bf16[256,128]{1,0:T(8,128)(2,1)S(1)}, f32[256,128]{1,0:T(8,128)S(1)}, f3...) custom-call(bf16[256,896]{1,0:T(8,128)(2,1)S(1)} %get-tuple-element., ...), custom_call_target="tpu_custom_call" | custom-call | flops 41943040 | bytes 83886 | tf_op jit(solution)/shard_map/local/pallas_call | solution.py:30
  27.1 2.1 %collective-permute-start.9 = (bf16[40,640]{1,0:T(8,128)(2,1)S(1)}, bf16[40,640]{1,0:T(8,128)(2,1)S(1)}, u32[]{:S(2)}, u32[]{:S(2)}) collective-permute-start(bf16[40,640]{1,0:T(8,128)(2,1)S(1)} %get-tuple-element.41), channel_id=1, source_target_pairs={{0,16},{8,24},{16,0},{24,8},{1,17},{9,25},{17,1},{25,9},{2,18},{10... | collective-permute-start | bytes 153608 | tf_op jit(solution)/shard_map/ppermute | solution.py:44
  29.2 1.4 %collective-permute-start.10 = (bf16[40,640]{1,0:T(8,128)(2,1)S(1)}, bf16[40,640]{1,0:T(8,128)(2,1)S(1)}, u32[]{:S(2)}, u32[]{:S(2)}) collective-permute-start(bf16[40,640]{1,0:T(8,128)(2,1)S(1)} %get-tuple-element.42), channel_id=1, source_target_pairs={{0,24},{8,0},{16,8},{24,16},{1,25},{9,1},{17,9},{25,17},{2,26},{10... | collective-permute-start | bytes 153608 | tf_op jit(solution)/shard_map/ppermute | solution.py:44
  31.6 1.4 %collective-permute-done.8.q1 = bf16[40,640]{1,0:T(8,128)(2,1)S(1)} collective-permute-done((bf16[40,640]{1,0:T(8,128)(2,1)S(1)}, bf16[40,640]{1,0:T(8,128)(2,1)S(1)}, u32[]{:S(2)}, u32[]{:S(2)}) %collective-permute-start.8) | collective-permute-done | bytes 51232 | tf_op jit(solution)/shard_map/ppermute | solution.py:44
  33.8 2.3 %collective-permute-start.11 = (bf16[40,640]{1,0:T(8,128)(2,1)S(1)}, bf16[40,640]{1,0:T(8,128)(2,1)S(1)}, u32[]{:S(2)}, u32[]{:S(2)}) collective-permute-start(bf16[40,640]{1,0:T(8,128)(2,1)S(1)} %rowtotal.1.row), channel_id=1, source_target_pairs={{0,32},{32,0},{64,96},{96,64},{128,160},{160,128},{192,224},{224,1... | collective-permute-start | bytes 153608 | tf_op jit(solution)/shard_map/ppermute | solution.py:333
  36.2 2.1 %collective-permute-done.11.other = bf16[40,640]{1,0:T(8,128)(2,1)S(1)} collective-permute-done((bf16[40,640]{1,0:T(8,128)(2,1)S(1)}, bf16[40,640]{1,0:T(8,128)(2,1)S(1)}, u32[]{:S(2)}, u32[]{:S(2)}) %collective-permute-start.11) | collective-permute-done | bytes 51232 | tf_op jit(solution)/shard_map/ppermute | solution.py:333
  38.3 3.2 %collective-permute-start.12 = (bf16[40,640]{1,0:T(8,128)(2,1)S(1)}, bf16[40,640]{1,0:T(8,128)(2,1)S(1)}, u32[]{:S(2)}, u32[]{:S(2)}) collective-permute-start(bf16[40,640]{1,0:T(8,128)(2,1)S(1)} %pairtotal.1), channel_id=1, source_target_pairs={{0,64},{32,96},{128,192},{160,224},{1,65},{33,97},{129,193},{161,2... | collective-permute-start | bytes 153608 | tf_op jit(solution)/shard_map/ppermute | solution.py:335
  41.5 1.8 %collective-permute-done.12.previous = bf16[40,640]{1,0:T(8,128)(2,1)S(1)} collective-permute-done((bf16[40,640]{1,0:T(8,128)(2,1)S(1)}, bf16[40,640]{1,0:T(8,128)(2,1)S(1)}, u32[]{:S(2)}, u32[]{:S(2)}) %collective-permute-start.12) | collective-permute-done | bytes 51232 | tf_op jit(solution)/shard_map/ppermute | solution.py:335
  44.0 1.3 %collective-permute-start.13 = (bf16[40,640]{1,0:T(8,128)(2,1)S(1)}, bf16[40,640]{1,0:T(8,128)(2,1)S(1)}, u32[]{:S(2)}, u32[]{:S(2)}) collective-permute-start(bf16[40,640]{1,0:T(8,128)(2,1)S(1)} %quadtotal.1), channel_id=1, source_target_pairs={{64,128},{96,160},{65,129},{97,161},{66,130},{98,162},{67,131},{99... | collective-permute-start | bytes 153608 | tf_op jit(solution)/shard_map/ppermute | solution.py:337
  45.3 11.2 %collective-permute-done.13.low = bf16[40,640]{1,0:T(8,128)(2,1)S(1)} collective-permute-done((bf16[40,640]{1,0:T(8,128)(2,1)S(1)}, bf16[40,640]{1,0:T(8,128)(2,1)S(1)}, u32[]{:S(2)}, u32[]{:S(2)}) %collective-permute-start.13) | collective-permute-done | bytes 51232 | tf_op jit(solution)/shard_map/ppermute | solution.py:337
  56.6 1.6 %collective-permute-start.15 = (bf16[32,640]{1,0:T(8,128)(2,1)S(1)}, bf16[32,640]{1,0:T(8,128)(2,1)S(1)}, u32[]{:S(2)}, u32[]{:S(2)}) collective-permute-start(bf16[32,640]{1,0:T(8,128)(2,1)S(1)} %get-tuple-element.49), channel_id=1, source_target_pairs={{0,8},{8,16},{16,24},{24,0},{1,9},{9,17},{17,25},{25,1},{2,10},{10... | collective-permute-start | bytes 122888 | tf_op jit(solution)/shard_map/ppermute | solution.py:44
  58.2 2.7 %collective-permute-start.16 = (bf16[32,640]{1,0:T(8,128)(2,1)S(1)}, bf16[32,640]{1,0:T(8,128)(2,1)S(1)}, u32[]{:S(2)}, u32[]{:S(2)}) collective-permute-start(bf16[32,640]{1,0:T(8,128)(2,1)S(1)} %get-tuple-element.50), channel_id=1, source_target_pairs={{0,16},{8,24},{16,0},{24,8},{1,17},{9,25},{17,1},{25,9},{2,18},{10... | collective-permute-start | bytes 122888 | tf_op jit(solution)/shard_map/ppermute | solution.py:44
  61.9 1.8 %collective-permute-done.16.e2 = bf16[32,640]{1,0:T(8,128)(2,1)S(1)} collective-permute-done((bf16[32,640]{1,0:T(8,128)(2,1)S(1)}, bf16[32,640]{1,0:T(8,128)(2,1)S(1)}, u32[]{:S(2)}, u32[]{:S(2)}) %collective-permute-start.16) | collective-permute-done | bytes 40992 | tf_op jit(solution)/shard_map/ppermute | solution.py:44
  66.8 1.4 %collective-permute-done.18.came = bf16[128,2688]{1,0:T(8,128)(2,1)S(1)} collective-permute-done((bf16[128,2688]{1,0:T(8,128)(2,1)S(1)}, bf16[128,2688]{1,0:T(8,128)(2,1)S(1)}, u32[]{:S(2)}, u32[]{:S(2)}) %collective-permute-start.18) | collective-permute-done | bytes 688160 | tf_op jit(solution)/shard_map/ppermute | solution.py:44
  68.6 2.1 %collective-permute-start.20 = (bf16[32,2688]{1,0:T(8,128)(2,1)S(1)}, bf16[32,2688]{1,0:T(8,128)(2,1)S(1)}, u32[]{:S(2)}, u32[]{:S(2)}) collective-permute-start(bf16[32,2688]{1,0:T(8,128)(2,1)S(1)} %get-tuple-element.57), channel_id=1, source_target_pairs={{0,4},{2,6},{4,0},{6,2},{1,5},{3,7},{5,1},{7,3},{8,12},{10,14},{12... | collective-permute-start | bytes 516104 | tf_op jit(solution)/shard_map/ppermute | solution.py:44
  71.8 8.1 %collective-permute-done.19.g1 = bf16[32,2688]{1,0:T(8,128)(2,1)S(1)} collective-permute-done((bf16[32,2688]{1,0:T(8,128)(2,1)S(1)}, bf16[32,2688]{1,0:T(8,128)(2,1)S(1)}, u32[]{:S(2)}, u32[]{:S(2)}) %collective-permute-start.19) | collective-permute-done | bytes 172064 | tf_op jit(solution)/shard_map/ppermute | solution.py:44
  (52 shorter events, 14.7 us)
Async XLA Ops:
  0.0 10.3 %collective-permute-start.2 = (bf16[32,2560]{1,0:T(8,128)(2,1)}, bf16[32,2560]{1,0:T(8,128)(2,1)S(1)}, u32[]{:S(2)}, u32[]{:S(2)}) collective-permute-start(bf16[32,2560]{1,0:T(8,128)(2,1)} %t0.1), channel_id=1, source_target_pairs={{0,6},{2,0},{4,2},{6,4},{1,7},{3,1},{5,3},{7,5},{8,14},{10,8},{12,... | collective-permute-start | bytes 491528 | tf_op jit(solution)/shard_map/ppermute | solution.py:44
  3.0 8.8 %collective-permute-start.1 = (bf16[32,2560]{1,0:T(8,128)(2,1)}, bf16[32,2560]{1,0:T(8,128)(2,1)S(1)}, u32[]{:S(2)}, u32[]{:S(2)}) collective-permute-start(bf16[32,2560]{1,0:T(8,128)(2,1)} %t0.1), channel_id=1, source_target_pairs={{0,4},{2,6},{4,0},{6,2},{1,5},{3,7},{5,1},{7,3},{8,12},{10,14},{12... | collective-permute-start | bytes 491528 | tf_op jit(solution)/shard_map/ppermute | solution.py:44
  3.6 10.3 %collective-permute-start = (bf16[32,2560]{1,0:T(8,128)(2,1)}, bf16[32,2560]{1,0:T(8,128)(2,1)S(1)}, u32[]{:S(2)}, u32[]{:S(2)}) collective-permute-start(bf16[32,2560]{1,0:T(8,128)(2,1)} %t0.1), channel_id=1, source_target_pairs={{0,2},{2,4},{4,6},{6,0},{1,3},{3,5},{5,7},{7,1},{8,10},{10,12},{12... | collective-permute-start | bytes 491528 | tf_op jit(solution)/shard_map/ppermute | solution.py:44
  4.6 9.8 %collective-permute-start.3 = (bf16[32,2560]{1,0:T(8,128)(2,1)}, bf16[32,2560]{1,0:T(8,128)(2,1)S(1)}, u32[]{:S(2)}, u32[]{:S(2)}) collective-permute-start(bf16[32,2560]{1,0:T(8,128)(2,1)} %t0.1), channel_id=1, source_target_pairs={{0,1},{1,0},{2,3},{3,2},{4,5},{5,4},{6,7},{7,6},{8,9},{9,8},{10,11... | collective-permute-start | bytes 491528 | tf_op jit(solution)/shard_map/ppermute | solution.py:44
  4.6 11.2 %copy-start.2 = (bf16[32,2560]{1,0:T(8,128)(2,1)S(1)}, bf16[32,2560]{1,0:T(8,128)(2,1)}, u32[]{:S(2)}) copy-start(bf16[32,2560]{1,0:T(8,128)(2,1)} %t0.1) | copy-start | bytes 491524
  13.9 1.4 %collective-permute-start.4 = (bf16[32,2560]{1,0:T(8,128)(2,1)S(1)}, bf16[32,2560]{1,0:T(8,128)(2,1)S(1)}, u32[]{:S(2)}, u32[]{:S(2)}) collective-permute-start(bf16[32,2560]{1,0:T(8,128)(2,1)S(1)} %collective-permute-done.t1), channel_id=1, source_target_pairs={{0,1},{1,0},{2,3},{3,2},{4,5},{5,4},{6,7},{7,6},{8,9},{9,8},{10,11... | collective-permute-start | bytes 491528 | tf_op jit(solution)/shard_map/ppermute | solution.py:44
  13.9 1.6 %collective-permute-start.5 = (bf16[32,2560]{1,0:T(8,128)(2,1)S(1)}, bf16[32,2560]{1,0:T(8,128)(2,1)S(1)}, u32[]{:S(2)}, u32[]{:S(2)}) collective-permute-start(bf16[32,2560]{1,0:T(8,128)(2,1)S(1)} %collective-permute-done.1.t2), channel_id=1, source_target_pairs={{0,1},{1,0},{2,3},{3,2},{4,5},{5,4},{6,7},{7,6},{8,9},{9,8},{10,11... | collective-permute-start | bytes 491528 | tf_op jit(solution)/shard_map/ppermute | solution.py:44
  14.4 1.4 %collective-permute-start.6 = (bf16[32,2560]{1,0:T(8,128)(2,1)S(1)}, bf16[32,2560]{1,0:T(8,128)(2,1)S(1)}, u32[]{:S(2)}, u32[]{:S(2)}) collective-permute-start(bf16[32,2560]{1,0:T(8,128)(2,1)S(1)} %collective-permute-done.2.t3), channel_id=1, source_target_pairs={{0,1},{1,0},{2,3},{3,2},{4,5},{5,4},{6,7},{7,6},{8,9},{9,8},{10,11... | collective-permute-start | bytes 491528 | tf_op jit(solution)/shard_map/ppermute | solution.py:44
  17.8 7.7 %collective-permute-start.7 = (bf16[8,896]{1,0:T(8,128)(2,1)S(1)}, bf16[8,896]{1,0:T(8,128)(2,1)S(1)}, u32[]{:S(2)}, u32[]{:S(2)}) collective-permute-start(bf16[8,896]{1,0:T(8,128)(2,1)S(1)} %get-tuple-element.36), channel_id=1, source_target_pairs={{0,8},{8,16},{16,24},{24,32},{32,40},{40,48},{48,56},{56,64},{64,7... | collective-permute-start | bytes 43016 | tf_op jit(solution)/shard_map/ppermute | solution.py:316
  22.4 42.4 %copy-start = (bf16[640,2560]{1,0:T(8,128)(2,1)S(1)}, bf16[640,2560]{1,0:T(8,128)(2,1)}, u32[]{:S(2)}) copy-start(bf16[640,2560]{1,0:T(8,128)(2,1)} %w.3) | copy-start | bytes 9830404
  27.0 5.9 %collective-permute-start.8 = (bf16[40,640]{1,0:T(8,128)(2,1)S(1)}, bf16[40,640]{1,0:T(8,128)(2,1)S(1)}, u32[]{:S(2)}, u32[]{:S(2)}) collective-permute-start(bf16[40,640]{1,0:T(8,128)(2,1)S(1)} %get-tuple-element.40), channel_id=1, source_target_pairs={{0,8},{8,16},{16,24},{24,0},{1,9},{9,17},{17,25},{25,1},{2,10},{10... | collective-permute-start | bytes 153608 | tf_op jit(solution)/shard_map/ppermute | solution.py:44
  27.1 5.9 %collective-permute-start.9 = (bf16[40,640]{1,0:T(8,128)(2,1)S(1)}, bf16[40,640]{1,0:T(8,128)(2,1)S(1)}, u32[]{:S(2)}, u32[]{:S(2)}) collective-permute-start(bf16[40,640]{1,0:T(8,128)(2,1)S(1)} %get-tuple-element.41), channel_id=1, source_target_pairs={{0,16},{8,24},{16,0},{24,8},{1,17},{9,25},{17,1},{25,9},{2,18},{10... | collective-permute-start | bytes 153608 | tf_op jit(solution)/shard_map/ppermute | solution.py:44
  29.2 4.6 %collective-permute-start.10 = (bf16[40,640]{1,0:T(8,128)(2,1)S(1)}, bf16[40,640]{1,0:T(8,128)(2,1)S(1)}, u32[]{:S(2)}, u32[]{:S(2)}) collective-permute-start(bf16[40,640]{1,0:T(8,128)(2,1)S(1)} %get-tuple-element.42), channel_id=1, source_target_pairs={{0,24},{8,0},{16,8},{24,16},{1,25},{9,1},{17,9},{25,17},{2,26},{10... | collective-permute-start | bytes 153608 | tf_op jit(solution)/shard_map/ppermute | solution.py:44
  33.8 4.4 %collective-permute-start.11 = (bf16[40,640]{1,0:T(8,128)(2,1)S(1)}, bf16[40,640]{1,0:T(8,128)(2,1)S(1)}, u32[]{:S(2)}, u32[]{:S(2)}) collective-permute-start(bf16[40,640]{1,0:T(8,128)(2,1)S(1)} %rowtotal.1.row), channel_id=1, source_target_pairs={{0,32},{32,0},{64,96},{96,64},{128,160},{160,128},{192,224},{224,1... | collective-permute-start | bytes 153608 | tf_op jit(solution)/shard_map/ppermute | solution.py:333
  38.3 4.9 %collective-permute-start.12 = (bf16[40,640]{1,0:T(8,128)(2,1)S(1)}, bf16[40,640]{1,0:T(8,128)(2,1)S(1)}, u32[]{:S(2)}, u32[]{:S(2)}) collective-permute-start(bf16[40,640]{1,0:T(8,128)(2,1)S(1)} %pairtotal.1), channel_id=1, source_target_pairs={{0,64},{32,96},{128,192},{160,224},{1,65},{33,97},{129,193},{161,2... | collective-permute-start | bytes 153608 | tf_op jit(solution)/shard_map/ppermute | solution.py:335
  43.3 2.0 %collective-permute-start.14 = (bf16[40,640]{1,0:T(8,128)(2,1)S(1)}, bf16[40,640]{1,0:T(8,128)(2,1)S(1)}, u32[]{:S(2)}, u32[]{:S(2)}) collective-permute-start(bf16[40,640]{1,0:T(8,128)(2,1)S(1)} %quadtotal.1), channel_id=1, source_target_pairs={{64,192},{96,224},{65,193},{97,225},{66,194},{98,226},{67,195},{99... | collective-permute-start | bytes 153608 | tf_op jit(solution)/shard_map/ppermute | solution.py:338
  44.0 12.5 %collective-permute-start.13 = (bf16[40,640]{1,0:T(8,128)(2,1)S(1)}, bf16[40,640]{1,0:T(8,128)(2,1)S(1)}, u32[]{:S(2)}, u32[]{:S(2)}) collective-permute-start(bf16[40,640]{1,0:T(8,128)(2,1)S(1)} %quadtotal.1), channel_id=1, source_target_pairs={{64,128},{96,160},{65,129},{97,161},{66,130},{98,162},{67,131},{99... | collective-permute-start | bytes 153608 | tf_op jit(solution)/shard_map/ppermute | solution.py:337
  56.6 5.3 %collective-permute-start.15 = (bf16[32,640]{1,0:T(8,128)(2,1)S(1)}, bf16[32,640]{1,0:T(8,128)(2,1)S(1)}, u32[]{:S(2)}, u32[]{:S(2)}) collective-permute-start(bf16[32,640]{1,0:T(8,128)(2,1)S(1)} %get-tuple-element.49), channel_id=1, source_target_pairs={{0,8},{8,16},{16,24},{24,0},{1,9},{9,17},{17,25},{25,1},{2,10},{10... | collective-permute-start | bytes 122888 | tf_op jit(solution)/shard_map/ppermute | solution.py:44
  58.2 5.5 %collective-permute-start.16 = (bf16[32,640]{1,0:T(8,128)(2,1)S(1)}, bf16[32,640]{1,0:T(8,128)(2,1)S(1)}, u32[]{:S(2)}, u32[]{:S(2)}) collective-permute-start(bf16[32,640]{1,0:T(8,128)(2,1)S(1)} %get-tuple-element.50), channel_id=1, source_target_pairs={{0,16},{8,24},{16,0},{24,8},{1,17},{9,25},{17,1},{25,9},{2,18},{10... | collective-permute-start | bytes 122888 | tf_op jit(solution)/shard_map/ppermute | solution.py:44
  60.8 4.0 %collective-permute-start.17 = (bf16[32,640]{1,0:T(8,128)(2,1)S(1)}, bf16[32,640]{1,0:T(8,128)(2,1)S(1)}, u32[]{:S(2)}, u32[]{:S(2)}) collective-permute-start(bf16[32,640]{1,0:T(8,128)(2,1)S(1)} %get-tuple-element.51), channel_id=1, source_target_pairs={{0,24},{8,0},{16,8},{24,16},{1,25},{9,1},{17,9},{25,17},{2,26},{10... | collective-permute-start | bytes 122888 | tf_op jit(solution)/shard_map/ppermute | solution.py:44
  66.0 2.2 %collective-permute-start.18 = (bf16[128,2688]{1,0:T(8,128)(2,1)S(1)}, bf16[128,2688]{1,0:T(8,128)(2,1)S(1)}, u32[]{:S(2)}, u32[]{:S(2)}) collective-permute-start(bf16[128,2688]{1,0:T(8,128)(2,1)S(1)} %get-tuple-element.54), channel_id=1, source_target_pairs={{0,1},{1,0},{2,3},{3,2},{4,5},{5,4},{6,7},{7,6},{8,9},{9,8},{10,11... | collective-permute-start | bytes 2064392 | tf_op jit(solution)/shard_map/ppermute | solution.py:44
  68.5 11.4 %collective-permute-start.19 = (bf16[32,2688]{1,0:T(8,128)(2,1)S(1)}, bf16[32,2688]{1,0:T(8,128)(2,1)S(1)}, u32[]{:S(2)}, u32[]{:S(2)}) collective-permute-start(bf16[32,2688]{1,0:T(8,128)(2,1)S(1)} %get-tuple-element.56), channel_id=1, source_target_pairs={{0,2},{2,4},{4,6},{6,0},{1,3},{3,5},{5,7},{7,1},{8,10},{10,12},{12... | collective-permute-start | bytes 516104 | tf_op jit(solution)/shard_map/ppermute | solution.py:44
  68.6 11.3 %collective-permute-start.20 = (bf16[32,2688]{1,0:T(8,128)(2,1)S(1)}, bf16[32,2688]{1,0:T(8,128)(2,1)S(1)}, u32[]{:S(2)}, u32[]{:S(2)}) collective-permute-start(bf16[32,2688]{1,0:T(8,128)(2,1)S(1)} %get-tuple-element.57), channel_id=1, source_target_pairs={{0,4},{2,6},{4,0},{6,2},{1,5},{3,7},{5,1},{7,3},{8,12},{10,14},{12... | collective-permute-start | bytes 516104 | tf_op jit(solution)/shard_map/ppermute | solution.py:44
  70.7 9.8 %collective-permute-start.21 = (bf16[32,2688]{1,0:T(8,128)(2,1)S(1)}, bf16[32,2688]{1,0:T(8,128)(2,1)S(1)}, u32[]{:S(2)}, u32[]{:S(2)}) collective-permute-start(bf16[32,2688]{1,0:T(8,128)(2,1)S(1)} %get-tuple-element.58), channel_id=1, source_target_pairs={{0,6},{2,0},{4,2},{6,4},{1,7},{3,1},{5,3},{7,5},{8,14},{10,8},{12,... | collective-permute-start | bytes 516104 | tf_op jit(solution)/shard_map/ppermute | solution.py:44
  (7 other events, 49.4 us)

commit v4 on v3

--- a/solution.py
+++ b/solution.py
@@ -221,18 +221,19 @@
 
 
 def quad_total_kernel(row, other, previous, out):
-    pack(out, *follow(unpack(previous), two_rows(row, other)[2]))
-
-
-def incoming_kernel(q0, q1, q2, q3, row, other, previous, low, high, e0, e1, e2, e3, held, ready):
+    first = lax.axis_index("z") < 2
+    mine, theirs = two_rows(row, other)[2], unpack(previous)
+    pack(out, *follow(choose(first, mine, theirs), choose(first, theirs, mine)))
+
+
+def incoming_kernel(q0, q1, q2, q3, row, other, previous, quad, e0, e1, e2, e3, held, ready):
     z, x = lax.axis_index("z"), lax.axis_index("x")
     load_rows((q0, q1, q2, q3), held)
     odd, theirs, _ = two_rows(row, other)
     carry = choose(odd, theirs, (jnp.zeros((32, WIDTH), F32), jnp.ones((1, WIDTH), F32)))
     second = lax.rem(z, 4) >= 2
     carry = choose(second, follow(unpack(previous), carry), carry)
-    quad = choose(second, unpack(high), unpack(low))
-    carry, _ = choose(z >= 4, follow(quad, carry), carry)
+    carry, _ = choose(z >= 4, follow(unpack(quad), carry), carry)
     ready[0] = carry
     for k in range(3):
         carry = carry * factor_of(held, k) + held[k, 0:32, :]
@@ -332,14 +333,13 @@
     (row,) = call(row_total_kernel, piece, [*rows, inside], scratch=[((4, PIECE, WIDTH), F32)], name="rowtotal")
     other = lax.ppermute(row, "z", [(i, i ^ 1) for i in range(8)])
     (two,) = call(pair_total_kernel, piece, [row, other], name="pairtotal")
-    previous = lax.ppermute(two, "z", [(0, 2), (1, 3), (4, 6), (5, 7)])
+    previous = lax.ppermute(two, "z", [(0, 2), (1, 3), (2, 0), (3, 1), (4, 6), (5, 7)])
     (four,) = call(quad_total_kernel, piece, [row, other, previous], name="quadtotal")
-    low = lax.ppermute(four, "z", [(2, 4), (3, 5)])
-    high = lax.ppermute(four, "z", [(2, 6), (3, 7)])
+    quad = lax.ppermute(four, "z", [(0, 7), (1, 6), (2, 5), (3, 4)])
     e0, e1, e2, e3 = call(
         incoming_kernel,
         [((32, WIDTH), BF)] * 4,
-        [*rows, row, other, previous, low, high],
+        [*rows, row, other, previous, quad],
         scratch=[((4, PIECE, WIDTH), F32), ((4, 32, WIDTH), F32)],
         name="incoming",
     )

time: 81.4 us -> 79.7 us (0.979)
  the two profiles are of different devices: /device:TPU:160 before, /device:TPU:1 now
where the time goes in v4:
time: 79.7 us; the launch traced here: 79.5 us
  starting transfers between devices  43.1 us (54%)
  waiting for transfers between devices  23.3 us (29%)
  Pallas kernels  8.74 us (11%)
  local copies, waits for them, and re-layouts  4.15 us (5%)
    ppermute x17, starting transfers between devices, shifted(): lax.ppermute(value, axis, [(i, (i + steps) % size) for i in range(size)])  26.6 us
    ppermute x17, waiting for transfers between devices, shifted(): lax.ppermute(value, axis, [(i, (i + steps) % size) for i in range(size)])  19.1 us
    pallas_call x12, Pallas kernels, call(): pl.pallas_call(body, out_shape=[jax.ShapeDtypeStruct(s, t) for s, t in ou...  8.74 us
    ppermute x1, starting transfers between devices, body(): lax.ppermute(two, 'z', [(0, 2), (1, 3), (2, 0), (3, 1), (4, 6), (5, 7)])  5.92 us
    ppermute x1, starting transfers between devices, body(): quad = lax.ppermute(four, 'z', [(0, 7), (1, 6), (2, 5), (3, 4)])  5.65 us
    unnamed x19, local copies, waits for them, and re-layouts  4.15 us
    ppermute x1, starting transfers between devices, body(): tail = lax.ppermute(tail, SEQ, [(i, i + 1) for i in range(31)])  3.12 us
    ppermute x1, starting transfers between devices, body(): other = lax.ppermute(row, 'z', [(i, i ^ 1) for i in range(8)])  1.75 us
  transfers between devices with their start and end apart: 21, of which 15 were waited for; matrix products, arithmetic and copies ran while one was open for 5% of the time, Pallas kernels for 4%

profile of v4, /device:TPU:1, one launch (start us, length us, event | category | flops | bytes accessed | tf_op | source)
XLA Modules:
  0.0 79.5 jit_solution(12190830190122655242)
XLA Ops:
  0.0 3.6 %collective-permute-start.2 = (bf16[32,2560]{1,0:T(8,128)(2,1)}, bf16[32,2560]{1,0:T(8,128)(2,1)S(1)}, u32[]{:S(2)}, u32[]{:S(2)}) collective-permute-start(bf16[32,2560]{1,0:T(8,128)(2,1)} %t0.1), channel_id=1, source_target_pairs={{0,6},{2,0},{4,2},{6,4},{1,7},{3,1},{5,3},{7,5},{8,14},{10,8},{12,... | collective-permute-start | bytes 491528 | tf_op jit(solution)/shard_map/ppermute | solution.py:44
  4.6 1.5 %collective-permute-start.3 = (bf16[32,2560]{1,0:T(8,128)(2,1)}, bf16[32,2560]{1,0:T(8,128)(2,1)S(1)}, u32[]{:S(2)}, u32[]{:S(2)}) collective-permute-start(bf16[32,2560]{1,0:T(8,128)(2,1)} %t0.1), channel_id=1, source_target_pairs={{0,1},{1,0},{2,3},{3,2},{4,5},{5,4},{6,7},{7,6},{8,9},{9,8},{10,11... | collective-permute-start | bytes 491528 | tf_op jit(solution)/shard_map/ppermute | solution.py:44
  6.1 4.1 %copy.11 = bf16[320,8,2,640]{3,1,2,0:T(8,128)(2,1)S(1)} copy(bf16[320,8,2,640]{3,2,1,0:T(2,128)(2,1)} %bitcast.10) | data formatting | bytes 13107200
  10.2 4.7 %collective-permute-done.t1 = bf16[32,2560]{1,0:T(8,128)(2,1)S(1)} collective-permute-done((bf16[32,2560]{1,0:T(8,128)(2,1)}, bf16[32,2560]{1,0:T(8,128)(2,1)S(1)}, u32[]{:S(2)}, u32[]{:S(2)}) %collective-permute-start) | collective-permute-done | bytes 163872 | tf_op jit(solution)/shard_map/ppermute | solution.py:44
  17.0 1.9 %project.1 = (bf16[256,2560]{1,0:T(8,128)(2,1)S(1)}, bf16[256,896]{1,0:T(8,128)(2,1)S(1)}, bf16[8,896]{1,0:T(8,128)(2,1)S(1)}, f32[256,128]{1,0:T(8,128)S(1)}) custom-call(bf16[32,2560]{1,0:T(8,128)(2,1)S(1)} %copy-done.2, bf16[32,2560]{1,0:T(8,128)(2,1)S(1)} %collective-permute-done.t1, bf16[32,2560]{1,0:T(8,128)(2,1)S(1)} %collective-permute-done.1.t2, ...), custom_call_target="tpu_custom_call" | custom-call | flops 1342177280 | bytes 2684354 | tf_op jit(solution)/shard_map/project/pallas_call | solution.py:30
  19.0 3.1 %collective-permute-start.7 = (bf16[8,896]{1,0:T(8,128)(2,1)S(1)}, bf16[8,896]{1,0:T(8,128)(2,1)S(1)}, u32[]{:S(2)}, u32[]{:S(2)}) collective-permute-start(bf16[8,896]{1,0:T(8,128)(2,1)S(1)} %get-tuple-element.36), channel_id=1, source_target_pairs={{0,8},{8,16},{16,24},{24,32},{32,40},{40,48},{48,56},{56,64},{64,7... | collective-permute-start | bytes 43016 | tf_op jit(solution)/shard_map/ppermute | solution.py:317
  22.2 1.2 %gate.1.before = f32[256,640]{1,0:T(8,128)S(1)} custom-call(bf16[256,2560]{1,0:T(8,128)(2,1)S(1)} %get-tuple-element.38.tokens, bf16[2560,1280]{1,0:T(8,128)(2,1)S(1)} %bitcast.6), custom_call_target="tpu_custom_call" | custom-call | flops 838860800 | bytes 1677721 | tf_op jit(solution)/shard_map/gate/pallas_call | solution.py:30
  23.4 1.5 %local.1 = (bf16[256,640]{1,0:T(8,128)(2,1)S(1)}, bf16[256,128]{1,0:T(8,128)(2,1)S(1)}, bf16[256,128]{1,0:T(8,128)(2,1)S(1)}, f32[256,128]{1,0:T(8,128)S(1)}, f3...) custom-call(bf16[256,896]{1,0:T(8,128)(2,1)S(1)} %get-tuple-element., ...), custom_call_target="tpu_custom_call" | custom-call | flops 41943040 | bytes 83886 | tf_op jit(solution)/shard_map/local/pallas_call | solution.py:30
  24.9 1.3 %collective-permute-start.8 = (bf16[40,640]{1,0:T(8,128)(2,1)S(1)}, bf16[40,640]{1,0:T(8,128)(2,1)S(1)}, u32[]{:S(2)}, u32[]{:S(2)}) collective-permute-start(bf16[40,640]{1,0:T(8,128)(2,1)S(1)} %get-tuple-element.40), channel_id=1, source_target_pairs={{0,8},{8,16},{16,24},{24,0},{1,9},{9,17},{17,25},{25,1},{2,10},{10... | collective-permute-start | bytes 153608 | tf_op jit(solution)/shard_map/ppermute | solution.py:44
  26.2 2.8 %collective-permute-start.9 = (bf16[40,640]{1,0:T(8,128)(2,1)S(1)}, bf16[40,640]{1,0:T(8,128)(2,1)S(1)}, u32[]{:S(2)}, u32[]{:S(2)}) collective-permute-start(bf16[40,640]{1,0:T(8,128)(2,1)S(1)} %get-tuple-element.41), channel_id=1, source_target_pairs={{0,16},{8,24},{16,0},{24,8},{1,17},{9,25},{17,1},{25,9},{2,18},{10... | collective-permute-start | bytes 153608 | tf_op jit(solution)/shard_map/ppermute | solution.py:44
  31.1 1.3 %collective-permute-done.10.q3 = bf16[40,640]{1,0:T(8,128)(2,1)S(1)} collective-permute-done((bf16[40,640]{1,0:T(8,128)(2,1)S(1)}, bf16[40,640]{1,0:T(8,128)(2,1)S(1)}, u32[]{:S(2)}, u32[]{:S(2)}) %collective-permute-start.10) | collective-permute-done | bytes 51232 | tf_op jit(solution)/shard_map/ppermute | solution.py:44
  32.5 1.8 %collective-permute-start.11 = (bf16[40,640]{1,0:T(8,128)(2,1)S(1)}, bf16[40,640]{1,0:T(8,128)(2,1)S(1)}, u32[]{:S(2)}, u32[]{:S(2)}) collective-permute-start(bf16[40,640]{1,0:T(8,128)(2,1)S(1)} %rowtotal.1.row), channel_id=1, source_target_pairs={{0,32},{32,0},{64,96},{96,64},{128,160},{160,128},{192,224},{224,1... | collective-permute-start | bytes 153608 | tf_op jit(solution)/shard_map/ppermute | solution.py:334
  34.2 1.5 %collective-permute-done.11.other = bf16[40,640]{1,0:T(8,128)(2,1)S(1)} collective-permute-done((bf16[40,640]{1,0:T(8,128)(2,1)S(1)}, bf16[40,640]{1,0:T(8,128)(2,1)S(1)}, u32[]{:S(2)}, u32[]{:S(2)}) %collective-permute-start.11) | collective-permute-done | bytes 51232 | tf_op jit(solution)/shard_map/ppermute | solution.py:334
  35.8 5.9 %collective-permute-start.12 = (bf16[40,640]{1,0:T(8,128)(2,1)S(1)}, bf16[40,640]{1,0:T(8,128)(2,1)S(1)}, u32[]{:S(2)}, u32[]{:S(2)}) collective-permute-start(bf16[40,640]{1,0:T(8,128)(2,1)S(1)} %pairtotal.1), channel_id=1, source_target_pairs={{0,64},{32,96},{64,0},{96,32},{128,192},{160,224},{1,65},{33,97},{... | collective-permute-start | bytes 153608 | tf_op jit(solution)/shard_map/ppermute | solution.py:336
  41.7 1.5 %collective-permute-done.12.previous = bf16[40,640]{1,0:T(8,128)(2,1)S(1)} collective-permute-done((bf16[40,640]{1,0:T(8,128)(2,1)S(1)}, bf16[40,640]{1,0:T(8,128)(2,1)S(1)}, u32[]{:S(2)}, u32[]{:S(2)}) %collective-permute-start.12) | collective-permute-done | bytes 51232 | tf_op jit(solution)/shard_map/ppermute | solution.py:336
  43.2 5.7 %collective-permute-start.13 = (bf16[40,640]{1,0:T(8,128)(2,1)S(1)}, bf16[40,640]{1,0:T(8,128)(2,1)S(1)}, u32[]{:S(2)}, u32[]{:S(2)}) collective-permute-start(bf16[40,640]{1,0:T(8,128)(2,1)S(1)} %quadtotal.1), channel_id=1, source_target_pairs={{0,224},{32,192},{64,160},{96,128},{1,225},{33,193},{65,161},{97,1... | collective-permute-start | bytes 153608 | tf_op jit(solution)/shard_map/ppermute | solution.py:338
  48.9 1.2 %collective-permute-done.13.quad = bf16[40,640]{1,0:T(8,128)(2,1)S(1)} collective-permute-done((bf16[40,640]{1,0:T(8,128)(2,1)S(1)}, bf16[40,640]{1,0:T(8,128)(2,1)S(1)}, u32[]{:S(2)}, u32[]{:S(2)}) %collective-permute-start.13) | collective-permute-done | bytes 51232 | tf_op jit(solution)/shard_map/ppermute | solution.py:338
  51.2 2.4 %collective-permute-start.15 = (bf16[32,640]{1,0:T(8,128)(2,1)S(1)}, bf16[32,640]{1,0:T(8,128)(2,1)S(1)}, u32[]{:S(2)}, u32[]{:S(2)}) collective-permute-start(bf16[32,640]{1,0:T(8,128)(2,1)S(1)} %get-tuple-element.50), channel_id=1, source_target_pairs={{0,16},{8,24},{16,0},{24,8},{1,17},{9,25},{17,1},{25,9},{2,18},{10... | collective-permute-start | bytes 122888 | tf_op jit(solution)/shard_map/ppermute | solution.py:44
  54.3 1.2 %collective-permute-done.15.e2 = bf16[32,640]{1,0:T(8,128)(2,1)S(1)} collective-permute-done((bf16[32,640]{1,0:T(8,128)(2,1)S(1)}, bf16[32,640]{1,0:T(8,128)(2,1)S(1)}, u32[]{:S(2)}, u32[]{:S(2)}) %collective-permute-start.15) | collective-permute-done | bytes 40992 | tf_op jit(solution)/shard_map/ppermute | solution.py:44
  56.5 1.2 %gated.1 = (bf16[256,640]{1,0:T(8,128)(2,1)S(1)}, f32[256,128]{1,0:T(8,128)S(1)}, bf16[128,2688]{1,0:T(8,128)(2,1)S(1)}) custom-call(bf16[32,640]{1,0:T(8,128)(2,1)S(1)} %get-tuple-element.48.e0, bf16[32,640]{1,0:T(8,128)(2,1)S(1)} %collective-permute-done.14.e1, bf16[32,640]{1,0:T(8,128)(2,1)S(1)} %collective-permute-done.15.e2, ...), custom_call_target="tpu_custom_call" | custom-call | flops 419430400 | bytes 838860 | tf_op jit(solution)/shard_map/gated/pallas_call | solution.py:30
  57.7 8.1 %collective-permute-start.17 = (bf16[128,2688]{1,0:T(8,128)(2,1)S(1)}, bf16[128,2688]{1,0:T(8,128)(2,1)S(1)}, u32[]{:S(2)}, u32[]{:S(2)}) collective-permute-start(bf16[128,2688]{1,0:T(8,128)(2,1)S(1)} %get-tuple-element.54), channel_id=1, source_target_pairs={{0,1},{1,0},{2,3},{3,2},{4,5},{5,4},{6,7},{7,6},{8,9},{9,8},{10,11... | collective-permute-start | bytes 2064392 | tf_op jit(solution)/shard_map/ppermute | solution.py:44
  67.8 1.5 %collective-permute-start.19 = (bf16[32,2688]{1,0:T(8,128)(2,1)S(1)}, bf16[32,2688]{1,0:T(8,128)(2,1)S(1)}, u32[]{:S(2)}, u32[]{:S(2)}) collective-permute-start(bf16[32,2688]{1,0:T(8,128)(2,1)S(1)} %get-tuple-element.57), channel_id=1, source_target_pairs={{0,4},{2,6},{4,0},{6,2},{1,5},{3,7},{5,1},{7,3},{8,12},{10,14},{12... | collective-permute-start | bytes 516104 | tf_op jit(solution)/shard_map/ppermute | solution.py:44
  69.3 1.4 %collective-permute-start.20 = (bf16[32,2688]{1,0:T(8,128)(2,1)S(1)}, bf16[32,2688]{1,0:T(8,128)(2,1)S(1)}, u32[]{:S(2)}, u32[]{:S(2)}) collective-permute-start(bf16[32,2688]{1,0:T(8,128)(2,1)S(1)} %get-tuple-element.58), channel_id=1, source_target_pairs={{0,6},{2,0},{4,2},{6,4},{1,7},{3,1},{5,3},{7,5},{8,14},{10,8},{12,... | collective-permute-start | bytes 516104 | tf_op jit(solution)/shard_map/ppermute | solution.py:44
  70.8 7.5 %collective-permute-done.18.g1 = bf16[32,2688]{1,0:T(8,128)(2,1)S(1)} collective-permute-done((bf16[32,2688]{1,0:T(8,128)(2,1)S(1)}, bf16[32,2688]{1,0:T(8,128)(2,1)S(1)}, u32[]{:S(2)}, u32[]{:S(2)}) %collective-permute-start.18) | collective-permute-done | bytes 172064 | tf_op jit(solution)/shard_map/ppermute | solution.py:44
  (50 shorter events, 11.5 us)
Async XLA Ops:
  0.0 10.2 %collective-permute-start.2 = (bf16[32,2560]{1,0:T(8,128)(2,1)}, bf16[32,2560]{1,0:T(8,128)(2,1)S(1)}, u32[]{:S(2)}, u32[]{:S(2)}) collective-permute-start(bf16[32,2560]{1,0:T(8,128)(2,1)} %t0.1), channel_id=1, source_target_pairs={{0,6},{2,0},{4,2},{6,4},{1,7},{3,1},{5,3},{7,5},{8,14},{10,8},{12,... | collective-permute-start | bytes 491528 | tf_op jit(solution)/shard_map/ppermute | solution.py:44
  3.6 6.7 %collective-permute-start.1 = (bf16[32,2560]{1,0:T(8,128)(2,1)}, bf16[32,2560]{1,0:T(8,128)(2,1)S(1)}, u32[]{:S(2)}, u32[]{:S(2)}) collective-permute-start(bf16[32,2560]{1,0:T(8,128)(2,1)} %t0.1), channel_id=1, source_target_pairs={{0,4},{2,6},{4,0},{6,2},{1,5},{3,7},{5,1},{7,3},{8,12},{10,14},{12... | collective-permute-start | bytes 491528 | tf_op jit(solution)/shard_map/ppermute | solution.py:44
  3.9 11.0 %collective-permute-start = (bf16[32,2560]{1,0:T(8,128)(2,1)}, bf16[32,2560]{1,0:T(8,128)(2,1)S(1)}, u32[]{:S(2)}, u32[]{:S(2)}) collective-permute-start(bf16[32,2560]{1,0:T(8,128)(2,1)} %t0.1), channel_id=1, source_target_pairs={{0,2},{2,4},{4,6},{6,0},{1,3},{3,5},{5,7},{7,1},{8,10},{10,12},{12... | collective-permute-start | bytes 491528 | tf_op jit(solution)/shard_map/ppermute | solution.py:44
  4.6 11.3 %collective-permute-start.3 = (bf16[32,2560]{1,0:T(8,128)(2,1)}, bf16[32,2560]{1,0:T(8,128)(2,1)S(1)}, u32[]{:S(2)}, u32[]{:S(2)}) collective-permute-start(bf16[32,2560]{1,0:T(8,128)(2,1)} %t0.1), channel_id=1, source_target_pairs={{0,1},{1,0},{2,3},{3,2},{4,5},{5,4},{6,7},{7,6},{8,9},{9,8},{10,11... | collective-permute-start | bytes 491528 | tf_op jit(solution)/shard_map/ppermute | solution.py:44
  6.1 10.9 %copy-start.2 = (bf16[32,2560]{1,0:T(8,128)(2,1)S(1)}, bf16[32,2560]{1,0:T(8,128)(2,1)}, u32[]{:S(2)}) copy-start(bf16[32,2560]{1,0:T(8,128)(2,1)} %t0.1) | copy-start | bytes 491524
  6.1 10.9 %copy-start.3 = (bf16[2560,10]{0,1:T(8,128)(2,1)S(1)}, bf16[2560,10]{0,1:T(8,128)(2,1)}, u32[]{:S(2)}) copy-start(bf16[2560,10]{0,1:T(8,128)(2,1)} %param.13) | copy-start | bytes 153604
  14.9 1.5 %collective-permute-start.4 = (bf16[32,2560]{1,0:T(8,128)(2,1)S(1)}, bf16[32,2560]{1,0:T(8,128)(2,1)S(1)}, u32[]{:S(2)}, u32[]{:S(2)}) collective-permute-start(bf16[32,2560]{1,0:T(8,128)(2,1)S(1)} %collective-permute-done.t1), channel_id=1, source_target_pairs={{0,1},{1,0},{2,3},{3,2},{4,5},{5,4},{6,7},{7,6},{8,9},{9,8},{10,11... | collective-permute-start | bytes 491528 | tf_op jit(solution)/shard_map/ppermute | solution.py:44
  15.4 1.4 %collective-permute-start.5 = (bf16[32,2560]{1,0:T(8,128)(2,1)S(1)}, bf16[32,2560]{1,0:T(8,128)(2,1)S(1)}, u32[]{:S(2)}, u32[]{:S(2)}) collective-permute-start(bf16[32,2560]{1,0:T(8,128)(2,1)S(1)} %collective-permute-done.1.t2), channel_id=1, source_target_pairs={{0,1},{1,0},{2,3},{3,2},{4,5},{5,4},{6,7},{7,6},{8,9},{9,8},{10,11... | collective-permute-start | bytes 491528 | tf_op jit(solution)/shard_map/ppermute | solution.py:44
  15.4 1.6 %collective-permute-start.6 = (bf16[32,2560]{1,0:T(8,128)(2,1)S(1)}, bf16[32,2560]{1,0:T(8,128)(2,1)S(1)}, u32[]{:S(2)}, u32[]{:S(2)}) collective-permute-start(bf16[32,2560]{1,0:T(8,128)(2,1)S(1)} %collective-permute-done.2.t3), channel_id=1, source_target_pairs={{0,1},{1,0},{2,3},{3,2},{4,5},{5,4},{6,7},{7,6},{8,9},{9,8},{10,11... | collective-permute-start | bytes 491528 | tf_op jit(solution)/shard_map/ppermute | solution.py:44
  19.0 4.4 %collective-permute-start.7 = (bf16[8,896]{1,0:T(8,128)(2,1)S(1)}, bf16[8,896]{1,0:T(8,128)(2,1)S(1)}, u32[]{:S(2)}, u32[]{:S(2)}) collective-permute-start(bf16[8,896]{1,0:T(8,128)(2,1)S(1)} %get-tuple-element.36), channel_id=1, source_target_pairs={{0,8},{8,16},{16,24},{24,32},{32,40},{40,48},{48,56},{56,64},{64,7... | collective-permute-start | bytes 43016 | tf_op jit(solution)/shard_map/ppermute | solution.py:317
  23.4 33.1 %copy-start = (bf16[640,2560]{1,0:T(8,128)(2,1)S(1)}, bf16[640,2560]{1,0:T(8,128)(2,1)}, u32[]{:S(2)}) copy-start(bf16[640,2560]{1,0:T(8,128)(2,1)} %w.3) | copy-start | bytes 9830404
  24.9 5.9 %collective-permute-start.8 = (bf16[40,640]{1,0:T(8,128)(2,1)S(1)}, bf16[40,640]{1,0:T(8,128)(2,1)S(1)}, u32[]{:S(2)}, u32[]{:S(2)}) collective-permute-start(bf16[40,640]{1,0:T(8,128)(2,1)S(1)} %get-tuple-element.40), channel_id=1, source_target_pairs={{0,8},{8,16},{16,24},{24,0},{1,9},{9,17},{17,25},{25,1},{2,10},{10... | collective-permute-start | bytes 153608 | tf_op jit(solution)/shard_map/ppermute | solution.py:44
  26.2 4.9 %collective-permute-start.9 = (bf16[40,640]{1,0:T(8,128)(2,1)S(1)}, bf16[40,640]{1,0:T(8,128)(2,1)S(1)}, u32[]{:S(2)}, u32[]{:S(2)}) collective-permute-start(bf16[40,640]{1,0:T(8,128)(2,1)S(1)} %get-tuple-element.41), channel_id=1, source_target_pairs={{0,16},{8,24},{16,0},{24,8},{1,17},{9,25},{17,1},{25,9},{2,18},{10... | collective-permute-start | bytes 153608 | tf_op jit(solution)/shard_map/ppermute | solution.py:44
  29.0 3.4 %collective-permute-start.10 = (bf16[40,640]{1,0:T(8,128)(2,1)S(1)}, bf16[40,640]{1,0:T(8,128)(2,1)S(1)}, u32[]{:S(2)}, u32[]{:S(2)}) collective-permute-start(bf16[40,640]{1,0:T(8,128)(2,1)S(1)} %get-tuple-element.42), channel_id=1, source_target_pairs={{0,24},{8,0},{16,8},{24,16},{1,25},{9,1},{17,9},{25,17},{2,26},{10... | collective-permute-start | bytes 153608 | tf_op jit(solution)/shard_map/ppermute | solution.py:44
  32.5 3.3 %collective-permute-start.11 = (bf16[40,640]{1,0:T(8,128)(2,1)S(1)}, bf16[40,640]{1,0:T(8,128)(2,1)S(1)}, u32[]{:S(2)}, u32[]{:S(2)}) collective-permute-start(bf16[40,640]{1,0:T(8,128)(2,1)S(1)} %rowtotal.1.row), channel_id=1, source_target_pairs={{0,32},{32,0},{64,96},{96,64},{128,160},{160,128},{192,224},{224,1... | collective-permute-start | bytes 153608 | tf_op jit(solution)/shard_map/ppermute | solution.py:334
  35.8 7.4 %collective-permute-start.12 = (bf16[40,640]{1,0:T(8,128)(2,1)S(1)}, bf16[40,640]{1,0:T(8,128)(2,1)S(1)}, u32[]{:S(2)}, u32[]{:S(2)}) collective-permute-start(bf16[40,640]{1,0:T(8,128)(2,1)S(1)} %pairtotal.1), channel_id=1, source_target_pairs={{0,64},{32,96},{64,0},{96,32},{128,192},{160,224},{1,65},{33,97},{... | collective-permute-start | bytes 153608 | tf_op jit(solution)/shard_map/ppermute | solution.py:336
  43.2 6.8 %collective-permute-start.13 = (bf16[40,640]{1,0:T(8,128)(2,1)S(1)}, bf16[40,640]{1,0:T(8,128)(2,1)S(1)}, u32[]{:S(2)}, u32[]{:S(2)}) collective-permute-start(bf16[40,640]{1,0:T(8,128)(2,1)S(1)} %quadtotal.1), channel_id=1, source_target_pairs={{0,224},{32,192},{64,160},{96,128},{1,225},{33,193},{65,161},{97,1... | collective-permute-start | bytes 153608 | tf_op jit(solution)/shard_map/ppermute | solution.py:338
  50.2 4.1 %collective-permute-start.14 = (bf16[32,640]{1,0:T(8,128)(2,1)S(1)}, bf16[32,640]{1,0:T(8,128)(2,1)S(1)}, u32[]{:S(2)}, u32[]{:S(2)}) collective-permute-start(bf16[32,640]{1,0:T(8,128)(2,1)S(1)} %get-tuple-element.49), channel_id=1, source_target_pairs={{0,8},{8,16},{16,24},{24,0},{1,9},{9,17},{17,25},{25,1},{2,10},{10... | collective-permute-start | bytes 122888 | tf_op jit(solution)/shard_map/ppermute | solution.py:44
  51.2 4.4 %collective-permute-start.15 = (bf16[32,640]{1,0:T(8,128)(2,1)S(1)}, bf16[32,640]{1,0:T(8,128)(2,1)S(1)}, u32[]{:S(2)}, u32[]{:S(2)}) collective-permute-start(bf16[32,640]{1,0:T(8,128)(2,1)S(1)} %get-tuple-element.50), channel_id=1, source_target_pairs={{0,16},{8,24},{16,0},{24,8},{1,17},{9,25},{17,1},{25,9},{2,18},{10... | collective-permute-start | bytes 122888 | tf_op jit(solution)/shard_map/ppermute | solution.py:44
  53.6 2.9 %collective-permute-start.16 = (bf16[32,640]{1,0:T(8,128)(2,1)S(1)}, bf16[32,640]{1,0:T(8,128)(2,1)S(1)}, u32[]{:S(2)}, u32[]{:S(2)}) collective-permute-start(bf16[32,640]{1,0:T(8,128)(2,1)S(1)} %get-tuple-element.51), channel_id=1, source_target_pairs={{0,24},{8,0},{16,8},{24,16},{1,25},{9,1},{17,9},{25,17},{2,26},{10... | collective-permute-start | bytes 122888 | tf_op jit(solution)/shard_map/ppermute | solution.py:44
  57.7 9.9 %collective-permute-start.17 = (bf16[128,2688]{1,0:T(8,128)(2,1)S(1)}, bf16[128,2688]{1,0:T(8,128)(2,1)S(1)}, u32[]{:S(2)}, u32[]{:S(2)}) collective-permute-start(bf16[128,2688]{1,0:T(8,128)(2,1)S(1)} %get-tuple-element.54), channel_id=1, source_target_pairs={{0,1},{1,0},{2,3},{3,2},{4,5},{5,4},{6,7},{7,6},{8,9},{9,8},{10,11... | collective-permute-start | bytes 2064392 | tf_op jit(solution)/shard_map/ppermute | solution.py:44
  67.7 10.5 %collective-permute-start.18 = (bf16[32,2688]{1,0:T(8,128)(2,1)S(1)}, bf16[32,2688]{1,0:T(8,128)(2,1)S(1)}, u32[]{:S(2)}, u32[]{:S(2)}) collective-permute-start(bf16[32,2688]{1,0:T(8,128)(2,1)S(1)} %get-tuple-element.56), channel_id=1, source_target_pairs={{0,2},{2,4},{4,6},{6,0},{1,3},{3,5},{5,7},{7,1},{8,10},{10,12},{12... | collective-permute-start | bytes 516104 | tf_op jit(solution)/shard_map/ppermute | solution.py:44
  67.8 10.4 %collective-permute-start.19 = (bf16[32,2688]{1,0:T(8,128)(2,1)S(1)}, bf16[32,2688]{1,0:T(8,128)(2,1)S(1)}, u32[]{:S(2)}, u32[]{:S(2)}) collective-permute-start(bf16[32,2688]{1,0:T(8,128)(2,1)S(1)} %get-tuple-element.57), channel_id=1, source_target_pairs={{0,4},{2,6},{4,0},{6,2},{1,5},{3,7},{5,1},{7,3},{8,12},{10,14},{12... | collective-permute-start | bytes 516104 | tf_op jit(solution)/shard_map/ppermute | solution.py:44
  69.3 9.3 %collective-permute-start.20 = (bf16[32,2688]{1,0:T(8,128)(2,1)S(1)}, bf16[32,2688]{1,0:T(8,128)(2,1)S(1)}, u32[]{:S(2)}, u32[]{:S(2)}) collective-permute-start(bf16[32,2688]{1,0:T(8,128)(2,1)S(1)} %get-tuple-element.58), channel_id=1, source_target_pairs={{0,6},{2,0},{4,2},{6,4},{1,7},{3,1},{5,3},{7,5},{8,14},{10,8},{12,... | collective-permute-start | bytes 516104 | tf_op jit(solution)/shard_map/ppermute | solution.py:44
  (6 other events, 25.8 us)

commit v5 on v4

--- a/solution.py
+++ b/solution.py
@@ -39,9 +39,12 @@
     )(*args)
 
 
-def shifted(value, axis, steps):
-    size = lax.axis_size(axis)
-    return lax.ppermute(value, axis, [(i, (i + steps) % size) for i in range(size)])
+def swapped(value, axis, mask):
+    return lax.ppermute(value, axis, [(i, i ^ mask) for i in range(lax.axis_size(axis))])
+
+
+def other_index(index, mask):
+    return lax.bitwise_xor(index, jnp.int32(mask))
 
 
 def row_at(index, rows):
@@ -51,7 +54,7 @@
 def project_kernel(t0, t1, t2, t3, o0, o1, o2, o3, w, w_bc, w_dt, early, all_out, pre_out, tail_out, dt_out, w_steps):
     y, c = lax.axis_index("y"), lax.axis_index("c")
     for d, (own, other) in enumerate(((t0, o0), (t1, o1), (t2, o2), (t3, o3))):
-        source = lax.rem(y + 4 - d, 4)
+        source = other_index(y, d)
         all_out[row_at(source * 2 + c, ROWS), :] = own[...]
         all_out[row_at(source * 2 + 1 - c, ROWS), :] = other[...]
     tokens = all_out[...]
@@ -152,7 +155,7 @@
         for out in (p0, p1, p2, p3):
             out[32:40, cols] = extra
     for d, out in enumerate((p0, p1, p2, p3)):
-        out[0:32, :] = state[row_at(lax.rem(x + d, 4), 32), :].astype(BF)
+        out[0:32, :] = state[row_at(other_index(x, d), 32), :].astype(BF)
 
 
 def inside_kernel(v, b, c, step, cum, out):
@@ -178,7 +181,7 @@
 def load_rows(pieces, held):
     x = lax.axis_index("x")
     for d, piece in enumerate(pieces):
-        held[lax.rem(x + 4 - d, 4)] = piece[...].astype(F32)
+        held[other_index(x, d)] = piece[...].astype(F32)
 
 
 def factor_of(held, k):
@@ -221,7 +224,7 @@
 
 
 def quad_total_kernel(row, other, previous, out):
-    first = lax.axis_index("z") < 2
+    first = lax.rem(lax.axis_index("z"), 4) < 2
     mine, theirs = two_rows(row, other)[2], unpack(previous)
     pack(out, *follow(choose(first, mine, theirs), choose(first, theirs, mine)))
 
@@ -239,13 +242,13 @@
         carry = carry * factor_of(held, k) + held[k, 0:32, :]
         ready[k + 1] = carry
     for d, out in enumerate((e0, e1, e2, e3)):
-        out[...] = ready[lax.rem(x + d, 4)].astype(BF)
+        out[...] = ready[other_index(x, d)].astype(BF)
 
 
 def gated_kernel(e0, e1, e2, e3, c, cum, inside, gate, gain, w, g_out, sq_out, send_out, state, pick):
     x, core = lax.axis_index("x"), lax.axis_index("c")
     for d, piece in enumerate((e0, e1, e2, e3)):
-        state[row_at(lax.rem(x + 4 - d, 4), 32), :] = piece[...]
+        state[row_at(other_index(x, d), 32), :] = piece[...]
     grown = jnp.exp(cum[...])
     squares = jnp.zeros((BLOCK, 128), F32)
     for pair in range(5):
@@ -287,7 +290,7 @@
 def pair_kernel(own, came, f0, f1, f2, f3):
     y = lax.axis_index("y")
     for d, out in enumerate((f0, f1, f2, f3)):
-        rows = row_at(lax.rem(y + d, 4), ROWS)
+        rows = row_at(other_index(y, d), ROWS)
         total = own[rows, :] + came[rows, :].astype(F32)
         out[:, :MODEL] = total[:, :MODEL].astype(out.dtype)
         both = jnp.sum(total[:, MODEL:], axis=1, keepdims=True)
@@ -301,10 +304,10 @@
 
 
 def body(tokens, w_xz, w_bc, w_dt, dt_bias, a_log, conv_x, conv_bc, norm_gain, w_out):
-    near = [tokens] + [shifted(tokens, "y", d) for d in (1, 2, 3)]
+    near = [tokens] + [swapped(tokens, "y", d) for d in (1, 2, 3)]
     w_both = w_xz.reshape(MODEL, 2 * WIDTH)
     near[1:] = [lax.optimization_barrier((piece, w_both))[0] for piece in near[1:]]
-    far = [shifted(piece, "c", 1) for piece in near]
+    far = [swapped(piece, "c", 1) for piece in near]
     gain = norm_gain[None]
     everything, pre, tail, dt_pre = call(
         project_kernel,
@@ -325,17 +328,17 @@
         flops=2 * BLOCK * STATE * WIDTH,
         name="local",
     )
-    rows = [p0] + [shifted(piece, "x", d) for d, piece in ((1, p1), (2, p2), (3, p3))]
+    rows = [p0] + [swapped(piece, "x", d) for d, piece in ((1, p1), (2, p2), (3, p3))]
     (inside,) = call(
         inside_kernel, [((BLOCK, WIDTH), F32)], [v, b, c, step, cum], flops=20 * BLOCK * BLOCK * 256, name="inside"
     )
     piece = [((PIECE, WIDTH), BF)]
     (row,) = call(row_total_kernel, piece, [*rows, inside], scratch=[((4, PIECE, WIDTH), F32)], name="rowtotal")
-    other = lax.ppermute(row, "z", [(i, i ^ 1) for i in range(8)])
+    other = swapped(row, "z", 1)
     (two,) = call(pair_total_kernel, piece, [row, other], name="pairtotal")
-    previous = lax.ppermute(two, "z", [(0, 2), (1, 3), (2, 0), (3, 1), (4, 6), (5, 7)])
+    previous = swapped(two, "z", 2)
     (four,) = call(quad_total_kernel, piece, [row, other, previous], name="quadtotal")
-    quad = lax.ppermute(four, "z", [(0, 7), (1, 6), (2, 5), (3, 4)])
+    quad = swapped(four, "z", 7)
     e0, e1, e2, e3 = call(
         incoming_kernel,
         [((32, WIDTH), BF)] * 4,
@@ -343,7 +346,7 @@
         scratch=[((4, PIECE, WIDTH), F32), ((4, 32, WIDTH), F32)],
         name="incoming",
     )
-    states = [e0] + [shifted(piece, "x", d) for d, piece in ((1, e1), (2, e2), (3, e3))]
+    states = [e0] + [swapped(piece, "x", d) for d, piece in ((1, e1), (2, e2), (3, e3))]
     g, squares, send = call(
         gated_kernel,
         [((BLOCK, WIDTH), BF), ((BLOCK, 128), F32), ((128, WIDE), BF)],
@@ -352,12 +355,12 @@
         flops=2 * 128 * WIDTH * MODEL,
         name="gated",
     )
-    came = shifted(send, "c", 1)
+    came = swapped(send, "c", 1)
     (own,) = call(
         own_kernel, [((128, WIDE), F32)], [g, squares, w_out], scratch=[((128, WIDTH), BF)], flops=2 * 128 * WIDTH * MODEL, name="own"
     )
     f0, f1, f2, f3 = call(pair_kernel, [((ROWS, WIDE), F32)] + [((ROWS, WIDE), BF)] * 3, [own, came], name="pair")
-    parts = [f0] + [shifted(piece, "y", d) for d, piece in ((1, f1), (2, f2), (3, f3))]
+    parts = [f0] + [swapped(piece, "y", d) for d, piece in ((1, f1), (2, f2), (3, f3))]
     (out,) = call(finish_kernel, [((ROWS, MODEL), BF)], parts, name="finish")
     return out
 

time: 79.7 us -> 79.4 us (level)
  starting transfers between devices: 43.1 us -> 41.9 us
  waiting for transfers between devices: 23.3 us -> 24.3 us
    ppermute x20, waiting for transfers between devices: 23.3 us -> 24.3 us  [swapped(): lax.ppermute(value, axis, [(i, i ^ mask) for i in range(lax.axis_size(axi...]
    ppermute x20, starting transfers between devices: 40 us -> 39 us  [swapped(): lax.ppermute(value, axis, [(i, i ^ mask) for i in range(lax.axis_size(axi...]
  transfers between devices with their start and end apart: 21 -> 21, of which waited for: 15 -> 14; matrix products, arithmetic and copies ran while one was open for 5% -> 5% of each run, Pallas kernels for 4% -> 4%
where the time goes in v5:
time: 79.4 us; the launch traced here: 79.3 us
  starting transfers between devices  41.9 us (53%)
  waiting for transfers between devices  24.3 us (31%)
  Pallas kernels  8.71 us (11%)
  local copies, waits for them, and re-layouts  4.15 us (5%)
    ppermute x20, starting transfers between devices, swapped(): lax.ppermute(value, axis, [(i, i ^ mask) for i in range(lax.axis_size(axi...  39 us
    ppermute x20, waiting for transfers between devices, swapped(): lax.ppermute(value, axis, [(i, i ^ mask) for i in range(lax.axis_size(axi...  24.3 us
    pallas_call x12, Pallas kernels, call(): pl.pallas_call(body, out_shape=[jax.ShapeDtypeStruct(s, t) for s, t in ou...  8.71 us
    unnamed x19, local copies, waits for them, and re-layouts  4.15 us
    ppermute x1, starting transfers between devices, body(): tail = lax.ppermute(tail, SEQ, [(i, i + 1) for i in range(31)])  2.96 us
  transfers between devices with their start and end apart: 21, of which 14 were waited for; matrix products, arithmetic and copies ran while one was open for 5% of the time, Pallas kernels for 4%

profile of v5, /device:TPU:1, one launch (start us, length us, event | category | flops | bytes accessed | tf_op | source)
XLA Modules:
  0.0 79.3 jit_solution(13723983985456458883)
XLA Ops:
  0.0 3.6 %collective-permute-start.2 = (bf16[32,2560]{1,0:T(8,128)(2,1)}, bf16[32,2560]{1,0:T(8,128)(2,1)S(1)}, u32[]{:S(2)}, u32[]{:S(2)}) collective-permute-start(bf16[32,2560]{1,0:T(8,128)(2,1)} %t0.1), channel_id=1, source_target_pairs={{0,6},{2,4},{4,2},{6,0},{1,7},{3,5},{5,3},{7,1},{8,14},{10,12},{12... | collective-permute-start | bytes 491528 | tf_op jit(solution)/shard_map/ppermute | solution.py:43
  4.1 3.2 %collective-permute-start.3 = (bf16[32,2560]{1,0:T(8,128)(2,1)}, bf16[32,2560]{1,0:T(8,128)(2,1)S(1)}, u32[]{:S(2)}, u32[]{:S(2)}) collective-permute-start(bf16[32,2560]{1,0:T(8,128)(2,1)} %t0.1), channel_id=1, source_target_pairs={{0,1},{1,0},{2,3},{3,2},{4,5},{5,4},{6,7},{7,6},{8,9},{9,8},{10,11... | collective-permute-start | bytes 491528 | tf_op jit(solution)/shard_map/ppermute | solution.py:43
  7.3 4.1 %copy.11 = bf16[320,8,2,640]{3,1,2,0:T(8,128)(2,1)S(1)} copy(bf16[320,8,2,640]{3,2,1,0:T(2,128)(2,1)} %bitcast.10) | data formatting | bytes 13107200
  11.4 2.0 %collective-permute-start.4 = (bf16[32,2560]{1,0:T(8,128)(2,1)S(1)}, bf16[32,2560]{1,0:T(8,128)(2,1)S(1)}, u32[]{:S(2)}, u32[]{:S(2)}) collective-permute-start(bf16[32,2560]{1,0:T(8,128)(2,1)S(1)} %collective-permute-done.t1), channel_id=1, source_target_pairs={{0,1},{1,0},{2,3},{3,2},{4,5},{5,4},{6,7},{7,6},{8,9},{9,8},{10,11... | collective-permute-start | bytes 491528 | tf_op jit(solution)/shard_map/ppermute | solution.py:43
  15.1 1.9 %project.1 = (bf16[256,2560]{1,0:T(8,128)(2,1)S(1)}, bf16[256,896]{1,0:T(8,128)(2,1)S(1)}, bf16[8,896]{1,0:T(8,128)(2,1)S(1)}, f32[256,128]{1,0:T(8,128)S(1)}) custom-call(bf16[32,2560]{1,0:T(8,128)(2,1)S(1)} %copy-done.2, bf16[32,2560]{1,0:T(8,128)(2,1)S(1)} %collective-permute-done.t1, bf16[32,2560]{1,0:T(8,128)(2,1)S(1)} %collective-permute-done.1.t2, ...), custom_call_target="tpu_custom_call" | custom-call | flops 1342177280 | bytes 2684354 | tf_op jit(solution)/shard_map/project/pallas_call | solution.py:30
  17.0 3.0 %collective-permute-start.7 = (bf16[8,896]{1,0:T(8,128)(2,1)S(1)}, bf16[8,896]{1,0:T(8,128)(2,1)S(1)}, u32[]{:S(2)}, u32[]{:S(2)}) collective-permute-start(bf16[8,896]{1,0:T(8,128)(2,1)S(1)} %get-tuple-element.36), channel_id=1, source_target_pairs={{0,8},{8,16},{16,24},{24,32},{32,40},{40,48},{48,56},{56,64},{64,7... | collective-permute-start | bytes 43016 | tf_op jit(solution)/shard_map/ppermute | solution.py:320
  21.3 1.4 %local.1 = (bf16[256,640]{1,0:T(8,128)(2,1)S(1)}, bf16[256,128]{1,0:T(8,128)(2,1)S(1)}, bf16[256,128]{1,0:T(8,128)(2,1)S(1)}, f32[256,128]{1,0:T(8,128)S(1)}, f3...) custom-call(bf16[256,896]{1,0:T(8,128)(2,1)S(1)} %get-tuple-element., ...), custom_call_target="tpu_custom_call" | custom-call | flops 41943040 | bytes 83886 | tf_op jit(solution)/shard_map/local/pallas_call | solution.py:30
  22.8 1.3 %collective-permute-start.8 = (bf16[40,640]{1,0:T(8,128)(2,1)S(1)}, bf16[40,640]{1,0:T(8,128)(2,1)S(1)}, u32[]{:S(2)}, u32[]{:S(2)}) collective-permute-start(bf16[40,640]{1,0:T(8,128)(2,1)S(1)} %get-tuple-element.40), channel_id=1, source_target_pairs={{0,8},{8,0},{16,24},{24,16},{1,9},{9,1},{17,25},{25,17},{2,10},{10... | collective-permute-start | bytes 153608 | tf_op jit(solution)/shard_map/ppermute | solution.py:43
  24.1 2.8 %collective-permute-start.9 = (bf16[40,640]{1,0:T(8,128)(2,1)S(1)}, bf16[40,640]{1,0:T(8,128)(2,1)S(1)}, u32[]{:S(2)}, u32[]{:S(2)}) collective-permute-start(bf16[40,640]{1,0:T(8,128)(2,1)S(1)} %get-tuple-element.41), channel_id=1, source_target_pairs={{0,16},{8,24},{16,0},{24,8},{1,17},{9,25},{17,1},{25,9},{2,18},{10... | collective-permute-start | bytes 153608 | tf_op jit(solution)/shard_map/ppermute | solution.py:43
  28.9 2.4 %collective-permute-done.10.q3 = bf16[40,640]{1,0:T(8,128)(2,1)S(1)} collective-permute-done((bf16[40,640]{1,0:T(8,128)(2,1)S(1)}, bf16[40,640]{1,0:T(8,128)(2,1)S(1)}, u32[]{:S(2)}, u32[]{:S(2)}) %collective-permute-start.10) | collective-permute-done | bytes 51232 | tf_op jit(solution)/shard_map/ppermute | solution.py:43
  31.4 2.4 %collective-permute-start.11 = (bf16[40,640]{1,0:T(8,128)(2,1)S(1)}, bf16[40,640]{1,0:T(8,128)(2,1)S(1)}, u32[]{:S(2)}, u32[]{:S(2)}) collective-permute-start(bf16[40,640]{1,0:T(8,128)(2,1)S(1)} %rowtotal.1.row), channel_id=1, source_target_pairs={{0,32},{32,0},{64,96},{96,64},{128,160},{160,128},{192,224},{224,1... | collective-permute-start | bytes 153608 | tf_op jit(solution)/shard_map/ppermute | solution.py:43
  33.7 1.5 %collective-permute-done.11.other = bf16[40,640]{1,0:T(8,128)(2,1)S(1)} collective-permute-done((bf16[40,640]{1,0:T(8,128)(2,1)S(1)}, bf16[40,640]{1,0:T(8,128)(2,1)S(1)}, u32[]{:S(2)}, u32[]{:S(2)}) %collective-permute-start.11) | collective-permute-done | bytes 51232 | tf_op jit(solution)/shard_map/ppermute | solution.py:43
  35.3 3.6 %collective-permute-start.12 = (bf16[40,640]{1,0:T(8,128)(2,1)S(1)}, bf16[40,640]{1,0:T(8,128)(2,1)S(1)}, u32[]{:S(2)}, u32[]{:S(2)}) collective-permute-start(bf16[40,640]{1,0:T(8,128)(2,1)S(1)} %pairtotal.1), channel_id=1, source_target_pairs={{0,64},{32,96},{64,0},{96,32},{128,192},{160,224},{192,128},{224,1... | collective-permute-start | bytes 153608 | tf_op jit(solution)/shard_map/ppermute | solution.py:43
  38.9 1.5 %collective-permute-done.12.previous = bf16[40,640]{1,0:T(8,128)(2,1)S(1)} collective-permute-done((bf16[40,640]{1,0:T(8,128)(2,1)S(1)}, bf16[40,640]{1,0:T(8,128)(2,1)S(1)}, u32[]{:S(2)}, u32[]{:S(2)}) %collective-permute-start.12) | collective-permute-done | bytes 51232 | tf_op jit(solution)/shard_map/ppermute | solution.py:43
  40.4 3.4 %collective-permute-start.13 = (bf16[40,640]{1,0:T(8,128)(2,1)S(1)}, bf16[40,640]{1,0:T(8,128)(2,1)S(1)}, u32[]{:S(2)}, u32[]{:S(2)}) collective-permute-start(bf16[40,640]{1,0:T(8,128)(2,1)S(1)} %quadtotal.1), channel_id=1, source_target_pairs={{0,224},{32,192},{64,160},{96,128},{128,96},{160,64},{192,32},{224... | collective-permute-start | bytes 153608 | tf_op jit(solution)/shard_map/ppermute | solution.py:43
  43.9 1.5 %collective-permute-done.13.quad = bf16[40,640]{1,0:T(8,128)(2,1)S(1)} collective-permute-done((bf16[40,640]{1,0:T(8,128)(2,1)S(1)}, bf16[40,640]{1,0:T(8,128)(2,1)S(1)}, u32[]{:S(2)}, u32[]{:S(2)}) %collective-permute-start.13) | collective-permute-done | bytes 51232 | tf_op jit(solution)/shard_map/ppermute | solution.py:43
  45.8 3.6 %collective-permute-start.15 = (bf16[32,640]{1,0:T(8,128)(2,1)S(1)}, bf16[32,640]{1,0:T(8,128)(2,1)S(1)}, u32[]{:S(2)}, u32[]{:S(2)}) collective-permute-start(bf16[32,640]{1,0:T(8,128)(2,1)S(1)} %get-tuple-element.50), channel_id=1, source_target_pairs={{0,16},{8,24},{16,0},{24,8},{1,17},{9,25},{17,1},{25,9},{2,18},{10... | collective-permute-start | bytes 122888 | tf_op jit(solution)/shard_map/ppermute | solution.py:43
  49.4 1.7 %collective-permute-done.15.e2 = bf16[32,640]{1,0:T(8,128)(2,1)S(1)} collective-permute-done((bf16[32,640]{1,0:T(8,128)(2,1)S(1)}, bf16[32,640]{1,0:T(8,128)(2,1)S(1)}, u32[]{:S(2)}, u32[]{:S(2)}) %collective-permute-start.15) | collective-permute-done | bytes 40992 | tf_op jit(solution)/shard_map/ppermute | solution.py:43
  51.2 2.2 %collective-permute-done.16.e3 = bf16[32,640]{1,0:T(8,128)(2,1)S(1)} collective-permute-done((bf16[32,640]{1,0:T(8,128)(2,1)S(1)}, bf16[32,640]{1,0:T(8,128)(2,1)S(1)}, u32[]{:S(2)}, u32[]{:S(2)}) %collective-permute-start.16) | collective-permute-done | bytes 40992 | tf_op jit(solution)/shard_map/ppermute | solution.py:43
  54.6 7.8 %collective-permute-start.17 = (bf16[128,2688]{1,0:T(8,128)(2,1)S(1)}, bf16[128,2688]{1,0:T(8,128)(2,1)S(1)}, u32[]{:S(2)}, u32[]{:S(2)}) collective-permute-start(bf16[128,2688]{1,0:T(8,128)(2,1)S(1)} %get-tuple-element.54), channel_id=1, source_target_pairs={{0,1},{1,0},{2,3},{3,2},{4,5},{5,4},{6,7},{7,6},{8,9},{9,8},{10,11... | collective-permute-start | bytes 2064392 | tf_op jit(solution)/shard_map/ppermute | solution.py:43
  65.4 2.6 %collective-permute-start.19 = (bf16[32,2688]{1,0:T(8,128)(2,1)S(1)}, bf16[32,2688]{1,0:T(8,128)(2,1)S(1)}, u32[]{:S(2)}, u32[]{:S(2)}) collective-permute-start(bf16[32,2688]{1,0:T(8,128)(2,1)S(1)} %get-tuple-element.57), channel_id=1, source_target_pairs={{0,4},{2,6},{4,0},{6,2},{1,5},{3,7},{5,1},{7,3},{8,12},{10,14},{12... | collective-permute-start | bytes 516104 | tf_op jit(solution)/shard_map/ppermute | solution.py:43
  68.3 1.7 %collective-permute-done.18.g1 = bf16[32,2688]{1,0:T(8,128)(2,1)S(1)} collective-permute-done((bf16[32,2688]{1,0:T(8,128)(2,1)S(1)}, bf16[32,2688]{1,0:T(8,128)(2,1)S(1)}, u32[]{:S(2)}, u32[]{:S(2)}) %collective-permute-start.18) | collective-permute-done | bytes 172064 | tf_op jit(solution)/shard_map/ppermute | solution.py:43
  70.0 5.8 %collective-permute-done.19.g2 = bf16[32,2688]{1,0:T(8,128)(2,1)S(1)} collective-permute-done((bf16[32,2688]{1,0:T(8,128)(2,1)S(1)}, bf16[32,2688]{1,0:T(8,128)(2,1)S(1)}, u32[]{:S(2)}, u32[]{:S(2)}) %collective-permute-start.19) | collective-permute-done | bytes 172064 | tf_op jit(solution)/shard_map/ppermute | solution.py:43
  75.9 2.7 %collective-permute-done.20.g3 = bf16[32,2688]{1,0:T(8,128)(2,1)S(1)} collective-permute-done((bf16[32,2688]{1,0:T(8,128)(2,1)S(1)}, bf16[32,2688]{1,0:T(8,128)(2,1)S(1)}, u32[]{:S(2)}, u32[]{:S(2)}) %collective-permute-start.20) | collective-permute-done | bytes 172064 | tf_op jit(solution)/shard_map/ppermute | solution.py:43
  (50 shorter events, 11.4 us)
Async XLA Ops:
  0.0 11.4 %collective-permute-start.2 = (bf16[32,2560]{1,0:T(8,128)(2,1)}, bf16[32,2560]{1,0:T(8,128)(2,1)S(1)}, u32[]{:S(2)}, u32[]{:S(2)}) collective-permute-start(bf16[32,2560]{1,0:T(8,128)(2,1)} %t0.1), channel_id=1, source_target_pairs={{0,6},{2,4},{4,2},{6,0},{1,7},{3,5},{5,3},{7,1},{8,14},{10,12},{12... | collective-permute-start | bytes 491528 | tf_op jit(solution)/shard_map/ppermute | solution.py:43
  3.6 7.9 %collective-permute-start.1 = (bf16[32,2560]{1,0:T(8,128)(2,1)}, bf16[32,2560]{1,0:T(8,128)(2,1)S(1)}, u32[]{:S(2)}, u32[]{:S(2)}) collective-permute-start(bf16[32,2560]{1,0:T(8,128)(2,1)} %t0.1), channel_id=1, source_target_pairs={{0,4},{2,6},{4,0},{6,2},{1,5},{3,7},{5,1},{7,3},{8,12},{10,14},{12... | collective-permute-start | bytes 491528 | tf_op jit(solution)/shard_map/ppermute | solution.py:43
  3.9 7.5 %collective-permute-start = (bf16[32,2560]{1,0:T(8,128)(2,1)}, bf16[32,2560]{1,0:T(8,128)(2,1)S(1)}, u32[]{:S(2)}, u32[]{:S(2)}) collective-permute-start(bf16[32,2560]{1,0:T(8,128)(2,1)} %t0.1), channel_id=1, source_target_pairs={{0,2},{2,0},{4,6},{6,4},{1,3},{3,1},{5,7},{7,5},{8,10},{10,8},{12,... | collective-permute-start | bytes 491528 | tf_op jit(solution)/shard_map/ppermute | solution.py:43
  4.1 9.8 %collective-permute-start.3 = (bf16[32,2560]{1,0:T(8,128)(2,1)}, bf16[32,2560]{1,0:T(8,128)(2,1)S(1)}, u32[]{:S(2)}, u32[]{:S(2)}) collective-permute-start(bf16[32,2560]{1,0:T(8,128)(2,1)} %t0.1), channel_id=1, source_target_pairs={{0,1},{1,0},{2,3},{3,2},{4,5},{5,4},{6,7},{7,6},{8,9},{9,8},{10,11... | collective-permute-start | bytes 491528 | tf_op jit(solution)/shard_map/ppermute | solution.py:43
  7.3 7.8 %copy-start.2 = (bf16[32,2560]{1,0:T(8,128)(2,1)S(1)}, bf16[32,2560]{1,0:T(8,128)(2,1)}, u32[]{:S(2)}) copy-start(bf16[32,2560]{1,0:T(8,128)(2,1)} %t0.1) | copy-start | bytes 491524
  7.3 7.8 %copy-start.3 = (bf16[2560,10]{0,1:T(8,128)(2,1)S(1)}, bf16[2560,10]{0,1:T(8,128)(2,1)}, u32[]{:S(2)}) copy-start(bf16[2560,10]{0,1:T(8,128)(2,1)} %param.13) | copy-start | bytes 153604
  11.4 3.0 %collective-permute-start.4 = (bf16[32,2560]{1,0:T(8,128)(2,1)S(1)}, bf16[32,2560]{1,0:T(8,128)(2,1)S(1)}, u32[]{:S(2)}, u32[]{:S(2)}) collective-permute-start(bf16[32,2560]{1,0:T(8,128)(2,1)S(1)} %collective-permute-done.t1), channel_id=1, source_target_pairs={{0,1},{1,0},{2,3},{3,2},{4,5},{5,4},{6,7},{7,6},{8,9},{9,8},{10,11... | collective-permute-start | bytes 491528 | tf_op jit(solution)/shard_map/ppermute | solution.py:43
  13.5 1.4 %collective-permute-start.5 = (bf16[32,2560]{1,0:T(8,128)(2,1)S(1)}, bf16[32,2560]{1,0:T(8,128)(2,1)S(1)}, u32[]{:S(2)}, u32[]{:S(2)}) collective-permute-start(bf16[32,2560]{1,0:T(8,128)(2,1)S(1)} %collective-permute-done.1.t2), channel_id=1, source_target_pairs={{0,1},{1,0},{2,3},{3,2},{4,5},{5,4},{6,7},{7,6},{8,9},{9,8},{10,11... | collective-permute-start | bytes 491528 | tf_op jit(solution)/shard_map/ppermute | solution.py:43
  13.6 1.5 %collective-permute-start.6 = (bf16[32,2560]{1,0:T(8,128)(2,1)S(1)}, bf16[32,2560]{1,0:T(8,128)(2,1)S(1)}, u32[]{:S(2)}, u32[]{:S(2)}) collective-permute-start(bf16[32,2560]{1,0:T(8,128)(2,1)S(1)} %collective-permute-done.2.t3), channel_id=1, source_target_pairs={{0,1},{1,0},{2,3},{3,2},{4,5},{5,4},{6,7},{7,6},{8,9},{9,8},{10,11... | collective-permute-start | bytes 491528 | tf_op jit(solution)/shard_map/ppermute | solution.py:43
  17.0 4.2 %collective-permute-start.7 = (bf16[8,896]{1,0:T(8,128)(2,1)S(1)}, bf16[8,896]{1,0:T(8,128)(2,1)S(1)}, u32[]{:S(2)}, u32[]{:S(2)}) collective-permute-start(bf16[8,896]{1,0:T(8,128)(2,1)S(1)} %get-tuple-element.36), channel_id=1, source_target_pairs={{0,8},{8,16},{16,24},{24,32},{32,40},{40,48},{48,56},{56,64},{64,7... | collective-permute-start | bytes 43016 | tf_op jit(solution)/shard_map/ppermute | solution.py:320
  21.3 32.2 %copy-start = (bf16[640,2560]{1,0:T(8,128)(2,1)S(1)}, bf16[640,2560]{1,0:T(8,128)(2,1)}, u32[]{:S(2)}) copy-start(bf16[640,2560]{1,0:T(8,128)(2,1)} %w.3) | copy-start | bytes 9830404
  22.8 5.1 %collective-permute-start.8 = (bf16[40,640]{1,0:T(8,128)(2,1)S(1)}, bf16[40,640]{1,0:T(8,128)(2,1)S(1)}, u32[]{:S(2)}, u32[]{:S(2)}) collective-permute-start(bf16[40,640]{1,0:T(8,128)(2,1)S(1)} %get-tuple-element.40), channel_id=1, source_target_pairs={{0,8},{8,0},{16,24},{24,16},{1,9},{9,1},{17,25},{25,17},{2,10},{10... | collective-permute-start | bytes 153608 | tf_op jit(solution)/shard_map/ppermute | solution.py:43
  24.1 4.8 %collective-permute-start.9 = (bf16[40,640]{1,0:T(8,128)(2,1)S(1)}, bf16[40,640]{1,0:T(8,128)(2,1)S(1)}, u32[]{:S(2)}, u32[]{:S(2)}) collective-permute-start(bf16[40,640]{1,0:T(8,128)(2,1)S(1)} %get-tuple-element.41), channel_id=1, source_target_pairs={{0,16},{8,24},{16,0},{24,8},{1,17},{9,25},{17,1},{25,9},{2,18},{10... | collective-permute-start | bytes 153608 | tf_op jit(solution)/shard_map/ppermute | solution.py:43
  26.9 4.4 %collective-permute-start.10 = (bf16[40,640]{1,0:T(8,128)(2,1)S(1)}, bf16[40,640]{1,0:T(8,128)(2,1)S(1)}, u32[]{:S(2)}, u32[]{:S(2)}) collective-permute-start(bf16[40,640]{1,0:T(8,128)(2,1)S(1)} %get-tuple-element.42), channel_id=1, source_target_pairs={{0,24},{8,16},{16,8},{24,0},{1,25},{9,17},{17,9},{25,1},{2,26},{10... | collective-permute-start | bytes 153608 | tf_op jit(solution)/shard_map/ppermute | solution.py:43
  31.4 3.9 %collective-permute-start.11 = (bf16[40,640]{1,0:T(8,128)(2,1)S(1)}, bf16[40,640]{1,0:T(8,128)(2,1)S(1)}, u32[]{:S(2)}, u32[]{:S(2)}) collective-permute-start(bf16[40,640]{1,0:T(8,128)(2,1)S(1)} %rowtotal.1.row), channel_id=1, source_target_pairs={{0,32},{32,0},{64,96},{96,64},{128,160},{160,128},{192,224},{224,1... | collective-permute-start | bytes 153608 | tf_op jit(solution)/shard_map/ppermute | solution.py:43
  35.3 5.1 %collective-permute-start.12 = (bf16[40,640]{1,0:T(8,128)(2,1)S(1)}, bf16[40,640]{1,0:T(8,128)(2,1)S(1)}, u32[]{:S(2)}, u32[]{:S(2)}) collective-permute-start(bf16[40,640]{1,0:T(8,128)(2,1)S(1)} %pairtotal.1), channel_id=1, source_target_pairs={{0,64},{32,96},{64,0},{96,32},{128,192},{160,224},{192,128},{224,1... | collective-permute-start | bytes 153608 | tf_op jit(solution)/shard_map/ppermute | solution.py:43
  40.4 4.9 %collective-permute-start.13 = (bf16[40,640]{1,0:T(8,128)(2,1)S(1)}, bf16[40,640]{1,0:T(8,128)(2,1)S(1)}, u32[]{:S(2)}, u32[]{:S(2)}) collective-permute-start(bf16[40,640]{1,0:T(8,128)(2,1)S(1)} %quadtotal.1), channel_id=1, source_target_pairs={{0,224},{32,192},{64,160},{96,128},{128,96},{160,64},{192,32},{224... | collective-permute-start | bytes 153608 | tf_op jit(solution)/shard_map/ppermute | solution.py:43
  45.5 3.9 %collective-permute-start.14 = (bf16[32,640]{1,0:T(8,128)(2,1)S(1)}, bf16[32,640]{1,0:T(8,128)(2,1)S(1)}, u32[]{:S(2)}, u32[]{:S(2)}) collective-permute-start(bf16[32,640]{1,0:T(8,128)(2,1)S(1)} %get-tuple-element.49), channel_id=1, source_target_pairs={{0,8},{8,0},{16,24},{24,16},{1,9},{9,1},{17,25},{25,17},{2,10},{10... | collective-permute-start | bytes 122888 | tf_op jit(solution)/shard_map/ppermute | solution.py:43
  45.8 5.4 %collective-permute-start.15 = (bf16[32,640]{1,0:T(8,128)(2,1)S(1)}, bf16[32,640]{1,0:T(8,128)(2,1)S(1)}, u32[]{:S(2)}, u32[]{:S(2)}) collective-permute-start(bf16[32,640]{1,0:T(8,128)(2,1)S(1)} %get-tuple-element.50), channel_id=1, source_target_pairs={{0,16},{8,24},{16,0},{24,8},{1,17},{9,25},{17,1},{25,9},{2,18},{10... | collective-permute-start | bytes 122888 | tf_op jit(solution)/shard_map/ppermute | solution.py:43
  49.4 4.1 %collective-permute-start.16 = (bf16[32,640]{1,0:T(8,128)(2,1)S(1)}, bf16[32,640]{1,0:T(8,128)(2,1)S(1)}, u32[]{:S(2)}, u32[]{:S(2)}) collective-permute-start(bf16[32,640]{1,0:T(8,128)(2,1)S(1)} %get-tuple-element.51), channel_id=1, source_target_pairs={{0,24},{8,16},{16,8},{24,0},{1,25},{9,17},{17,9},{25,1},{2,26},{10... | collective-permute-start | bytes 122888 | tf_op jit(solution)/shard_map/ppermute | solution.py:43
  54.6 9.5 %collective-permute-start.17 = (bf16[128,2688]{1,0:T(8,128)(2,1)S(1)}, bf16[128,2688]{1,0:T(8,128)(2,1)S(1)}, u32[]{:S(2)}, u32[]{:S(2)}) collective-permute-start(bf16[128,2688]{1,0:T(8,128)(2,1)S(1)} %get-tuple-element.54), channel_id=1, source_target_pairs={{0,1},{1,0},{2,3},{3,2},{4,5},{5,4},{6,7},{7,6},{8,9},{9,8},{10,11... | collective-permute-start | bytes 2064392 | tf_op jit(solution)/shard_map/ppermute | solution.py:43
  64.4 5.6 %collective-permute-start.18 = (bf16[32,2688]{1,0:T(8,128)(2,1)S(1)}, bf16[32,2688]{1,0:T(8,128)(2,1)S(1)}, u32[]{:S(2)}, u32[]{:S(2)}) collective-permute-start(bf16[32,2688]{1,0:T(8,128)(2,1)S(1)} %get-tuple-element.56), channel_id=1, source_target_pairs={{0,2},{2,0},{4,6},{6,4},{1,3},{3,1},{5,7},{7,5},{8,10},{10,8},{12,... | collective-permute-start | bytes 516104 | tf_op jit(solution)/shard_map/ppermute | solution.py:43
  65.4 10.4 %collective-permute-start.19 = (bf16[32,2688]{1,0:T(8,128)(2,1)S(1)}, bf16[32,2688]{1,0:T(8,128)(2,1)S(1)}, u32[]{:S(2)}, u32[]{:S(2)}) collective-permute-start(bf16[32,2688]{1,0:T(8,128)(2,1)S(1)} %get-tuple-element.57), channel_id=1, source_target_pairs={{0,4},{2,6},{4,0},{6,2},{1,5},{3,7},{5,1},{7,3},{8,12},{10,14},{12... | collective-permute-start | bytes 516104 | tf_op jit(solution)/shard_map/ppermute | solution.py:43
  68.0 10.5 %collective-permute-start.20 = (bf16[32,2688]{1,0:T(8,128)(2,1)S(1)}, bf16[32,2688]{1,0:T(8,128)(2,1)S(1)}, u32[]{:S(2)}, u32[]{:S(2)}) collective-permute-start(bf16[32,2688]{1,0:T(8,128)(2,1)S(1)} %get-tuple-element.58), channel_id=1, source_target_pairs={{0,6},{2,4},{4,2},{6,0},{1,7},{3,5},{5,3},{7,1},{8,14},{10,12},{12... | collective-permute-start | bytes 516104 | tf_op jit(solution)/shard_map/ppermute | solution.py:43
  (6 other events, 19.6 us)

commit v6 on v5

--- a/solution.py
+++ b/solution.py
@@ -20,6 +20,8 @@
 MODEL = 2560
 WIDE = MODEL + 128
 PIECE = 40
+MASKS = (0, 2, 1, 3)
+TOKEN_MASKS = (0, 1, 3, 2)
 
 
 def whole(count):
@@ -43,6 +45,10 @@
     return lax.ppermute(value, axis, [(i, i ^ mask) for i in range(lax.axis_size(axis))])
 
 
+def exchanged(pieces, axis, masks):
+    return [swapped(piece, axis, mask) if mask else piece for mask, piece in zip(masks, pieces)]
+
+
 def other_index(index, mask):
     return lax.bitwise_xor(index, jnp.int32(mask))
 
@@ -53,7 +59,7 @@
 
 def project_kernel(t0, t1, t2, t3, o0, o1, o2, o3, w, w_bc, w_dt, early, all_out, pre_out, tail_out, dt_out, w_steps):
     y, c = lax.axis_index("y"), lax.axis_index("c")
-    for d, (own, other) in enumerate(((t0, o0), (t1, o1), (t2, o2), (t3, o3))):
+    for d, own, other in zip(TOKEN_MASKS, (t0, t1, t2, t3), (o0, o1, o2, o3)):
         source = other_index(y, d)
         all_out[row_at(source * 2 + c, ROWS), :] = own[...]
         all_out[row_at(source * 2 + 1 - c, ROWS), :] = other[...]
@@ -154,7 +160,7 @@
         extra = decay_rows(spread(factor, pair))
         for out in (p0, p1, p2, p3):
             out[32:40, cols] = extra
-    for d, out in enumerate((p0, p1, p2, p3)):
+    for d, out in zip(MASKS, (p0, p1, p2, p3)):
         out[0:32, :] = state[row_at(other_index(x, d), 32), :].astype(BF)
 
 
@@ -180,7 +186,7 @@
 
 def load_rows(pieces, held):
     x = lax.axis_index("x")
-    for d, piece in enumerate(pieces):
+    for d, piece in zip(MASKS, pieces):
         held[other_index(x, d)] = piece[...].astype(F32)
 
 
@@ -241,13 +247,13 @@
     for k in range(3):
         carry = carry * factor_of(held, k) + held[k, 0:32, :]
         ready[k + 1] = carry
-    for d, out in enumerate((e0, e1, e2, e3)):
+    for d, out in zip(MASKS, (e0, e1, e2, e3)):
         out[...] = ready[other_index(x, d)].astype(BF)
 
 
 def gated_kernel(e0, e1, e2, e3, c, cum, inside, gate, gain, w, g_out, sq_out, send_out, state, pick):
     x, core = lax.axis_index("x"), lax.axis_index("c")
-    for d, piece in enumerate((e0, e1, e2, e3)):
+    for d, piece in zip(MASKS, (e0, e1, e2, e3)):
         state[row_at(other_index(x, d), 32), :] = piece[...]
     grown = jnp.exp(cum[...])
     squares = jnp.zeros((BLOCK, 128), F32)
@@ -289,7 +295,7 @@
 
 def pair_kernel(own, came, f0, f1, f2, f3):
     y = lax.axis_index("y")
-    for d, out in enumerate((f0, f1, f2, f3)):
+    for d, out in zip(MASKS, (f0, f1, f2, f3)):
         rows = row_at(other_index(y, d), ROWS)
         total = own[rows, :] + came[rows, :].astype(F32)
         out[:, :MODEL] = total[:, :MODEL].astype(out.dtype)
@@ -304,7 +310,7 @@
 
 
 def body(tokens, w_xz, w_bc, w_dt, dt_bias, a_log, conv_x, conv_bc, norm_gain, w_out):
-    near = [tokens] + [swapped(tokens, "y", d) for d in (1, 2, 3)]
+    near = exchanged([tokens] * 4, "y", TOKEN_MASKS)
     w_both = w_xz.reshape(MODEL, 2 * WIDTH)
     near[1:] = [lax.optimization_barrier((piece, w_both))[0] for piece in near[1:]]
     far = [swapped(piece, "c", 1) for piece in near]
@@ -328,7 +334,7 @@
         flops=2 * BLOCK * STATE * WIDTH,
         name="local",
     )
-    rows = [p0] + [swapped(piece, "x", d) for d, piece in ((1, p1), (2, p2), (3, p3))]
+    rows = exchanged([p0, p1, p2, p3], "x", MASKS)
     (inside,) = call(
         inside_kernel, [((BLOCK, WIDTH), F32)], [v, b, c, step, cum], flops=20 * BLOCK * BLOCK * 256, name="inside"
     )
@@ -346,7 +352,7 @@
         scratch=[((4, PIECE, WIDTH), F32), ((4, 32, WIDTH), F32)],
         name="incoming",
     )
-    states = [e0] + [swapped(piece, "x", d) for d, piece in ((1, e1), (2, e2), (3, e3))]
+    states = exchanged([e0, e1, e2, e3], "x", MASKS)
     g, squares, send = call(
         gated_kernel,
         [((BLOCK, WIDTH), BF), ((BLOCK, 128), F32), ((128, WIDE), BF)],
@@ -360,7 +366,7 @@
         own_kernel, [((128, WIDE), F32)], [g, squares, w_out], scratch=[((128, WIDTH), BF)], flops=2 * 128 * WIDTH * MODEL, name="own"
     )
     f0, f1, f2, f3 = call(pair_kernel, [((ROWS, WIDE), F32)] + [((ROWS, WIDE), BF)] * 3, [own, came], name="pair")
-    parts = [f0] + [swapped(piece, "y", d) for d, piece in ((1, f1), (2, f2), (3, f3))]
+    parts = exchanged([f0, f1, f2, f3], "y", MASKS)
     (out,) = call(finish_kernel, [((ROWS, MODEL), BF)], parts, name="finish")
     return out
 

time: 79.4 us -> 76 us (0.957)
  starting transfers between devices: 41.9 us -> 40 us
  waiting for transfers between devices: 24.3 us -> 22.8 us
    ppermute x20, starting transfers between devices: 39 us -> 37.4 us  [swapped(): lax.ppermute(value, axis, [(i, i ^ mask) for i in range(lax.axis_size(axi...]
    ppermute x20, waiting for transfers between devices: 24.3 us -> 22.8 us  [swapped(): lax.ppermute(value, axis, [(i, i ^ mask) for i in range(lax.axis_size(axi...]
  transfers between devices with their start and end apart: 21 -> 21, of which waited for: 14 -> 16; matrix products, arithmetic and copies ran while one was open for 5% -> 5% of each run, Pallas kernels for 4% -> 4%
where the time goes in v6:
time: 76 us; the launch traced here: 75.9 us
  starting transfers between devices  40 us (53%)
  waiting for transfers between devices  22.8 us (30%)
  Pallas kernels  8.72 us (11%)
  local copies, waits for them, and re-layouts  4.15 us (5%)
    ppermute x20, starting transfers between devices, swapped(): lax.ppermute(value, axis, [(i, i ^ mask) for i in range(lax.axis_size(axi...  37.4 us
    ppermute x20, waiting for transfers between devices, swapped(): lax.ppermute(value, axis, [(i, i ^ mask) for i in range(lax.axis_size(axi...  22.8 us
    pallas_call x12, Pallas kernels, call(): pl.pallas_call(body, out_shape=[jax.ShapeDtypeStruct(s, t) for s, t in ou...  8.72 us
    unnamed x19, local copies, waits for them, and re-layouts  4.15 us
    ppermute x1, starting transfers between devices, body(): tail = lax.ppermute(tail, SEQ, [(i, i + 1) for i in range(31)])  2.61 us
  transfers between devices with their start and end apart: 21, of which 16 were waited for; matrix products, arithmetic and copies ran while one was open for 5% of the time, Pallas kernels for 4%

profile of v6, /device:TPU:1, one launch (start us, length us, event | category | flops | bytes accessed | tf_op | source)
XLA Modules:
  0.0 75.9 jit_solution(14821904898710783482)
XLA Ops:
  0.0 3.7 %collective-permute-start.2 = (bf16[32,2560]{1,0:T(8,128)(2,1)}, bf16[32,2560]{1,0:T(8,128)(2,1)S(1)}, u32[]{:S(2)}, u32[]{:S(2)}) collective-permute-start(bf16[32,2560]{1,0:T(8,128)(2,1)} %t0.1), channel_id=1, source_target_pairs={{0,4},{2,6},{4,0},{6,2},{1,5},{3,7},{5,1},{7,3},{8,12},{10,14},{12... | collective-permute-start | bytes 491528 | tf_op jit(solution)/shard_map/ppermute | solution.py:45
  4.5 2.2 %collective-permute-start.3 = (bf16[32,2560]{1,0:T(8,128)(2,1)}, bf16[32,2560]{1,0:T(8,128)(2,1)S(1)}, u32[]{:S(2)}, u32[]{:S(2)}) collective-permute-start(bf16[32,2560]{1,0:T(8,128)(2,1)} %t0.1), channel_id=1, source_target_pairs={{0,1},{1,0},{2,3},{3,2},{4,5},{5,4},{6,7},{7,6},{8,9},{9,8},{10,11... | collective-permute-start | bytes 491528 | tf_op jit(solution)/shard_map/ppermute | solution.py:45
  6.7 4.1 %copy.11 = bf16[320,8,2,640]{3,1,2,0:T(8,128)(2,1)S(1)} copy(bf16[320,8,2,640]{3,2,1,0:T(2,128)(2,1)} %bitcast.10) | data formatting | bytes 13107200
  10.8 2.0 %collective-permute-done.1.t2 = bf16[32,2560]{1,0:T(8,128)(2,1)S(1)} collective-permute-done((bf16[32,2560]{1,0:T(8,128)(2,1)}, bf16[32,2560]{1,0:T(8,128)(2,1)S(1)}, u32[]{:S(2)}, u32[]{:S(2)}) %collective-permute-start.1) | collective-permute-done | bytes 163872 | tf_op jit(solution)/shard_map/ppermute | solution.py:45
  15.2 1.9 %project.1 = (bf16[256,2560]{1,0:T(8,128)(2,1)S(1)}, bf16[256,896]{1,0:T(8,128)(2,1)S(1)}, bf16[8,896]{1,0:T(8,128)(2,1)S(1)}, f32[256,128]{1,0:T(8,128)S(1)}) custom-call(bf16[32,2560]{1,0:T(8,128)(2,1)S(1)} %copy-done.2, bf16[32,2560]{1,0:T(8,128)(2,1)S(1)} %collective-permute-done.t1, bf16[32,2560]{1,0:T(8,128)(2,1)S(1)} %collective-permute-done.1.t2, ...), custom_call_target="tpu_custom_call" | custom-call | flops 1342177280 | bytes 2684354 | tf_op jit(solution)/shard_map/project/pallas_call | solution.py:32
  17.1 2.6 %collective-permute-start.7 = (bf16[8,896]{1,0:T(8,128)(2,1)S(1)}, bf16[8,896]{1,0:T(8,128)(2,1)S(1)}, u32[]{:S(2)}, u32[]{:S(2)}) collective-permute-start(bf16[8,896]{1,0:T(8,128)(2,1)S(1)} %get-tuple-element.36), channel_id=1, source_target_pairs={{0,8},{8,16},{16,24},{24,32},{32,40},{40,48},{48,56},{56,64},{64,7... | collective-permute-start | bytes 43016 | tf_op jit(solution)/shard_map/ppermute | solution.py:326
  21.0 1.4 %local.1 = (bf16[256,640]{1,0:T(8,128)(2,1)S(1)}, bf16[256,128]{1,0:T(8,128)(2,1)S(1)}, bf16[256,128]{1,0:T(8,128)(2,1)S(1)}, f32[256,128]{1,0:T(8,128)S(1)}, f3...) custom-call(bf16[256,896]{1,0:T(8,128)(2,1)S(1)} %get-tuple-element., ...), custom_call_target="tpu_custom_call" | custom-call | flops 41943040 | bytes 83886 | tf_op jit(solution)/shard_map/local/pallas_call | solution.py:32
  22.5 2.9 %collective-permute-start.8 = (bf16[40,640]{1,0:T(8,128)(2,1)S(1)}, bf16[40,640]{1,0:T(8,128)(2,1)S(1)}, u32[]{:S(2)}, u32[]{:S(2)}) collective-permute-start(bf16[40,640]{1,0:T(8,128)(2,1)S(1)} %get-tuple-element.40), channel_id=1, source_target_pairs={{0,16},{8,24},{16,0},{24,8},{1,17},{9,25},{17,1},{25,9},{2,18},{10... | collective-permute-start | bytes 153608 | tf_op jit(solution)/shard_map/ppermute | solution.py:45
  27.2 1.4 %collective-permute-done.9.q2 = bf16[40,640]{1,0:T(8,128)(2,1)S(1)} collective-permute-done((bf16[40,640]{1,0:T(8,128)(2,1)S(1)}, bf16[40,640]{1,0:T(8,128)(2,1)S(1)}, u32[]{:S(2)}, u32[]{:S(2)}) %collective-permute-start.9) | collective-permute-done | bytes 51232 | tf_op jit(solution)/shard_map/ppermute | solution.py:45
  28.6 1.5 %collective-permute-done.10.q3 = bf16[40,640]{1,0:T(8,128)(2,1)S(1)} collective-permute-done((bf16[40,640]{1,0:T(8,128)(2,1)S(1)}, bf16[40,640]{1,0:T(8,128)(2,1)S(1)}, u32[]{:S(2)}, u32[]{:S(2)}) %collective-permute-start.10) | collective-permute-done | bytes 51232 | tf_op jit(solution)/shard_map/ppermute | solution.py:45
  30.2 1.9 %collective-permute-start.11 = (bf16[40,640]{1,0:T(8,128)(2,1)S(1)}, bf16[40,640]{1,0:T(8,128)(2,1)S(1)}, u32[]{:S(2)}, u32[]{:S(2)}) collective-permute-start(bf16[40,640]{1,0:T(8,128)(2,1)S(1)} %rowtotal.1.row), channel_id=1, source_target_pairs={{0,32},{32,0},{64,96},{96,64},{128,160},{160,128},{192,224},{224,1... | collective-permute-start | bytes 153608 | tf_op jit(solution)/shard_map/ppermute | solution.py:45
  32.2 1.5 %collective-permute-done.11.other = bf16[40,640]{1,0:T(8,128)(2,1)S(1)} collective-permute-done((bf16[40,640]{1,0:T(8,128)(2,1)S(1)}, bf16[40,640]{1,0:T(8,128)(2,1)S(1)}, u32[]{:S(2)}, u32[]{:S(2)}) %collective-permute-start.11) | collective-permute-done | bytes 51232 | tf_op jit(solution)/shard_map/ppermute | solution.py:45
  33.7 4.5 %collective-permute-start.12 = (bf16[40,640]{1,0:T(8,128)(2,1)S(1)}, bf16[40,640]{1,0:T(8,128)(2,1)S(1)}, u32[]{:S(2)}, u32[]{:S(2)}) collective-permute-start(bf16[40,640]{1,0:T(8,128)(2,1)S(1)} %pairtotal.1), channel_id=1, source_target_pairs={{0,64},{32,96},{64,0},{96,32},{128,192},{160,224},{192,128},{224,1... | collective-permute-start | bytes 153608 | tf_op jit(solution)/shard_map/ppermute | solution.py:45
  38.2 1.5 %collective-permute-done.12.previous = bf16[40,640]{1,0:T(8,128)(2,1)S(1)} collective-permute-done((bf16[40,640]{1,0:T(8,128)(2,1)S(1)}, bf16[40,640]{1,0:T(8,128)(2,1)S(1)}, u32[]{:S(2)}, u32[]{:S(2)}) %collective-permute-start.12) | collective-permute-done | bytes 51232 | tf_op jit(solution)/shard_map/ppermute | solution.py:45
  39.8 3.2 %collective-permute-start.13 = (bf16[40,640]{1,0:T(8,128)(2,1)S(1)}, bf16[40,640]{1,0:T(8,128)(2,1)S(1)}, u32[]{:S(2)}, u32[]{:S(2)}) collective-permute-start(bf16[40,640]{1,0:T(8,128)(2,1)S(1)} %quadtotal.1), channel_id=1, source_target_pairs={{0,224},{32,192},{64,160},{96,128},{128,96},{160,64},{192,32},{224... | collective-permute-start | bytes 153608 | tf_op jit(solution)/shard_map/ppermute | solution.py:45
  43.0 1.5 %collective-permute-done.13.quad = bf16[40,640]{1,0:T(8,128)(2,1)S(1)} collective-permute-done((bf16[40,640]{1,0:T(8,128)(2,1)S(1)}, bf16[40,640]{1,0:T(8,128)(2,1)S(1)}, u32[]{:S(2)}, u32[]{:S(2)}) %collective-permute-start.13) | collective-permute-done | bytes 51232 | tf_op jit(solution)/shard_map/ppermute | solution.py:45
  44.6 1.2 %collective-permute-start.14 = (bf16[32,640]{1,0:T(8,128)(2,1)S(1)}, bf16[32,640]{1,0:T(8,128)(2,1)S(1)}, u32[]{:S(2)}, u32[]{:S(2)}) collective-permute-start(bf16[32,640]{1,0:T(8,128)(2,1)S(1)} %get-tuple-element.49), channel_id=1, source_target_pairs={{0,16},{8,24},{16,0},{24,8},{1,17},{9,25},{17,1},{25,9},{2,18},{10... | collective-permute-start | bytes 122888 | tf_op jit(solution)/shard_map/ppermute | solution.py:45
  45.8 1.8 %collective-permute-start.15 = (bf16[32,640]{1,0:T(8,128)(2,1)S(1)}, bf16[32,640]{1,0:T(8,128)(2,1)S(1)}, u32[]{:S(2)}, u32[]{:S(2)}) collective-permute-start(bf16[32,640]{1,0:T(8,128)(2,1)S(1)} %get-tuple-element.50), channel_id=1, source_target_pairs={{0,8},{8,0},{16,24},{24,16},{1,9},{9,1},{17,25},{25,17},{2,10},{10... | collective-permute-start | bytes 122888 | tf_op jit(solution)/shard_map/ppermute | solution.py:45
  49.4 2.2 %collective-permute-done.16.e3 = bf16[32,640]{1,0:T(8,128)(2,1)S(1)} collective-permute-done((bf16[32,640]{1,0:T(8,128)(2,1)S(1)}, bf16[32,640]{1,0:T(8,128)(2,1)S(1)}, u32[]{:S(2)}, u32[]{:S(2)}) %collective-permute-start.16) | collective-permute-done | bytes 40992 | tf_op jit(solution)/shard_map/ppermute | solution.py:45
  51.7 1.2 %gated.1 = (bf16[256,640]{1,0:T(8,128)(2,1)S(1)}, f32[256,128]{1,0:T(8,128)S(1)}, bf16[128,2688]{1,0:T(8,128)(2,1)S(1)}) custom-call(bf16[32,640]{1,0:T(8,128)(2,1)S(1)} %get-tuple-element.48.e0, bf16[32,640]{1,0:T(8,128)(2,1)S(1)} %collective-permute-done.14.e1, bf16[32,640]{1,0:T(8,128)(2,1)S(1)} %collective-permute-done.15.e2, ...), custom_call_target="tpu_custom_call" | custom-call | flops 419430400 | bytes 838860 | tf_op jit(solution)/shard_map/gated/pallas_call | solution.py:32
  52.9 9.2 %collective-permute-start.17 = (bf16[128,2688]{1,0:T(8,128)(2,1)S(1)}, bf16[128,2688]{1,0:T(8,128)(2,1)S(1)}, u32[]{:S(2)}, u32[]{:S(2)}) collective-permute-start(bf16[128,2688]{1,0:T(8,128)(2,1)S(1)} %get-tuple-element.54), channel_id=1, source_target_pairs={{0,1},{1,0},{2,3},{3,2},{4,5},{5,4},{6,7},{7,6},{8,9},{9,8},{10,11... | collective-permute-start | bytes 2064392 | tf_op jit(solution)/shard_map/ppermute | solution.py:45
  64.1 1.9 %collective-permute-start.18 = (bf16[32,2688]{1,0:T(8,128)(2,1)S(1)}, bf16[32,2688]{1,0:T(8,128)(2,1)S(1)}, u32[]{:S(2)}, u32[]{:S(2)}) collective-permute-start(bf16[32,2688]{1,0:T(8,128)(2,1)S(1)} %get-tuple-element.56), channel_id=1, source_target_pairs={{0,4},{2,6},{4,0},{6,2},{1,5},{3,7},{5,1},{7,3},{8,12},{10,14},{12... | collective-permute-start | bytes 516104 | tf_op jit(solution)/shard_map/ppermute | solution.py:45
  67.6 3.6 %collective-permute-done.18.g1 = bf16[32,2688]{1,0:T(8,128)(2,1)S(1)} collective-permute-done((bf16[32,2688]{1,0:T(8,128)(2,1)S(1)}, bf16[32,2688]{1,0:T(8,128)(2,1)S(1)}, u32[]{:S(2)}, u32[]{:S(2)}) %collective-permute-start.18) | collective-permute-done | bytes 172064 | tf_op jit(solution)/shard_map/ppermute | solution.py:45
  71.2 3.7 %collective-permute-done.19.g2 = bf16[32,2688]{1,0:T(8,128)(2,1)S(1)} collective-permute-done((bf16[32,2688]{1,0:T(8,128)(2,1)S(1)}, bf16[32,2688]{1,0:T(8,128)(2,1)S(1)}, u32[]{:S(2)}, u32[]{:S(2)}) %collective-permute-start.19) | collective-permute-done | bytes 172064 | tf_op jit(solution)/shard_map/ppermute | solution.py:45
  (50 shorter events, 13.0 us)
Async XLA Ops:
  0.0 10.8 %collective-permute-start.2 = (bf16[32,2560]{1,0:T(8,128)(2,1)}, bf16[32,2560]{1,0:T(8,128)(2,1)S(1)}, u32[]{:S(2)}, u32[]{:S(2)}) collective-permute-start(bf16[32,2560]{1,0:T(8,128)(2,1)} %t0.1), channel_id=1, source_target_pairs={{0,4},{2,6},{4,0},{6,2},{1,5},{3,7},{5,1},{7,3},{8,12},{10,14},{12... | collective-permute-start | bytes 491528 | tf_op jit(solution)/shard_map/ppermute | solution.py:45
  3.7 9.0 %collective-permute-start.1 = (bf16[32,2560]{1,0:T(8,128)(2,1)}, bf16[32,2560]{1,0:T(8,128)(2,1)S(1)}, u32[]{:S(2)}, u32[]{:S(2)}) collective-permute-start(bf16[32,2560]{1,0:T(8,128)(2,1)} %t0.1), channel_id=1, source_target_pairs={{0,6},{2,4},{4,2},{6,0},{1,7},{3,5},{5,3},{7,1},{8,14},{10,12},{12... | collective-permute-start | bytes 491528 | tf_op jit(solution)/shard_map/ppermute | solution.py:45
  4.5 8.3 %collective-permute-start = (bf16[32,2560]{1,0:T(8,128)(2,1)}, bf16[32,2560]{1,0:T(8,128)(2,1)S(1)}, u32[]{:S(2)}, u32[]{:S(2)}) collective-permute-start(bf16[32,2560]{1,0:T(8,128)(2,1)} %t0.1), channel_id=1, source_target_pairs={{0,2},{2,0},{4,6},{6,4},{1,3},{3,1},{5,7},{7,5},{8,10},{10,8},{12,... | collective-permute-start | bytes 491528 | tf_op jit(solution)/shard_map/ppermute | solution.py:45
  4.5 9.5 %collective-permute-start.3 = (bf16[32,2560]{1,0:T(8,128)(2,1)}, bf16[32,2560]{1,0:T(8,128)(2,1)S(1)}, u32[]{:S(2)}, u32[]{:S(2)}) collective-permute-start(bf16[32,2560]{1,0:T(8,128)(2,1)} %t0.1), channel_id=1, source_target_pairs={{0,1},{1,0},{2,3},{3,2},{4,5},{5,4},{6,7},{7,6},{8,9},{9,8},{10,11... | collective-permute-start | bytes 491528 | tf_op jit(solution)/shard_map/ppermute | solution.py:45
  6.7 8.5 %copy-start.2 = (bf16[32,2560]{1,0:T(8,128)(2,1)S(1)}, bf16[32,2560]{1,0:T(8,128)(2,1)}, u32[]{:S(2)}) copy-start(bf16[32,2560]{1,0:T(8,128)(2,1)} %t0.1) | copy-start | bytes 491524
  6.7 8.5 %copy-start.3 = (bf16[2560,10]{0,1:T(8,128)(2,1)S(1)}, bf16[2560,10]{0,1:T(8,128)(2,1)}, u32[]{:S(2)}) copy-start(bf16[2560,10]{0,1:T(8,128)(2,1)} %param.13) | copy-start | bytes 153604
  12.8 1.8 %collective-permute-start.4 = (bf16[32,2560]{1,0:T(8,128)(2,1)S(1)}, bf16[32,2560]{1,0:T(8,128)(2,1)S(1)}, u32[]{:S(2)}, u32[]{:S(2)}) collective-permute-start(bf16[32,2560]{1,0:T(8,128)(2,1)S(1)} %collective-permute-done.t1), channel_id=1, source_target_pairs={{0,1},{1,0},{2,3},{3,2},{4,5},{5,4},{6,7},{7,6},{8,9},{9,8},{10,11... | collective-permute-start | bytes 491528 | tf_op jit(solution)/shard_map/ppermute | solution.py:45
  13.5 1.4 %collective-permute-start.5 = (bf16[32,2560]{1,0:T(8,128)(2,1)S(1)}, bf16[32,2560]{1,0:T(8,128)(2,1)S(1)}, u32[]{:S(2)}, u32[]{:S(2)}) collective-permute-start(bf16[32,2560]{1,0:T(8,128)(2,1)S(1)} %collective-permute-done.1.t2), channel_id=1, source_target_pairs={{0,1},{1,0},{2,3},{3,2},{4,5},{5,4},{6,7},{7,6},{8,9},{9,8},{10,11... | collective-permute-start | bytes 491528 | tf_op jit(solution)/shard_map/ppermute | solution.py:45
  13.5 1.6 %collective-permute-start.6 = (bf16[32,2560]{1,0:T(8,128)(2,1)S(1)}, bf16[32,2560]{1,0:T(8,128)(2,1)S(1)}, u32[]{:S(2)}, u32[]{:S(2)}) collective-permute-start(bf16[32,2560]{1,0:T(8,128)(2,1)S(1)} %collective-permute-done.2.t3), channel_id=1, source_target_pairs={{0,1},{1,0},{2,3},{3,2},{4,5},{5,4},{6,7},{7,6},{8,9},{9,8},{10,11... | collective-permute-start | bytes 491528 | tf_op jit(solution)/shard_map/ppermute | solution.py:45
  17.1 3.9 %collective-permute-start.7 = (bf16[8,896]{1,0:T(8,128)(2,1)S(1)}, bf16[8,896]{1,0:T(8,128)(2,1)S(1)}, u32[]{:S(2)}, u32[]{:S(2)}) collective-permute-start(bf16[8,896]{1,0:T(8,128)(2,1)S(1)} %get-tuple-element.36), channel_id=1, source_target_pairs={{0,8},{8,16},{16,24},{24,32},{32,40},{40,48},{48,56},{56,64},{64,7... | collective-permute-start | bytes 43016 | tf_op jit(solution)/shard_map/ppermute | solution.py:326
  21.0 30.7 %copy-start = (bf16[640,2560]{1,0:T(8,128)(2,1)S(1)}, bf16[640,2560]{1,0:T(8,128)(2,1)}, u32[]{:S(2)}) copy-start(bf16[640,2560]{1,0:T(8,128)(2,1)} %w.3) | copy-start | bytes 9830404
  22.5 4.7 %collective-permute-start.8 = (bf16[40,640]{1,0:T(8,128)(2,1)S(1)}, bf16[40,640]{1,0:T(8,128)(2,1)S(1)}, u32[]{:S(2)}, u32[]{:S(2)}) collective-permute-start(bf16[40,640]{1,0:T(8,128)(2,1)S(1)} %get-tuple-element.40), channel_id=1, source_target_pairs={{0,16},{8,24},{16,0},{24,8},{1,17},{9,25},{17,1},{25,9},{2,18},{10... | collective-permute-start | bytes 153608 | tf_op jit(solution)/shard_map/ppermute | solution.py:45
  25.4 3.3 %collective-permute-start.9 = (bf16[40,640]{1,0:T(8,128)(2,1)S(1)}, bf16[40,640]{1,0:T(8,128)(2,1)S(1)}, u32[]{:S(2)}, u32[]{:S(2)}) collective-permute-start(bf16[40,640]{1,0:T(8,128)(2,1)S(1)} %get-tuple-element.41), channel_id=1, source_target_pairs={{0,8},{8,0},{16,24},{24,16},{1,9},{9,1},{17,25},{25,17},{2,10},{10... | collective-permute-start | bytes 153608 | tf_op jit(solution)/shard_map/ppermute | solution.py:45
  26.0 4.2 %collective-permute-start.10 = (bf16[40,640]{1,0:T(8,128)(2,1)S(1)}, bf16[40,640]{1,0:T(8,128)(2,1)S(1)}, u32[]{:S(2)}, u32[]{:S(2)}) collective-permute-start(bf16[40,640]{1,0:T(8,128)(2,1)S(1)} %get-tuple-element.42), channel_id=1, source_target_pairs={{0,24},{8,16},{16,8},{24,0},{1,25},{9,17},{17,9},{25,1},{2,26},{10... | collective-permute-start | bytes 153608 | tf_op jit(solution)/shard_map/ppermute | solution.py:45
  30.2 3.4 %collective-permute-start.11 = (bf16[40,640]{1,0:T(8,128)(2,1)S(1)}, bf16[40,640]{1,0:T(8,128)(2,1)S(1)}, u32[]{:S(2)}, u32[]{:S(2)}) collective-permute-start(bf16[40,640]{1,0:T(8,128)(2,1)S(1)} %rowtotal.1.row), channel_id=1, source_target_pairs={{0,32},{32,0},{64,96},{96,64},{128,160},{160,128},{192,224},{224,1... | collective-permute-start | bytes 153608 | tf_op jit(solution)/shard_map/ppermute | solution.py:45
  33.7 6.0 %collective-permute-start.12 = (bf16[40,640]{1,0:T(8,128)(2,1)S(1)}, bf16[40,640]{1,0:T(8,128)(2,1)S(1)}, u32[]{:S(2)}, u32[]{:S(2)}) collective-permute-start(bf16[40,640]{1,0:T(8,128)(2,1)S(1)} %pairtotal.1), channel_id=1, source_target_pairs={{0,64},{32,96},{64,0},{96,32},{128,192},{160,224},{192,128},{224,1... | collective-permute-start | bytes 153608 | tf_op jit(solution)/shard_map/ppermute | solution.py:45
  39.8 4.7 %collective-permute-start.13 = (bf16[40,640]{1,0:T(8,128)(2,1)S(1)}, bf16[40,640]{1,0:T(8,128)(2,1)S(1)}, u32[]{:S(2)}, u32[]{:S(2)}) collective-permute-start(bf16[40,640]{1,0:T(8,128)(2,1)S(1)} %quadtotal.1), channel_id=1, source_target_pairs={{0,224},{32,192},{64,160},{96,128},{128,96},{160,64},{192,32},{224... | collective-permute-start | bytes 153608 | tf_op jit(solution)/shard_map/ppermute | solution.py:45
  44.6 4.4 %collective-permute-start.14 = (bf16[32,640]{1,0:T(8,128)(2,1)S(1)}, bf16[32,640]{1,0:T(8,128)(2,1)S(1)}, u32[]{:S(2)}, u32[]{:S(2)}) collective-permute-start(bf16[32,640]{1,0:T(8,128)(2,1)S(1)} %get-tuple-element.49), channel_id=1, source_target_pairs={{0,16},{8,24},{16,0},{24,8},{1,17},{9,25},{17,1},{25,9},{2,18},{10... | collective-permute-start | bytes 122888 | tf_op jit(solution)/shard_map/ppermute | solution.py:45
  45.8 3.6 %collective-permute-start.15 = (bf16[32,640]{1,0:T(8,128)(2,1)S(1)}, bf16[32,640]{1,0:T(8,128)(2,1)S(1)}, u32[]{:S(2)}, u32[]{:S(2)}) collective-permute-start(bf16[32,640]{1,0:T(8,128)(2,1)S(1)} %get-tuple-element.50), channel_id=1, source_target_pairs={{0,8},{8,0},{16,24},{24,16},{1,9},{9,1},{17,25},{25,17},{2,10},{10... | collective-permute-start | bytes 122888 | tf_op jit(solution)/shard_map/ppermute | solution.py:45
  47.6 4.1 %collective-permute-start.16 = (bf16[32,640]{1,0:T(8,128)(2,1)S(1)}, bf16[32,640]{1,0:T(8,128)(2,1)S(1)}, u32[]{:S(2)}, u32[]{:S(2)}) collective-permute-start(bf16[32,640]{1,0:T(8,128)(2,1)S(1)} %get-tuple-element.51), channel_id=1, source_target_pairs={{0,24},{8,16},{16,8},{24,0},{1,25},{9,17},{17,9},{25,1},{2,26},{10... | collective-permute-start | bytes 122888 | tf_op jit(solution)/shard_map/ppermute | solution.py:45
  52.9 11.0 %collective-permute-start.17 = (bf16[128,2688]{1,0:T(8,128)(2,1)S(1)}, bf16[128,2688]{1,0:T(8,128)(2,1)S(1)}, u32[]{:S(2)}, u32[]{:S(2)}) collective-permute-start(bf16[128,2688]{1,0:T(8,128)(2,1)S(1)} %get-tuple-element.54), channel_id=1, source_target_pairs={{0,1},{1,0},{2,3},{3,2},{4,5},{5,4},{6,7},{7,6},{8,9},{9,8},{10,11... | collective-permute-start | bytes 2064392 | tf_op jit(solution)/shard_map/ppermute | solution.py:45
  64.1 7.1 %collective-permute-start.18 = (bf16[32,2688]{1,0:T(8,128)(2,1)S(1)}, bf16[32,2688]{1,0:T(8,128)(2,1)S(1)}, u32[]{:S(2)}, u32[]{:S(2)}) collective-permute-start(bf16[32,2688]{1,0:T(8,128)(2,1)S(1)} %get-tuple-element.56), channel_id=1, source_target_pairs={{0,4},{2,6},{4,0},{6,2},{1,5},{3,7},{5,1},{7,3},{8,12},{10,14},{12... | collective-permute-start | bytes 516104 | tf_op jit(solution)/shard_map/ppermute | solution.py:45
  65.9 9.0 %collective-permute-start.19 = (bf16[32,2688]{1,0:T(8,128)(2,1)S(1)}, bf16[32,2688]{1,0:T(8,128)(2,1)S(1)}, u32[]{:S(2)}, u32[]{:S(2)}) collective-permute-start(bf16[32,2688]{1,0:T(8,128)(2,1)S(1)} %get-tuple-element.57), channel_id=1, source_target_pairs={{0,2},{2,0},{4,6},{6,4},{1,3},{3,1},{5,7},{7,5},{8,10},{10,8},{12,... | collective-permute-start | bytes 516104 | tf_op jit(solution)/shard_map/ppermute | solution.py:45
  67.1 8.0 %collective-permute-start.20 = (bf16[32,2688]{1,0:T(8,128)(2,1)S(1)}, bf16[32,2688]{1,0:T(8,128)(2,1)S(1)}, u32[]{:S(2)}, u32[]{:S(2)}) collective-permute-start(bf16[32,2688]{1,0:T(8,128)(2,1)S(1)} %get-tuple-element.58), channel_id=1, source_target_pairs={{0,6},{2,4},{4,2},{6,0},{1,7},{3,5},{5,3},{7,1},{8,14},{10,12},{12... | collective-permute-start | bytes 516104 | tf_op jit(solution)/shard_map/ppermute | solution.py:45
  (6 other events, 20.9 us)

commit v7 on v6

--- a/solution.py
+++ b/solution.py
@@ -19,7 +19,7 @@
 PRE = WIDTH + 2 * STATE
 MODEL = 2560
 WIDE = MODEL + 128
-PIECE = 40
+PIECE = 168
 MASKS = (0, 2, 1, 3)
 TOKEN_MASKS = (0, 1, 3, 2)
 
@@ -76,7 +76,7 @@
     dt_out[...] = lax.dot_general(tokens, w_steps[...], (((1,), (1,)), ((), ())), preferred_element_type=F32)
 
 
-def gate_kernel(tokens, w, out):
+def gate_kernel(tokens, w, before, out):
     for lo, hi in ((0, 256), (256, 512), (512, WIDTH)):
         gate = jnp.dot(tokens[...], w[:, WIDTH + lo : WIDTH + hi], preferred_element_type=F32)
         out[:, lo:hi] = jax.nn.silu(gate.astype(BF).astype(F32))
@@ -95,36 +95,32 @@
     return high, (value - high.astype(F32)).astype(BF)
 
 
-def decay_rows(factor):
-    high, low = halves(factor)
-    row = lax.broadcasted_iota(jnp.int32, factor.shape, 0)
-    return jnp.where(row == 0, high.astype(F32), jnp.where(row == 1, low.astype(F32), 0.0)).astype(BF)
-
-
-def local_kernel(
+def mixed(ext, first, kernel, lo, rows):
+    total = jnp.zeros((rows, 128), F32)
+    for k in range(4):
+        total = total + kernel[k : k + 1, lo : lo + 128].astype(F32) * ext[5 + k : 5 + k + rows, first : first + 128]
+    return jax.nn.silu(total).astype(BF)
+
+
+def prepare_kernel(
     pre,
-    tail,
     dt_pre,
     conv_x,
     conv_bc,
     bias,
     a_log,
-    before,
     v_out,
     b_out,
     c_out,
     dt_out,
     cum_out,
-    p0,
-    p1,
-    p2,
-    p3,
+    weight_out,
+    factor_out,
+    state_out,
     ext,
-    state,
     small,
 ):
-    x = lax.axis_index("x")
-    ext[0:8, :] = tail[...].astype(F32)
+    ext[0:8, :] = jnp.zeros((8, PRE), F32)
     ext[8 : 8 + BLOCK, :] = pre[...].astype(F32)
     small[...] = jnp.zeros(small.shape, F32)
     small[0:1, 0 : bias.shape[1]] = bias[...]
@@ -138,34 +134,62 @@
     dt_out[...] = step
     cum_out[...] = cum
     last = cum[BLOCK - 1 : BLOCK, :]
-    tail_weight = jnp.exp(last - cum) * step
-
-    def mixed(first, kernel, lo):
-        total = jnp.zeros((BLOCK, 128), F32)
-        for k in range(4):
-            total = total + kernel[k : k + 1, lo : lo + 128].astype(F32) * ext[5 + k : 5 + k + BLOCK, first : first + 128]
-        return jax.nn.silu(total).astype(BF)
-
-    b = mixed(WIDTH, conv_bc, 0)
+    weight = jnp.exp(last - cum) * step
+    weight_out[...] = weight[0:8, :]
+    factor_out[...] = jnp.broadcast_to(jnp.exp(last), (8, 128))
+    weight = jnp.where(row >= 3, weight, 0.0)
+    b = mixed(ext, WIDTH, conv_bc, 0, BLOCK)
     b_out[...] = b
-    c_out[...] = mixed(WIDTH + STATE, conv_bc, STATE)
-    factor = jnp.broadcast_to(jnp.exp(last), (8, 128))
+    c_out[...] = mixed(ext, WIDTH + STATE, conv_bc, STATE, BLOCK)
     b_rows = b.astype(F32).T.astype(BF)
     for pair in range(5):
         cols = slice(128 * pair, 128 * pair + 128)
-        v = mixed(128 * pair, conv_x, 128 * pair)
+        v = mixed(ext, 128 * pair, conv_x, 128 * pair, BLOCK)
         v_out[:, cols] = v
-        scaled = (spread(tail_weight, pair) * v.astype(F32)).astype(BF)
-        state[:, cols] = jnp.dot(b_rows, scaled, preferred_element_type=F32)
-        extra = decay_rows(spread(factor, pair))
-        for out in (p0, p1, p2, p3):
-            out[32:40, cols] = extra
+        scaled = (spread(weight, pair) * v.astype(F32)).astype(BF)
+        state_out[:, cols] = jnp.dot(b_rows, scaled, preferred_element_type=F32)
+
+
+def decay_rows(factor):
+    high, low = halves(factor)
+    row = lax.broadcasted_iota(jnp.int32, (8, 128), 0)
+    return jnp.where(row == 0, high.astype(F32), jnp.where(row == 1, low.astype(F32), 0.0)).astype(BF)
+
+
+def local_kernel(tail, pre, conv_x, conv_bc, weight, factor, main, v_out, b_out, c_out, p0, p1, p2, p3, ext, state):
+    x = lax.axis_index("x")
+    first = jnp.logical_and(lax.axis_index("z") == 0, x == 0)
+    ext[0:8, :] = jnp.where(first, 0.0, tail[...].astype(F32))
+    ext[8:16, :] = pre[0:8, :].astype(F32)
+    b = mixed(ext, WIDTH, conv_bc, 0, 8)
+    b_out[...] = b
+    c_out[...] = mixed(ext, WIDTH + STATE, conv_bc, STATE, 8)
+    b_rows = jnp.broadcast_to(b.astype(F32)[None], (16, 8, 128)).reshape(128, 128).T
+    extra = decay_rows(factor[0:1, :])
+    for pair in range(5):
+        cols = slice(128 * pair, 128 * pair + 128)
+        v = mixed(ext, 128 * pair, conv_x, 128 * pair, 8)
+        v_out[:, cols] = v
+        scaled = (spread(weight[...], pair) * v.astype(F32)).astype(BF).astype(F32)
+        total = main[:, cols]
+        for k in range(3):
+            total = total + b_rows[:, k : k + 1] * scaled[k : k + 1, :]
+        state[:, cols] = total
     for d, out in zip(MASKS, (p0, p1, p2, p3)):
-        out[0:32, :] = state[row_at(other_index(x, d), 32), :].astype(BF)
-
-
-def inside_kernel(v, b, c, step, cum, out):
-    scores = jnp.dot(c[...], b[...].astype(F32).T.astype(BF), preferred_element_type=F32)
+        rows = row_at(other_index(x, d), 32)
+        for pair in range(5):
+            out[32 * pair : 32 * pair + 32, :] = state[rows, 128 * pair : 128 * pair + 128].astype(BF)
+        out[160:168, :] = extra
+
+
+def inside_kernel(v, b, c, v_first, b_first, c_first, step, cum, out, c_out, values, b_all):
+    values[...] = v[...]
+    values[0:8, :] = v_first[...]
+    b_all[...] = b[...]
+    b_all[0:8, :] = b_first[...]
+    c_out[...] = c[...]
+    c_out[0:8, :] = c_first[...]
+    scores = jnp.dot(c_out[...], b_all[...].astype(F32).T.astype(BF), preferred_element_type=F32)
     t = lax.broadcasted_iota(jnp.int32, (BLOCK, BLOCK), 0)
     s = lax.broadcasted_iota(jnp.int32, (BLOCK, BLOCK), 1)
     scores = jnp.where(t >= s, scores, 0.0)
@@ -175,7 +199,7 @@
     lane = lax.broadcasted_iota(jnp.int32, (BLOCK, 128), 1)
     for pair in range(5):
         cols = slice(128 * pair, 128 * pair + 128)
-        value = v[:, cols]
+        value = values[:, cols]
         parts = []
         for h in (2 * pair, 2 * pair + 1):
             differ = jnp.broadcast_to(cum_all[:, h : h + 1], (BLOCK, BLOCK)) - cum_rows[h : h + 1, :]
@@ -190,33 +214,34 @@
         held[other_index(x, d)] = piece[...].astype(F32)
 
 
-def factor_of(held, k):
-    return held[k, 32:33, :] + held[k, 33:34, :]
-
-
-def pack(out, total, factor):
-    out[0:32, :] = total.astype(BF)
-    out[32:40, :] = decay_rows(jnp.broadcast_to(factor, (8, WIDTH)))
+def split(piece):
+    return [piece[32 * k : 32 * k + 32] for k in range(5)], piece[160:161] + piece[161:162]
 
 
 def unpack(ref):
-    return ref[0:32, :].astype(F32), ref[32:33, :].astype(F32) + ref[33:34, :].astype(F32)
+    return split(ref[...].astype(F32))
+
+
+def pack(out, item):
+    for k, part in enumerate(item[0]):
+        out[32 * k : 32 * k + 32, :] = part.astype(BF)
+    out[160:168, :] = decay_rows(item[1])
 
 
 def follow(earlier, later):
-    return earlier[0] * later[1] + later[0], earlier[1] * later[1]
+    return [e * spread(later[1], k) + l for k, (e, l) in enumerate(zip(earlier[0], later[0]))], earlier[1] * later[1]
 
 
 def choose(test, yes, no):
-    return jnp.where(test, yes[0], no[0]), jnp.where(test, yes[1], no[1])
-
-
-def row_total_kernel(q0, q1, q2, q3, before, out, held):
+    return [jnp.where(test, y, n) for y, n in zip(yes[0], no[0])], jnp.where(test, yes[1], no[1])
+
+
+def row_total_kernel(q0, q1, q2, q3, before, before_too, out, held):
     load_rows((q0, q1, q2, q3), held)
-    total = held[0, 0:32, :], factor_of(held, 0)
+    total = split(held[0])
     for k in range(1, 4):
-        total = follow(total, (held[k, 0:32, :], factor_of(held, k)))
-    pack(out, *total)
+        total = follow(total, split(held[k]))
+    pack(out, total)
 
 
 def two_rows(row, other):
@@ -226,27 +251,28 @@
 
 
 def pair_total_kernel(row, other, out):
-    pack(out, *two_rows(row, other)[2])
+    pack(out, two_rows(row, other)[2])
 
 
 def quad_total_kernel(row, other, previous, out):
     first = lax.rem(lax.axis_index("z"), 4) < 2
     mine, theirs = two_rows(row, other)[2], unpack(previous)
-    pack(out, *follow(choose(first, mine, theirs), choose(first, theirs, mine)))
+    pack(out, follow(choose(first, mine, theirs), choose(first, theirs, mine)))
 
 
 def incoming_kernel(q0, q1, q2, q3, row, other, previous, quad, e0, e1, e2, e3, held, ready):
     z, x = lax.axis_index("z"), lax.axis_index("x")
     load_rows((q0, q1, q2, q3), held)
     odd, theirs, _ = two_rows(row, other)
-    carry = choose(odd, theirs, (jnp.zeros((32, WIDTH), F32), jnp.ones((1, WIDTH), F32)))
+    carry = choose(odd, theirs, ([jnp.zeros((32, 128), F32)] * 5, jnp.ones((1, 128), F32)))
     second = lax.rem(z, 4) >= 2
     carry = choose(second, follow(unpack(previous), carry), carry)
-    carry, _ = choose(z >= 4, follow(unpack(quad), carry), carry)
-    ready[0] = carry
-    for k in range(3):
-        carry = carry * factor_of(held, k) + held[k, 0:32, :]
-        ready[k + 1] = carry
+    carry = choose(z >= 4, follow(unpack(quad), carry), carry)
+    for k in range(4):
+        for j, part in enumerate(carry[0]):
+            ready[k, :, 128 * j : 128 * j + 128] = part
+        if k < 3:
+            carry = follow(carry, split(held[k]))
     for d, out in zip(MASKS, (e0, e1, e2, e3)):
         out[...] = ready[other_index(x, d)].astype(BF)
 
@@ -323,23 +349,37 @@
         flops=2 * BLOCK * MODEL * 1024,
         name="project",
     )
-    tail = lax.ppermute(tail, SEQ, [(i, i + 1) for i in range(31)])
-    (gate,) = call(gate_kernel, [((BLOCK, WIDTH), F32)], [everything, w_both], flops=2 * BLOCK * MODEL * WIDTH, name="gate")
-    v, b, c, step, cum, p0, p1, p2, p3 = call(
+    tail = lax.ppermute(tail, SEQ, [(i, (i + 1) % 32) for i in range(32)])
+    v, b, c, step, cum, weight, factor, main = call(
+        prepare_kernel,
+        [((BLOCK, WIDTH), BF), ((BLOCK, STATE), BF), ((BLOCK, STATE), BF), ((BLOCK, 128), F32), ((BLOCK, 128), F32)]
+        + [((8, 128), F32), ((8, 128), F32), ((STATE, WIDTH), F32)],
+        [pre, dt_pre, conv_x, conv_bc, dt_bias[None], a_log[None]],
+        scratch=[((BLOCK + 8, PRE), F32), ((8, 128), F32)],
+        flops=2 * BLOCK * STATE * WIDTH,
+        name="prepare",
+    )
+    v_first, b_first, c_first, p0, p1, p2, p3 = call(
         local_kernel,
-        [((BLOCK, WIDTH), BF), ((BLOCK, STATE), BF), ((BLOCK, STATE), BF), ((BLOCK, 128), F32), ((BLOCK, 128), F32)]
-        + [((PIECE, WIDTH), BF)] * 4,
-        [pre, tail, dt_pre, conv_x, conv_bc, dt_bias[None], a_log[None], gate],
-        scratch=[((BLOCK + 8, PRE), F32), ((STATE, WIDTH), F32), ((8, 128), F32)],
-        flops=2 * BLOCK * STATE * WIDTH,
+        [((8, WIDTH), BF), ((8, STATE), BF), ((8, STATE), BF)] + [((PIECE, 128), BF)] * 4,
+        [tail, pre, conv_x, conv_bc, weight, factor, main],
+        scratch=[((16, PRE), F32), ((STATE, WIDTH), F32)],
         name="local",
     )
     rows = exchanged([p0, p1, p2, p3], "x", MASKS)
-    (inside,) = call(
-        inside_kernel, [((BLOCK, WIDTH), F32)], [v, b, c, step, cum], flops=20 * BLOCK * BLOCK * 256, name="inside"
-    )
-    piece = [((PIECE, WIDTH), BF)]
-    (row,) = call(row_total_kernel, piece, [*rows, inside], scratch=[((4, PIECE, WIDTH), F32)], name="rowtotal")
+    inside, c_all = call(
+        inside_kernel,
+        [((BLOCK, WIDTH), F32), ((BLOCK, STATE), BF)],
+        [v, b, c, v_first, b_first, c_first, step, cum],
+        scratch=[((BLOCK, WIDTH), BF), ((BLOCK, STATE), BF)],
+        flops=20 * BLOCK * BLOCK * 256,
+        name="inside",
+    )
+    (gate,) = call(
+        gate_kernel, [((BLOCK, WIDTH), F32)], [everything, w_both, v_first], flops=2 * BLOCK * MODEL * WIDTH, name="gate"
+    )
+    piece = [((PIECE, 128), BF)]
+    (row,) = call(row_total_kernel, piece, [*rows, inside, gate], scratch=[((4, PIECE, 128), F32)], name="rowtotal")
     other = swapped(row, "z", 1)
     (two,) = call(pair_total_kernel, piece, [row, other], name="pairtotal")
     previous = swapped(two, "z", 2)
@@ -349,14 +389,14 @@
         incoming_kernel,
         [((32, WIDTH), BF)] * 4,
         [*rows, row, other, previous, quad],
-        scratch=[((4, PIECE, WIDTH), F32), ((4, 32, WIDTH), F32)],
+        scratch=[((4, PIECE, 128), F32), ((4, 32, WIDTH), F32)],
         name="incoming",
     )
     states = exchanged([e0, e1, e2, e3], "x", MASKS)
     g, squares, send = call(
         gated_kernel,
         [((BLOCK, WIDTH), BF), ((BLOCK, 128), F32), ((128, WIDE), BF)],
-        [*states, c, cum, inside, gate, gain, w_out],
+        [*states, c_all, cum, inside, gate, gain, w_out],
         scratch=[((STATE, WIDTH), BF), ((128, WIDTH), BF)],
         flops=2 * 128 * WIDTH * MODEL,
         name="gated",

time: 76 us -> 73.3 us (0.964)
  starting transfers between devices: 40 us -> 28.7 us
  waiting for transfers between devices: 22.8 us -> 30.8 us
    ppermute x20, starting transfers between devices: 37.4 us -> 27.9 us  [swapped(): lax.ppermute(value, axis, [(i, i ^ mask) for i in range(lax.axis_size(axi...]
    ppermute x1, waiting for transfers between devices: 0.01 us -> 6.27 us  [body(): tail = lax.ppermute(tail, SEQ, [(i, (i + 1) % 32) for i in range(32)])]
    ppermute x1, starting transfers between devices: 2.61 us -> 0.79 us  [body(): tail = lax.ppermute(tail, SEQ, [(i, (i + 1) % 32) for i in range(32)])]
    ppermute x20, waiting for transfers between devices: 22.8 us -> 24.6 us  [swapped(): lax.ppermute(value, axis, [(i, i ^ mask) for i in range(lax.axis_size(axi...]
    pallas_call x12 -> x13, Pallas kernels: 8.72 us -> 9.25 us  [call(): pl.pallas_call(body, out_shape=[jax.ShapeDtypeStruct(s, t) for s, t in ou...]
  transfers between devices with their start and end apart: 21 -> 21, of which waited for: 16 -> 15; matrix products, arithmetic and copies ran while one was open for 5% -> 6% of each run, Pallas kernels for 4% -> 6%
where the time goes in v7:
time: 73.3 us; the launch traced here: 73.2 us
  waiting for transfers between devices  30.8 us (42%)
  starting transfers between devices  28.7 us (39%)
  Pallas kernels  9.25 us (13%)
  local copies, waits for them, and re-layouts  4.15 us (6%)
    ppermute x20, starting transfers between devices, swapped(): lax.ppermute(value, axis, [(i, i ^ mask) for i in range(lax.axis_size(axi...  27.9 us
    ppermute x20, waiting for transfers between devices, swapped(): lax.ppermute(value, axis, [(i, i ^ mask) for i in range(lax.axis_size(axi...  24.6 us
    pallas_call x13, Pallas kernels, call(): pl.pallas_call(body, out_shape=[jax.ShapeDtypeStruct(s, t) for s, t in ou...  9.25 us
    ppermute x1, waiting for transfers between devices, body(): tail = lax.ppermute(tail, SEQ, [(i, (i + 1) % 32) for i in range(32)])  6.27 us
    unnamed x19, local copies, waits for them, and re-layouts  4.15 us
  transfers between devices with their start and end apart: 21, of which 15 were waited for; matrix products, arithmetic and copies ran while one was open for 6% of the time, Pallas kernels for 6%

profile of v7, /device:TPU:1, one launch (start us, length us, event | category | flops | bytes accessed | tf_op | source)
XLA Modules:
  0.0 73.2 jit_solution(17912068470346452635)
XLA Ops:
  0.0 3.7 %collective-permute-start.2 = (bf16[32,2560]{1,0:T(8,128)(2,1)}, bf16[32,2560]{1,0:T(8,128)(2,1)S(1)}, u32[]{:S(2)}, u32[]{:S(2)}) collective-permute-start(bf16[32,2560]{1,0:T(8,128)(2,1)} %t0.1), channel_id=1, source_target_pairs={{0,4},{2,6},{4,0},{6,2},{1,5},{3,7},{5,1},{7,3},{8,12},{10,14},{12... | collective-permute-start | bytes 491528 | tf_op jit(solution)/shard_map/ppermute | solution.py:45
  4.5 2.2 %collective-permute-start.3 = (bf16[32,2560]{1,0:T(8,128)(2,1)}, bf16[32,2560]{1,0:T(8,128)(2,1)S(1)}, u32[]{:S(2)}, u32[]{:S(2)}) collective-permute-start(bf16[32,2560]{1,0:T(8,128)(2,1)} %t0.1), channel_id=1, source_target_pairs={{0,1},{1,0},{2,3},{3,2},{4,5},{5,4},{6,7},{7,6},{8,9},{9,8},{10,11... | collective-permute-start | bytes 491528 | tf_op jit(solution)/shard_map/ppermute | solution.py:45
  6.7 4.1 %copy.11 = bf16[320,8,2,640]{3,1,2,0:T(8,128)(2,1)S(1)} copy(bf16[320,8,2,640]{3,2,1,0:T(2,128)(2,1)} %bitcast.10) | data formatting | bytes 13107200
  10.8 2.0 %collective-permute-done.1.t2 = bf16[32,2560]{1,0:T(8,128)(2,1)S(1)} collective-permute-done((bf16[32,2560]{1,0:T(8,128)(2,1)}, bf16[32,2560]{1,0:T(8,128)(2,1)S(1)}, u32[]{:S(2)}, u32[]{:S(2)}) %collective-permute-start.1) | collective-permute-done | bytes 163872 | tf_op jit(solution)/shard_map/ppermute | solution.py:45
  15.2 1.9 %project.1 = (bf16[256,2560]{1,0:T(8,128)(2,1)S(1)}, bf16[256,896]{1,0:T(8,128)(2,1)S(1)}, bf16[8,896]{1,0:T(8,128)(2,1)S(1)}, f32[256,128]{1,0:T(8,128)S(1)}) custom-call(bf16[32,2560]{1,0:T(8,128)(2,1)S(1)} %copy-done.2, bf16[32,2560]{1,0:T(8,128)(2,1)S(1)} %collective-permute-done.t1, bf16[32,2560]{1,0:T(8,128)(2,1)S(1)} %collective-permute-done.1.t2, ...), custom_call_target="tpu_custom_call" | custom-call | flops 1342177280 | bytes 2684354 | tf_op jit(solution)/shard_map/project/pallas_call | solution.py:32
  18.0 1.4 %prepare.1 = (bf16[256,640]{1,0:T(8,128)(2,1)S(1)}, bf16[256,128]{1,0:T(8,128)(2,1)S(1)}, bf16[256,128]{1,0:T(8,128)(2,1)S(1)}, f32[256,128]{1,0:T(8,128)S(1)}, ...) custom-call(bf16[256,896]{1,0:T(8,128)(2,1)S(1)} %get-tuple-element.44.pre, ...), custom_call_target="tpu_custom_call" | custom-call | flops 41943040 | bytes 83886 | tf_op jit(solution)/shard_map/prepare/pallas_call | solution.py:32
  19.3 6.3 %collective-permute-done.7.tail = bf16[8,896]{1,0:T(8,128)(2,1)S(1)} collective-permute-done((bf16[8,896]{1,0:T(8,128)(2,1)S(1)}, bf16[8,896]{1,0:T(8,128)(2,1)S(1)}, u32[]{:S(2)}, u32[]{:S(2)}) %collective-permute-start.7) | collective-permute-done | bytes 14368 | tf_op jit(solution)/shard_map/ppermute | solution.py:352
  26.1 3.1 %collective-permute-start.10 = (bf16[168,128]{1,0:T(8,128)(2,1)S(1)}, bf16[168,128]{1,0:T(8,128)(2,1)S(1)}, u32[]{:S(2)}, u32[]{:S(2)}) collective-permute-start(bf16[168,128]{1,0:T(8,128)(2,1)S(1)} %get-tuple-element.52), channel_id=1, source_target_pairs={{0,24},{8,16},{16,8},{24,0},{1,25},{9,17},{17,9},{25,1},{2,26},{10... | collective-permute-start | bytes 129032 | tf_op jit(solution)/shard_map/ppermute | solution.py:45
  29.2 1.2 %gate.1.before_too = f32[256,640]{1,0:T(8,128)S(1)} custom-call(bf16[256,2560]{1,0:T(8,128)(2,1)S(1)} %get-tuple-element.62.tokens, bf16[2560,1280]{1,0:T(8,128)(2,1)S(1)} %bitcast.6, bf16[8,640]{1,0:T(8,128)(2,1)S(1)} %get-tuple-element.56.v_first.before), custom_call_target="tpu_custom_call" | custom-call | flops 838860800 | bytes 1677721 | tf_op jit(solution)/shard_map/gate/pallas_call | solution.py:32
  30.5 1.0 %inside.1 = (f32[256,640]{1,0:T(8,128)S(1)}, bf16[256,128]{1,0:T(8,128)(2,1)S(1)}) custom-call(bf16[256,640]{1,0:T(8,128)(2,1)S(1)} %get-tuple-element.53.v, bf16[256,128]{1,0:T(8,128)(2,1)S(1)} %get-tuple-element.54.b, bf16[256,128]{1,0:T(8,128)(2,1)S(1)} %get-tuple-element.55.c, bf16[8,640]{1,0:T(8,128)(2,1)S(1)} %get-tuple-element.56.v_first.before, ...), custom_call_target="tpu_custom_call" | custom-call | flops 335544320 | bytes 671088 | tf_op jit(solution)/shard_map/inside/pallas_call | solution.py:32
  31.8 2.9 %collective-permute-done.11.other = bf16[168,128]{1,0:T(8,128)(2,1)S(1)} collective-permute-done((bf16[168,128]{1,0:T(8,128)(2,1)S(1)}, bf16[168,128]{1,0:T(8,128)(2,1)S(1)}, u32[]{:S(2)}, u32[]{:S(2)}) %collective-permute-start.11) | collective-permute-done | bytes 43040 | tf_op jit(solution)/shard_map/ppermute | solution.py:45
  35.0 3.8 %collective-permute-done.12.previous = bf16[168,128]{1,0:T(8,128)(2,1)S(1)} collective-permute-done((bf16[168,128]{1,0:T(8,128)(2,1)S(1)}, bf16[168,128]{1,0:T(8,128)(2,1)S(1)}, u32[]{:S(2)}, u32[]{:S(2)}) %collective-permute-start.12) | collective-permute-done | bytes 43040 | tf_op jit(solution)/shard_map/ppermute | solution.py:45
  38.9 1.3 %collective-permute-start.13 = (bf16[168,128]{1,0:T(8,128)(2,1)S(1)}, bf16[168,128]{1,0:T(8,128)(2,1)S(1)}, u32[]{:S(2)}, u32[]{:S(2)}) collective-permute-start(bf16[168,128]{1,0:T(8,128)(2,1)S(1)} %quadtotal.1), channel_id=1, source_target_pairs={{0,224},{32,192},{64,160},{96,128},{128,96},{160,64},{192,32},{224... | collective-permute-start | bytes 129032 | tf_op jit(solution)/shard_map/ppermute | solution.py:45
  40.2 2.9 %collective-permute-done.13.quad = bf16[168,128]{1,0:T(8,128)(2,1)S(1)} collective-permute-done((bf16[168,128]{1,0:T(8,128)(2,1)S(1)}, bf16[168,128]{1,0:T(8,128)(2,1)S(1)}, u32[]{:S(2)}, u32[]{:S(2)}) %collective-permute-start.13) | collective-permute-done | bytes 43040 | tf_op jit(solution)/shard_map/ppermute | solution.py:45
  44.0 1.9 %collective-permute-start.15 = (bf16[32,640]{1,0:T(8,128)(2,1)S(1)}, bf16[32,640]{1,0:T(8,128)(2,1)S(1)}, u32[]{:S(2)}, u32[]{:S(2)}) collective-permute-start(bf16[32,640]{1,0:T(8,128)(2,1)S(1)} %get-tuple-element.65), channel_id=1, source_target_pairs={{0,8},{8,0},{16,24},{24,16},{1,9},{9,1},{17,25},{25,17},{2,10},{10... | collective-permute-start | bytes 122888 | tf_op jit(solution)/shard_map/ppermute | solution.py:45
  46.6 1.1 %collective-permute-done.14.e1 = bf16[32,640]{1,0:T(8,128)(2,1)S(1)} collective-permute-done((bf16[32,640]{1,0:T(8,128)(2,1)S(1)}, bf16[32,640]{1,0:T(8,128)(2,1)S(1)}, u32[]{:S(2)}, u32[]{:S(2)}) %collective-permute-start.14) | collective-permute-done | bytes 40992 | tf_op jit(solution)/shard_map/ppermute | solution.py:45
  48.0 1.9 %collective-permute-done.16.e3 = bf16[32,640]{1,0:T(8,128)(2,1)S(1)} collective-permute-done((bf16[32,640]{1,0:T(8,128)(2,1)S(1)}, bf16[32,640]{1,0:T(8,128)(2,1)S(1)}, u32[]{:S(2)}, u32[]{:S(2)}) %collective-permute-start.16) | collective-permute-done | bytes 40992 | tf_op jit(solution)/shard_map/ppermute | solution.py:45
  50.0 1.2 %gated.1 = (bf16[256,640]{1,0:T(8,128)(2,1)S(1)}, f32[256,128]{1,0:T(8,128)S(1)}, bf16[128,2688]{1,0:T(8,128)(2,1)S(1)}) custom-call(bf16[32,640]{1,0:T(8,128)(2,1)S(1)} %get-tuple-element.63.e0, bf16[32,640]{1,0:T(8,128)(2,1)S(1)} %collective-permute-done.14.e1, bf16[32,640]{1,0:T(8,128)(2,1)S(1)} %collective-permute-done.15.e2, ...), custom_call_target="tpu_custom_call" | custom-call | flops 419430400 | bytes 838860 | tf_op jit(solution)/shard_map/gated/pallas_call | solution.py:32
  51.2 8.1 %collective-permute-start.17 = (bf16[128,2688]{1,0:T(8,128)(2,1)S(1)}, bf16[128,2688]{1,0:T(8,128)(2,1)S(1)}, u32[]{:S(2)}, u32[]{:S(2)}) collective-permute-start(bf16[128,2688]{1,0:T(8,128)(2,1)S(1)} %get-tuple-element.70), channel_id=1, source_target_pairs={{0,1},{1,0},{2,3},{3,2},{4,5},{5,4},{6,7},{7,6},{8,9},{9,8},{10,11... | collective-permute-start | bytes 2064392 | tf_op jit(solution)/shard_map/ppermute | solution.py:45
  60.0 1.1 %collective-permute-done.17.came = bf16[128,2688]{1,0:T(8,128)(2,1)S(1)} collective-permute-done((bf16[128,2688]{1,0:T(8,128)(2,1)S(1)}, bf16[128,2688]{1,0:T(8,128)(2,1)S(1)}, u32[]{:S(2)}, u32[]{:S(2)}) %collective-permute-start.17) | collective-permute-done | bytes 688160 | tf_op jit(solution)/shard_map/ppermute | solution.py:45
  61.3 1.9 %collective-permute-start.18 = (bf16[32,2688]{1,0:T(8,128)(2,1)S(1)}, bf16[32,2688]{1,0:T(8,128)(2,1)S(1)}, u32[]{:S(2)}, u32[]{:S(2)}) collective-permute-start(bf16[32,2688]{1,0:T(8,128)(2,1)S(1)} %get-tuple-element.72), channel_id=1, source_target_pairs={{0,4},{2,6},{4,0},{6,2},{1,5},{3,7},{5,1},{7,3},{8,12},{10,14},{12... | collective-permute-start | bytes 516104 | tf_op jit(solution)/shard_map/ppermute | solution.py:45
  63.2 1.1 %collective-permute-start.19 = (bf16[32,2688]{1,0:T(8,128)(2,1)S(1)}, bf16[32,2688]{1,0:T(8,128)(2,1)S(1)}, u32[]{:S(2)}, u32[]{:S(2)}) collective-permute-start(bf16[32,2688]{1,0:T(8,128)(2,1)S(1)} %get-tuple-element.73), channel_id=1, source_target_pairs={{0,2},{2,0},{4,6},{6,4},{1,3},{3,1},{5,7},{7,5},{8,10},{10,8},{12,... | collective-permute-start | bytes 516104 | tf_op jit(solution)/shard_map/ppermute | solution.py:45
  64.9 3.6 %collective-permute-done.18.g1 = bf16[32,2688]{1,0:T(8,128)(2,1)S(1)} collective-permute-done((bf16[32,2688]{1,0:T(8,128)(2,1)S(1)}, bf16[32,2688]{1,0:T(8,128)(2,1)S(1)}, u32[]{:S(2)}, u32[]{:S(2)}) %collective-permute-start.18) | collective-permute-done | bytes 172064 | tf_op jit(solution)/shard_map/ppermute | solution.py:45
  68.5 3.7 %collective-permute-done.19.g2 = bf16[32,2688]{1,0:T(8,128)(2,1)S(1)} collective-permute-done((bf16[32,2688]{1,0:T(8,128)(2,1)S(1)}, bf16[32,2688]{1,0:T(8,128)(2,1)S(1)}, u32[]{:S(2)}, u32[]{:S(2)}) %collective-permute-start.19) | collective-permute-done | bytes 172064 | tf_op jit(solution)/shard_map/ppermute | solution.py:45
  (51 shorter events, 9.5 us)
Async XLA Ops:
  0.0 10.8 %collective-permute-start.2 = (bf16[32,2560]{1,0:T(8,128)(2,1)}, bf16[32,2560]{1,0:T(8,128)(2,1)S(1)}, u32[]{:S(2)}, u32[]{:S(2)}) collective-permute-start(bf16[32,2560]{1,0:T(8,128)(2,1)} %t0.1), channel_id=1, source_target_pairs={{0,4},{2,6},{4,0},{6,2},{1,5},{3,7},{5,1},{7,3},{8,12},{10,14},{12... | collective-permute-start | bytes 491528 | tf_op jit(solution)/shard_map/ppermute | solution.py:45
  3.7 9.0 %collective-permute-start.1 = (bf16[32,2560]{1,0:T(8,128)(2,1)}, bf16[32,2560]{1,0:T(8,128)(2,1)S(1)}, u32[]{:S(2)}, u32[]{:S(2)}) collective-permute-start(bf16[32,2560]{1,0:T(8,128)(2,1)} %t0.1), channel_id=1, source_target_pairs={{0,6},{2,4},{4,2},{6,0},{1,7},{3,5},{5,3},{7,1},{8,14},{10,12},{12... | collective-permute-start | bytes 491528 | tf_op jit(solution)/shard_map/ppermute | solution.py:45
  4.5 8.3 %collective-permute-start = (bf16[32,2560]{1,0:T(8,128)(2,1)}, bf16[32,2560]{1,0:T(8,128)(2,1)S(1)}, u32[]{:S(2)}, u32[]{:S(2)}) collective-permute-start(bf16[32,2560]{1,0:T(8,128)(2,1)} %t0.1), channel_id=1, source_target_pairs={{0,2},{2,0},{4,6},{6,4},{1,3},{3,1},{5,7},{7,5},{8,10},{10,8},{12,... | collective-permute-start | bytes 491528 | tf_op jit(solution)/shard_map/ppermute | solution.py:45
  4.5 9.5 %collective-permute-start.3 = (bf16[32,2560]{1,0:T(8,128)(2,1)}, bf16[32,2560]{1,0:T(8,128)(2,1)S(1)}, u32[]{:S(2)}, u32[]{:S(2)}) collective-permute-start(bf16[32,2560]{1,0:T(8,128)(2,1)} %t0.1), channel_id=1, source_target_pairs={{0,1},{1,0},{2,3},{3,2},{4,5},{5,4},{6,7},{7,6},{8,9},{9,8},{10,11... | collective-permute-start | bytes 491528 | tf_op jit(solution)/shard_map/ppermute | solution.py:45
  6.7 8.5 %copy-start.2 = (bf16[32,2560]{1,0:T(8,128)(2,1)S(1)}, bf16[32,2560]{1,0:T(8,128)(2,1)}, u32[]{:S(2)}) copy-start(bf16[32,2560]{1,0:T(8,128)(2,1)} %t0.1) | copy-start | bytes 491524
  6.7 8.5 %copy-start.3 = (bf16[2560,10]{0,1:T(8,128)(2,1)S(1)}, bf16[2560,10]{0,1:T(8,128)(2,1)}, u32[]{:S(2)}) copy-start(bf16[2560,10]{0,1:T(8,128)(2,1)} %param.13) | copy-start | bytes 153604
  12.8 1.8 %collective-permute-start.4 = (bf16[32,2560]{1,0:T(8,128)(2,1)S(1)}, bf16[32,2560]{1,0:T(8,128)(2,1)S(1)}, u32[]{:S(2)}, u32[]{:S(2)}) collective-permute-start(bf16[32,2560]{1,0:T(8,128)(2,1)S(1)} %collective-permute-done.t1), channel_id=1, source_target_pairs={{0,1},{1,0},{2,3},{3,2},{4,5},{5,4},{6,7},{7,6},{8,9},{9,8},{10,11... | collective-permute-start | bytes 491528 | tf_op jit(solution)/shard_map/ppermute | solution.py:45
  13.5 1.4 %collective-permute-start.5 = (bf16[32,2560]{1,0:T(8,128)(2,1)S(1)}, bf16[32,2560]{1,0:T(8,128)(2,1)S(1)}, u32[]{:S(2)}, u32[]{:S(2)}) collective-permute-start(bf16[32,2560]{1,0:T(8,128)(2,1)S(1)} %collective-permute-done.1.t2), channel_id=1, source_target_pairs={{0,1},{1,0},{2,3},{3,2},{4,5},{5,4},{6,7},{7,6},{8,9},{9,8},{10,11... | collective-permute-start | bytes 491528 | tf_op jit(solution)/shard_map/ppermute | solution.py:45
  13.5 1.6 %collective-permute-start.6 = (bf16[32,2560]{1,0:T(8,128)(2,1)S(1)}, bf16[32,2560]{1,0:T(8,128)(2,1)S(1)}, u32[]{:S(2)}, u32[]{:S(2)}) collective-permute-start(bf16[32,2560]{1,0:T(8,128)(2,1)S(1)} %collective-permute-done.2.t3), channel_id=1, source_target_pairs={{0,1},{1,0},{2,3},{3,2},{4,5},{5,4},{6,7},{7,6},{8,9},{9,8},{10,11... | collective-permute-start | bytes 491528 | tf_op jit(solution)/shard_map/ppermute | solution.py:45
  17.2 8.5 %collective-permute-start.7 = (bf16[8,896]{1,0:T(8,128)(2,1)S(1)}, bf16[8,896]{1,0:T(8,128)(2,1)S(1)}, u32[]{:S(2)}, u32[]{:S(2)}) collective-permute-start(bf16[8,896]{1,0:T(8,128)(2,1)S(1)} %get-tuple-element.43), channel_id=1, source_target_pairs={{0,8},{8,16},{16,24},{24,32},{32,40},{40,48},{48,56},{56,64},{64,7... | collective-permute-start | bytes 43016 | tf_op jit(solution)/shard_map/ppermute | solution.py:352
  25.9 5.6 %collective-permute-start.8 = (bf16[168,128]{1,0:T(8,128)(2,1)S(1)}, bf16[168,128]{1,0:T(8,128)(2,1)S(1)}, u32[]{:S(2)}, u32[]{:S(2)}) collective-permute-start(bf16[168,128]{1,0:T(8,128)(2,1)S(1)} %get-tuple-element.50), channel_id=1, source_target_pairs={{0,16},{8,24},{16,0},{24,8},{1,17},{9,25},{17,1},{25,9},{2,18},{10... | collective-permute-start | bytes 129032 | tf_op jit(solution)/shard_map/ppermute | solution.py:45
  26.0 5.5 %collective-permute-start.9 = (bf16[168,128]{1,0:T(8,128)(2,1)S(1)}, bf16[168,128]{1,0:T(8,128)(2,1)S(1)}, u32[]{:S(2)}, u32[]{:S(2)}) collective-permute-start(bf16[168,128]{1,0:T(8,128)(2,1)S(1)} %get-tuple-element.51), channel_id=1, source_target_pairs={{0,8},{8,0},{16,24},{24,16},{1,9},{9,1},{17,25},{25,17},{2,10},{10... | collective-permute-start | bytes 129032 | tf_op jit(solution)/shard_map/ppermute | solution.py:45
  26.1 5.4 %collective-permute-start.10 = (bf16[168,128]{1,0:T(8,128)(2,1)S(1)}, bf16[168,128]{1,0:T(8,128)(2,1)S(1)}, u32[]{:S(2)}, u32[]{:S(2)}) collective-permute-start(bf16[168,128]{1,0:T(8,128)(2,1)S(1)} %get-tuple-element.52), channel_id=1, source_target_pairs={{0,24},{8,16},{16,8},{24,0},{1,25},{9,17},{17,9},{25,1},{2,26},{10... | collective-permute-start | bytes 129032 | tf_op jit(solution)/shard_map/ppermute | solution.py:45
  30.4 19.5 %copy-start = (bf16[640,2560]{1,0:T(8,128)(2,1)S(1)}, bf16[640,2560]{1,0:T(8,128)(2,1)}, u32[]{:S(2)}) copy-start(bf16[640,2560]{1,0:T(8,128)(2,1)} %w.3) | copy-start | bytes 9830404
  31.7 3.0 %collective-permute-start.11 = (bf16[168,128]{1,0:T(8,128)(2,1)S(1)}, bf16[168,128]{1,0:T(8,128)(2,1)S(1)}, u32[]{:S(2)}, u32[]{:S(2)}) collective-permute-start(bf16[168,128]{1,0:T(8,128)(2,1)S(1)} %rowtotal.1.row), channel_id=1, source_target_pairs={{0,32},{32,0},{64,96},{96,64},{128,160},{160,128},{192,224},{224,1... | collective-permute-start | bytes 129032 | tf_op jit(solution)/shard_map/ppermute | solution.py:45
  34.7 4.0 %collective-permute-start.12 = (bf16[168,128]{1,0:T(8,128)(2,1)S(1)}, bf16[168,128]{1,0:T(8,128)(2,1)S(1)}, u32[]{:S(2)}, u32[]{:S(2)}) collective-permute-start(bf16[168,128]{1,0:T(8,128)(2,1)S(1)} %pairtotal.1), channel_id=1, source_target_pairs={{0,64},{32,96},{64,0},{96,32},{128,192},{160,224},{192,128},{224,1... | collective-permute-start | bytes 129032 | tf_op jit(solution)/shard_map/ppermute | solution.py:45
  38.9 4.2 %collective-permute-start.13 = (bf16[168,128]{1,0:T(8,128)(2,1)S(1)}, bf16[168,128]{1,0:T(8,128)(2,1)S(1)}, u32[]{:S(2)}, u32[]{:S(2)}) collective-permute-start(bf16[168,128]{1,0:T(8,128)(2,1)S(1)} %quadtotal.1), channel_id=1, source_target_pairs={{0,224},{32,192},{64,160},{96,128},{128,96},{160,64},{192,32},{224... | collective-permute-start | bytes 129032 | tf_op jit(solution)/shard_map/ppermute | solution.py:45
  43.3 4.4 %collective-permute-start.14 = (bf16[32,640]{1,0:T(8,128)(2,1)S(1)}, bf16[32,640]{1,0:T(8,128)(2,1)S(1)}, u32[]{:S(2)}, u32[]{:S(2)}) collective-permute-start(bf16[32,640]{1,0:T(8,128)(2,1)S(1)} %get-tuple-element.64), channel_id=1, source_target_pairs={{0,16},{8,24},{16,0},{24,8},{1,17},{9,25},{17,1},{25,9},{2,18},{10... | collective-permute-start | bytes 122888 | tf_op jit(solution)/shard_map/ppermute | solution.py:45
  44.0 4.0 %collective-permute-start.15 = (bf16[32,640]{1,0:T(8,128)(2,1)S(1)}, bf16[32,640]{1,0:T(8,128)(2,1)S(1)}, u32[]{:S(2)}, u32[]{:S(2)}) collective-permute-start(bf16[32,640]{1,0:T(8,128)(2,1)S(1)} %get-tuple-element.65), channel_id=1, source_target_pairs={{0,8},{8,0},{16,24},{24,16},{1,9},{9,1},{17,25},{25,17},{2,10},{10... | collective-permute-start | bytes 122888 | tf_op jit(solution)/shard_map/ppermute | solution.py:45
  45.9 4.1 %collective-permute-start.16 = (bf16[32,640]{1,0:T(8,128)(2,1)S(1)}, bf16[32,640]{1,0:T(8,128)(2,1)S(1)}, u32[]{:S(2)}, u32[]{:S(2)}) collective-permute-start(bf16[32,640]{1,0:T(8,128)(2,1)S(1)} %get-tuple-element.66), channel_id=1, source_target_pairs={{0,24},{8,16},{16,8},{24,0},{1,25},{9,17},{17,9},{25,1},{2,26},{10... | collective-permute-start | bytes 122888 | tf_op jit(solution)/shard_map/ppermute | solution.py:45
  51.2 9.9 %collective-permute-start.17 = (bf16[128,2688]{1,0:T(8,128)(2,1)S(1)}, bf16[128,2688]{1,0:T(8,128)(2,1)S(1)}, u32[]{:S(2)}, u32[]{:S(2)}) collective-permute-start(bf16[128,2688]{1,0:T(8,128)(2,1)S(1)} %get-tuple-element.70), channel_id=1, source_target_pairs={{0,1},{1,0},{2,3},{3,2},{4,5},{5,4},{6,7},{7,6},{8,9},{9,8},{10,11... | collective-permute-start | bytes 2064392 | tf_op jit(solution)/shard_map/ppermute | solution.py:45
  61.3 7.1 %collective-permute-start.18 = (bf16[32,2688]{1,0:T(8,128)(2,1)S(1)}, bf16[32,2688]{1,0:T(8,128)(2,1)S(1)}, u32[]{:S(2)}, u32[]{:S(2)}) collective-permute-start(bf16[32,2688]{1,0:T(8,128)(2,1)S(1)} %get-tuple-element.72), channel_id=1, source_target_pairs={{0,4},{2,6},{4,0},{6,2},{1,5},{3,7},{5,1},{7,3},{8,12},{10,14},{12... | collective-permute-start | bytes 516104 | tf_op jit(solution)/shard_map/ppermute | solution.py:45
  63.2 9.0 %collective-permute-start.19 = (bf16[32,2688]{1,0:T(8,128)(2,1)S(1)}, bf16[32,2688]{1,0:T(8,128)(2,1)S(1)}, u32[]{:S(2)}, u32[]{:S(2)}) collective-permute-start(bf16[32,2688]{1,0:T(8,128)(2,1)S(1)} %get-tuple-element.73), channel_id=1, source_target_pairs={{0,2},{2,0},{4,6},{6,4},{1,3},{3,1},{5,7},{7,5},{8,10},{10,8},{12,... | collective-permute-start | bytes 516104 | tf_op jit(solution)/shard_map/ppermute | solution.py:45
  64.4 8.0 %collective-permute-start.20 = (bf16[32,2688]{1,0:T(8,128)(2,1)S(1)}, bf16[32,2688]{1,0:T(8,128)(2,1)S(1)}, u32[]{:S(2)}, u32[]{:S(2)}) collective-permute-start(bf16[32,2688]{1,0:T(8,128)(2,1)S(1)} %get-tuple-element.74), channel_id=1, source_target_pairs={{0,6},{2,4},{4,2},{6,0},{1,7},{3,5},{5,3},{7,1},{8,14},{10,12},{12... | collective-permute-start | bytes 516104 | tf_op jit(solution)/shard_map/ppermute | solution.py:45
  (6 other events, 26.9 us)

commit v8 on v7

--- a/solution.py
+++ b/solution.py
@@ -21,6 +21,8 @@
 WIDE = MODEL + 128
 PIECE = 168
 MASKS = (0, 2, 1, 3)
+FIRST = (2,)
+REST = (1, 3, 0)
 TOKEN_MASKS = (0, 1, 3, 2)
 
 
@@ -28,7 +30,7 @@
     return [pl.BlockSpec(memory_space=pltpu.VMEM)] * count
 
 
-def call(body, outs, args, scratch=(), flops=0, name=None):
+def call(body, outs, args, scratch=(), flops=0):
     return pl.pallas_call(
         body,
         out_shape=[jax.ShapeDtypeStruct(s, t) for s, t in outs],
@@ -37,7 +39,6 @@
         scratch_shapes=[pltpu.VMEM(s, t) for s, t in scratch],
         compiler_params=pltpu.CompilerParams(vmem_limit_bytes=24 << 20),
         cost_estimate=pl.CostEstimate(flops=flops, transcendentals=0, bytes_accessed=flops // 500),
-        name=name,
     )(*args)
 
 
@@ -57,15 +58,13 @@
     return pl.ds(pl.multiple_of(index * rows, rows), rows)
 
 
-def project_kernel(t0, t1, t2, t3, o0, o1, o2, o3, w, w_bc, w_dt, early, all_out, pre_out, tail_out, dt_out, w_steps):
+def project_kernel(t0, t1, t2, t3, o0, o1, o2, o3, w, w_bc, early, all_out, pre_out, tail_out):
     y, c = lax.axis_index("y"), lax.axis_index("c")
     for d, own, other in zip(TOKEN_MASKS, (t0, t1, t2, t3), (o0, o1, o2, o3)):
         source = other_index(y, d)
         all_out[row_at(source * 2 + c, ROWS), :] = own[...]
         all_out[row_at(source * 2 + 1 - c, ROWS), :] = other[...]
     tokens = all_out[...]
-    w_steps[...] = jnp.zeros(w_steps.shape, BF)
-    w_steps[0 : w_dt.shape[0], :] = w_dt[...]
     for lo, hi in ((0, 256), (256, 512), (512, WIDTH)):
         part = jnp.dot(tokens, w[:, lo:hi], preferred_element_type=F32).astype(BF)
         pre_out[:, lo:hi] = part
@@ -73,7 +72,6 @@
     part = jnp.dot(tokens, w_bc[...], preferred_element_type=F32).astype(BF)
     pre_out[:, WIDTH:] = part
     tail_out[:, WIDTH:] = part[BLOCK - 8 :]
-    dt_out[...] = lax.dot_general(tokens, w_steps[...], (((1,), (1,)), ((), ())), preferred_element_type=F32)
 
 
 def gate_kernel(tokens, w, before, out):
@@ -104,7 +102,8 @@
 
 def prepare_kernel(
     pre,
-    dt_pre,
+    tokens,
+    w_dt,
     conv_x,
     conv_bc,
     bias,
@@ -119,13 +118,17 @@
     state_out,
     ext,
     small,
+    w_steps,
 ):
+    w_steps[...] = jnp.zeros(w_steps.shape, BF)
+    w_steps[0 : w_dt.shape[0], :] = w_dt[...]
+    dt_pre = lax.dot_general(tokens[...], w_steps[...], (((1,), (1,)), ((), ())), preferred_element_type=F32)
     ext[0:8, :] = jnp.zeros((8, PRE), F32)
     ext[8 : 8 + BLOCK, :] = pre[...].astype(F32)
     small[...] = jnp.zeros(small.shape, F32)
     small[0:1, 0 : bias.shape[1]] = bias[...]
     small[1:2, 0 : bias.shape[1]] = a_log[...]
-    step = jax.nn.softplus(dt_pre[...] + small[0:1, :])
+    step = jax.nn.softplus(dt_pre + small[0:1, :])
     decay = step * (-jnp.exp(small[1:2, :]))
     row = lax.broadcasted_iota(jnp.int32, decay.shape, 0)
     cum = decay
@@ -277,53 +280,56 @@
         out[...] = ready[other_index(x, d)].astype(BF)
 
 
-def gated_kernel(e0, e1, e2, e3, c, cum, inside, gate, gain, w, g_out, sq_out, send_out, state, pick):
-    x, core = lax.axis_index("x"), lax.axis_index("c")
-    for d, piece in zip(MASKS, (e0, e1, e2, e3)):
-        state[row_at(other_index(x, d), 32), :] = piece[...]
-    grown = jnp.exp(cum[...])
-    squares = jnp.zeros((BLOCK, 128), F32)
-    for pair in range(5):
-        cols = slice(128 * pair, 128 * pair + 128)
-        came = jnp.dot(c[...], state[:, cols], preferred_element_type=F32)
-        gated = (inside[:, cols] + spread(grown, pair) * came) * gate[:, cols]
-        squares = squares + gated * gated
-        g_out[:, cols] = (gated * gain[:, cols]).astype(BF)
-    sq_out[...] = jnp.broadcast_to(jnp.sum(squares, axis=1, keepdims=True), (BLOCK, 128))
-    for k in range(4):
-        rows = row_at(2 * k + 1 - core, ROWS)
-        pick[32 * k : 32 * k + 32, :] = g_out[rows, :]
-        send_out[32 * k : 32 * k + 32, MODEL:] = square_cols(sq_out[rows, :])
-    left = pick[...]
-    for n in range(10):
-        cols = slice(256 * n, 256 * n + 256)
-        send_out[:, cols] = jnp.dot(left, w[:, cols], preferred_element_type=F32).astype(BF)
-
-
 def square_cols(total):
     high, low = halves(total)
     lane = lax.broadcasted_iota(jnp.int32, total.shape, 1)
     return jnp.where(lane == 0, high.astype(F32), jnp.where(lane == 1, low.astype(F32), 0.0)).astype(BF)
 
 
-def own_kernel(g, sq, w, out, pick):
-    core = lax.axis_index("c")
-    lane = lax.broadcasted_iota(jnp.int32, (ROWS, 128), 1)
-    for k in range(4):
-        rows = row_at(2 * k + core, ROWS)
-        pick[32 * k : 32 * k + 32, :] = g[rows, :]
-        out[32 * k : 32 * k + 32, MODEL:] = jnp.where(lane == 0, sq[rows, :], 0.0)
-    left = pick[...]
+def project_rows(masks, side, state, c, cum, inside, gate, gain, w, out):
+    y = lax.axis_index("y")
+    rows = [row_at(2 * other_index(y, mask) + side, ROWS) for mask in masks]
+
+    def picked(ref, cols):
+        return jnp.concatenate([ref[r, cols] for r in rows], axis=0)
+
+    states = picked(c, slice(0, STATE))
+    grown = jnp.exp(picked(cum, slice(0, 128)))
+    squares = jnp.zeros(grown.shape, F32)
+    left = []
+    for pair in range(5):
+        cols = slice(128 * pair, 128 * pair + 128)
+        came = jnp.dot(states, state[:, cols], preferred_element_type=F32)
+        gated = (picked(inside, cols) + spread(grown, pair) * came) * picked(gate, cols)
+        squares = squares + gated * gated
+        left.append((gated * gain[:, cols]).astype(BF))
+    left = jnp.concatenate(left, axis=1)
     for n in range(10):
-        cols = slice(256 * n, 256 * n + 256)
-        out[:, cols] = jnp.dot(left, w[:, cols], preferred_element_type=F32)
-
-
-def pair_kernel(own, came, f0, f1, f2, f3):
-    y = lax.axis_index("y")
-    for d, out in zip(MASKS, (f0, f1, f2, f3)):
-        rows = row_at(other_index(y, d), ROWS)
-        total = own[rows, :] + came[rows, :].astype(F32)
+        part = jnp.dot(left, w[:, 256 * n : 256 * n + 256], preferred_element_type=F32)
+        out[:, 256 * n : 256 * n + 256] = part.astype(out.dtype)
+    out[:, MODEL:] = square_cols(jnp.broadcast_to(jnp.sum(squares, axis=1, keepdims=True), squares.shape)).astype(out.dtype)
+
+
+def send_kernel(e0, e1, e2, e3, c, cum, inside, gate, gain, w, state, out):
+    x = lax.axis_index("x")
+    for d, piece in zip(MASKS, (e0, e1, e2, e3)):
+        state[row_at(other_index(x, d), 32), :] = piece[...]
+    project_rows(FIRST + REST, 1 - lax.axis_index("c"), state, c, cum, inside, gate, gain, w, out)
+
+
+def keep_first_kernel(state, c, cum, inside, gate, gain, w, out):
+    project_rows(FIRST, lax.axis_index("c"), state, c, cum, inside, gate, gain, w, out)
+
+
+def keep_rest_kernel(state, c, cum, inside, gate, gain, w, before, out):
+    project_rows(REST, lax.axis_index("c"), state, c, cum, inside, gate, gain, w, out)
+
+
+def pair_kernel(own, came, *outs):
+    skip = came.shape[0] - own.shape[0] if len(outs) > 1 else 0
+    for k, out in enumerate(outs):
+        mine, theirs = slice(ROWS * k, ROWS * k + ROWS), slice(skip + ROWS * k, skip + ROWS * k + ROWS)
+        total = own[mine, :] + came[theirs, :].astype(F32)
         out[:, :MODEL] = total[:, :MODEL].astype(out.dtype)
         both = jnp.sum(total[:, MODEL:], axis=1, keepdims=True)
         out[:, MODEL:] = square_cols(jnp.broadcast_to(both, (ROWS, 128))).astype(out.dtype)
@@ -341,30 +347,26 @@
     near[1:] = [lax.optimization_barrier((piece, w_both))[0] for piece in near[1:]]
     far = [swapped(piece, "c", 1) for piece in near]
     gain = norm_gain[None]
-    everything, pre, tail, dt_pre = call(
+    everything, pre, tail = call(
         project_kernel,
-        [((BLOCK, MODEL), BF), ((BLOCK, PRE), BF), ((8, PRE), BF), ((BLOCK, 128), F32)],
-        [*near, *far, w_both, w_bc, w_dt.T, gain],
-        scratch=[((128, MODEL), BF)],
+        [((BLOCK, MODEL), BF), ((BLOCK, PRE), BF), ((8, PRE), BF)],
+        [*near, *far, w_both, w_bc, gain],
         flops=2 * BLOCK * MODEL * 1024,
-        name="project",
     )
     tail = lax.ppermute(tail, SEQ, [(i, (i + 1) % 32) for i in range(32)])
     v, b, c, step, cum, weight, factor, main = call(
         prepare_kernel,
         [((BLOCK, WIDTH), BF), ((BLOCK, STATE), BF), ((BLOCK, STATE), BF), ((BLOCK, 128), F32), ((BLOCK, 128), F32)]
         + [((8, 128), F32), ((8, 128), F32), ((STATE, WIDTH), F32)],
-        [pre, dt_pre, conv_x, conv_bc, dt_bias[None], a_log[None]],
-        scratch=[((BLOCK + 8, PRE), F32), ((8, 128), F32)],
+        [pre, everything, w_dt.T, conv_x, conv_bc, dt_bias[None], a_log[None]],
+        scratch=[((BLOCK + 8, PRE), F32), ((8, 128), F32), ((128, MODEL), BF)],
         flops=2 * BLOCK * STATE * WIDTH,
-        name="prepare",
     )
     v_first, b_first, c_first, p0, p1, p2, p3 = call(
         local_kernel,
         [((8, WIDTH), BF), ((8, STATE), BF), ((8, STATE), BF)] + [((PIECE, 128), BF)] * 4,
         [tail, pre, conv_x, conv_bc, weight, factor, main],
         scratch=[((16, PRE), F32), ((STATE, WIDTH), F32)],
-        name="local",
     )
     rows = exchanged([p0, p1, p2, p3], "x", MASKS)
     inside, c_all = call(
@@ -373,41 +375,34 @@
         [v, b, c, v_first, b_first, c_first, step, cum],
         scratch=[((BLOCK, WIDTH), BF), ((BLOCK, STATE), BF)],
         flops=20 * BLOCK * BLOCK * 256,
-        name="inside",
-    )
-    (gate,) = call(
-        gate_kernel, [((BLOCK, WIDTH), F32)], [everything, w_both, v_first], flops=2 * BLOCK * MODEL * WIDTH, name="gate"
-    )
+    )
+    (gate,) = call(gate_kernel, [((BLOCK, WIDTH), F32)], [everything, w_both, v_first], flops=2 * BLOCK * MODEL * WIDTH)
     piece = [((PIECE, 128), BF)]
-    (row,) = call(row_total_kernel, piece, [*rows, inside, gate], scratch=[((4, PIECE, 128), F32)], name="rowtotal")
+    (row,) = call(row_total_kernel, piece, [*rows, inside, gate], scratch=[((4, PIECE, 128), F32)])
     other = swapped(row, "z", 1)
-    (two,) = call(pair_total_kernel, piece, [row, other], name="pairtotal")
+    (two,) = call(pair_total_kernel, piece, [row, other])
     previous = swapped(two, "z", 2)
-    (four,) = call(quad_total_kernel, piece, [row, other, previous], name="quadtotal")
+    (four,) = call(quad_total_kernel, piece, [row, other, previous])
     quad = swapped(four, "z", 7)
     e0, e1, e2, e3 = call(
         incoming_kernel,
         [((32, WIDTH), BF)] * 4,
         [*rows, row, other, previous, quad],
         scratch=[((4, PIECE, 128), F32), ((4, 32, WIDTH), F32)],
-        name="incoming",
     )
     states = exchanged([e0, e1, e2, e3], "x", MASKS)
-    g, squares, send = call(
-        gated_kernel,
-        [((BLOCK, WIDTH), BF), ((BLOCK, 128), F32), ((128, WIDE), BF)],
-        [*states, c_all, cum, inside, gate, gain, w_out],
-        scratch=[((STATE, WIDTH), BF), ((128, WIDTH), BF)],
-        flops=2 * 128 * WIDTH * MODEL,
-        name="gated",
-    )
+    shared = [c_all, cum, inside, gate, gain, w_out]
+    flops = 2 * 96 * WIDTH * MODEL
+    state, send = call(send_kernel, [((STATE, WIDTH), BF), ((128, WIDE), BF)], [*states, *shared], flops=flops)
     came = swapped(send, "c", 1)
-    (own,) = call(
-        own_kernel, [((128, WIDE), F32)], [g, squares, w_out], scratch=[((128, WIDTH), BF)], flops=2 * 128 * WIDTH * MODEL, name="own"
-    )
-    f0, f1, f2, f3 = call(pair_kernel, [((ROWS, WIDE), F32)] + [((ROWS, WIDE), BF)] * 3, [own, came], name="pair")
-    parts = exchanged([f0, f1, f2, f3], "y", MASKS)
-    (out,) = call(finish_kernel, [((ROWS, MODEL), BF)], parts, name="finish")
+    (own,) = call(keep_first_kernel, [((ROWS, WIDE), F32)], [state, *shared], flops=flops)
+    (first,) = call(pair_kernel, [((ROWS, WIDE), BF)], [own, came])
+    arrived = swapped(first, "y", FIRST[0])
+    (own,) = call(keep_rest_kernel, [((96, WIDE), F32)], [state, *shared, first], flops=flops)
+    one, three, here = call(pair_kernel, [((ROWS, WIDE), BF), ((ROWS, WIDE), BF), ((ROWS, WIDE), F32)], [own, came])
+    (out,) = call(
+        finish_kernel, [((ROWS, MODEL), BF)], [here, arrived, swapped(one, "y", REST[0]), swapped(three, "y", REST[1])]
+    )
     return out
 
 
@@ -425,4 +420,5 @@
         P(HEAD),
         P(HEAD, None),
     )
+
     return jax.shard_map(body, mesh=split, in_specs=in_specs, out_specs=P(ALL, None), check_vma=False)

time: 73.3 us -> 74 us (level)
  Pallas kernels: 9.25 us -> 10.2 us
  waiting for transfers between devices: 30.8 us -> 30 us
    pallas_call x13 -> x15, Pallas kernels: 9.25 us -> 10.2 us  [call(): pl.pallas_call(body, out_shape=[jax.ShapeDtypeStruct(s, t) for s, t in ou...]
  transfers between devices with their start and end apart: 21 -> 21, of which waited for: 15 -> 15; matrix products, arithmetic and copies ran while one was open for 6% -> 6% of each run, Pallas kernels for 6% -> 7%
where the time goes in v8:
time: 74 us; the launch traced here: 73.9 us
  waiting for transfers between devices  30 us (41%)
  starting transfers between devices  29.3 us (40%)
  Pallas kernels  10.2 us (14%)
  local copies, waits for them, and re-layouts  4.14 us (6%)
    ppermute x20, starting transfers between devices, swapped(): lax.ppermute(value, axis, [(i, i ^ mask) for i in range(lax.axis_size(axi...  28.5 us
    ppermute x20, waiting for transfers between devices, swapped(): lax.ppermute(value, axis, [(i, i ^ mask) for i in range(lax.axis_size(axi...  24.3 us
    pallas_call x15, Pallas kernels, call(): pl.pallas_call(body, out_shape=[jax.ShapeDtypeStruct(s, t) for s, t in ou...  10.2 us
    ppermute x1, waiting for transfers between devices, body(): tail = lax.ppermute(tail, SEQ, [(i, (i + 1) % 32) for i in range(32)])  5.7 us
    unnamed x19, local copies, waits for them, and re-layouts  4.14 us
  transfers between devices with their start and end apart: 21, of which 15 were waited for; matrix products, arithmetic and copies ran while one was open for 6% of the time, Pallas kernels for 7%

profile of v8, /device:TPU:1, one launch (start us, length us, event | category | flops | bytes accessed | tf_op | source)
XLA Modules:
  0.0 73.9 jit_solution(13769969891007742508)
XLA Ops:
  0.0 3.7 %collective-permute-start.2 = (bf16[32,2560]{1,0:T(8,128)(2,1)}, bf16[32,2560]{1,0:T(8,128)(2,1)S(1)}, u32[]{:S(2)}, u32[]{:S(2)}) collective-permute-start(bf16[32,2560]{1,0:T(8,128)(2,1)} %t0.1), channel_id=1, source_target_pairs={{0,4},{2,6},{4,0},{6,2},{1,5},{3,7},{5,1},{7,3},{8,12},{10,14},{12... | collective-permute-start | bytes 491528 | tf_op jit(solution)/shard_map/ppermute | solution.py:46
  4.5 2.2 %collective-permute-start.3 = (bf16[32,2560]{1,0:T(8,128)(2,1)}, bf16[32,2560]{1,0:T(8,128)(2,1)S(1)}, u32[]{:S(2)}, u32[]{:S(2)}) collective-permute-start(bf16[32,2560]{1,0:T(8,128)(2,1)} %t0.1), channel_id=1, source_target_pairs={{0,1},{1,0},{2,3},{3,2},{4,5},{5,4},{6,7},{7,6},{8,9},{9,8},{10,11... | collective-permute-start | bytes 491528 | tf_op jit(solution)/shard_map/ppermute | solution.py:46
  6.7 4.1 %copy.11 = bf16[320,8,2,640]{3,1,2,0:T(8,128)(2,1)S(1)} copy(bf16[320,8,2,640]{3,2,1,0:T(2,128)(2,1)} %bitcast.10) | data formatting | bytes 13107200
  10.8 2.0 %collective-permute-done.1.t2 = bf16[32,2560]{1,0:T(8,128)(2,1)S(1)} collective-permute-done((bf16[32,2560]{1,0:T(8,128)(2,1)}, bf16[32,2560]{1,0:T(8,128)(2,1)S(1)}, u32[]{:S(2)}, u32[]{:S(2)}) %collective-permute-start.1) | collective-permute-done | bytes 163872 | tf_op jit(solution)/shard_map/ppermute | solution.py:46
  15.2 1.6 %shard_map.100 = (bf16[256,2560]{1,0:T(8,128)(2,1)S(1)}, bf16[256,896]{1,0:T(8,128)(2,1)S(1)}, bf16[8,896]{1,0:T(8,128)(2,1)S(1)}) custom-call(bf16[32,2560]{1,0:T(8,128)(2,1)S(1)} %copy-done.2, bf16[32,2560]{1,0:T(8,128)(2,1)S(1)} %collective-permute-done.t1, bf16[32,2560]{1,0:T(8,128)(2,1)S(1)} %collective-permute-done.1.t2, ...), custom_call_target="tpu_custom_call" | custom-call | flops 1342177280 | bytes 2684354 | tf_op jit(solution)/shard_map/pallas_call | solution.py:34
  17.6 1.9 %shard_map.101 = (bf16[256,640]{1,0:T(8,128)(2,1)S(1)}, bf16[256,128]{1,0:T(8,128)(2,1)S(1)}, bf16[256,128]{1,0:T(8,128)(2,1)S(1)}, f32[256,128]{1,0:T(8,128)S(1...) custom-call(bf16[256,896]{1,0:T(8,128)(2,1)S(1)} %get-tuple-element.41.pre, ...), custom_call_target="tpu_custom_call" | custom-call | flops 41943040 | bytes 83886 | tf_op jit(solution)/shard_map/pallas_call | solution.py:34
  19.5 5.7 %collective-permute-done.7.tail = bf16[8,896]{1,0:T(8,128)(2,1)S(1)} collective-permute-done((bf16[8,896]{1,0:T(8,128)(2,1)S(1)}, bf16[8,896]{1,0:T(8,128)(2,1)S(1)}, u32[]{:S(2)}, u32[]{:S(2)}) %collective-permute-start.7) | collective-permute-done | bytes 14368 | tf_op jit(solution)/shard_map/ppermute | solution.py:356
  25.7 3.1 %collective-permute-start.10 = (bf16[168,128]{1,0:T(8,128)(2,1)S(1)}, bf16[168,128]{1,0:T(8,128)(2,1)S(1)}, u32[]{:S(2)}, u32[]{:S(2)}) collective-permute-start(bf16[168,128]{1,0:T(8,128)(2,1)S(1)} %get-tuple-element.49), channel_id=1, source_target_pairs={{0,24},{8,16},{16,8},{24,0},{1,25},{9,17},{17,9},{25,1},{2,26},{10... | collective-permute-start | bytes 129032 | tf_op jit(solution)/shard_map/ppermute | solution.py:46
  28.9 1.2 %shard_map.104.before_too.gate = f32[256,640]{1,0:T(8,128)S(1)} custom-call(bf16[256,2560]{1,0:T(8,128)(2,1)S(1)} %get-tuple-element.42.tokens, bf16[2560,1280]{1,0:T(8,128)(2,1)S(1)} %bitcast.6, bf16[8,640]{1,0:T(8,128)(2,1)S(1)} %get-tuple-element.53.v_first.before), custom_call_target="tpu_custom_call" | custom-call | flops 838860800 | bytes 1677721 | tf_op jit(solution)/shard_map/pallas_call | solution.py:34
  30.1 1.0 %shard_map.103 = (f32[256,640]{1,0:T(8,128)S(1)}, bf16[256,128]{1,0:T(8,128)(2,1)S(1)}) custom-call(bf16[256,640]{1,0:T(8,128)(2,1)S(1)} %get-tuple-element.50.v, bf16[256,128]{1,0:T(8,128)(2,1)S(1)} %get-tuple-element.51.b, bf16[256,128]{1,0:T(8,128)(2,1)S(1)} %get-tuple-element.52.c, bf16[8,640]{1,0:T(8,128)(2,1)S(1)} %get-tuple-element.53.v_first.before, ...), custom_call_target="tpu_custom_call" | custom-call | flops 335544320 | bytes 671088 | tf_op jit(solution)/shard_map/pallas_call | solution.py:34
  31.4 2.9 %collective-permute-done.11.other = bf16[168,128]{1,0:T(8,128)(2,1)S(1)} collective-permute-done((bf16[168,128]{1,0:T(8,128)(2,1)S(1)}, bf16[168,128]{1,0:T(8,128)(2,1)S(1)}, u32[]{:S(2)}, u32[]{:S(2)}) %collective-permute-start.11) | collective-permute-done | bytes 43040 | tf_op jit(solution)/shard_map/ppermute | solution.py:46
  35.1 3.3 %collective-permute-done.12.previous = bf16[168,128]{1,0:T(8,128)(2,1)S(1)} collective-permute-done((bf16[168,128]{1,0:T(8,128)(2,1)S(1)}, bf16[168,128]{1,0:T(8,128)(2,1)S(1)}, u32[]{:S(2)}, u32[]{:S(2)}) %collective-permute-start.12) | collective-permute-done | bytes 43040 | tf_op jit(solution)/shard_map/ppermute | solution.py:46
  38.5 1.3 %collective-permute-start.13 = (bf16[168,128]{1,0:T(8,128)(2,1)S(1)}, bf16[168,128]{1,0:T(8,128)(2,1)S(1)}, u32[]{:S(2)}, u32[]{:S(2)}) collective-permute-start(bf16[168,128]{1,0:T(8,128)(2,1)S(1)} %shard_map.107), channel_id=1, source_target_pairs={{0,224},{32,192},{64,160},{96,128},{128,96},{160,64},{192,32},{224... | collective-permute-start | bytes 129032 | tf_op jit(solution)/shard_map/ppermute | solution.py:46
  39.8 2.9 %collective-permute-done.13.quad = bf16[168,128]{1,0:T(8,128)(2,1)S(1)} collective-permute-done((bf16[168,128]{1,0:T(8,128)(2,1)S(1)}, bf16[168,128]{1,0:T(8,128)(2,1)S(1)}, u32[]{:S(2)}, u32[]{:S(2)}) %collective-permute-start.13) | collective-permute-done | bytes 43040 | tf_op jit(solution)/shard_map/ppermute | solution.py:46
  43.6 1.9 %collective-permute-start.15 = (bf16[32,640]{1,0:T(8,128)(2,1)S(1)}, bf16[32,640]{1,0:T(8,128)(2,1)S(1)}, u32[]{:S(2)}, u32[]{:S(2)}) collective-permute-start(bf16[32,640]{1,0:T(8,128)(2,1)S(1)} %get-tuple-element.61), channel_id=1, source_target_pairs={{0,8},{8,0},{16,24},{24,16},{1,9},{9,1},{17,25},{25,17},{2,10},{10... | collective-permute-start | bytes 122888 | tf_op jit(solution)/shard_map/ppermute | solution.py:46
  46.2 1.1 %collective-permute-done.14.e1 = bf16[32,640]{1,0:T(8,128)(2,1)S(1)} collective-permute-done((bf16[32,640]{1,0:T(8,128)(2,1)S(1)}, bf16[32,640]{1,0:T(8,128)(2,1)S(1)}, u32[]{:S(2)}, u32[]{:S(2)}) %collective-permute-start.14) | collective-permute-done | bytes 40992 | tf_op jit(solution)/shard_map/ppermute | solution.py:46
  47.6 2.0 %collective-permute-done.16.e3 = bf16[32,640]{1,0:T(8,128)(2,1)S(1)} collective-permute-done((bf16[32,640]{1,0:T(8,128)(2,1)S(1)}, bf16[32,640]{1,0:T(8,128)(2,1)S(1)}, u32[]{:S(2)}, u32[]{:S(2)}) %collective-permute-start.16) | collective-permute-done | bytes 40992 | tf_op jit(solution)/shard_map/ppermute | solution.py:46
  50.6 8.2 %collective-permute-start.17 = (bf16[128,2688]{1,0:T(8,128)(2,1)S(1)}, bf16[128,2688]{1,0:T(8,128)(2,1)S(1)}, u32[]{:S(2)}, u32[]{:S(2)}) collective-permute-start(bf16[128,2688]{1,0:T(8,128)(2,1)S(1)} %get-tuple-element.65), channel_id=1, source_target_pairs={{0,1},{1,0},{2,3},{3,2},{4,5},{5,4},{6,7},{7,6},{8,9},{9,8},{10,11... | collective-permute-start | bytes 2064392 | tf_op jit(solution)/shard_map/ppermute | solution.py:46
  61.6 1.2 %collective-permute-start.19 = (bf16[32,2688]{1,0:T(8,128)(2,1)S(1)}, bf16[32,2688]{1,0:T(8,128)(2,1)S(1)}, u32[]{:S(2)}, u32[]{:S(2)}) collective-permute-start(bf16[32,2688]{1,0:T(8,128)(2,1)S(1)} %get-tuple-element.67), channel_id=1, source_target_pairs={{0,2},{2,0},{4,6},{6,4},{1,3},{3,1},{5,7},{7,5},{8,10},{10,8},{12,... | collective-permute-start | bytes 516104 | tf_op jit(solution)/shard_map/ppermute | solution.py:46
  62.8 1.4 %collective-permute-start.20 = (bf16[32,2688]{1,0:T(8,128)(2,1)S(1)}, bf16[32,2688]{1,0:T(8,128)(2,1)S(1)}, u32[]{:S(2)}, u32[]{:S(2)}) collective-permute-start(bf16[32,2688]{1,0:T(8,128)(2,1)S(1)} %get-tuple-element.68), channel_id=1, source_target_pairs={{0,6},{2,4},{4,2},{6,0},{1,7},{3,5},{5,3},{7,1},{8,14},{10,12},{12... | collective-permute-start | bytes 516104 | tf_op jit(solution)/shard_map/ppermute | solution.py:46
  64.2 1.1 %collective-permute-start.18 = (bf16[32,2688]{1,0:T(8,128)(2,1)S(1)}, bf16[32,2688]{1,0:T(8,128)(2,1)S(1)}, u32[]{:S(2)}, u32[]{:S(2)}) collective-permute-start(bf16[32,2688]{1,0:T(8,128)(2,1)S(1)} %shard_map.111.before), channel_id=1, source_target_pairs={{0,4},{2,6},{4,0},{6,2},{1,5},{3,7},{5,1},{7,3},{8,12},{10,14},{12... | collective-permute-start | bytes 516104 | tf_op jit(solution)/shard_map/ppermute | solution.py:46
  65.3 2.0 %collective-permute-done.19.g2 = bf16[32,2688]{1,0:T(8,128)(2,1)S(1)} collective-permute-done((bf16[32,2688]{1,0:T(8,128)(2,1)S(1)}, bf16[32,2688]{1,0:T(8,128)(2,1)S(1)}, u32[]{:S(2)}, u32[]{:S(2)}) %collective-permute-start.19) | collective-permute-done | bytes 172064 | tf_op jit(solution)/shard_map/ppermute | solution.py:46
  67.3 2.0 %collective-permute-done.20.g3 = bf16[32,2688]{1,0:T(8,128)(2,1)S(1)} collective-permute-done((bf16[32,2688]{1,0:T(8,128)(2,1)S(1)}, bf16[32,2688]{1,0:T(8,128)(2,1)S(1)}, u32[]{:S(2)}, u32[]{:S(2)}) %collective-permute-start.20) | collective-permute-done | bytes 172064 | tf_op jit(solution)/shard_map/ppermute | solution.py:46
  69.3 3.8 %collective-permute-done.18.g1 = bf16[32,2688]{1,0:T(8,128)(2,1)S(1)} collective-permute-done((bf16[32,2688]{1,0:T(8,128)(2,1)S(1)}, bf16[32,2688]{1,0:T(8,128)(2,1)S(1)}, u32[]{:S(2)}, u32[]{:S(2)}) %collective-permute-start.18) | collective-permute-done | bytes 172064 | tf_op jit(solution)/shard_map/ppermute | solution.py:46
  (53 shorter events, 12.1 us)
Async XLA Ops:
  0.0 10.8 %collective-permute-start.2 = (bf16[32,2560]{1,0:T(8,128)(2,1)}, bf16[32,2560]{1,0:T(8,128)(2,1)S(1)}, u32[]{:S(2)}, u32[]{:S(2)}) collective-permute-start(bf16[32,2560]{1,0:T(8,128)(2,1)} %t0.1), channel_id=1, source_target_pairs={{0,4},{2,6},{4,0},{6,2},{1,5},{3,7},{5,1},{7,3},{8,12},{10,14},{12... | collective-permute-start | bytes 491528 | tf_op jit(solution)/shard_map/ppermute | solution.py:46
  3.7 9.0 %collective-permute-start.1 = (bf16[32,2560]{1,0:T(8,128)(2,1)}, bf16[32,2560]{1,0:T(8,128)(2,1)S(1)}, u32[]{:S(2)}, u32[]{:S(2)}) collective-permute-start(bf16[32,2560]{1,0:T(8,128)(2,1)} %t0.1), channel_id=1, source_target_pairs={{0,6},{2,4},{4,2},{6,0},{1,7},{3,5},{5,3},{7,1},{8,14},{10,12},{12... | collective-permute-start | bytes 491528 | tf_op jit(solution)/shard_map/ppermute | solution.py:46
  4.5 8.3 %collective-permute-start = (bf16[32,2560]{1,0:T(8,128)(2,1)}, bf16[32,2560]{1,0:T(8,128)(2,1)S(1)}, u32[]{:S(2)}, u32[]{:S(2)}) collective-permute-start(bf16[32,2560]{1,0:T(8,128)(2,1)} %t0.1), channel_id=1, source_target_pairs={{0,2},{2,0},{4,6},{6,4},{1,3},{3,1},{5,7},{7,5},{8,10},{10,8},{12,... | collective-permute-start | bytes 491528 | tf_op jit(solution)/shard_map/ppermute | solution.py:46
  4.5 9.6 %collective-permute-start.3 = (bf16[32,2560]{1,0:T(8,128)(2,1)}, bf16[32,2560]{1,0:T(8,128)(2,1)S(1)}, u32[]{:S(2)}, u32[]{:S(2)}) collective-permute-start(bf16[32,2560]{1,0:T(8,128)(2,1)} %t0.1), channel_id=1, source_target_pairs={{0,1},{1,0},{2,3},{3,2},{4,5},{5,4},{6,7},{7,6},{8,9},{9,8},{10,11... | collective-permute-start | bytes 491528 | tf_op jit(solution)/shard_map/ppermute | solution.py:46
  6.7 8.5 %copy-start.1 = (bf16[2560,256]{1,0:T(8,128)(2,1)S(1)}, bf16[2560,256]{1,0:T(8,128)(2,1)}, u32[]{:S(2)}) copy-start(bf16[2560,256]{1,0:T(8,128)(2,1)} %w_bc.1) | copy-start | bytes 3932164
  6.7 8.5 %copy-start.2 = (bf16[32,2560]{1,0:T(8,128)(2,1)S(1)}, bf16[32,2560]{1,0:T(8,128)(2,1)}, u32[]{:S(2)}) copy-start(bf16[32,2560]{1,0:T(8,128)(2,1)} %t0.1) | copy-start | bytes 491524
  12.8 1.8 %collective-permute-start.4 = (bf16[32,2560]{1,0:T(8,128)(2,1)S(1)}, bf16[32,2560]{1,0:T(8,128)(2,1)S(1)}, u32[]{:S(2)}, u32[]{:S(2)}) collective-permute-start(bf16[32,2560]{1,0:T(8,128)(2,1)S(1)} %collective-permute-done.t1), channel_id=1, source_target_pairs={{0,1},{1,0},{2,3},{3,2},{4,5},{5,4},{6,7},{7,6},{8,9},{9,8},{10,11... | collective-permute-start | bytes 491528 | tf_op jit(solution)/shard_map/ppermute | solution.py:46
  13.5 1.4 %collective-permute-start.5 = (bf16[32,2560]{1,0:T(8,128)(2,1)S(1)}, bf16[32,2560]{1,0:T(8,128)(2,1)S(1)}, u32[]{:S(2)}, u32[]{:S(2)}) collective-permute-start(bf16[32,2560]{1,0:T(8,128)(2,1)S(1)} %collective-permute-done.1.t2), channel_id=1, source_target_pairs={{0,1},{1,0},{2,3},{3,2},{4,5},{5,4},{6,7},{7,6},{8,9},{9,8},{10,11... | collective-permute-start | bytes 491528 | tf_op jit(solution)/shard_map/ppermute | solution.py:46
  13.5 1.6 %collective-permute-start.6 = (bf16[32,2560]{1,0:T(8,128)(2,1)S(1)}, bf16[32,2560]{1,0:T(8,128)(2,1)S(1)}, u32[]{:S(2)}, u32[]{:S(2)}) collective-permute-start(bf16[32,2560]{1,0:T(8,128)(2,1)S(1)} %collective-permute-done.2.t3), channel_id=1, source_target_pairs={{0,1},{1,0},{2,3},{3,2},{4,5},{5,4},{6,7},{7,6},{8,9},{9,8},{10,11... | collective-permute-start | bytes 491528 | tf_op jit(solution)/shard_map/ppermute | solution.py:46
  16.8 8.5 %collective-permute-start.7 = (bf16[8,896]{1,0:T(8,128)(2,1)S(1)}, bf16[8,896]{1,0:T(8,128)(2,1)S(1)}, u32[]{:S(2)}, u32[]{:S(2)}) collective-permute-start(bf16[8,896]{1,0:T(8,128)(2,1)S(1)} %get-tuple-element.40), channel_id=1, source_target_pairs={{0,8},{8,16},{16,24},{24,32},{32,40},{40,48},{48,56},{56,64},{64,7... | collective-permute-start | bytes 43016 | tf_op jit(solution)/shard_map/ppermute | solution.py:356
  25.5 5.6 %collective-permute-start.8 = (bf16[168,128]{1,0:T(8,128)(2,1)S(1)}, bf16[168,128]{1,0:T(8,128)(2,1)S(1)}, u32[]{:S(2)}, u32[]{:S(2)}) collective-permute-start(bf16[168,128]{1,0:T(8,128)(2,1)S(1)} %get-tuple-element.47), channel_id=1, source_target_pairs={{0,16},{8,24},{16,0},{24,8},{1,17},{9,25},{17,1},{25,9},{2,18},{10... | collective-permute-start | bytes 129032 | tf_op jit(solution)/shard_map/ppermute | solution.py:46
  25.6 5.5 %collective-permute-start.9 = (bf16[168,128]{1,0:T(8,128)(2,1)S(1)}, bf16[168,128]{1,0:T(8,128)(2,1)S(1)}, u32[]{:S(2)}, u32[]{:S(2)}) collective-permute-start(bf16[168,128]{1,0:T(8,128)(2,1)S(1)} %get-tuple-element.48), channel_id=1, source_target_pairs={{0,8},{8,0},{16,24},{24,16},{1,9},{9,1},{17,25},{25,17},{2,10},{10... | collective-permute-start | bytes 129032 | tf_op jit(solution)/shard_map/ppermute | solution.py:46
  25.7 5.4 %collective-permute-start.10 = (bf16[168,128]{1,0:T(8,128)(2,1)S(1)}, bf16[168,128]{1,0:T(8,128)(2,1)S(1)}, u32[]{:S(2)}, u32[]{:S(2)}) collective-permute-start(bf16[168,128]{1,0:T(8,128)(2,1)S(1)} %get-tuple-element.49), channel_id=1, source_target_pairs={{0,24},{8,16},{16,8},{24,0},{1,25},{9,17},{17,9},{25,1},{2,26},{10... | collective-permute-start | bytes 129032 | tf_op jit(solution)/shard_map/ppermute | solution.py:46
  30.1 19.5 %copy-start = (bf16[640,2560]{1,0:T(8,128)(2,1)S(1)}, bf16[640,2560]{1,0:T(8,128)(2,1)}, u32[]{:S(2)}) copy-start(bf16[640,2560]{1,0:T(8,128)(2,1)} %w.5) | copy-start | bytes 9830404
  31.3 3.0 %collective-permute-start.11 = (bf16[168,128]{1,0:T(8,128)(2,1)S(1)}, bf16[168,128]{1,0:T(8,128)(2,1)S(1)}, u32[]{:S(2)}, u32[]{:S(2)}) collective-permute-start(bf16[168,128]{1,0:T(8,128)(2,1)S(1)} %shard_map.105.row), channel_id=1, source_target_pairs={{0,32},{32,0},{64,96},{96,64},{128,160},{160,128},{192,224},{224,1... | collective-permute-start | bytes 129032 | tf_op jit(solution)/shard_map/ppermute | solution.py:46
  34.4 4.0 %collective-permute-start.12 = (bf16[168,128]{1,0:T(8,128)(2,1)S(1)}, bf16[168,128]{1,0:T(8,128)(2,1)S(1)}, u32[]{:S(2)}, u32[]{:S(2)}) collective-permute-start(bf16[168,128]{1,0:T(8,128)(2,1)S(1)} %shard_map.106), channel_id=1, source_target_pairs={{0,64},{32,96},{64,0},{96,32},{128,192},{160,224},{192,128},{224,1... | collective-permute-start | bytes 129032 | tf_op jit(solution)/shard_map/ppermute | solution.py:46
  38.5 4.2 %collective-permute-start.13 = (bf16[168,128]{1,0:T(8,128)(2,1)S(1)}, bf16[168,128]{1,0:T(8,128)(2,1)S(1)}, u32[]{:S(2)}, u32[]{:S(2)}) collective-permute-start(bf16[168,128]{1,0:T(8,128)(2,1)S(1)} %shard_map.107), channel_id=1, source_target_pairs={{0,224},{32,192},{64,160},{96,128},{128,96},{160,64},{192,32},{224... | collective-permute-start | bytes 129032 | tf_op jit(solution)/shard_map/ppermute | solution.py:46
  42.9 4.4 %collective-permute-start.14 = (bf16[32,640]{1,0:T(8,128)(2,1)S(1)}, bf16[32,640]{1,0:T(8,128)(2,1)S(1)}, u32[]{:S(2)}, u32[]{:S(2)}) collective-permute-start(bf16[32,640]{1,0:T(8,128)(2,1)S(1)} %get-tuple-element.60), channel_id=1, source_target_pairs={{0,16},{8,24},{16,0},{24,8},{1,17},{9,25},{17,1},{25,9},{2,18},{10... | collective-permute-start | bytes 122888 | tf_op jit(solution)/shard_map/ppermute | solution.py:46
  43.6 3.9 %collective-permute-start.15 = (bf16[32,640]{1,0:T(8,128)(2,1)S(1)}, bf16[32,640]{1,0:T(8,128)(2,1)S(1)}, u32[]{:S(2)}, u32[]{:S(2)}) collective-permute-start(bf16[32,640]{1,0:T(8,128)(2,1)S(1)} %get-tuple-element.61), channel_id=1, source_target_pairs={{0,8},{8,0},{16,24},{24,16},{1,9},{9,1},{17,25},{25,17},{2,10},{10... | collective-permute-start | bytes 122888 | tf_op jit(solution)/shard_map/ppermute | solution.py:46
  45.5 4.1 %collective-permute-start.16 = (bf16[32,640]{1,0:T(8,128)(2,1)S(1)}, bf16[32,640]{1,0:T(8,128)(2,1)S(1)}, u32[]{:S(2)}, u32[]{:S(2)}) collective-permute-start(bf16[32,640]{1,0:T(8,128)(2,1)S(1)} %get-tuple-element.62), channel_id=1, source_target_pairs={{0,24},{8,16},{16,8},{24,0},{1,25},{9,17},{17,9},{25,1},{2,26},{10... | collective-permute-start | bytes 122888 | tf_op jit(solution)/shard_map/ppermute | solution.py:46
  50.6 9.9 %collective-permute-start.17 = (bf16[128,2688]{1,0:T(8,128)(2,1)S(1)}, bf16[128,2688]{1,0:T(8,128)(2,1)S(1)}, u32[]{:S(2)}, u32[]{:S(2)}) collective-permute-start(bf16[128,2688]{1,0:T(8,128)(2,1)S(1)} %get-tuple-element.65), channel_id=1, source_target_pairs={{0,1},{1,0},{2,3},{3,2},{4,5},{5,4},{6,7},{7,6},{8,9},{9,8},{10,11... | collective-permute-start | bytes 2064392 | tf_op jit(solution)/shard_map/ppermute | solution.py:46
  61.6 5.6 %collective-permute-start.19 = (bf16[32,2688]{1,0:T(8,128)(2,1)S(1)}, bf16[32,2688]{1,0:T(8,128)(2,1)S(1)}, u32[]{:S(2)}, u32[]{:S(2)}) collective-permute-start(bf16[32,2688]{1,0:T(8,128)(2,1)S(1)} %get-tuple-element.67), channel_id=1, source_target_pairs={{0,2},{2,0},{4,6},{6,4},{1,3},{3,1},{5,7},{7,5},{8,10},{10,8},{12,... | collective-permute-start | bytes 516104 | tf_op jit(solution)/shard_map/ppermute | solution.py:46
  62.8 6.5 %collective-permute-start.20 = (bf16[32,2688]{1,0:T(8,128)(2,1)S(1)}, bf16[32,2688]{1,0:T(8,128)(2,1)S(1)}, u32[]{:S(2)}, u32[]{:S(2)}) collective-permute-start(bf16[32,2688]{1,0:T(8,128)(2,1)S(1)} %get-tuple-element.68), channel_id=1, source_target_pairs={{0,6},{2,4},{4,2},{6,0},{1,7},{3,5},{5,3},{7,1},{8,14},{10,12},{12... | collective-permute-start | bytes 516104 | tf_op jit(solution)/shard_map/ppermute | solution.py:46
  64.2 8.9 %collective-permute-start.18 = (bf16[32,2688]{1,0:T(8,128)(2,1)S(1)}, bf16[32,2688]{1,0:T(8,128)(2,1)S(1)}, u32[]{:S(2)}, u32[]{:S(2)}) collective-permute-start(bf16[32,2688]{1,0:T(8,128)(2,1)S(1)} %shard_map.111.before), channel_id=1, source_target_pairs={{0,4},{2,6},{4,0},{6,2},{1,5},{3,7},{5,1},{7,3},{8,12},{10,14},{12... | collective-permute-start | bytes 516104 | tf_op jit(solution)/shard_map/ppermute | solution.py:46
  (6 other events, 24.9 us)

commit v9 on v8

--- a/solution.py
+++ b/solution.py
@@ -58,20 +58,36 @@
     return pl.ds(pl.multiple_of(index * rows, rows), rows)
 
 
-def project_kernel(t0, t1, t2, t3, o0, o1, o2, o3, w, w_bc, early, all_out, pre_out, tail_out):
+def gain_kernel(gain, out):
+    out[...] = gain[...]
+
+
+def project_into(tokens, w, w_bc, out):
+    for lo, hi in ((0, 256), (256, 512), (512, WIDTH)):
+        out[:, lo:hi] = jnp.dot(tokens[...], w[:, lo:hi], preferred_element_type=F32).astype(BF)
+    out[:, WIDTH:] = jnp.dot(tokens[...], w_bc[...], preferred_element_type=F32).astype(BF)
+
+
+def project_early_kernel(t0, t1, t2, t3, o0, o3, w, w_bc, out, tokens):
+    for k, piece in enumerate((t0, t1, t2, t3, o0, o3)):
+        tokens[32 * k : 32 * k + 32, :] = piece[...]
+    project_into(tokens, w, w_bc, out)
+
+
+def project_kernel(t0, t1, t2, t3, o0, o1, o2, o3, part, w, w_bc, early, all_out, pre_out, tail_out, late, rest):
     y, c = lax.axis_index("y"), lax.axis_index("c")
-    for d, own, other in zip(TOKEN_MASKS, (t0, t1, t2, t3), (o0, o1, o2, o3)):
-        source = other_index(y, d)
-        all_out[row_at(source * 2 + c, ROWS), :] = own[...]
-        all_out[row_at(source * 2 + 1 - c, ROWS), :] = other[...]
-    tokens = all_out[...]
-    for lo, hi in ((0, 256), (256, 512), (512, WIDTH)):
-        part = jnp.dot(tokens, w[:, lo:hi], preferred_element_type=F32).astype(BF)
-        pre_out[:, lo:hi] = part
-        tail_out[:, lo:hi] = part[BLOCK - 8 :]
-    part = jnp.dot(tokens, w_bc[...], preferred_element_type=F32).astype(BF)
-    pre_out[:, WIDTH:] = part
-    tail_out[:, WIDTH:] = part[BLOCK - 8 :]
+    near = [row_at(other_index(y, mask) * 2 + c, ROWS) for mask in TOKEN_MASKS]
+    far = [row_at(other_index(y, mask) * 2 + 1 - c, ROWS) for mask in TOKEN_MASKS]
+    late[0:32, :] = o1[...]
+    late[32:64, :] = o2[...]
+    project_into(late, w, w_bc, rest)
+    for rows, piece in zip(near + far, (t0, t1, t2, t3, o0, o1, o2, o3)):
+        all_out[rows, :] = piece[...]
+    for k, rows in enumerate(near + [far[0], far[3]]):
+        pre_out[rows, :] = part[32 * k : 32 * k + 32, :]
+    for k, rows in enumerate(far[1:3]):
+        pre_out[rows, :] = rest[32 * k : 32 * k + 32, :]
+    tail_out[...] = pre_out[BLOCK - 8 :, :]
 
 
 def gate_kernel(tokens, w, before, out):
@@ -342,16 +358,27 @@
 
 
 def body(tokens, w_xz, w_bc, w_dt, dt_bias, a_log, conv_x, conv_bc, norm_gain, w_out):
-    near = exchanged([tokens] * 4, "y", TOKEN_MASKS)
     w_both = w_xz.reshape(MODEL, 2 * WIDTH)
-    near[1:] = [lax.optimization_barrier((piece, w_both))[0] for piece in near[1:]]
-    far = [swapped(piece, "c", 1) for piece in near]
-    gain = norm_gain[None]
+    near, far = [tokens], [swapped(tokens, "c", 1)]
+    for mask in TOKEN_MASKS[1:]:
+        near.append(swapped(tokens, "y", mask))
+    near[3], w_both = lax.optimization_barrier((near[3], w_both))
+    for mask, piece in zip(TOKEN_MASKS[1:], near[1:]):
+        far.append(swapped(piece, "c", 1))
+    (gain,) = call(gain_kernel, [((1, WIDTH), F32)], [norm_gain[None]])
+    (part,) = call(
+        project_early_kernel,
+        [((192, PRE), BF)],
+        [*near, far[0], far[3], w_both, w_bc],
+        scratch=[((192, MODEL), BF)],
+        flops=2 * 192 * MODEL * 1024,
+    )
     everything, pre, tail = call(
         project_kernel,
         [((BLOCK, MODEL), BF), ((BLOCK, PRE), BF), ((8, PRE), BF)],
-        [*near, *far, w_both, w_bc, gain],
-        flops=2 * BLOCK * MODEL * 1024,
+        [*near, *far, part, w_both, w_bc, gain],
+        scratch=[((64, MODEL), BF), ((64, PRE), BF)],
+        flops=2 * 64 * MODEL * 1024,
     )
     tail = lax.ppermute(tail, SEQ, [(i, (i + 1) % 32) for i in range(32)])
     v, b, c, step, cum, weight, factor, main = call(

time: 74 us -> 73.5 us (level)
  waiting for transfers between devices: 30 us -> 28.6 us
    ppermute x20, waiting for transfers between devices: 24.3 us -> 22.9 us  [swapped(): lax.ppermute(value, axis, [(i, i ^ mask) for i in range(lax.axis_size(axi...]
    pallas_call x15 -> x17, Pallas kernels: 10.2 us -> 10.7 us  [call(): pl.pallas_call(body, out_shape=[jax.ShapeDtypeStruct(s, t) for s, t in ou...]
  transfers between devices with their start and end apart: 21 -> 21, of which waited for: 15 -> 12; matrix products, arithmetic and copies ran while one was open for 6% -> 6% of each run, Pallas kernels for 7% -> 8%
where the time goes in v9:
time: 73.5 us
  starting transfers between devices  29.6 us (40%)
  waiting for transfers between devices  28.6 us (39%)
  Pallas kernels  10.7 us (15%)
  local copies, waits for them, and re-layouts  4.15 us (6%)
    ppermute x20, starting transfers between devices, swapped(): lax.ppermute(value, axis, [(i, i ^ mask) for i in range(lax.axis_size(axi...  28.9 us
    ppermute x20, waiting for transfers between devices, swapped(): lax.ppermute(value, axis, [(i, i ^ mask) for i in range(lax.axis_size(axi...  22.9 us
    pallas_call x17, Pallas kernels, call(): pl.pallas_call(body, out_shape=[jax.ShapeDtypeStruct(s, t) for s, t in ou...  10.7 us
    ppermute x1, waiting for transfers between devices, body(): tail = lax.ppermute(tail, SEQ, [(i, (i + 1) % 32) for i in range(32)])  5.69 us
    unnamed x19, local copies, waits for them, and re-layouts  4.14 us
  transfers between devices with their start and end apart: 21, of which 12 were waited for; matrix products, arithmetic and copies ran while one was open for 6% of the time, Pallas kernels for 8%

profile of v9, /device:TPU:1, one launch (start us, length us, event | category | flops | bytes accessed | tf_op | source)
XLA Modules:
  0.0 73.5 jit_solution(12260674485041448576)
XLA Ops:
  0.0 3.7 %collective-permute-start.2 = (bf16[32,2560]{1,0:T(8,128)(2,1)}, bf16[32,2560]{1,0:T(8,128)(2,1)S(1)}, u32[]{:S(2)}, u32[]{:S(2)}) collective-permute-start(bf16[32,2560]{1,0:T(8,128)(2,1)} %t0.3), channel_id=1, source_target_pairs={{0,4},{2,6},{4,0},{6,2},{1,5},{3,7},{5,1},{7,3},{8,12},{10,14},{12... | collective-permute-start | bytes 491528 | tf_op jit(solution)/shard_map/ppermute | solution.py:46
  4.5 2.2 %collective-permute-start.3 = (bf16[32,2560]{1,0:T(8,128)(2,1)}, bf16[32,2560]{1,0:T(8,128)(2,1)S(1)}, u32[]{:S(2)}, u32[]{:S(2)}) collective-permute-start(bf16[32,2560]{1,0:T(8,128)(2,1)} %t0.3), channel_id=1, source_target_pairs={{0,1},{1,0},{2,3},{3,2},{4,5},{5,4},{6,7},{7,6},{8,9},{9,8},{10,11... | collective-permute-start | bytes 491528 | tf_op jit(solution)/shard_map/ppermute | solution.py:46
  6.7 4.1 %copy.11 = bf16[320,8,2,640]{3,1,2,0:T(8,128)(2,1)S(1)} copy(bf16[320,8,2,640]{3,2,1,0:T(2,128)(2,1)} %bitcast.11) | data formatting | bytes 13107200
  11.1 1.7 %collective-permute-done.1.t2 = bf16[32,2560]{1,0:T(8,128)(2,1)S(1)} collective-permute-done((bf16[32,2560]{1,0:T(8,128)(2,1)}, bf16[32,2560]{1,0:T(8,128)(2,1)S(1)}, u32[]{:S(2)}, u32[]{:S(2)}) %collective-permute-start.1) | collective-permute-done | bytes 163872 | tf_op jit(solution)/shard_map/ppermute | solution.py:46
  13.6 1.2 %shard_map.100.part = bf16[192,896]{1,0:T(8,128)(2,1)S(1)} custom-call(bf16[32,2560]{1,0:T(8,128)(2,1)S(1)} %copy-done.2, bf16[32,2560]{1,0:T(8,128)(2,1)S(1)} %collective-permute-done.t1, bf16[32,2560]{1,0:T(8,128)(2,1)S(1)} %collective-permute-done.1.t2, bf16[32,2560]{1,0:T(8,128)(2,1)S(1)} %collective-permute-done.2.t3, ...), custom_call_target="tpu_custom_call" | custom-call | flops 1006632960 | bytes 2013265 | tf_op jit(solution)/shard_map/pallas_call | solution.py:34
  16.6 1.9 %shard_map.103 = (bf16[256,640]{1,0:T(8,128)(2,1)S(1)}, bf16[256,128]{1,0:T(8,128)(2,1)S(1)}, bf16[256,128]{1,0:T(8,128)(2,1)S(1)}, f32[256,128]{1,0:T(8,128)S(1...) custom-call(bf16[256,896]{1,0:T(8,128)(2,1)S(1)} %get-tuple-element.39.pre, ...), custom_call_target="tpu_custom_call" | custom-call | flops 41943040 | bytes 83886 | tf_op jit(solution)/shard_map/pallas_call | solution.py:34
  18.5 5.7 %collective-permute-done.7.tail = bf16[8,896]{1,0:T(8,128)(2,1)S(1)} collective-permute-done((bf16[8,896]{1,0:T(8,128)(2,1)S(1)}, bf16[8,896]{1,0:T(8,128)(2,1)S(1)}, u32[]{:S(2)}, u32[]{:S(2)}) %collective-permute-start.7) | collective-permute-done | bytes 14368 | tf_op jit(solution)/shard_map/ppermute | solution.py:383
  24.7 3.1 %collective-permute-start.10 = (bf16[168,128]{1,0:T(8,128)(2,1)S(1)}, bf16[168,128]{1,0:T(8,128)(2,1)S(1)}, u32[]{:S(2)}, u32[]{:S(2)}) collective-permute-start(bf16[168,128]{1,0:T(8,128)(2,1)S(1)} %get-tuple-element.47), channel_id=1, source_target_pairs={{0,24},{8,16},{16,8},{24,0},{1,25},{9,17},{17,9},{25,1},{2,26},{10... | collective-permute-start | bytes 129032 | tf_op jit(solution)/shard_map/ppermute | solution.py:46
  27.8 1.2 %shard_map.106.before_too.gate = f32[256,640]{1,0:T(8,128)S(1)} custom-call(bf16[256,2560]{1,0:T(8,128)(2,1)S(1)} %get-tuple-element.40.tokens, bf16[2560,1280]{1,0:T(8,128)(2,1)S(1)} %bitcast.7, bf16[8,640]{1,0:T(8,128)(2,1)S(1)} %get-tuple-element.51.v_first.before), custom_call_target="tpu_custom_call" | custom-call | flops 838860800 | bytes 1677721 | tf_op jit(solution)/shard_map/pallas_call | solution.py:34
  29.1 1.0 %shard_map.105 = (f32[256,640]{1,0:T(8,128)S(1)}, bf16[256,128]{1,0:T(8,128)(2,1)S(1)}) custom-call(bf16[256,640]{1,0:T(8,128)(2,1)S(1)} %get-tuple-element.48.v, bf16[256,128]{1,0:T(8,128)(2,1)S(1)} %get-tuple-element.49.b, bf16[256,128]{1,0:T(8,128)(2,1)S(1)} %get-tuple-element.50.c, bf16[8,640]{1,0:T(8,128)(2,1)S(1)} %get-tuple-element.51.v_first.before, ...), custom_call_target="tpu_custom_call" | custom-call | flops 335544320 | bytes 671088 | tf_op jit(solution)/shard_map/pallas_call | solution.py:34
  30.4 2.9 %collective-permute-done.11.other = bf16[168,128]{1,0:T(8,128)(2,1)S(1)} collective-permute-done((bf16[168,128]{1,0:T(8,128)(2,1)S(1)}, bf16[168,128]{1,0:T(8,128)(2,1)S(1)}, u32[]{:S(2)}, u32[]{:S(2)}) %collective-permute-start.11) | collective-permute-done | bytes 43040 | tf_op jit(solution)/shard_map/ppermute | solution.py:46
  34.1 3.3 %collective-permute-done.12.previous = bf16[168,128]{1,0:T(8,128)(2,1)S(1)} collective-permute-done((bf16[168,128]{1,0:T(8,128)(2,1)S(1)}, bf16[168,128]{1,0:T(8,128)(2,1)S(1)}, u32[]{:S(2)}, u32[]{:S(2)}) %collective-permute-start.12) | collective-permute-done | bytes 43040 | tf_op jit(solution)/shard_map/ppermute | solution.py:46
  37.5 1.3 %collective-permute-start.13 = (bf16[168,128]{1,0:T(8,128)(2,1)S(1)}, bf16[168,128]{1,0:T(8,128)(2,1)S(1)}, u32[]{:S(2)}, u32[]{:S(2)}) collective-permute-start(bf16[168,128]{1,0:T(8,128)(2,1)S(1)} %shard_map.109), channel_id=1, source_target_pairs={{0,224},{32,192},{64,160},{96,128},{128,96},{160,64},{192,32},{224... | collective-permute-start | bytes 129032 | tf_op jit(solution)/shard_map/ppermute | solution.py:46
  38.8 2.9 %collective-permute-done.13.quad = bf16[168,128]{1,0:T(8,128)(2,1)S(1)} collective-permute-done((bf16[168,128]{1,0:T(8,128)(2,1)S(1)}, bf16[168,128]{1,0:T(8,128)(2,1)S(1)}, u32[]{:S(2)}, u32[]{:S(2)}) %collective-permute-start.13) | collective-permute-done | bytes 43040 | tf_op jit(solution)/shard_map/ppermute | solution.py:46
  42.5 2.0 %collective-permute-start.15 = (bf16[32,640]{1,0:T(8,128)(2,1)S(1)}, bf16[32,640]{1,0:T(8,128)(2,1)S(1)}, u32[]{:S(2)}, u32[]{:S(2)}) collective-permute-start(bf16[32,640]{1,0:T(8,128)(2,1)S(1)} %get-tuple-element.59), channel_id=1, source_target_pairs={{0,8},{8,0},{16,24},{24,16},{1,9},{9,1},{17,25},{25,17},{2,10},{10... | collective-permute-start | bytes 122888 | tf_op jit(solution)/shard_map/ppermute | solution.py:46
  45.2 1.1 %collective-permute-done.14.e1 = bf16[32,640]{1,0:T(8,128)(2,1)S(1)} collective-permute-done((bf16[32,640]{1,0:T(8,128)(2,1)S(1)}, bf16[32,640]{1,0:T(8,128)(2,1)S(1)}, u32[]{:S(2)}, u32[]{:S(2)}) %collective-permute-start.14) | collective-permute-done | bytes 40992 | tf_op jit(solution)/shard_map/ppermute | solution.py:46
  46.4 2.2 %collective-permute-done.16.e3 = bf16[32,640]{1,0:T(8,128)(2,1)S(1)} collective-permute-done((bf16[32,640]{1,0:T(8,128)(2,1)S(1)}, bf16[32,640]{1,0:T(8,128)(2,1)S(1)}, u32[]{:S(2)}, u32[]{:S(2)}) %collective-permute-start.16) | collective-permute-done | bytes 40992 | tf_op jit(solution)/shard_map/ppermute | solution.py:46
  49.5 7.9 %collective-permute-start.17 = (bf16[128,2688]{1,0:T(8,128)(2,1)S(1)}, bf16[128,2688]{1,0:T(8,128)(2,1)S(1)}, u32[]{:S(2)}, u32[]{:S(2)}) collective-permute-start(bf16[128,2688]{1,0:T(8,128)(2,1)S(1)} %get-tuple-element.63), channel_id=1, source_target_pairs={{0,1},{1,0},{2,3},{3,2},{4,5},{5,4},{6,7},{7,6},{8,9},{9,8},{10,11... | collective-permute-start | bytes 2064392 | tf_op jit(solution)/shard_map/ppermute | solution.py:46
  60.3 1.6 %collective-permute-start.19 = (bf16[32,2688]{1,0:T(8,128)(2,1)S(1)}, bf16[32,2688]{1,0:T(8,128)(2,1)S(1)}, u32[]{:S(2)}, u32[]{:S(2)}) collective-permute-start(bf16[32,2688]{1,0:T(8,128)(2,1)S(1)} %get-tuple-element.65), channel_id=1, source_target_pairs={{0,2},{2,0},{4,6},{6,4},{1,3},{3,1},{5,7},{7,5},{8,10},{10,8},{12,... | collective-permute-start | bytes 516104 | tf_op jit(solution)/shard_map/ppermute | solution.py:46
  61.9 1.9 %collective-permute-start.20 = (bf16[32,2688]{1,0:T(8,128)(2,1)S(1)}, bf16[32,2688]{1,0:T(8,128)(2,1)S(1)}, u32[]{:S(2)}, u32[]{:S(2)}) collective-permute-start(bf16[32,2688]{1,0:T(8,128)(2,1)S(1)} %get-tuple-element.66), channel_id=1, source_target_pairs={{0,6},{2,4},{4,2},{6,0},{1,7},{3,5},{5,3},{7,1},{8,14},{10,12},{12... | collective-permute-start | bytes 516104 | tf_op jit(solution)/shard_map/ppermute | solution.py:46
  63.8 1.1 %collective-permute-start.18 = (bf16[32,2688]{1,0:T(8,128)(2,1)S(1)}, bf16[32,2688]{1,0:T(8,128)(2,1)S(1)}, u32[]{:S(2)}, u32[]{:S(2)}) collective-permute-start(bf16[32,2688]{1,0:T(8,128)(2,1)S(1)} %shard_map.113.before), channel_id=1, source_target_pairs={{0,4},{2,6},{4,0},{6,2},{1,5},{3,7},{5,1},{7,3},{8,12},{10,14},{12... | collective-permute-start | bytes 516104 | tf_op jit(solution)/shard_map/ppermute | solution.py:46
  64.9 1.2 %collective-permute-done.19.g2 = bf16[32,2688]{1,0:T(8,128)(2,1)S(1)} collective-permute-done((bf16[32,2688]{1,0:T(8,128)(2,1)S(1)}, bf16[32,2688]{1,0:T(8,128)(2,1)S(1)}, u32[]{:S(2)}, u32[]{:S(2)}) %collective-permute-start.19) | collective-permute-done | bytes 172064 | tf_op jit(solution)/shard_map/ppermute | solution.py:46
  66.1 4.6 %collective-permute-done.20.g3 = bf16[32,2688]{1,0:T(8,128)(2,1)S(1)} collective-permute-done((bf16[32,2688]{1,0:T(8,128)(2,1)S(1)}, bf16[32,2688]{1,0:T(8,128)(2,1)S(1)}, u32[]{:S(2)}, u32[]{:S(2)}) %collective-permute-start.20) | collective-permute-done | bytes 172064 | tf_op jit(solution)/shard_map/ppermute | solution.py:46
  70.7 2.0 %collective-permute-done.18.g1 = bf16[32,2688]{1,0:T(8,128)(2,1)S(1)} collective-permute-done((bf16[32,2688]{1,0:T(8,128)(2,1)S(1)}, bf16[32,2688]{1,0:T(8,128)(2,1)S(1)}, u32[]{:S(2)}, u32[]{:S(2)}) %collective-permute-start.18) | collective-permute-done | bytes 172064 | tf_op jit(solution)/shard_map/ppermute | solution.py:46
  (55 shorter events, 11.4 us)
Async XLA Ops:
  0.0 10.8 %collective-permute-start.2 = (bf16[32,2560]{1,0:T(8,128)(2,1)}, bf16[32,2560]{1,0:T(8,128)(2,1)S(1)}, u32[]{:S(2)}, u32[]{:S(2)}) collective-permute-start(bf16[32,2560]{1,0:T(8,128)(2,1)} %t0.3), channel_id=1, source_target_pairs={{0,4},{2,6},{4,0},{6,2},{1,5},{3,7},{5,1},{7,3},{8,12},{10,14},{12... | collective-permute-start | bytes 491528 | tf_op jit(solution)/shard_map/ppermute | solution.py:46
  3.7 9.0 %collective-permute-start.1 = (bf16[32,2560]{1,0:T(8,128)(2,1)}, bf16[32,2560]{1,0:T(8,128)(2,1)S(1)}, u32[]{:S(2)}, u32[]{:S(2)}) collective-permute-start(bf16[32,2560]{1,0:T(8,128)(2,1)} %t0.3), channel_id=1, source_target_pairs={{0,6},{2,4},{4,2},{6,0},{1,7},{3,5},{5,3},{7,1},{8,14},{10,12},{12... | collective-permute-start | bytes 491528 | tf_op jit(solution)/shard_map/ppermute | solution.py:46
  4.5 9.0 %collective-permute-start = (bf16[32,2560]{1,0:T(8,128)(2,1)}, bf16[32,2560]{1,0:T(8,128)(2,1)S(1)}, u32[]{:S(2)}, u32[]{:S(2)}) collective-permute-start(bf16[32,2560]{1,0:T(8,128)(2,1)} %t0.3), channel_id=1, source_target_pairs={{0,2},{2,0},{4,6},{6,4},{1,3},{3,1},{5,7},{7,5},{8,10},{10,8},{12,... | collective-permute-start | bytes 491528 | tf_op jit(solution)/shard_map/ppermute | solution.py:46
  4.5 9.1 %collective-permute-start.3 = (bf16[32,2560]{1,0:T(8,128)(2,1)}, bf16[32,2560]{1,0:T(8,128)(2,1)S(1)}, u32[]{:S(2)}, u32[]{:S(2)}) collective-permute-start(bf16[32,2560]{1,0:T(8,128)(2,1)} %t0.3), channel_id=1, source_target_pairs={{0,1},{1,0},{2,3},{3,2},{4,5},{5,4},{6,7},{7,6},{8,9},{9,8},{10,11... | collective-permute-start | bytes 491528 | tf_op jit(solution)/shard_map/ppermute | solution.py:46
  6.7 6.9 %copy-start.1 = (bf16[2560,256]{1,0:T(8,128)(2,1)S(1)}, bf16[2560,256]{1,0:T(8,128)(2,1)}, u32[]{:S(2)}) copy-start(bf16[2560,256]{1,0:T(8,128)(2,1)} %w_bc.3) | copy-start | bytes 3932164
  6.7 6.9 %copy-start.2 = (bf16[32,2560]{1,0:T(8,128)(2,1)S(1)}, bf16[32,2560]{1,0:T(8,128)(2,1)}, u32[]{:S(2)}) copy-start(bf16[32,2560]{1,0:T(8,128)(2,1)} %t0.3) | copy-start | bytes 491524
  10.8 2.8 %collective-permute-start.6 = (bf16[32,2560]{1,0:T(8,128)(2,1)S(1)}, bf16[32,2560]{1,0:T(8,128)(2,1)S(1)}, u32[]{:S(2)}, u32[]{:S(2)}) collective-permute-start(bf16[32,2560]{1,0:T(8,128)(2,1)S(1)} %collective-permute-done.2.t3), channel_id=1, source_target_pairs={{0,1},{1,0},{2,3},{3,2},{4,5},{5,4},{6,7},{7,6},{8,9},{9,8},{10,11... | collective-permute-start | bytes 491528 | tf_op jit(solution)/shard_map/ppermute | solution.py:46
  12.8 2.1 %collective-permute-start.5 = (bf16[32,2560]{1,0:T(8,128)(2,1)S(1)}, bf16[32,2560]{1,0:T(8,128)(2,1)S(1)}, u32[]{:S(2)}, u32[]{:S(2)}) collective-permute-start(bf16[32,2560]{1,0:T(8,128)(2,1)S(1)} %collective-permute-done.1.t2), channel_id=1, source_target_pairs={{0,1},{1,0},{2,3},{3,2},{4,5},{5,4},{6,7},{7,6},{8,9},{9,8},{10,11... | collective-permute-start | bytes 491528 | tf_op jit(solution)/shard_map/ppermute | solution.py:46
  13.5 1.4 %collective-permute-start.4 = (bf16[32,2560]{1,0:T(8,128)(2,1)S(1)}, bf16[32,2560]{1,0:T(8,128)(2,1)S(1)}, u32[]{:S(2)}, u32[]{:S(2)}) collective-permute-start(bf16[32,2560]{1,0:T(8,128)(2,1)S(1)} %collective-permute-done.t1), channel_id=1, source_target_pairs={{0,1},{1,0},{2,3},{3,2},{4,5},{5,4},{6,7},{7,6},{8,9},{9,8},{10,11... | collective-permute-start | bytes 491528 | tf_op jit(solution)/shard_map/ppermute | solution.py:46
  15.8 8.4 %collective-permute-start.7 = (bf16[8,896]{1,0:T(8,128)(2,1)S(1)}, bf16[8,896]{1,0:T(8,128)(2,1)S(1)}, u32[]{:S(2)}, u32[]{:S(2)}) collective-permute-start(bf16[8,896]{1,0:T(8,128)(2,1)S(1)} %get-tuple-element.38), channel_id=1, source_target_pairs={{0,8},{8,16},{16,24},{24,32},{32,40},{40,48},{48,56},{56,64},{64,7... | collective-permute-start | bytes 43016 | tf_op jit(solution)/shard_map/ppermute | solution.py:383
  24.5 5.6 %collective-permute-start.8 = (bf16[168,128]{1,0:T(8,128)(2,1)S(1)}, bf16[168,128]{1,0:T(8,128)(2,1)S(1)}, u32[]{:S(2)}, u32[]{:S(2)}) collective-permute-start(bf16[168,128]{1,0:T(8,128)(2,1)S(1)} %get-tuple-element.45), channel_id=1, source_target_pairs={{0,16},{8,24},{16,0},{24,8},{1,17},{9,25},{17,1},{25,9},{2,18},{10... | collective-permute-start | bytes 129032 | tf_op jit(solution)/shard_map/ppermute | solution.py:46
  24.6 5.5 %collective-permute-start.9 = (bf16[168,128]{1,0:T(8,128)(2,1)S(1)}, bf16[168,128]{1,0:T(8,128)(2,1)S(1)}, u32[]{:S(2)}, u32[]{:S(2)}) collective-permute-start(bf16[168,128]{1,0:T(8,128)(2,1)S(1)} %get-tuple-element.46), channel_id=1, source_target_pairs={{0,8},{8,0},{16,24},{24,16},{1,9},{9,1},{17,25},{25,17},{2,10},{10... | collective-permute-start | bytes 129032 | tf_op jit(solution)/shard_map/ppermute | solution.py:46
  24.7 5.4 %collective-permute-start.10 = (bf16[168,128]{1,0:T(8,128)(2,1)S(1)}, bf16[168,128]{1,0:T(8,128)(2,1)S(1)}, u32[]{:S(2)}, u32[]{:S(2)}) collective-permute-start(bf16[168,128]{1,0:T(8,128)(2,1)S(1)} %get-tuple-element.47), channel_id=1, source_target_pairs={{0,24},{8,16},{16,8},{24,0},{1,25},{9,17},{17,9},{25,1},{2,26},{10... | collective-permute-start | bytes 129032 | tf_op jit(solution)/shard_map/ppermute | solution.py:46
  29.0 19.5 %copy-start = (bf16[640,2560]{1,0:T(8,128)(2,1)S(1)}, bf16[640,2560]{1,0:T(8,128)(2,1)}, u32[]{:S(2)}) copy-start(bf16[640,2560]{1,0:T(8,128)(2,1)} %w.5) | copy-start | bytes 9830404
  30.3 3.0 %collective-permute-start.11 = (bf16[168,128]{1,0:T(8,128)(2,1)S(1)}, bf16[168,128]{1,0:T(8,128)(2,1)S(1)}, u32[]{:S(2)}, u32[]{:S(2)}) collective-permute-start(bf16[168,128]{1,0:T(8,128)(2,1)S(1)} %shard_map.107.row), channel_id=1, source_target_pairs={{0,32},{32,0},{64,96},{96,64},{128,160},{160,128},{192,224},{224,1... | collective-permute-start | bytes 129032 | tf_op jit(solution)/shard_map/ppermute | solution.py:46
  33.3 4.0 %collective-permute-start.12 = (bf16[168,128]{1,0:T(8,128)(2,1)S(1)}, bf16[168,128]{1,0:T(8,128)(2,1)S(1)}, u32[]{:S(2)}, u32[]{:S(2)}) collective-permute-start(bf16[168,128]{1,0:T(8,128)(2,1)S(1)} %shard_map.108), channel_id=1, source_target_pairs={{0,64},{32,96},{64,0},{96,32},{128,192},{160,224},{192,128},{224,1... | collective-permute-start | bytes 129032 | tf_op jit(solution)/shard_map/ppermute | solution.py:46
  37.5 4.2 %collective-permute-start.13 = (bf16[168,128]{1,0:T(8,128)(2,1)S(1)}, bf16[168,128]{1,0:T(8,128)(2,1)S(1)}, u32[]{:S(2)}, u32[]{:S(2)}) collective-permute-start(bf16[168,128]{1,0:T(8,128)(2,1)S(1)} %shard_map.109), channel_id=1, source_target_pairs={{0,224},{32,192},{64,160},{96,128},{128,96},{160,64},{192,32},{224... | collective-permute-start | bytes 129032 | tf_op jit(solution)/shard_map/ppermute | solution.py:46
  41.9 4.4 %collective-permute-start.14 = (bf16[32,640]{1,0:T(8,128)(2,1)S(1)}, bf16[32,640]{1,0:T(8,128)(2,1)S(1)}, u32[]{:S(2)}, u32[]{:S(2)}) collective-permute-start(bf16[32,640]{1,0:T(8,128)(2,1)S(1)} %get-tuple-element.58), channel_id=1, source_target_pairs={{0,16},{8,24},{16,0},{24,8},{1,17},{9,25},{17,1},{25,9},{2,18},{10... | collective-permute-start | bytes 122888 | tf_op jit(solution)/shard_map/ppermute | solution.py:46
  42.5 3.9 %collective-permute-start.15 = (bf16[32,640]{1,0:T(8,128)(2,1)S(1)}, bf16[32,640]{1,0:T(8,128)(2,1)S(1)}, u32[]{:S(2)}, u32[]{:S(2)}) collective-permute-start(bf16[32,640]{1,0:T(8,128)(2,1)S(1)} %get-tuple-element.59), channel_id=1, source_target_pairs={{0,8},{8,0},{16,24},{24,16},{1,9},{9,1},{17,25},{25,17},{2,10},{10... | collective-permute-start | bytes 122888 | tf_op jit(solution)/shard_map/ppermute | solution.py:46
  44.5 4.1 %collective-permute-start.16 = (bf16[32,640]{1,0:T(8,128)(2,1)S(1)}, bf16[32,640]{1,0:T(8,128)(2,1)S(1)}, u32[]{:S(2)}, u32[]{:S(2)}) collective-permute-start(bf16[32,640]{1,0:T(8,128)(2,1)S(1)} %get-tuple-element.60), channel_id=1, source_target_pairs={{0,24},{8,16},{16,8},{24,0},{1,25},{9,17},{17,9},{25,1},{2,26},{10... | collective-permute-start | bytes 122888 | tf_op jit(solution)/shard_map/ppermute | solution.py:46
  49.5 9.6 %collective-permute-start.17 = (bf16[128,2688]{1,0:T(8,128)(2,1)S(1)}, bf16[128,2688]{1,0:T(8,128)(2,1)S(1)}, u32[]{:S(2)}, u32[]{:S(2)}) collective-permute-start(bf16[128,2688]{1,0:T(8,128)(2,1)S(1)} %get-tuple-element.63), channel_id=1, source_target_pairs={{0,1},{1,0},{2,3},{3,2},{4,5},{5,4},{6,7},{7,6},{8,9},{9,8},{10,11... | collective-permute-start | bytes 2064392 | tf_op jit(solution)/shard_map/ppermute | solution.py:46
  60.3 5.7 %collective-permute-start.19 = (bf16[32,2688]{1,0:T(8,128)(2,1)S(1)}, bf16[32,2688]{1,0:T(8,128)(2,1)S(1)}, u32[]{:S(2)}, u32[]{:S(2)}) collective-permute-start(bf16[32,2688]{1,0:T(8,128)(2,1)S(1)} %get-tuple-element.65), channel_id=1, source_target_pairs={{0,2},{2,0},{4,6},{6,4},{1,3},{3,1},{5,7},{7,5},{8,10},{10,8},{12,... | collective-permute-start | bytes 516104 | tf_op jit(solution)/shard_map/ppermute | solution.py:46
  61.9 8.8 %collective-permute-start.20 = (bf16[32,2688]{1,0:T(8,128)(2,1)S(1)}, bf16[32,2688]{1,0:T(8,128)(2,1)S(1)}, u32[]{:S(2)}, u32[]{:S(2)}) collective-permute-start(bf16[32,2688]{1,0:T(8,128)(2,1)S(1)} %get-tuple-element.66), channel_id=1, source_target_pairs={{0,6},{2,4},{4,2},{6,0},{1,7},{3,5},{5,3},{7,1},{8,14},{10,12},{12... | collective-permute-start | bytes 516104 | tf_op jit(solution)/shard_map/ppermute | solution.py:46
  63.8 8.9 %collective-permute-start.18 = (bf16[32,2688]{1,0:T(8,128)(2,1)S(1)}, bf16[32,2688]{1,0:T(8,128)(2,1)S(1)}, u32[]{:S(2)}, u32[]{:S(2)}) collective-permute-start(bf16[32,2688]{1,0:T(8,128)(2,1)S(1)} %shard_map.113.before), channel_id=1, source_target_pairs={{0,4},{2,6},{4,0},{6,2},{1,5},{3,7},{5,1},{7,3},{8,12},{10,14},{12... | collective-permute-start | bytes 516104 | tf_op jit(solution)/shard_map/ppermute | solution.py:46
  (6 other events, 15.4 us)

commit v10 on v9

--- a/solution.py
+++ b/solution.py
@@ -74,15 +74,13 @@
     project_into(tokens, w, w_bc, out)
 
 
-def project_kernel(t0, t1, t2, t3, o0, o1, o2, o3, part, w, w_bc, early, all_out, pre_out, tail_out, late, rest):
+def project_kernel(o1, o2, part, w, w_bc, early, pre_out, tail_out, late, rest):
     y, c = lax.axis_index("y"), lax.axis_index("c")
     near = [row_at(other_index(y, mask) * 2 + c, ROWS) for mask in TOKEN_MASKS]
     far = [row_at(other_index(y, mask) * 2 + 1 - c, ROWS) for mask in TOKEN_MASKS]
     late[0:32, :] = o1[...]
     late[32:64, :] = o2[...]
     project_into(late, w, w_bc, rest)
-    for rows, piece in zip(near + far, (t0, t1, t2, t3, o0, o1, o2, o3)):
-        all_out[rows, :] = piece[...]
     for k, rows in enumerate(near + [far[0], far[3]]):
         pre_out[rows, :] = part[32 * k : 32 * k + 32, :]
     for k, rows in enumerate(far[1:3]):
@@ -118,12 +116,20 @@
 
 def prepare_kernel(
     pre,
-    tokens,
+    t0,
+    t1,
+    t2,
+    t3,
+    o0,
+    o1,
+    o2,
+    o3,
     w_dt,
     conv_x,
     conv_bc,
     bias,
     a_log,
+    tokens,
     v_out,
     b_out,
     c_out,
@@ -136,6 +142,10 @@
     small,
     w_steps,
 ):
+    y, c = lax.axis_index("y"), lax.axis_index("c")
+    for mask, own, other in zip(TOKEN_MASKS, (t0, t1, t2, t3), (o0, o1, o2, o3)):
+        tokens[row_at(other_index(y, mask) * 2 + c, ROWS), :] = own[...]
+        tokens[row_at(other_index(y, mask) * 2 + 1 - c, ROWS), :] = other[...]
     w_steps[...] = jnp.zeros(w_steps.shape, BF)
     w_steps[0 : w_dt.shape[0], :] = w_dt[...]
     dt_pre = lax.dot_general(tokens[...], w_steps[...], (((1,), (1,)), ((), ())), preferred_element_type=F32)
@@ -302,7 +312,7 @@
     return jnp.where(lane == 0, high.astype(F32), jnp.where(lane == 1, low.astype(F32), 0.0)).astype(BF)
 
 
-def project_rows(masks, side, state, c, cum, inside, gate, gain, w, out):
+def project_rows(masks, side, state, c, cum, inside, gate, gain, w, *outs):
     y = lax.axis_index("y")
     rows = [row_at(2 * other_index(y, mask) + side, ROWS) for mask in masks]
 
@@ -320,17 +330,25 @@
         squares = squares + gated * gated
         left.append((gated * gain[:, cols]).astype(BF))
     left = jnp.concatenate(left, axis=1)
+    sums = square_cols(jnp.broadcast_to(jnp.sum(squares, axis=1, keepdims=True), squares.shape))
     for n in range(10):
-        part = jnp.dot(left, w[:, 256 * n : 256 * n + 256], preferred_element_type=F32)
-        out[:, 256 * n : 256 * n + 256] = part.astype(out.dtype)
-    out[:, MODEL:] = square_cols(jnp.broadcast_to(jnp.sum(squares, axis=1, keepdims=True), squares.shape)).astype(out.dtype)
-
-
-def send_kernel(e0, e1, e2, e3, c, cum, inside, gate, gain, w, state, out):
+        cols = slice(256 * n, 256 * n + 256)
+        part = jnp.dot(left, w[:, cols], preferred_element_type=F32)
+        first = 0
+        for out in outs:
+            out[:, cols] = part[first : first + out.shape[0]].astype(out.dtype)
+            first += out.shape[0]
+    first = 0
+    for out in outs:
+        out[:, MODEL:] = sums[first : first + out.shape[0]].astype(out.dtype)
+        first += out.shape[0]
+
+
+def send_kernel(e0, e1, e2, e3, c, cum, inside, gate, gain, w, state, out, out_rest):
     x = lax.axis_index("x")
     for d, piece in zip(MASKS, (e0, e1, e2, e3)):
         state[row_at(other_index(x, d), 32), :] = piece[...]
-    project_rows(FIRST + REST, 1 - lax.axis_index("c"), state, c, cum, inside, gate, gain, w, out)
+    project_rows(FIRST + REST, 1 - lax.axis_index("c"), state, c, cum, inside, gate, gain, w, out, out_rest)
 
 
 def keep_first_kernel(state, c, cum, inside, gate, gain, w, out):
@@ -342,10 +360,9 @@
 
 
 def pair_kernel(own, came, *outs):
-    skip = came.shape[0] - own.shape[0] if len(outs) > 1 else 0
     for k, out in enumerate(outs):
-        mine, theirs = slice(ROWS * k, ROWS * k + ROWS), slice(skip + ROWS * k, skip + ROWS * k + ROWS)
-        total = own[mine, :] + came[theirs, :].astype(F32)
+        rows = slice(ROWS * k, ROWS * k + ROWS)
+        total = own[rows, :] + came[rows, :].astype(F32)
         out[:, :MODEL] = total[:, :MODEL].astype(out.dtype)
         both = jnp.sum(total[:, MODEL:], axis=1, keepdims=True)
         out[:, MODEL:] = square_cols(jnp.broadcast_to(both, (ROWS, 128))).astype(out.dtype)
@@ -373,19 +390,19 @@
         scratch=[((192, MODEL), BF)],
         flops=2 * 192 * MODEL * 1024,
     )
-    everything, pre, tail = call(
+    pre, tail = call(
         project_kernel,
-        [((BLOCK, MODEL), BF), ((BLOCK, PRE), BF), ((8, PRE), BF)],
-        [*near, *far, part, w_both, w_bc, gain],
+        [((BLOCK, PRE), BF), ((8, PRE), BF)],
+        [far[1], far[2], part, w_both, w_bc, gain],
         scratch=[((64, MODEL), BF), ((64, PRE), BF)],
         flops=2 * 64 * MODEL * 1024,
     )
     tail = lax.ppermute(tail, SEQ, [(i, (i + 1) % 32) for i in range(32)])
-    v, b, c, step, cum, weight, factor, main = call(
+    everything, v, b, c, step, cum, weight, factor, main = call(
         prepare_kernel,
-        [((BLOCK, WIDTH), BF), ((BLOCK, STATE), BF), ((BLOCK, STATE), BF), ((BLOCK, 128), F32), ((BLOCK, 128), F32)]
+        [((BLOCK, MODEL), BF), ((BLOCK, WIDTH), BF), ((BLOCK, STATE), BF), ((BLOCK, STATE), BF), ((BLOCK, 128), F32), ((BLOCK, 128), F32)]
         + [((8, 128), F32), ((8, 128), F32), ((STATE, WIDTH), F32)],
-        [pre, everything, w_dt.T, conv_x, conv_bc, dt_bias[None], a_log[None]],
+        [pre, *near, *far, w_dt.T, conv_x, conv_bc, dt_bias[None], a_log[None]],
         scratch=[((BLOCK + 8, PRE), F32), ((8, 128), F32), ((128, MODEL), BF)],
         flops=2 * BLOCK * STATE * WIDTH,
     )
@@ -420,13 +437,18 @@
     states = exchanged([e0, e1, e2, e3], "x", MASKS)
     shared = [c_all, cum, inside, gate, gain, w_out]
     flops = 2 * 96 * WIDTH * MODEL
-    state, send = call(send_kernel, [((STATE, WIDTH), BF), ((128, WIDE), BF)], [*states, *shared], flops=flops)
+    state, send, send_rest = call(
+        send_kernel, [((STATE, WIDTH), BF), ((ROWS, WIDE), BF), ((96, WIDE), BF)], [*states, *shared], flops=flops
+    )
     came = swapped(send, "c", 1)
+    came_rest = swapped(send_rest, "c", 1)
     (own,) = call(keep_first_kernel, [((ROWS, WIDE), F32)], [state, *shared], flops=flops)
     (first,) = call(pair_kernel, [((ROWS, WIDE), BF)], [own, came])
     arrived = swapped(first, "y", FIRST[0])
     (own,) = call(keep_rest_kernel, [((96, WIDE), F32)], [state, *shared, first], flops=flops)
-    one, three, here = call(pair_kernel, [((ROWS, WIDE), BF), ((ROWS, WIDE), BF), ((ROWS, WIDE), F32)], [own, came])
+    one, three, here = call(
+        pair_kernel, [((ROWS, WIDE), BF), ((ROWS, WIDE), BF), ((ROWS, WIDE), F32)], [own, came_rest]
+    )
     (out,) = call(
         finish_kernel, [((ROWS, MODEL), BF)], [here, arrived, swapped(one, "y", REST[0]), swapped(three, "y", REST[1])]
     )

time: 73.5 us -> 71.8 us (0.977)
  waiting for transfers between devices: 28.6 us -> 27.1 us
    ppermute x20 -> x21, waiting for transfers between devices: 22.9 us -> 21.5 us  [swapped(): lax.ppermute(value, axis, [(i, i ^ mask) for i in range(lax.axis_size(axi...]
    ppermute x20 -> x21, starting transfers between devices: 28.9 us -> 28.7 us  [swapped(): lax.ppermute(value, axis, [(i, i ^ mask) for i in range(lax.axis_size(axi...]
  transfers between devices with their start and end apart: 21 -> 22, of which waited for: 12 -> 11; matrix products, arithmetic and copies ran while one was open for 6% -> 6% of each run, Pallas kernels for 8% -> 10%
where the time goes in v10:
time: 71.8 us; the launch traced here: 71.7 us
  starting transfers between devices  29.4 us (41%)
  waiting for transfers between devices  27.1 us (38%)
  Pallas kernels  10.7 us (15%)
  local copies, waits for them, and re-layouts  4.15 us (6%)
    ppermute x21, starting transfers between devices, swapped(): lax.ppermute(value, axis, [(i, i ^ mask) for i in range(lax.axis_size(axi...  28.7 us
    ppermute x21, waiting for transfers between devices, swapped(): lax.ppermute(value, axis, [(i, i ^ mask) for i in range(lax.axis_size(axi...  21.5 us
    pallas_call x17, Pallas kernels, call(): pl.pallas_call(body, out_shape=[jax.ShapeDtypeStruct(s, t) for s, t in ou...  10.7 us
    ppermute x1, waiting for transfers between devices, body(): tail = lax.ppermute(tail, SEQ, [(i, (i + 1) % 32) for i in range(32)])  5.63 us
    unnamed x19, local copies, waits for them, and re-layouts  4.14 us
  transfers between devices with their start and end apart: 22, of which 11 were waited for; matrix products, arithmetic and copies ran while one was open for 6% of the time, Pallas kernels for 10%

profile of v10, /device:TPU:1, one launch (start us, length us, event | category | flops | bytes accessed | tf_op | source)
XLA Modules:
  0.0 71.7 jit_solution(12172533784082669936)
XLA Ops:
  0.0 3.7 %collective-permute-start.4 = (bf16[32,2560]{1,0:T(8,128)(2,1)}, bf16[32,2560]{1,0:T(8,128)(2,1)S(1)}, u32[]{:S(2)}, u32[]{:S(2)}) collective-permute-start(bf16[32,2560]{1,0:T(8,128)(2,1)} %t0.3), channel_id=1, source_target_pairs={{0,4},{2,6},{4,0},{6,2},{1,5},{3,7},{5,1},{7,3},{8,12},{10,14},{12... | collective-permute-start | bytes 491528 | tf_op jit(solution)/shard_map/ppermute | solution.py:46
  4.5 2.2 %collective-permute-start.5 = (bf16[32,2560]{1,0:T(8,128)(2,1)}, bf16[32,2560]{1,0:T(8,128)(2,1)S(1)}, u32[]{:S(2)}, u32[]{:S(2)}) collective-permute-start(bf16[32,2560]{1,0:T(8,128)(2,1)} %t0.3), channel_id=1, source_target_pairs={{0,1},{1,0},{2,3},{3,2},{4,5},{5,4},{6,7},{7,6},{8,9},{9,8},{10,11... | collective-permute-start | bytes 491528 | tf_op jit(solution)/shard_map/ppermute | solution.py:46
  6.7 4.1 %copy.11 = bf16[320,8,2,640]{3,1,2,0:T(8,128)(2,1)S(1)} copy(bf16[320,8,2,640]{3,2,1,0:T(2,128)(2,1)} %bitcast.11) | data formatting | bytes 13107200
  11.1 1.7 %collective-permute-done.2.t2 = bf16[32,2560]{1,0:T(8,128)(2,1)S(1)} collective-permute-done((bf16[32,2560]{1,0:T(8,128)(2,1)}, bf16[32,2560]{1,0:T(8,128)(2,1)S(1)}, u32[]{:S(2)}, u32[]{:S(2)}) %collective-permute-start.2) | collective-permute-done | bytes 163872 | tf_op jit(solution)/shard_map/ppermute | solution.py:46
  13.6 1.2 %shard_map.100.part = bf16[192,896]{1,0:T(8,128)(2,1)S(1)} custom-call(bf16[32,2560]{1,0:T(8,128)(2,1)S(1)} %copy-done.2, bf16[32,2560]{1,0:T(8,128)(2,1)S(1)} %collective-permute-done.t1, bf16[32,2560]{1,0:T(8,128)(2,1)S(1)} %collective-permute-done.2.t2, bf16[32,2560]{1,0:T(8,128)(2,1)S(1)} %collective-permute-done.4.t3, ...), custom_call_target="tpu_custom_call" | custom-call | flops 1006632960 | bytes 2013265 | tf_op jit(solution)/shard_map/pallas_call | solution.py:34
  16.5 2.0 %shard_map.103 = (bf16[256,2560]{1,0:T(8,128)(2,1)S(1)}, bf16[256,640]{1,0:T(8,128)(2,1)S(1)}, bf16[256,128]{1,0:T(8,128)(2,1)S(1)}, bf16[256,128]{1,0:T(8,128)(...) custom-call(bf16[256,896]{1,0:T(8,128)(2,1)S(1)} %get-tuple-element., ...), custom_call_target="tpu_custom_call" | custom-call | flops 41943040 | bytes 83886 | tf_op jit(solution)/shard_map/pallas_call | solution.py:34
  18.5 5.6 %collective-permute-done.7.tail = bf16[8,896]{1,0:T(8,128)(2,1)S(1)} collective-permute-done((bf16[8,896]{1,0:T(8,128)(2,1)S(1)}, bf16[8,896]{1,0:T(8,128)(2,1)S(1)}, u32[]{:S(2)}, u32[]{:S(2)}) %collective-permute-start.7) | collective-permute-done | bytes 14368 | tf_op jit(solution)/shard_map/ppermute | solution.py:400
  24.6 3.1 %collective-permute-start.10 = (bf16[168,128]{1,0:T(8,128)(2,1)S(1)}, bf16[168,128]{1,0:T(8,128)(2,1)S(1)}, u32[]{:S(2)}, u32[]{:S(2)}) collective-permute-start(bf16[168,128]{1,0:T(8,128)(2,1)S(1)} %get-tuple-element.47), channel_id=1, source_target_pairs={{0,24},{8,16},{16,8},{24,0},{1,25},{9,17},{17,9},{25,1},{2,26},{10... | collective-permute-start | bytes 129032 | tf_op jit(solution)/shard_map/ppermute | solution.py:46
  27.8 1.2 %shard_map.106.before_too.gate = f32[256,640]{1,0:T(8,128)S(1)} custom-call(bf16[256,2560]{1,0:T(8,128)(2,1)S(1)} %get-tuple-element.57.tokens, bf16[2560,1280]{1,0:T(8,128)(2,1)S(1)} %bitcast.7, bf16[8,640]{1,0:T(8,128)(2,1)S(1)} %get-tuple-element.51.v_first.before), custom_call_target="tpu_custom_call" | custom-call | flops 838860800 | bytes 1677721 | tf_op jit(solution)/shard_map/pallas_call | solution.py:34
  29.0 1.0 %shard_map.105 = (f32[256,640]{1,0:T(8,128)S(1)}, bf16[256,128]{1,0:T(8,128)(2,1)S(1)}) custom-call(bf16[256,640]{1,0:T(8,128)(2,1)S(1)} %get-tuple-element.48.v, bf16[256,128]{1,0:T(8,128)(2,1)S(1)} %get-tuple-element.49.b, bf16[256,128]{1,0:T(8,128)(2,1)S(1)} %get-tuple-element.50.c, bf16[8,640]{1,0:T(8,128)(2,1)S(1)} %get-tuple-element.51.v_first.before, ...), custom_call_target="tpu_custom_call" | custom-call | flops 335544320 | bytes 671088 | tf_op jit(solution)/shard_map/pallas_call | solution.py:34
  30.3 2.9 %collective-permute-done.11.other = bf16[168,128]{1,0:T(8,128)(2,1)S(1)} collective-permute-done((bf16[168,128]{1,0:T(8,128)(2,1)S(1)}, bf16[168,128]{1,0:T(8,128)(2,1)S(1)}, u32[]{:S(2)}, u32[]{:S(2)}) %collective-permute-start.11) | collective-permute-done | bytes 43040 | tf_op jit(solution)/shard_map/ppermute | solution.py:46
  34.1 3.2 %collective-permute-done.12.previous = bf16[168,128]{1,0:T(8,128)(2,1)S(1)} collective-permute-done((bf16[168,128]{1,0:T(8,128)(2,1)S(1)}, bf16[168,128]{1,0:T(8,128)(2,1)S(1)}, u32[]{:S(2)}, u32[]{:S(2)}) %collective-permute-start.12) | collective-permute-done | bytes 43040 | tf_op jit(solution)/shard_map/ppermute | solution.py:46
  37.4 1.3 %collective-permute-start.13 = (bf16[168,128]{1,0:T(8,128)(2,1)S(1)}, bf16[168,128]{1,0:T(8,128)(2,1)S(1)}, u32[]{:S(2)}, u32[]{:S(2)}) collective-permute-start(bf16[168,128]{1,0:T(8,128)(2,1)S(1)} %shard_map.109), channel_id=1, source_target_pairs={{0,224},{32,192},{64,160},{96,128},{128,96},{160,64},{192,32},{224... | collective-permute-start | bytes 129032 | tf_op jit(solution)/shard_map/ppermute | solution.py:46
  38.7 2.9 %collective-permute-done.13.quad = bf16[168,128]{1,0:T(8,128)(2,1)S(1)} collective-permute-done((bf16[168,128]{1,0:T(8,128)(2,1)S(1)}, bf16[168,128]{1,0:T(8,128)(2,1)S(1)}, u32[]{:S(2)}, u32[]{:S(2)}) %collective-permute-start.13) | collective-permute-done | bytes 43040 | tf_op jit(solution)/shard_map/ppermute | solution.py:46
  42.4 2.0 %collective-permute-start.15 = (bf16[32,640]{1,0:T(8,128)(2,1)S(1)}, bf16[32,640]{1,0:T(8,128)(2,1)S(1)}, u32[]{:S(2)}, u32[]{:S(2)}) collective-permute-start(bf16[32,640]{1,0:T(8,128)(2,1)S(1)} %get-tuple-element.60), channel_id=1, source_target_pairs={{0,8},{8,0},{16,24},{24,16},{1,9},{9,1},{17,25},{25,17},{2,10},{10... | collective-permute-start | bytes 122888 | tf_op jit(solution)/shard_map/ppermute | solution.py:46
  45.2 1.1 %collective-permute-done.14.e1 = bf16[32,640]{1,0:T(8,128)(2,1)S(1)} collective-permute-done((bf16[32,640]{1,0:T(8,128)(2,1)S(1)}, bf16[32,640]{1,0:T(8,128)(2,1)S(1)}, u32[]{:S(2)}, u32[]{:S(2)}) %collective-permute-start.14) | collective-permute-done | bytes 40992 | tf_op jit(solution)/shard_map/ppermute | solution.py:46
  46.3 2.2 %collective-permute-done.16.e3 = bf16[32,640]{1,0:T(8,128)(2,1)S(1)} collective-permute-done((bf16[32,640]{1,0:T(8,128)(2,1)S(1)}, bf16[32,640]{1,0:T(8,128)(2,1)S(1)}, u32[]{:S(2)}, u32[]{:S(2)}) %collective-permute-start.16) | collective-permute-done | bytes 40992 | tf_op jit(solution)/shard_map/ppermute | solution.py:46
  48.5 1.0 %shard_map.111 = (bf16[128,640]{1,0:T(8,128)(2,1)S(1)}, bf16[32,2688]{1,0:T(8,128)(2,1)S(1)}, bf16[96,2688]{1,0:T(8,128)(2,1)S(1)}) custom-call(bf16[32,640]{1,0:T(8,128)(2,1)S(1)} %get-tuple-element.58.e0, bf16[32,640]{1,0:T(8,128)(2,1)S(1)} %collective-permute-done.14.e1, bf16[32,640]{1,0:T(8,128)(2,1)S(1)} %collective-permute-done.15.e2, ...), custom_call_target="tpu_custom_call" | custom-call | flops 314572800 | bytes 629145 | tf_op jit(solution)/shard_map/pallas_call | solution.py:34
  49.5 7.9 %collective-permute-start.18 = (bf16[96,2688]{1,0:T(8,128)(2,1)S(1)}, bf16[96,2688]{1,0:T(8,128)(2,1)S(1)}, u32[]{:S(2)}, u32[]{:S(2)}) collective-permute-start(bf16[96,2688]{1,0:T(8,128)(2,1)S(1)} %get-tuple-element.65), channel_id=1, source_target_pairs={{0,1},{1,0},{2,3},{3,2},{4,5},{5,4},{6,7},{7,6},{8,9},{9,8},{10,11... | collective-permute-start | bytes 1548296 | tf_op jit(solution)/shard_map/ppermute | solution.py:46
  59.2 2.8 %collective-permute-start.19 = (bf16[32,2688]{1,0:T(8,128)(2,1)S(1)}, bf16[32,2688]{1,0:T(8,128)(2,1)S(1)}, u32[]{:S(2)}, u32[]{:S(2)}) collective-permute-start(bf16[32,2688]{1,0:T(8,128)(2,1)S(1)} %shard_map.113.before), channel_id=1, source_target_pairs={{0,4},{2,6},{4,0},{6,2},{1,5},{3,7},{5,1},{7,3},{8,12},{10,14},{12... | collective-permute-start | bytes 516104 | tf_op jit(solution)/shard_map/ppermute | solution.py:46
  62.0 0.9 %shard_map.114.own = f32[96,2688]{1,0:T(8,128)S(1)} custom-call(bf16[128,640]{1,0:T(8,128)(2,1)S(1)} %get-tuple-element.63.state, bf16[256,128]{1,0:T(8,128)(2,1)S(1)} %get-tuple-element.62.c, f32[256,128]{1,0:T(8,128)S(1)} %get-tuple-element.55.cum, f32[256,640]{1,0:T(8,128)S(1)} %get-tuple-element.56.before.inside, ...), custom_call_target="tpu_custom_call" | custom-call | flops 314572800 | bytes 629145 | tf_op jit(solution)/shard_map/pallas_call | solution.py:34
  63.0 1.2 %collective-permute-start.20 = (bf16[32,2688]{1,0:T(8,128)(2,1)S(1)}, bf16[32,2688]{1,0:T(8,128)(2,1)S(1)}, u32[]{:S(2)}, u32[]{:S(2)}) collective-permute-start(bf16[32,2688]{1,0:T(8,128)(2,1)S(1)} %get-tuple-element.67), channel_id=1, source_target_pairs={{0,2},{2,0},{4,6},{6,4},{1,3},{3,1},{5,7},{7,5},{8,10},{10,8},{12,... | collective-permute-start | bytes 516104 | tf_op jit(solution)/shard_map/ppermute | solution.py:46
  64.4 1.9 %collective-permute-done.19.g1 = bf16[32,2688]{1,0:T(8,128)(2,1)S(1)} collective-permute-done((bf16[32,2688]{1,0:T(8,128)(2,1)S(1)}, bf16[32,2688]{1,0:T(8,128)(2,1)S(1)}, u32[]{:S(2)}, u32[]{:S(2)}) %collective-permute-start.19) | collective-permute-done | bytes 172064 | tf_op jit(solution)/shard_map/ppermute | solution.py:46
  66.3 4.6 %collective-permute-done.20.g2 = bf16[32,2688]{1,0:T(8,128)(2,1)S(1)} collective-permute-done((bf16[32,2688]{1,0:T(8,128)(2,1)S(1)}, bf16[32,2688]{1,0:T(8,128)(2,1)S(1)}, u32[]{:S(2)}, u32[]{:S(2)}) %collective-permute-start.20) | collective-permute-done | bytes 172064 | tf_op jit(solution)/shard_map/ppermute | solution.py:46
  (57 shorter events, 9.7 us)
Async XLA Ops:
  0.0 10.8 %collective-permute-start.4 = (bf16[32,2560]{1,0:T(8,128)(2,1)}, bf16[32,2560]{1,0:T(8,128)(2,1)S(1)}, u32[]{:S(2)}, u32[]{:S(2)}) collective-permute-start(bf16[32,2560]{1,0:T(8,128)(2,1)} %t0.3), channel_id=1, source_target_pairs={{0,4},{2,6},{4,0},{6,2},{1,5},{3,7},{5,1},{7,3},{8,12},{10,14},{12... | collective-permute-start | bytes 491528 | tf_op jit(solution)/shard_map/ppermute | solution.py:46
  3.7 9.0 %collective-permute-start.2 = (bf16[32,2560]{1,0:T(8,128)(2,1)}, bf16[32,2560]{1,0:T(8,128)(2,1)S(1)}, u32[]{:S(2)}, u32[]{:S(2)}) collective-permute-start(bf16[32,2560]{1,0:T(8,128)(2,1)} %t0.3), channel_id=1, source_target_pairs={{0,6},{2,4},{4,2},{6,0},{1,7},{3,5},{5,3},{7,1},{8,14},{10,12},{12... | collective-permute-start | bytes 491528 | tf_op jit(solution)/shard_map/ppermute | solution.py:46
  4.5 9.0 %collective-permute-start = (bf16[32,2560]{1,0:T(8,128)(2,1)}, bf16[32,2560]{1,0:T(8,128)(2,1)S(1)}, u32[]{:S(2)}, u32[]{:S(2)}) collective-permute-start(bf16[32,2560]{1,0:T(8,128)(2,1)} %t0.3), channel_id=1, source_target_pairs={{0,2},{2,0},{4,6},{6,4},{1,3},{3,1},{5,7},{7,5},{8,10},{10,8},{12,... | collective-permute-start | bytes 491528 | tf_op jit(solution)/shard_map/ppermute | solution.py:46
  4.5 9.1 %collective-permute-start.5 = (bf16[32,2560]{1,0:T(8,128)(2,1)}, bf16[32,2560]{1,0:T(8,128)(2,1)S(1)}, u32[]{:S(2)}, u32[]{:S(2)}) collective-permute-start(bf16[32,2560]{1,0:T(8,128)(2,1)} %t0.3), channel_id=1, source_target_pairs={{0,1},{1,0},{2,3},{3,2},{4,5},{5,4},{6,7},{7,6},{8,9},{9,8},{10,11... | collective-permute-start | bytes 491528 | tf_op jit(solution)/shard_map/ppermute | solution.py:46
  6.7 6.9 %copy-start.2 = (bf16[32,2560]{1,0:T(8,128)(2,1)S(1)}, bf16[32,2560]{1,0:T(8,128)(2,1)}, u32[]{:S(2)}) copy-start(bf16[32,2560]{1,0:T(8,128)(2,1)} %t0.3) | copy-start | bytes 491524
  10.8 2.8 %collective-permute-start.6 = (bf16[32,2560]{1,0:T(8,128)(2,1)S(1)}, bf16[32,2560]{1,0:T(8,128)(2,1)S(1)}, u32[]{:S(2)}, u32[]{:S(2)}) collective-permute-start(bf16[32,2560]{1,0:T(8,128)(2,1)S(1)} %collective-permute-done.4.t3), channel_id=1, source_target_pairs={{0,1},{1,0},{2,3},{3,2},{4,5},{5,4},{6,7},{7,6},{8,9},{9,8},{10,11... | collective-permute-start | bytes 491528 | tf_op jit(solution)/shard_map/ppermute | solution.py:46
  12.8 2.1 %collective-permute-start.3 = (bf16[32,2560]{1,0:T(8,128)(2,1)S(1)}, bf16[32,2560]{1,0:T(8,128)(2,1)S(1)}, u32[]{:S(2)}, u32[]{:S(2)}) collective-permute-start(bf16[32,2560]{1,0:T(8,128)(2,1)S(1)} %collective-permute-done.2.t2), channel_id=1, source_target_pairs={{0,1},{1,0},{2,3},{3,2},{4,5},{5,4},{6,7},{7,6},{8,9},{9,8},{10,11... | collective-permute-start | bytes 491528 | tf_op jit(solution)/shard_map/ppermute | solution.py:46
  13.5 1.4 %collective-permute-start.1 = (bf16[32,2560]{1,0:T(8,128)(2,1)S(1)}, bf16[32,2560]{1,0:T(8,128)(2,1)S(1)}, u32[]{:S(2)}, u32[]{:S(2)}) collective-permute-start(bf16[32,2560]{1,0:T(8,128)(2,1)S(1)} %collective-permute-done.t1), channel_id=1, source_target_pairs={{0,1},{1,0},{2,3},{3,2},{4,5},{5,4},{6,7},{7,6},{8,9},{9,8},{10,11... | collective-permute-start | bytes 491528 | tf_op jit(solution)/shard_map/ppermute | solution.py:46
  15.7 8.4 %collective-permute-start.7 = (bf16[8,896]{1,0:T(8,128)(2,1)S(1)}, bf16[8,896]{1,0:T(8,128)(2,1)S(1)}, u32[]{:S(2)}, u32[]{:S(2)}) collective-permute-start(bf16[8,896]{1,0:T(8,128)(2,1)S(1)} %get-tuple-element.39), channel_id=1, source_target_pairs={{0,8},{8,16},{16,24},{24,32},{32,40},{40,48},{48,56},{56,64},{64,7... | collective-permute-start | bytes 43016 | tf_op jit(solution)/shard_map/ppermute | solution.py:400
  24.4 5.6 %collective-permute-start.8 = (bf16[168,128]{1,0:T(8,128)(2,1)S(1)}, bf16[168,128]{1,0:T(8,128)(2,1)S(1)}, u32[]{:S(2)}, u32[]{:S(2)}) collective-permute-start(bf16[168,128]{1,0:T(8,128)(2,1)S(1)} %get-tuple-element.45), channel_id=1, source_target_pairs={{0,16},{8,24},{16,0},{24,8},{1,17},{9,25},{17,1},{25,9},{2,18},{10... | collective-permute-start | bytes 129032 | tf_op jit(solution)/shard_map/ppermute | solution.py:46
  24.5 5.5 %collective-permute-start.9 = (bf16[168,128]{1,0:T(8,128)(2,1)S(1)}, bf16[168,128]{1,0:T(8,128)(2,1)S(1)}, u32[]{:S(2)}, u32[]{:S(2)}) collective-permute-start(bf16[168,128]{1,0:T(8,128)(2,1)S(1)} %get-tuple-element.46), channel_id=1, source_target_pairs={{0,8},{8,0},{16,24},{24,16},{1,9},{9,1},{17,25},{25,17},{2,10},{10... | collective-permute-start | bytes 129032 | tf_op jit(solution)/shard_map/ppermute | solution.py:46
  24.6 5.4 %collective-permute-start.10 = (bf16[168,128]{1,0:T(8,128)(2,1)S(1)}, bf16[168,128]{1,0:T(8,128)(2,1)S(1)}, u32[]{:S(2)}, u32[]{:S(2)}) collective-permute-start(bf16[168,128]{1,0:T(8,128)(2,1)S(1)} %get-tuple-element.47), channel_id=1, source_target_pairs={{0,24},{8,16},{16,8},{24,0},{1,25},{9,17},{17,9},{25,1},{2,26},{10... | collective-permute-start | bytes 129032 | tf_op jit(solution)/shard_map/ppermute | solution.py:46
  29.0 19.5 %copy-start = (bf16[640,2560]{1,0:T(8,128)(2,1)S(1)}, bf16[640,2560]{1,0:T(8,128)(2,1)}, u32[]{:S(2)}) copy-start(bf16[640,2560]{1,0:T(8,128)(2,1)} %w.5) | copy-start | bytes 9830404
  30.2 3.0 %collective-permute-start.11 = (bf16[168,128]{1,0:T(8,128)(2,1)S(1)}, bf16[168,128]{1,0:T(8,128)(2,1)S(1)}, u32[]{:S(2)}, u32[]{:S(2)}) collective-permute-start(bf16[168,128]{1,0:T(8,128)(2,1)S(1)} %shard_map.107.row), channel_id=1, source_target_pairs={{0,32},{32,0},{64,96},{96,64},{128,160},{160,128},{192,224},{224,1... | collective-permute-start | bytes 129032 | tf_op jit(solution)/shard_map/ppermute | solution.py:46
  33.3 4.0 %collective-permute-start.12 = (bf16[168,128]{1,0:T(8,128)(2,1)S(1)}, bf16[168,128]{1,0:T(8,128)(2,1)S(1)}, u32[]{:S(2)}, u32[]{:S(2)}) collective-permute-start(bf16[168,128]{1,0:T(8,128)(2,1)S(1)} %shard_map.108), channel_id=1, source_target_pairs={{0,64},{32,96},{64,0},{96,32},{128,192},{160,224},{192,128},{224,1... | collective-permute-start | bytes 129032 | tf_op jit(solution)/shard_map/ppermute | solution.py:46
  37.4 4.2 %collective-permute-start.13 = (bf16[168,128]{1,0:T(8,128)(2,1)S(1)}, bf16[168,128]{1,0:T(8,128)(2,1)S(1)}, u32[]{:S(2)}, u32[]{:S(2)}) collective-permute-start(bf16[168,128]{1,0:T(8,128)(2,1)S(1)} %shard_map.109), channel_id=1, source_target_pairs={{0,224},{32,192},{64,160},{96,128},{128,96},{160,64},{192,32},{224... | collective-permute-start | bytes 129032 | tf_op jit(solution)/shard_map/ppermute | solution.py:46
  41.8 4.4 %collective-permute-start.14 = (bf16[32,640]{1,0:T(8,128)(2,1)S(1)}, bf16[32,640]{1,0:T(8,128)(2,1)S(1)}, u32[]{:S(2)}, u32[]{:S(2)}) collective-permute-start(bf16[32,640]{1,0:T(8,128)(2,1)S(1)} %get-tuple-element.59), channel_id=1, source_target_pairs={{0,16},{8,24},{16,0},{24,8},{1,17},{9,25},{17,1},{25,9},{2,18},{10... | collective-permute-start | bytes 122888 | tf_op jit(solution)/shard_map/ppermute | solution.py:46
  42.4 3.9 %collective-permute-start.15 = (bf16[32,640]{1,0:T(8,128)(2,1)S(1)}, bf16[32,640]{1,0:T(8,128)(2,1)S(1)}, u32[]{:S(2)}, u32[]{:S(2)}) collective-permute-start(bf16[32,640]{1,0:T(8,128)(2,1)S(1)} %get-tuple-element.60), channel_id=1, source_target_pairs={{0,8},{8,0},{16,24},{24,16},{1,9},{9,1},{17,25},{25,17},{2,10},{10... | collective-permute-start | bytes 122888 | tf_op jit(solution)/shard_map/ppermute | solution.py:46
  44.5 4.1 %collective-permute-start.16 = (bf16[32,640]{1,0:T(8,128)(2,1)S(1)}, bf16[32,640]{1,0:T(8,128)(2,1)S(1)}, u32[]{:S(2)}, u32[]{:S(2)}) collective-permute-start(bf16[32,640]{1,0:T(8,128)(2,1)S(1)} %get-tuple-element.61), channel_id=1, source_target_pairs={{0,24},{8,16},{16,8},{24,0},{1,25},{9,17},{17,9},{25,1},{2,26},{10... | collective-permute-start | bytes 122888 | tf_op jit(solution)/shard_map/ppermute | solution.py:46
  49.5 13.4 %collective-permute-start.18 = (bf16[96,2688]{1,0:T(8,128)(2,1)S(1)}, bf16[96,2688]{1,0:T(8,128)(2,1)S(1)}, u32[]{:S(2)}, u32[]{:S(2)}) collective-permute-start(bf16[96,2688]{1,0:T(8,128)(2,1)S(1)} %get-tuple-element.65), channel_id=1, source_target_pairs={{0,1},{1,0},{2,3},{3,2},{4,5},{5,4},{6,7},{7,6},{8,9},{9,8},{10,11... | collective-permute-start | bytes 1548296 | tf_op jit(solution)/shard_map/ppermute | solution.py:46
  57.3 1.8 %collective-permute-start.17 = (bf16[32,2688]{1,0:T(8,128)(2,1)S(1)}, bf16[32,2688]{1,0:T(8,128)(2,1)S(1)}, u32[]{:S(2)}, u32[]{:S(2)}) collective-permute-start(bf16[32,2688]{1,0:T(8,128)(2,1)S(1)} %get-tuple-element.64), channel_id=1, source_target_pairs={{0,1},{1,0},{2,3},{3,2},{4,5},{5,4},{6,7},{7,6},{8,9},{9,8},{10,11... | collective-permute-start | bytes 516104 | tf_op jit(solution)/shard_map/ppermute | solution.py:46
  59.2 7.1 %collective-permute-start.19 = (bf16[32,2688]{1,0:T(8,128)(2,1)S(1)}, bf16[32,2688]{1,0:T(8,128)(2,1)S(1)}, u32[]{:S(2)}, u32[]{:S(2)}) collective-permute-start(bf16[32,2688]{1,0:T(8,128)(2,1)S(1)} %shard_map.113.before), channel_id=1, source_target_pairs={{0,4},{2,6},{4,0},{6,2},{1,5},{3,7},{5,1},{7,3},{8,12},{10,14},{12... | collective-permute-start | bytes 516104 | tf_op jit(solution)/shard_map/ppermute | solution.py:46
  63.0 7.9 %collective-permute-start.20 = (bf16[32,2688]{1,0:T(8,128)(2,1)S(1)}, bf16[32,2688]{1,0:T(8,128)(2,1)S(1)}, u32[]{:S(2)}, u32[]{:S(2)}) collective-permute-start(bf16[32,2688]{1,0:T(8,128)(2,1)S(1)} %get-tuple-element.67), channel_id=1, source_target_pairs={{0,2},{2,0},{4,6},{6,4},{1,3},{3,1},{5,7},{7,5},{8,10},{10,8},{12,... | collective-permute-start | bytes 516104 | tf_op jit(solution)/shard_map/ppermute | solution.py:46
  64.2 6.7 %collective-permute-start.21 = (bf16[32,2688]{1,0:T(8,128)(2,1)S(1)}, bf16[32,2688]{1,0:T(8,128)(2,1)S(1)}, u32[]{:S(2)}, u32[]{:S(2)}) collective-permute-start(bf16[32,2688]{1,0:T(8,128)(2,1)S(1)} %get-tuple-element.68), channel_id=1, source_target_pairs={{0,6},{2,4},{4,2},{6,0},{1,7},{3,5},{5,3},{7,1},{8,14},{10,12},{12... | collective-permute-start | bytes 516104 | tf_op jit(solution)/shard_map/ppermute | solution.py:46
  (7 other events, 22.0 us)

commit v11 on v10

--- a/solution.py
+++ b/solution.py
@@ -68,20 +68,22 @@
     out[:, WIDTH:] = jnp.dot(tokens[...], w_bc[...], preferred_element_type=F32).astype(BF)
 
 
-def project_early_kernel(t0, t1, t2, t3, o0, o3, w, w_bc, out, tokens):
-    for k, piece in enumerate((t0, t1, t2, t3, o0, o3)):
+def project_three_kernel(a, b, c, w, w_bc, out, tokens):
+    for k, piece in enumerate((a, b, c)):
         tokens[32 * k : 32 * k + 32, :] = piece[...]
     project_into(tokens, w, w_bc, out)
 
 
-def project_kernel(o1, o2, part, w, w_bc, early, pre_out, tail_out, late, rest):
+def project_kernel(o1, o2, part_zero, part, w, w_bc, early, pre_out, tail_out, late, rest):
     y, c = lax.axis_index("y"), lax.axis_index("c")
     near = [row_at(other_index(y, mask) * 2 + c, ROWS) for mask in TOKEN_MASKS]
     far = [row_at(other_index(y, mask) * 2 + 1 - c, ROWS) for mask in TOKEN_MASKS]
     late[0:32, :] = o1[...]
     late[32:64, :] = o2[...]
     project_into(late, w, w_bc, rest)
-    for k, rows in enumerate(near + [far[0], far[3]]):
+    for k, rows in enumerate((near[0], near[3], far[0])):
+        pre_out[rows, :] = part_zero[32 * k : 32 * k + 32, :]
+    for k, rows in enumerate((near[1], near[2], far[3])):
         pre_out[rows, :] = part[32 * k : 32 * k + 32, :]
     for k, rows in enumerate(far[1:3]):
         pre_out[rows, :] = rest[32 * k : 32 * k + 32, :]
@@ -279,7 +281,7 @@
     return odd, theirs, follow(choose(odd, theirs, mine), choose(odd, mine, theirs))
 
 
-def pair_total_kernel(row, other, out):
+def pair_total_kernel(row, other, before, out):
     pack(out, two_rows(row, other)[2])
 
 
@@ -312,21 +314,29 @@
     return jnp.where(lane == 0, high.astype(F32), jnp.where(lane == 1, low.astype(F32), 0.0)).astype(BF)
 
 
-def project_rows(masks, side, state, c, cum, inside, gate, gain, w, *outs):
-    y = lax.axis_index("y")
-    rows = [row_at(2 * other_index(y, mask) + side, ROWS) for mask in masks]
-
-    def picked(ref, cols):
-        return jnp.concatenate([ref[r, cols] for r in rows], axis=0)
-
-    states = picked(c, slice(0, STATE))
-    grown = jnp.exp(picked(cum, slice(0, 128)))
-    squares = jnp.zeros(grown.shape, F32)
+def order_kernel(c, cum, inside, gate, c_out, grown_out, inside_out, gate_out):
+    y, core = lax.axis_index("y"), lax.axis_index("c")
+    start = 0
+    for masks in (FIRST, REST):
+        for side, mask in [(side, mask) for side in (1 - core, core) for mask in masks]:
+            source = row_at(2 * other_index(y, mask) + side, ROWS)
+            rows = slice(start, start + 32)
+            start += 32
+            c_out[rows, :] = c[source, :]
+            inside_out[rows, :] = inside[source, :]
+            gate_out[rows, :] = gate[source, :]
+            grown = jnp.exp(cum[source, :])
+            for pair in range(5):
+                grown_out[rows, 128 * pair : 128 * pair + 128] = spread(grown, pair)
+
+
+def project_rows(rows, state, c, grown, inside, gate, gain, w, *outs):
+    squares = jnp.zeros((rows.stop - rows.start, 128), F32)
     left = []
     for pair in range(5):
         cols = slice(128 * pair, 128 * pair + 128)
-        came = jnp.dot(states, state[:, cols], preferred_element_type=F32)
-        gated = (picked(inside, cols) + spread(grown, pair) * came) * picked(gate, cols)
+        came = jnp.dot(c[rows, :], state[:, cols], preferred_element_type=F32)
+        gated = (inside[rows, cols] + grown[rows, cols] * came) * gate[rows, cols]
         squares = squares + gated * gated
         left.append((gated * gain[:, cols]).astype(BF))
     left = jnp.concatenate(left, axis=1)
@@ -344,19 +354,19 @@
         first += out.shape[0]
 
 
-def send_kernel(e0, e1, e2, e3, c, cum, inside, gate, gain, w, state, out, out_rest):
+def first_kernel(e0, e1, e2, e3, c, grown, inside, gate, gain, w, state, send, keep):
     x = lax.axis_index("x")
     for d, piece in zip(MASKS, (e0, e1, e2, e3)):
         state[row_at(other_index(x, d), 32), :] = piece[...]
-    project_rows(FIRST + REST, 1 - lax.axis_index("c"), state, c, cum, inside, gate, gain, w, out, out_rest)
-
-
-def keep_first_kernel(state, c, cum, inside, gate, gain, w, out):
-    project_rows(FIRST, lax.axis_index("c"), state, c, cum, inside, gate, gain, w, out)
-
-
-def keep_rest_kernel(state, c, cum, inside, gate, gain, w, before, out):
-    project_rows(REST, lax.axis_index("c"), state, c, cum, inside, gate, gain, w, out)
+    project_rows(slice(0, 64), state, c, grown, inside, gate, gain, w, send, keep)
+
+
+def send_rest_kernel(state, c, grown, inside, gate, gain, w, out):
+    project_rows(slice(64, 160), state, c, grown, inside, gate, gain, w, out)
+
+
+def keep_rest_kernel(state, c, grown, inside, gate, gain, w, before, out):
+    project_rows(slice(160, 256), state, c, grown, inside, gate, gain, w, out)
 
 
 def pair_kernel(own, came, *outs):
@@ -368,8 +378,12 @@
         out[:, MODEL:] = square_cols(jnp.broadcast_to(both, (ROWS, 128))).astype(out.dtype)
 
 
-def finish_kernel(f0, g1, g2, g3, out):
-    total = f0[...] + g1[...].astype(F32) + g2[...].astype(F32) + g3[...].astype(F32)
+def add_kernel(f0, g1, out):
+    out[...] = f0[...] + g1[...].astype(F32)
+
+
+def finish_kernel(f0, g2, g3, out):
+    total = f0[...] + g2[...].astype(F32) + g3[...].astype(F32)
     squares = jnp.sum(total[:, MODEL:], axis=1, keepdims=True)
     out[...] = (total[:, :MODEL] * lax.rsqrt(squares / DI + 1.0)).astype(BF)
 
@@ -383,17 +397,19 @@
     for mask, piece in zip(TOKEN_MASKS[1:], near[1:]):
         far.append(swapped(piece, "c", 1))
     (gain,) = call(gain_kernel, [((1, WIDTH), F32)], [norm_gain[None]])
-    (part,) = call(
-        project_early_kernel,
-        [((192, PRE), BF)],
-        [*near, far[0], far[3], w_both, w_bc],
-        scratch=[((192, MODEL), BF)],
-        flops=2 * 192 * MODEL * 1024,
-    )
+    parts = []
+    for pieces in ((near[0], near[3], far[0]), (near[1], near[2], far[3])):
+        parts += call(
+            project_three_kernel,
+            [((96, PRE), BF)],
+            [*pieces, w_both, w_bc],
+            scratch=[((96, MODEL), BF)],
+            flops=2 * 96 * MODEL * 1024,
+        )
     pre, tail = call(
         project_kernel,
         [((BLOCK, PRE), BF), ((8, PRE), BF)],
-        [far[1], far[2], part, w_both, w_bc, gain],
+        [far[1], far[2], *parts, w_both, w_bc, gain],
         scratch=[((64, MODEL), BF), ((64, PRE), BF)],
         flops=2 * 64 * MODEL * 1024,
     )
@@ -424,7 +440,12 @@
     piece = [((PIECE, 128), BF)]
     (row,) = call(row_total_kernel, piece, [*rows, inside, gate], scratch=[((4, PIECE, 128), F32)])
     other = swapped(row, "z", 1)
-    (two,) = call(pair_total_kernel, piece, [row, other])
+    c_all, grown, inside, gate = call(
+        order_kernel,
+        [((BLOCK, STATE), BF), ((BLOCK, WIDTH), F32), ((BLOCK, WIDTH), F32), ((BLOCK, WIDTH), F32)],
+        [c_all, cum, inside, gate],
+    )
+    (two,) = call(pair_total_kernel, piece, [row, other, c_all])
     previous = swapped(two, "z", 2)
     (four,) = call(quad_total_kernel, piece, [row, other, previous])
     quad = swapped(four, "z", 7)
@@ -435,22 +456,23 @@
         scratch=[((4, PIECE, 128), F32), ((4, 32, WIDTH), F32)],
     )
     states = exchanged([e0, e1, e2, e3], "x", MASKS)
-    shared = [c_all, cum, inside, gate, gain, w_out]
+    shared = [c_all, grown, inside, gate, gain, w_out]
     flops = 2 * 96 * WIDTH * MODEL
-    state, send, send_rest = call(
-        send_kernel, [((STATE, WIDTH), BF), ((ROWS, WIDE), BF), ((96, WIDE), BF)], [*states, *shared], flops=flops
+    state, send, own = call(
+        first_kernel, [((STATE, WIDTH), BF), ((ROWS, WIDE), BF), ((ROWS, WIDE), F32)], [*states, *shared], flops=flops
     )
     came = swapped(send, "c", 1)
+    (send_rest,) = call(send_rest_kernel, [((96, WIDE), BF)], [state, *shared], flops=flops)
     came_rest = swapped(send_rest, "c", 1)
-    (own,) = call(keep_first_kernel, [((ROWS, WIDE), F32)], [state, *shared], flops=flops)
     (first,) = call(pair_kernel, [((ROWS, WIDE), BF)], [own, came])
     arrived = swapped(first, "y", FIRST[0])
     (own,) = call(keep_rest_kernel, [((96, WIDE), F32)], [state, *shared, first], flops=flops)
     one, three, here = call(
         pair_kernel, [((ROWS, WIDE), BF), ((ROWS, WIDE), BF), ((ROWS, WIDE), F32)], [own, came_rest]
     )
+    (here,) = call(add_kernel, [((ROWS, WIDE), F32)], [here, arrived])
     (out,) = call(
-        finish_kernel, [((ROWS, MODEL), BF)], [here, arrived, swapped(one, "y", REST[0]), swapped(three, "y", REST[1])]
+        finish_kernel, [((ROWS, MODEL), BF)], [here, swapped(one, "y", REST[0]), swapped(three, "y", REST[1])]
     )
     return out
 

time: 71.8 us -> 73 us (1.017)
  Pallas kernels: 10.7 us -> 11.7 us
    pallas_call x17 -> x20, Pallas kernels: 10.7 us -> 11.7 us  [call(): pl.pallas_call(body, out_shape=[jax.ShapeDtypeStruct(s, t) for s, t in ou...]
where the time goes in v11:
time: 73 us; the launch traced here: 72.9 us
  starting transfers between devices  29.4 us (40%)
  waiting for transfers between devices  27.3 us (37%)
  Pallas kernels  11.7 us (16%)
  local copies, waits for them, and re-layouts  4.15 us (6%)
    ppermute x21, starting transfers between devices, swapped(): lax.ppermute(value, axis, [(i, i ^ mask) for i in range(lax.axis_size(axi...  28.7 us
    ppermute x21, waiting for transfers between devices, swapped(): lax.ppermute(value, axis, [(i, i ^ mask) for i in range(lax.axis_size(axi...  21.7 us
    pallas_call x20, Pallas kernels, call(): pl.pallas_call(body, out_shape=[jax.ShapeDtypeStruct(s, t) for s, t in ou...  11.7 us
    ppermute x1, waiting for transfers between devices, body(): tail = lax.ppermute(tail, SEQ, [(i, (i + 1) % 32) for i in range(32)])  5.63 us
    unnamed x19, local copies, waits for them, and re-layouts  4.14 us
  transfers between devices with their start and end apart: 22, of which 11 were waited for; matrix products, arithmetic and copies ran while one was open for 6% of the time, Pallas kernels for 10%

profile of v11, /device:TPU:1, one launch (start us, length us, event | category | flops | bytes accessed | tf_op | source)
XLA Modules:
  0.0 72.9 jit_solution(2748185343384326514)
XLA Ops:
  0.0 3.7 %collective-permute-start.4 = (bf16[32,2560]{1,0:T(8,128)(2,1)}, bf16[32,2560]{1,0:T(8,128)(2,1)S(1)}, u32[]{:S(2)}, u32[]{:S(2)}) collective-permute-start(bf16[32,2560]{1,0:T(8,128)(2,1)} %t0.1), channel_id=1, source_target_pairs={{0,4},{2,6},{4,0},{6,2},{1,5},{3,7},{5,1},{7,3},{8,12},{10,14},{12... | collective-permute-start | bytes 491528 | tf_op jit(solution)/shard_map/ppermute | solution.py:46
  4.5 2.2 %collective-permute-start.5 = (bf16[32,2560]{1,0:T(8,128)(2,1)}, bf16[32,2560]{1,0:T(8,128)(2,1)S(1)}, u32[]{:S(2)}, u32[]{:S(2)}) collective-permute-start(bf16[32,2560]{1,0:T(8,128)(2,1)} %t0.1), channel_id=1, source_target_pairs={{0,1},{1,0},{2,3},{3,2},{4,5},{5,4},{6,7},{7,6},{8,9},{9,8},{10,11... | collective-permute-start | bytes 491528 | tf_op jit(solution)/shard_map/ppermute | solution.py:46
  6.7 4.1 %copy.11 = bf16[320,8,2,640]{3,1,2,0:T(8,128)(2,1)S(1)} copy(bf16[320,8,2,640]{3,2,1,0:T(2,128)(2,1)} %bitcast.12) | data formatting | bytes 13107200
  11.1 1.7 %collective-permute-done.2.b.t2 = bf16[32,2560]{1,0:T(8,128)(2,1)S(1)} collective-permute-done((bf16[32,2560]{1,0:T(8,128)(2,1)}, bf16[32,2560]{1,0:T(8,128)(2,1)S(1)}, u32[]{:S(2)}, u32[]{:S(2)}) %collective-permute-start.2) | collective-permute-done | bytes 163872 | tf_op jit(solution)/shard_map/ppermute | solution.py:46
  13.6 0.9 %shard_map.100.part_zero = bf16[96,896]{1,0:T(8,128)(2,1)S(1)} custom-call(bf16[32,2560]{1,0:T(8,128)(2,1)S(1)} %copy-done.2, bf16[32,2560]{1,0:T(8,128)(2,1)S(1)} %collective-permute-done.4.b.t3, bf16[32,2560]{1,0:T(8,128)(2,1)S(1)} %collective-permute-done.5.c.o0, bf16[2560,1280]{1,0:T(8,128)(2,1)S(1)} %bitcast.5, bf16[2560,256]{1,0:T(8,128)(2,1)S(1)} %copy-done.1), custom_call_target="tpu_custom_call" | custom-call | flops 503316480 | bytes 1006632 | tf_op jit(solution)/shard_map/pallas_call | solution.py:34
  14.5 0.9 %shard_map.101.part = bf16[96,896]{1,0:T(8,128)(2,1)S(1)} custom-call(bf16[32,2560]{1,0:T(8,128)(2,1)S(1)} %collective-permute-done.a.t1, bf16[32,2560]{1,0:T(8,128)(2,1)S(1)} %collective-permute-done.2.b.t2, bf16[32,2560]{1,0:T(8,128)(2,1)S(1)} %collective-permute-done.6.c.o3, bf16[2560,1280]{1,0:T(8,128)(2,1)S(1)} %bitcast.6, bf16[2560,256]{1,0:T(8,128)(2,1)S(1)} %copy-done.1), custom_call_target="tpu_custom_call" | custom-call | flops 503316480 | bytes 1006632 | tf_op jit(solution)/shard_map/pallas_call | solution.py:34
  17.0 2.0 %shard_map.104 = (bf16[256,2560]{1,0:T(8,128)(2,1)S(1)}, bf16[256,640]{1,0:T(8,128)(2,1)S(1)}, bf16[256,128]{1,0:T(8,128)(2,1)S(1)}, bf16[256,128]{1,0:T(8,128)(...) custom-call(bf16[256,896]{1,0:T(8,128)(2,1)S(1)} %get-tuple-element., ...), custom_call_target="tpu_custom_call" | custom-call | flops 41943040 | bytes 83886 | tf_op jit(solution)/shard_map/pallas_call | solution.py:34
  19.1 5.6 %collective-permute-done.7.tail = bf16[8,896]{1,0:T(8,128)(2,1)S(1)} collective-permute-done((bf16[8,896]{1,0:T(8,128)(2,1)S(1)}, bf16[8,896]{1,0:T(8,128)(2,1)S(1)}, u32[]{:S(2)}, u32[]{:S(2)}) %collective-permute-start.7) | collective-permute-done | bytes 14368 | tf_op jit(solution)/shard_map/ppermute | solution.py:416
  25.2 3.1 %collective-permute-start.10 = (bf16[168,128]{1,0:T(8,128)(2,1)S(1)}, bf16[168,128]{1,0:T(8,128)(2,1)S(1)}, u32[]{:S(2)}, u32[]{:S(2)}) collective-permute-start(bf16[168,128]{1,0:T(8,128)(2,1)S(1)} %get-tuple-element.51), channel_id=1, source_target_pairs={{0,24},{8,16},{16,8},{24,0},{1,25},{9,17},{17,9},{25,1},{2,26},{10... | collective-permute-start | bytes 129032 | tf_op jit(solution)/shard_map/ppermute | solution.py:46
  28.3 1.2 %shard_map.107.before_too.gate = f32[256,640]{1,0:T(8,128)S(1)} custom-call(bf16[256,2560]{1,0:T(8,128)(2,1)S(1)} %get-tuple-element.61.tokens, bf16[2560,1280]{1,0:T(8,128)(2,1)S(1)} %bitcast.8, bf16[8,640]{1,0:T(8,128)(2,1)S(1)} %get-tuple-element.55.v_first.before), custom_call_target="tpu_custom_call" | custom-call | flops 838860800 | bytes 1677721 | tf_op jit(solution)/shard_map/pallas_call | solution.py:34
  29.5 1.0 %shard_map.106 = (f32[256,640]{1,0:T(8,128)S(1)}, bf16[256,128]{1,0:T(8,128)(2,1)S(1)}) custom-call(bf16[256,640]{1,0:T(8,128)(2,1)S(1)} %get-tuple-element.52.v, bf16[256,128]{1,0:T(8,128)(2,1)S(1)} %get-tuple-element.53.b, bf16[256,128]{1,0:T(8,128)(2,1)S(1)} %get-tuple-element.54.c, bf16[8,640]{1,0:T(8,128)(2,1)S(1)} %get-tuple-element.55.v_first.before, ...), custom_call_target="tpu_custom_call" | custom-call | flops 335544320 | bytes 671088 | tf_op jit(solution)/shard_map/pallas_call | solution.py:34
  31.4 2.3 %collective-permute-done.11.other = bf16[168,128]{1,0:T(8,128)(2,1)S(1)} collective-permute-done((bf16[168,128]{1,0:T(8,128)(2,1)S(1)}, bf16[168,128]{1,0:T(8,128)(2,1)S(1)}, u32[]{:S(2)}, u32[]{:S(2)}) %collective-permute-start.11) | collective-permute-done | bytes 43040 | tf_op jit(solution)/shard_map/ppermute | solution.py:46
  34.6 3.2 %collective-permute-done.12.previous = bf16[168,128]{1,0:T(8,128)(2,1)S(1)} collective-permute-done((bf16[168,128]{1,0:T(8,128)(2,1)S(1)}, bf16[168,128]{1,0:T(8,128)(2,1)S(1)}, u32[]{:S(2)}, u32[]{:S(2)}) %collective-permute-start.12) | collective-permute-done | bytes 43040 | tf_op jit(solution)/shard_map/ppermute | solution.py:46
  38.0 1.3 %collective-permute-start.13 = (bf16[168,128]{1,0:T(8,128)(2,1)S(1)}, bf16[168,128]{1,0:T(8,128)(2,1)S(1)}, u32[]{:S(2)}, u32[]{:S(2)}) collective-permute-start(bf16[168,128]{1,0:T(8,128)(2,1)S(1)} %shard_map.111), channel_id=1, source_target_pairs={{0,224},{32,192},{64,160},{96,128},{128,96},{160,64},{192,32},{224... | collective-permute-start | bytes 129032 | tf_op jit(solution)/shard_map/ppermute | solution.py:46
  39.2 2.9 %collective-permute-done.13.quad = bf16[168,128]{1,0:T(8,128)(2,1)S(1)} collective-permute-done((bf16[168,128]{1,0:T(8,128)(2,1)S(1)}, bf16[168,128]{1,0:T(8,128)(2,1)S(1)}, u32[]{:S(2)}, u32[]{:S(2)}) %collective-permute-start.13) | collective-permute-done | bytes 43040 | tf_op jit(solution)/shard_map/ppermute | solution.py:46
  43.0 2.0 %collective-permute-start.15 = (bf16[32,640]{1,0:T(8,128)(2,1)S(1)}, bf16[32,640]{1,0:T(8,128)(2,1)S(1)}, u32[]{:S(2)}, u32[]{:S(2)}) collective-permute-start(bf16[32,640]{1,0:T(8,128)(2,1)S(1)} %get-tuple-element.66), channel_id=1, source_target_pairs={{0,8},{8,0},{16,24},{24,16},{1,9},{9,1},{17,25},{25,17},{2,10},{10... | collective-permute-start | bytes 122888 | tf_op jit(solution)/shard_map/ppermute | solution.py:46
  45.7 1.1 %collective-permute-done.14.e1 = bf16[32,640]{1,0:T(8,128)(2,1)S(1)} collective-permute-done((bf16[32,640]{1,0:T(8,128)(2,1)S(1)}, bf16[32,640]{1,0:T(8,128)(2,1)S(1)}, u32[]{:S(2)}, u32[]{:S(2)}) %collective-permute-start.14) | collective-permute-done | bytes 40992 | tf_op jit(solution)/shard_map/ppermute | solution.py:46
  46.9 2.2 %collective-permute-done.16.e3 = bf16[32,640]{1,0:T(8,128)(2,1)S(1)} collective-permute-done((bf16[32,640]{1,0:T(8,128)(2,1)S(1)}, bf16[32,640]{1,0:T(8,128)(2,1)S(1)}, u32[]{:S(2)}, u32[]{:S(2)}) %collective-permute-start.16) | collective-permute-done | bytes 40992 | tf_op jit(solution)/shard_map/ppermute | solution.py:46
  50.7 7.9 %collective-permute-start.18 = (bf16[96,2688]{1,0:T(8,128)(2,1)S(1)}, bf16[96,2688]{1,0:T(8,128)(2,1)S(1)}, u32[]{:S(2)}, u32[]{:S(2)}) collective-permute-start(bf16[96,2688]{1,0:T(8,128)(2,1)S(1)} %shard_map.116), channel_id=1, source_target_pairs={{0,1},{1,0},{2,3},{3,2},{4,5},{5,4},{6,7},{7,6},{8,9},{9,8},{10,11... | collective-permute-start | bytes 1548296 | tf_op jit(solution)/shard_map/ppermute | solution.py:46
  58.7 1.7 %collective-permute-done.17.came = bf16[32,2688]{1,0:T(8,128)(2,1)S(1)} collective-permute-done((bf16[32,2688]{1,0:T(8,128)(2,1)S(1)}, bf16[32,2688]{1,0:T(8,128)(2,1)S(1)}, u32[]{:S(2)}, u32[]{:S(2)}) %collective-permute-start.17) | collective-permute-done | bytes 172064 | tf_op jit(solution)/shard_map/ppermute | solution.py:46
  60.5 2.7 %collective-permute-start.19 = (bf16[32,2688]{1,0:T(8,128)(2,1)S(1)}, bf16[32,2688]{1,0:T(8,128)(2,1)S(1)}, u32[]{:S(2)}, u32[]{:S(2)}) collective-permute-start(bf16[32,2688]{1,0:T(8,128)(2,1)S(1)} %shard_map.114.before), channel_id=1, source_target_pairs={{0,4},{2,6},{4,0},{6,2},{1,5},{3,7},{5,1},{7,3},{8,12},{10,14},{12... | collective-permute-start | bytes 516104 | tf_op jit(solution)/shard_map/ppermute | solution.py:46
  64.2 1.2 %collective-permute-start.20 = (bf16[32,2688]{1,0:T(8,128)(2,1)S(1)}, bf16[32,2688]{1,0:T(8,128)(2,1)S(1)}, u32[]{:S(2)}, u32[]{:S(2)}) collective-permute-start(bf16[32,2688]{1,0:T(8,128)(2,1)S(1)} %get-tuple-element.75), channel_id=1, source_target_pairs={{0,2},{2,0},{4,6},{6,4},{1,3},{3,1},{5,7},{7,5},{8,10},{10,8},{12,... | collective-permute-start | bytes 516104 | tf_op jit(solution)/shard_map/ppermute | solution.py:46
  65.6 2.0 %collective-permute-done.19.g1 = bf16[32,2688]{1,0:T(8,128)(2,1)S(1)} collective-permute-done((bf16[32,2688]{1,0:T(8,128)(2,1)S(1)}, bf16[32,2688]{1,0:T(8,128)(2,1)S(1)}, u32[]{:S(2)}, u32[]{:S(2)}) %collective-permute-start.19) | collective-permute-done | bytes 172064 | tf_op jit(solution)/shard_map/ppermute | solution.py:46
  67.6 4.5 %collective-permute-done.20.g2 = bf16[32,2688]{1,0:T(8,128)(2,1)S(1)} collective-permute-done((bf16[32,2688]{1,0:T(8,128)(2,1)S(1)}, bf16[32,2688]{1,0:T(8,128)(2,1)S(1)}, u32[]{:S(2)}, u32[]{:S(2)}) %collective-permute-start.20) | collective-permute-done | bytes 172064 | tf_op jit(solution)/shard_map/ppermute | solution.py:46
  (60 shorter events, 11.2 us)
Async XLA Ops:
  0.0 10.8 %collective-permute-start.4 = (bf16[32,2560]{1,0:T(8,128)(2,1)}, bf16[32,2560]{1,0:T(8,128)(2,1)S(1)}, u32[]{:S(2)}, u32[]{:S(2)}) collective-permute-start(bf16[32,2560]{1,0:T(8,128)(2,1)} %t0.1), channel_id=1, source_target_pairs={{0,4},{2,6},{4,0},{6,2},{1,5},{3,7},{5,1},{7,3},{8,12},{10,14},{12... | collective-permute-start | bytes 491528 | tf_op jit(solution)/shard_map/ppermute | solution.py:46
  3.7 9.0 %collective-permute-start.2 = (bf16[32,2560]{1,0:T(8,128)(2,1)}, bf16[32,2560]{1,0:T(8,128)(2,1)S(1)}, u32[]{:S(2)}, u32[]{:S(2)}) collective-permute-start(bf16[32,2560]{1,0:T(8,128)(2,1)} %t0.1), channel_id=1, source_target_pairs={{0,6},{2,4},{4,2},{6,0},{1,7},{3,5},{5,3},{7,1},{8,14},{10,12},{12... | collective-permute-start | bytes 491528 | tf_op jit(solution)/shard_map/ppermute | solution.py:46
  4.5 9.0 %collective-permute-start = (bf16[32,2560]{1,0:T(8,128)(2,1)}, bf16[32,2560]{1,0:T(8,128)(2,1)S(1)}, u32[]{:S(2)}, u32[]{:S(2)}) collective-permute-start(bf16[32,2560]{1,0:T(8,128)(2,1)} %t0.1), channel_id=1, source_target_pairs={{0,2},{2,0},{4,6},{6,4},{1,3},{3,1},{5,7},{7,5},{8,10},{10,8},{12,... | collective-permute-start | bytes 491528 | tf_op jit(solution)/shard_map/ppermute | solution.py:46
  4.5 9.1 %collective-permute-start.5 = (bf16[32,2560]{1,0:T(8,128)(2,1)}, bf16[32,2560]{1,0:T(8,128)(2,1)S(1)}, u32[]{:S(2)}, u32[]{:S(2)}) collective-permute-start(bf16[32,2560]{1,0:T(8,128)(2,1)} %t0.1), channel_id=1, source_target_pairs={{0,1},{1,0},{2,3},{3,2},{4,5},{5,4},{6,7},{7,6},{8,9},{9,8},{10,11... | collective-permute-start | bytes 491528 | tf_op jit(solution)/shard_map/ppermute | solution.py:46
  6.7 6.9 %copy-start.2 = (bf16[32,2560]{1,0:T(8,128)(2,1)S(1)}, bf16[32,2560]{1,0:T(8,128)(2,1)}, u32[]{:S(2)}) copy-start(bf16[32,2560]{1,0:T(8,128)(2,1)} %t0.1) | copy-start | bytes 491524
  10.8 3.7 %collective-permute-start.6 = (bf16[32,2560]{1,0:T(8,128)(2,1)S(1)}, bf16[32,2560]{1,0:T(8,128)(2,1)S(1)}, u32[]{:S(2)}, u32[]{:S(2)}) collective-permute-start(bf16[32,2560]{1,0:T(8,128)(2,1)S(1)} %collective-permute-done.4.b.t3), channel_id=1, source_target_pairs={{0,1},{1,0},{2,3},{3,2},{4,5},{5,4},{6,7},{7,6},{8,9},{9,8},{10,11... | collective-permute-start | bytes 491528 | tf_op jit(solution)/shard_map/ppermute | solution.py:46
  12.8 2.6 %collective-permute-start.3 = (bf16[32,2560]{1,0:T(8,128)(2,1)S(1)}, bf16[32,2560]{1,0:T(8,128)(2,1)S(1)}, u32[]{:S(2)}, u32[]{:S(2)}) collective-permute-start(bf16[32,2560]{1,0:T(8,128)(2,1)S(1)} %collective-permute-done.2.b.t2), channel_id=1, source_target_pairs={{0,1},{1,0},{2,3},{3,2},{4,5},{5,4},{6,7},{7,6},{8,9},{9,8},{10,11... | collective-permute-start | bytes 491528 | tf_op jit(solution)/shard_map/ppermute | solution.py:46
  13.5 1.9 %collective-permute-start.1 = (bf16[32,2560]{1,0:T(8,128)(2,1)S(1)}, bf16[32,2560]{1,0:T(8,128)(2,1)S(1)}, u32[]{:S(2)}, u32[]{:S(2)}) collective-permute-start(bf16[32,2560]{1,0:T(8,128)(2,1)S(1)} %collective-permute-done.a.t1), channel_id=1, source_target_pairs={{0,1},{1,0},{2,3},{3,2},{4,5},{5,4},{6,7},{7,6},{8,9},{9,8},{10,11... | collective-permute-start | bytes 491528 | tf_op jit(solution)/shard_map/ppermute | solution.py:46
  16.3 8.4 %collective-permute-start.7 = (bf16[8,896]{1,0:T(8,128)(2,1)S(1)}, bf16[8,896]{1,0:T(8,128)(2,1)S(1)}, u32[]{:S(2)}, u32[]{:S(2)}) collective-permute-start(bf16[8,896]{1,0:T(8,128)(2,1)S(1)} %get-tuple-element.43), channel_id=1, source_target_pairs={{0,8},{8,16},{16,24},{24,32},{32,40},{40,48},{48,56},{56,64},{64,7... | collective-permute-start | bytes 43016 | tf_op jit(solution)/shard_map/ppermute | solution.py:416
  25.0 5.6 %collective-permute-start.8 = (bf16[168,128]{1,0:T(8,128)(2,1)S(1)}, bf16[168,128]{1,0:T(8,128)(2,1)S(1)}, u32[]{:S(2)}, u32[]{:S(2)}) collective-permute-start(bf16[168,128]{1,0:T(8,128)(2,1)S(1)} %get-tuple-element.49), channel_id=1, source_target_pairs={{0,16},{8,24},{16,0},{24,8},{1,17},{9,25},{17,1},{25,9},{2,18},{10... | collective-permute-start | bytes 129032 | tf_op jit(solution)/shard_map/ppermute | solution.py:46
  25.1 5.5 %collective-permute-start.9 = (bf16[168,128]{1,0:T(8,128)(2,1)S(1)}, bf16[168,128]{1,0:T(8,128)(2,1)S(1)}, u32[]{:S(2)}, u32[]{:S(2)}) collective-permute-start(bf16[168,128]{1,0:T(8,128)(2,1)S(1)} %get-tuple-element.50), channel_id=1, source_target_pairs={{0,8},{8,0},{16,24},{24,16},{1,9},{9,1},{17,25},{25,17},{2,10},{10... | collective-permute-start | bytes 129032 | tf_op jit(solution)/shard_map/ppermute | solution.py:46
  25.2 5.4 %collective-permute-start.10 = (bf16[168,128]{1,0:T(8,128)(2,1)S(1)}, bf16[168,128]{1,0:T(8,128)(2,1)S(1)}, u32[]{:S(2)}, u32[]{:S(2)}) collective-permute-start(bf16[168,128]{1,0:T(8,128)(2,1)S(1)} %get-tuple-element.51), channel_id=1, source_target_pairs={{0,24},{8,16},{16,8},{24,0},{1,25},{9,17},{17,9},{25,1},{2,26},{10... | collective-permute-start | bytes 129032 | tf_op jit(solution)/shard_map/ppermute | solution.py:46
  29.5 19.5 %copy-start = (bf16[640,2560]{1,0:T(8,128)(2,1)S(1)}, bf16[640,2560]{1,0:T(8,128)(2,1)}, u32[]{:S(2)}) copy-start(bf16[640,2560]{1,0:T(8,128)(2,1)} %w.5) | copy-start | bytes 9830404
  30.7 3.0 %collective-permute-start.11 = (bf16[168,128]{1,0:T(8,128)(2,1)S(1)}, bf16[168,128]{1,0:T(8,128)(2,1)S(1)}, u32[]{:S(2)}, u32[]{:S(2)}) collective-permute-start(bf16[168,128]{1,0:T(8,128)(2,1)S(1)} %shard_map.108.row), channel_id=1, source_target_pairs={{0,32},{32,0},{64,96},{96,64},{128,160},{160,128},{192,224},{224,1... | collective-permute-start | bytes 129032 | tf_op jit(solution)/shard_map/ppermute | solution.py:46
  33.8 4.0 %collective-permute-start.12 = (bf16[168,128]{1,0:T(8,128)(2,1)S(1)}, bf16[168,128]{1,0:T(8,128)(2,1)S(1)}, u32[]{:S(2)}, u32[]{:S(2)}) collective-permute-start(bf16[168,128]{1,0:T(8,128)(2,1)S(1)} %shard_map.110), channel_id=1, source_target_pairs={{0,64},{32,96},{64,0},{96,32},{128,192},{160,224},{192,128},{224,1... | collective-permute-start | bytes 129032 | tf_op jit(solution)/shard_map/ppermute | solution.py:46
  38.0 4.2 %collective-permute-start.13 = (bf16[168,128]{1,0:T(8,128)(2,1)S(1)}, bf16[168,128]{1,0:T(8,128)(2,1)S(1)}, u32[]{:S(2)}, u32[]{:S(2)}) collective-permute-start(bf16[168,128]{1,0:T(8,128)(2,1)S(1)} %shard_map.111), channel_id=1, source_target_pairs={{0,224},{32,192},{64,160},{96,128},{128,96},{160,64},{192,32},{224... | collective-permute-start | bytes 129032 | tf_op jit(solution)/shard_map/ppermute | solution.py:46
  42.4 4.4 %collective-permute-start.14 = (bf16[32,640]{1,0:T(8,128)(2,1)S(1)}, bf16[32,640]{1,0:T(8,128)(2,1)S(1)}, u32[]{:S(2)}, u32[]{:S(2)}) collective-permute-start(bf16[32,640]{1,0:T(8,128)(2,1)S(1)} %get-tuple-element.65), channel_id=1, source_target_pairs={{0,16},{8,24},{16,0},{24,8},{1,17},{9,25},{17,1},{25,9},{2,18},{10... | collective-permute-start | bytes 122888 | tf_op jit(solution)/shard_map/ppermute | solution.py:46
  43.0 3.9 %collective-permute-start.15 = (bf16[32,640]{1,0:T(8,128)(2,1)S(1)}, bf16[32,640]{1,0:T(8,128)(2,1)S(1)}, u32[]{:S(2)}, u32[]{:S(2)}) collective-permute-start(bf16[32,640]{1,0:T(8,128)(2,1)S(1)} %get-tuple-element.66), channel_id=1, source_target_pairs={{0,8},{8,0},{16,24},{24,16},{1,9},{9,1},{17,25},{25,17},{2,10},{10... | collective-permute-start | bytes 122888 | tf_op jit(solution)/shard_map/ppermute | solution.py:46
  45.0 4.1 %collective-permute-start.16 = (bf16[32,640]{1,0:T(8,128)(2,1)S(1)}, bf16[32,640]{1,0:T(8,128)(2,1)S(1)}, u32[]{:S(2)}, u32[]{:S(2)}) collective-permute-start(bf16[32,640]{1,0:T(8,128)(2,1)S(1)} %get-tuple-element.67), channel_id=1, source_target_pairs={{0,24},{8,16},{16,8},{24,0},{1,25},{9,17},{17,9},{25,1},{2,26},{10... | collective-permute-start | bytes 122888 | tf_op jit(solution)/shard_map/ppermute | solution.py:46
  50.7 13.3 %collective-permute-start.18 = (bf16[96,2688]{1,0:T(8,128)(2,1)S(1)}, bf16[96,2688]{1,0:T(8,128)(2,1)S(1)}, u32[]{:S(2)}, u32[]{:S(2)}) collective-permute-start(bf16[96,2688]{1,0:T(8,128)(2,1)S(1)} %shard_map.116), channel_id=1, source_target_pairs={{0,1},{1,0},{2,3},{3,2},{4,5},{5,4},{6,7},{7,6},{8,9},{9,8},{10,11... | collective-permute-start | bytes 1548296 | tf_op jit(solution)/shard_map/ppermute | solution.py:46
  58.6 1.8 %collective-permute-start.17 = (bf16[32,2688]{1,0:T(8,128)(2,1)S(1)}, bf16[32,2688]{1,0:T(8,128)(2,1)S(1)}, u32[]{:S(2)}, u32[]{:S(2)}) collective-permute-start(bf16[32,2688]{1,0:T(8,128)(2,1)S(1)} %get-tuple-element.73), channel_id=1, source_target_pairs={{0,1},{1,0},{2,3},{3,2},{4,5},{5,4},{6,7},{7,6},{8,9},{9,8},{10,11... | collective-permute-start | bytes 516104 | tf_op jit(solution)/shard_map/ppermute | solution.py:46
  60.5 7.1 %collective-permute-start.19 = (bf16[32,2688]{1,0:T(8,128)(2,1)S(1)}, bf16[32,2688]{1,0:T(8,128)(2,1)S(1)}, u32[]{:S(2)}, u32[]{:S(2)}) collective-permute-start(bf16[32,2688]{1,0:T(8,128)(2,1)S(1)} %shard_map.114.before), channel_id=1, source_target_pairs={{0,4},{2,6},{4,0},{6,2},{1,5},{3,7},{5,1},{7,3},{8,12},{10,14},{12... | collective-permute-start | bytes 516104 | tf_op jit(solution)/shard_map/ppermute | solution.py:46
  64.2 8.0 %collective-permute-start.20 = (bf16[32,2688]{1,0:T(8,128)(2,1)S(1)}, bf16[32,2688]{1,0:T(8,128)(2,1)S(1)}, u32[]{:S(2)}, u32[]{:S(2)}) collective-permute-start(bf16[32,2688]{1,0:T(8,128)(2,1)S(1)} %get-tuple-element.75), channel_id=1, source_target_pairs={{0,2},{2,0},{4,6},{6,4},{1,3},{3,1},{5,7},{7,5},{8,10},{10,8},{12,... | collective-permute-start | bytes 516104 | tf_op jit(solution)/shard_map/ppermute | solution.py:46
  65.4 6.7 %collective-permute-start.21 = (bf16[32,2688]{1,0:T(8,128)(2,1)S(1)}, bf16[32,2688]{1,0:T(8,128)(2,1)S(1)}, u32[]{:S(2)}, u32[]{:S(2)}) collective-permute-start(bf16[32,2688]{1,0:T(8,128)(2,1)S(1)} %get-tuple-element.76), channel_id=1, source_target_pairs={{0,6},{2,4},{4,2},{6,0},{1,7},{3,5},{5,3},{7,1},{8,14},{10,12},{12... | collective-permute-start | bytes 516104 | tf_op jit(solution)/shard_map/ppermute | solution.py:46
  (7 other events, 22.0 us)
